TPU v7x, 32 devices: a whole 2x2x4 slice. The times are simulated.
32 devices in a mesh: grp: 8 (over z, core), sub: 4 (over y, x).
Axes of the slice: x: 2, y: 2, z: 4, core: 2. Of those that a mesh axis runs over, the one named last changes fastest.
Arguments:
- coarse_op: float32 [256, 64, 576], P(('grp', 'sub'))
- right_side: float32 [256, 64, 64], P(('grp', 'sub')), may hold values from -6 to 6
- owner_map: int32 [256], replicated, may hold values from 0 to 255, as said below
- neighbor_table: int32 [256, 8], replicated, may hold values from 0 to 255, as said below
Outputs:
- solution: float32 [256, 64, 64], P(('grp', 'sub'))
Inputs may be any that keep to these rules, and one draw needn't show every extreme that they name: `owner_map`: a permutation of 0 .. 255. `neighbor_table`: row t lists the neighbours of coarse site t on a periodic 4^4 lattice in the order +x, -x, +y, -y, +z, -z, +t, -t; lattice positions carry the site numbers in a permuted order.
All inputs are finite; a program needn't handle non-finite values.
Results may differ from a plain program's by a relative error of at most 0.0001.
Values sent between devices are 32-bit elements; how exact they have to be, the bound alone decides.
No kernel may reach another device: no remote copies, remote signals or barrier semaphores. Data moves between devices by JAX's collectives and lax.ppermute only.
A program may use at most 64 MiB of HBM per device.

v0:
```python
import jax
import jax.numpy as jnp
from jax import lax
from jax.sharding import PartitionSpec as P

ITERS = 3


def inner_product(first, second):
    return jnp.sum(first * second, axis=(0, 1))


def per_device(coarse_op, right_side, owner_map, neighbor_table):
    n_sub = lax.axis_size("sub")
    n_grp = lax.axis_size("grp")
    per_dev = coarse_op.shape[0]
    dof_count = coarse_op.shape[1]
    site_count = owner_map.shape[0]
    site_ids = jnp.arange(site_count, dtype=jnp.int32)
    inverse = jnp.sum(
        jnp.where(owner_map[None, :] == site_ids[:, None], site_ids[None, :], 0), axis=1
    )
    link = inverse[neighbor_table[owner_map]]
    op_rows = lax.all_gather(coarse_op, "grp", axis=0, tiled=True)
    rhs_rows = lax.all_to_all(right_side, "grp", split_axis=2, concat_axis=0, tiled=True)

    def reduce_sum(values):
        return lax.psum(values, "sub")

    row_count = op_rows.shape[0]
    local_rows = jnp.arange(row_count, dtype=jnp.int32)
    own_slots = (
        local_rows // per_dev * n_sub + lax.axis_index("sub")
    ) * per_dev + local_rows % per_dev
    target = link[own_slots]
    target_block = target // per_dev
    position = (target_block % n_sub * n_grp + target_block // n_sub) * per_dev + target % per_dev
    rhs_count = rhs_rows.shape[2]
    beta = jnp.sqrt(reduce_sum(inner_product(rhs_rows, rhs_rows)))
    krylov = [rhs_rows / beta]
    hess = jnp.zeros((ITERS + 1, ITERS, rhs_count), jnp.float32)
    for column in range(ITERS):
        apply_vector = krylov[column]
        piece = lax.all_gather(apply_vector, "sub", axis=0, tiled=True)
        count = piece.shape[0]
        select = (position[:, :, None] == jnp.arange(count, dtype=jnp.int32)[None, None, :]).astype(
            jnp.float32
        )
        nearby = jnp.einsum("lkr,rab->lkab", select, piece, precision=lax.Precision.HIGHEST)
        stacked = jnp.concatenate([apply_vector[:, None], nearby], axis=1).reshape(
            row_count, 9 * dof_count, rhs_count
        )
        image = jnp.einsum("sac,scr->sar", op_rows, stacked, precision=lax.Precision.HIGHEST)
        for index_i in range(column + 1):
            coeff = reduce_sum(inner_product(krylov[index_i], image))
            image = image - coeff * krylov[index_i]
            hess = hess.at[index_i, column].set(coeff)
        norm_sq = reduce_sum(inner_product(image, image))
        norm_value = jnp.sqrt(norm_sq)
        hess = hess.at[column + 1, column].set(norm_value)
        krylov.append(image / norm_value)
    gram_matrix = jnp.einsum("ijr,ikr->rjk", hess, hess, precision=lax.Precision.HIGHEST)
    projected = (beta[None, :] * hess[0]).T
    factor = jnp.linalg.cholesky(gram_matrix)
    halfway = jax.scipy.linalg.solve_triangular(factor, projected[..., None], lower=True)
    weights = jax.scipy.linalg.solve_triangular(factor, halfway, lower=True, trans=1)[..., 0]
    solution = jnp.zeros_like(rhs_rows)
    for column in range(ITERS):
        solution = solution + weights[:, column][None, None, :] * krylov[column]
    return lax.all_to_all(solution, "grp", split_axis=0, concat_axis=2, tiled=True)


def solution(mesh):
    placed = (P(("grp", "sub"), None, None), P(("grp", "sub"), None, None), P(), P())
    return jax.shard_map(
        per_device,
        mesh=mesh,
        in_specs=placed,
        out_specs=P(("grp", "sub"), None, None),
        check_vma=False,
    )
```

profile of v0, /device:TPU:0, one launch (start us, length us, event | category | flops | bytes accessed | tf_op | source)
XLA Modules:
  0.0 307.9 jit_solution(5895258015328376698)
XLA Ops:
  9.2 6.4 %all-to-all-start = ((f32[8,1,4096]{2,1,0:T(1,128)}), f32[8,1,4096]{2,1,0:T(1,128)S(1)}, u32[]{:S(2)}, u32[]{:S(2)}) async-start(f32[8,1,4096]{2,1,0:T(1,128)} %reshape.534), calls=%async_computation | async-start | bytes 262144 | tf_op jit(solution)/shard_map/all_to_all | solution.py:25
  16.7 13.1 %gather_fusion.1 = s32[2048]{0:T(1024)S(1)} fusion(s32[256]{0:T(256)S(1)} %select_reduce_fusion, s32[2048]{0:T(1024)S(1)} %broadcast_clamp_fusion), kind=kCustom, calls=%fused_computation.1 | custom fusion | bytes 24576 | tf_op jit(solution)/shard_map/gather | solution.py:23
  32.4 9.9 %psum.70 = f32[8]{0:T(128)S(1)} all-reduce(f32[8]{0:T(128)S(1)} %fusion.13), channel_id=1, replica_groups=mesh['grp'=8,'sub'=4] {'sub'}, use_global_device_ids=true, to_apply=%region_1.2 | all-reduce | flops 8 | bytes 64 | tf_op jit(solution)/shard_map/psum | solution.py:28
  42.5 11.9 %all_gather.12 = f32[256,64,8]{1,0,2:T(8,128)S(1)} all-gather(f32[64,64,8]{1,0,2:T(8,128)S(1)} %bitcast_divide_fusion), channel_id=1, replica_groups=mesh['grp'=8,'sub'=4] {'sub'}, dimensions={0}, use_global_device_ids=true | all-gather | bytes 655360 | tf_op jit(solution)/shard_map/all_gather | solution.py:44
  55.8 2.9 pad_maximum_fusion
  58.7 4.3 %copy.148 = f32[64,9,64,8]{0,3,2,1:T(8,128)S(1)} copy(f32[64,9,64,8]{2,1,3,0:T(8,128)} %pad_maximum_fusion) | data formatting | bytes 2359296 | tf_op jit(solution)/shard_map/concatenate | solution.py:50
  63.0 2.0 copy.149
  65.0 46.1 %all-gather.2.cloned.1.call-done = f32[64,64,576]{2,1,0:T(8,128)} async-done(((f32[8,64,576]{2,1,0:T(8,128)}), f32[64,64,576]{2,1,0:T(8,128)}) %all-gather.2.cloned.1.call-update) | async-done | bytes 9437200 | tf_op jit(solution)/shard_map/all_gather | solution.py:24
  111.1 13.0 %fusion.38 = f32[64,8,64]{2,1,0:T(8,128)S(1)} fusion(f32[64,576,8]{1,2,0:T(8,128)} %copy.149, f32[64,64,576]{2,1,0:T(8,128)} %all-gather.2.cloned.1.call-done), kind=kOutput, calls=%fused_computation.107 | convolution fusion | flops 226492416 | bytes 10747904 | tf_op jit(solution)/shard_map/sac,scr->sar/dot_general | solution.py:53
  124.3 9.8 %psum.71 = f32[8]{0:T(128)S(1)} all-reduce(f32[8]{0:T(128)S(1)} %fusion.12), channel_id=1, replica_groups=mesh['grp'=8,'sub'=4] {'sub'}, use_global_device_ids=true, to_apply=%region_4.5 | all-reduce | flops 8 | bytes 64 | tf_op jit(solution)/shard_map/psum | solution.py:28
  134.4 8.0 %psum.72 = f32[8]{0:T(128)S(1)} all-reduce(f32[8]{0:T(128)S(1)} %multiply_reduce_fusion.5), channel_id=1, replica_groups=mesh['grp'=8,'sub'=4] {'sub'}, use_global_device_ids=true, to_apply=%region_6.7 | all-reduce | flops 8 | bytes 64 | tf_op jit(solution)/shard_map/psum | solution.py:28
  142.5 13.0 %all_gather.14 = f32[256,64,8]{1,0,2:T(8,128)S(1)} all-gather(f32[64,64,8]{1,0,2:T(8,128)S(1)} %broadcast_divide_fusion.2), channel_id=1, replica_groups=mesh['grp'=8,'sub'=4] {'sub'}, dimensions={0}, use_global_device_ids=true | all-gather | bytes 655360 | tf_op jit(solution)/shard_map/all_gather | solution.py:44
  156.9 2.8 pad_maximum_fusion.1
  159.7 4.3 %copy.152 = f32[64,9,64,8]{0,3,2,1:T(8,128)S(1)} copy(f32[64,9,64,8]{2,1,3,0:T(8,128)} %pad_maximum_fusion.1) | data formatting | bytes 2359296 | tf_op jit(solution)/shard_map/concatenate | solution.py:50
  164.1 2.0 copy.153
  166.1 13.0 %fusion.39 = f32[64,8,64]{2,1,0:T(8,128)S(1)} fusion(f32[64,576,8]{1,2,0:T(8,128)} %copy.153, f32[64,64,576]{2,1,0:T(8,128)} %all-gather.2.cloned.1.call-done), kind=kOutput, calls=%fused_computation.108 | convolution fusion | flops 226492416 | bytes 10747904 | tf_op jit(solution)/shard_map/sac,scr->sar/dot_general | solution.py:53
  180.0 8.9 %psum.73 = f32[8]{0:T(128)S(1)} all-reduce(f32[8]{0:T(128)S(1)} %fusion.11), channel_id=1, replica_groups=mesh['grp'=8,'sub'=4] {'sub'}, use_global_device_ids=true, to_apply=%region_8.9 | all-reduce | flops 8 | bytes 64 | tf_op jit(solution)/shard_map/psum | solution.py:28
  189.2 8.7 %psum.74 = f32[8]{0:T(128)S(1)} all-reduce(f32[8]{0:T(128)S(1)} %get-tuple-element.115), channel_id=1, replica_groups=mesh['grp'=8,'sub'=4] {'sub'}, use_global_device_ids=true, to_apply=%region_10.11 | all-reduce | flops 8 | bytes 64 | tf_op jit(solution)/shard_map/psum | solution.py:28
  198.8 9.0 %psum.75 = f32[8]{0:T(128)S(1)} all-reduce(f32[8]{0:T(128)S(1)} %multiply_reduce_fusion.3), channel_id=1, replica_groups=mesh['grp'=8,'sub'=4] {'sub'}, use_global_device_ids=true, to_apply=%region_12.13 | all-reduce | flops 8 | bytes 64 | tf_op jit(solution)/shard_map/psum | solution.py:28
  207.9 11.6 %all_gather.15 = f32[256,64,8]{1,0,2:T(8,128)S(1)} all-gather(f32[64,64,8]{1,0,2:T(8,128)S(1)} %broadcast_divide_fusion.1), channel_id=1, replica_groups=mesh['grp'=8,'sub'=4] {'sub'}, dimensions={0}, use_global_device_ids=true | all-gather | bytes 655360 | tf_op jit(solution)/shard_map/all_gather | solution.py:44
  220.9 2.8 pad_maximum_fusion.2
  223.7 4.3 %copy.156 = f32[64,9,64,8]{0,3,2,1:T(8,128)S(1)} copy(f32[64,9,64,8]{2,1,3,0:T(8,128)} %pad_maximum_fusion.2) | data formatting | bytes 2359296 | tf_op jit(solution)/shard_map/concatenate | solution.py:50
  228.0 2.0 copy.157
  230.0 13.0 %fusion.40 = f32[64,8,64]{2,1,0:T(8,128)S(1)} fusion(f32[64,576,8]{1,2,0:T(8,128)} %copy.157, f32[64,64,576]{2,1,0:T(8,128)} %all-gather.2.cloned.1.call-done), kind=kOutput, calls=%fused_computation.109 | convolution fusion | flops 226492416 | bytes 10747904 | tf_op jit(solution)/shard_map/sac,scr->sar/dot_general | solution.py:53
  243.9 8.9 %psum.76 = f32[8]{0:T(128)S(1)} all-reduce(f32[8]{0:T(128)S(1)} %fusion.10), channel_id=1, replica_groups=mesh['grp'=8,'sub'=4] {'sub'}, use_global_device_ids=true, to_apply=%region_15.16 | all-reduce | flops 8 | bytes 64 | tf_op jit(solution)/shard_map/psum | solution.py:28
  253.0 8.7 %psum.77 = f32[8]{0:T(128)S(1)} all-reduce(f32[8]{0:T(128)S(1)} %get-tuple-element.113), channel_id=1, replica_groups=mesh['grp'=8,'sub'=4] {'sub'}, use_global_device_ids=true, to_apply=%region_17.18 | all-reduce | flops 8 | bytes 64 | tf_op jit(solution)/shard_map/psum | solution.py:28
  262.0 8.9 %psum.78 = f32[8]{0:T(128)S(1)} all-reduce(f32[8]{0:T(128)S(1)} %multiply_reduce_fusion.1), channel_id=1, replica_groups=mesh['grp'=8,'sub'=4] {'sub'}, use_global_device_ids=true, to_apply=%region_19.20 | all-reduce | flops 8 | bytes 64 | tf_op jit(solution)/shard_map/psum | solution.py:28
  271.1 8.1 %psum.79 = f32[8]{0:T(128)S(1)} all-reduce(f32[8]{0:T(128)S(1)} %multiply_reduce_fusion), channel_id=1, replica_groups=mesh['grp'=8,'sub'=4] {'sub'}, use_global_device_ids=true, to_apply=%region_21.22 | all-reduce | flops 8 | bytes 64 | tf_op jit(solution)/shard_map/psum | solution.py:28
  280.7 1.9 broadcast_select_fusion
  284.6 2.3 custom-call.11
  287.1 2.1 custom-call.12
  290.0 9.1 %all_to_all.39 = f32[8,1,4096]{2,1,0:T(1,128)S(1)} all-to-all(f32[8,1,4096]{2,1,0:T(1,128)S(1)} %reshape.536), channel_id=1, replica_groups=mesh['grp'=8,'sub'=4] {'grp'}, dimensions={0} | all-to-all | bytes 262144 | tf_op jit(solution)/shard_map/all_to_all | solution.py:70
  (88 shorter events, 21.3 us)
Async XLA Ops:
  6.5 9.0 %copy-start = (s32[256,8]{0,1:T(8,128)S(1)}, s32[256,8]{0,1:T(8,128)}, u32[]{:S(2)}) copy-start(s32[256,8]{0,1:T(8,128)} %param.25) | copy-start | bytes 24580
  6.5 9.2 %copy-start.1 = (s32[256]{0:T(256)S(1)}, s32[256]{0:T(256)}, u32[]{:S(2)}) copy-start(s32[256]{0:T(256)} %param.24) | copy-start | bytes 3076
  6.5 104.6 %all-gather.2.cloned.1.call-start = ((), (), s32[]{:S(2)}) async-start(), calls=%async_computation.2 | async-start | bytes 11796480 | tf_op jit(solution)/shard_map/all_gather | solution.py:24
  9.2 21.4 %all-to-all-start = ((f32[8,1,4096]{2,1,0:T(1,128)}), f32[8,1,4096]{2,1,0:T(1,128)S(1)}, u32[]{:S(2)}, u32[]{:S(2)}) async-start(f32[8,1,4096]{2,1,0:T(1,128)} %reshape.534), calls=%async_computation | async-start | bytes 262144 | tf_op jit(solution)/shard_map/all_to_all | solution.py:25
  166.1 13.2 %copy-start.2 = (s32[3]{0:T(128)S(1)}, s32[3]{0:T(128)}, u32[]{:S(2)}) copy-start(s32[3]{0:T(128)} %constant.393.clone.1) | copy-start | bytes 40
Sparse Core Ops, SparseCore 0:
  9.0 102.0 all-gather.1
where the time goes:
time: 309 us; the launch traced here: 308 us
  blocking collectives  135 us (44%)
  waiting for transfers between devices  46.8 us (15%)
  local copies, waits for them, and re-layouts  42.9 us (14%)
  matrix products  42.5 us (14%)
  other arithmetic  21.1 us (7%)
  between operations  13.7 us (4%)
  starting transfers between devices  6.36 us (2%)
    psum x10, blocking collectives, reduce_sum(): return lax.psum(values, 'sub')  89 us
    all_gather x1, waiting for transfers between devices, per_device(): op_rows = lax.all_gather(coarse_op, 'grp', axis=0, tiled=True)  46.1 us
    dot_general x3, matrix products, per_device(): jnp.einsum('sac,scr->sar', op_rows, stacked, precision=lax.Precision.HIGH...  38.9 us
    all_gather x3, blocking collectives, per_device(): piece = lax.all_gather(apply_vector, 'sub', axis=0, tiled=True)  36.5 us
    gather x3, local copies, waits for them, and re-layouts, per_device(): link = inverse[neighbor_table[owner_map]]  14 us
    concatenate x3, local copies, waits for them, and re-layouts, per_device(): jnp.concatenate([apply_vector[:, None], nearby], axis=1)  13 us
    all_to_all x1, blocking collectives, per_device(): lax.all_to_all(solution, 'grp', split_axis=0, concat_axis=2, tiled=True)  9.14 us
    concatenate x3, other arithmetic, per_device(): jnp.concatenate([apply_vector[:, None], nearby], axis=1)  8.55 us
  transfers between devices with their start and end apart: 2, of which 1 were waited for; matrix products, arithmetic and copies ran while one was open for 10% of the time, Pallas kernels for 0%

commit v1 on v0

v1 whole, which is shorter than its diff:
```python
import functools

import jax
import jax.numpy as jnp
from jax import lax
from jax.experimental import pallas as pl
from jax.experimental.pallas import tpu as pltpu
from jax.sharding import Mesh
from jax.sharding import PartitionSpec as P

F32 = jnp.float32
BF16 = jnp.bfloat16
CORES = 2
VMEM = pl.BlockSpec(memory_space=pltpu.VMEM)
SMEM = pl.BlockSpec(memory_space=pltpu.SMEM)
ANY = pl.BlockSpec(memory_space=pl.ANY)
PARAMS = pltpu.CompilerParams(vmem_limit_bytes=56 * 1024 * 1024)


def low_half(shape, dof):
    return lax.broadcasted_iota(jnp.int32, shape, 1) < dof


def lane_sum(values):
    return jnp.sum(values, axis=1, keepdims=True)


def split_bf16(values):
    high = values.astype(BF16)
    return high, (values - high.astype(F32)).astype(BF16)


def place(columns, shape):
    lane = lax.broadcasted_iota(jnp.int32, shape, 1)
    packed = jnp.zeros(shape, F32)
    for index, column in enumerate(columns):
        packed = jnp.where(lane == index, column, packed)
    return packed


def position_kernel(geometry, ids, owner, table, out, where):
    per_dev, n_sub, nz, hops = geometry
    me_z, me_c, me_s = ids[0], ids[1], ids[2]
    sites = owner.shape[0]

    def locate(slot):
        dev = slot // per_dev
        grp = dev // n_sub
        block = ((grp % CORES) ^ me_c) * nz + grp // CORES
        return (block * n_sub + ((dev % n_sub) ^ me_s)) * per_dev + slot % per_dev

    def fill(slot, carry):
        where[owner[slot]] = locate(slot)
        return carry

    lax.fori_loop(0, sites, fill, 0, unroll=8)

    def look(local, carry):
        dev = (me_z * CORES + me_c) * n_sub + ((local // per_dev) ^ me_s)
        slot = dev * per_dev + local % per_dev
        base = owner[slot] * hops
        out[local * (hops + 1)] = locate(slot)
        for hop in range(hops):
            out[local * (hops + 1) + 1 + hop] = where[table[base + hop]]
        return carry

    lax.fori_loop(0, n_sub * per_dev, look, 0, unroll=2)


def spread(dup, pair, values, dof):
    mask = low_half(values.shape, dof)
    rolled = pltpu.roll(values, dof, 1)
    dup[2 * pair] = jnp.where(mask, values, rolled)
    dup[2 * pair + 1] = jnp.where(mask, rolled, values)


def site_product(op, local, pos, dup, terms, dof):
    rows = dup.shape[1]
    mask = low_half((rows, 2 * dof), dof)
    tiles = []
    for first in range(0, terms - 1, 2):
        left = dup[pos[local * terms + first]]
        right = dup[pos[local * terms + first + 1]]
        tiles.append(jnp.where(mask, left, right))
    if terms % 2:
        tiles.append(dup[pos[local * terms + terms - 1]][:, :dof])
    high, low = split_bf16(jnp.concatenate(tiles, axis=1))
    op_high, op_low = split_bf16(op)
    product = lax.dot_general(
        jnp.concatenate([high, low], axis=0),
        jnp.concatenate([op_high, op_low], axis=0),
        (((1,), (1,)), ((), ())),
        preferred_element_type=F32,
    )
    total = product[:rows] + product[rows:]
    return total + pltpu.roll(total, dof, 1)


def apply_rows(ops, pos, dup, terms, dof, put):
    per_part = ops[0].shape[0]
    rows = dup.shape[1]
    mask = low_half((rows, 2 * dof), dof)
    if per_part % 2:
        for pair in range(len(ops) * per_part // 2):
            halves = [
                site_product(ops[i // per_part][i % per_part], i, pos, dup, terms, dof)
                for i in (2 * pair, 2 * pair + 1)
            ]
            put(pair, jnp.where(mask, halves[0], halves[1]))
        return
    base = 0
    for op in ops:

        def body(inner, carry, base=base, op=op):
            first = base + 2 * inner
            even = site_product(op[2 * inner], first, pos, dup, terms, dof)
            odd = site_product(op[2 * inner + 1], first + 1, pos, dup, terms, dof)
            put(base // 2 + inner, jnp.where(mask, even, odd))
            return carry

        lax.fori_loop(0, op.shape[0] // 2, body, 0, unroll=True)
        base += op.shape[0]


def start_copies(sources, targets, sems):
    copies = [
        pltpu.make_async_copy(source, target, sems.at[index])
        for index, (source, target) in enumerate(zip(sources, targets))
    ]
    for copy in copies:
        copy.start()
    return copies


def over_pairs(fields, step, init):
    n_pair = fields[0].shape[0]
    for half in range(2):
        init = lax.fori_loop(
            0, n_pair, lambda pair, carry, half=half: step(half, pair, carry), init, unroll=8
        )
    return init


def first_kernel(count, dof, terms, pos, own, par, *rest):
    ops, out = rest[:count], rest[count]
    held, sems, dup = rest[count + 1 : 2 * count + 1], rest[2 * count + 1], rest[2 * count + 2]
    copies = start_copies(ops, held, sems)
    n_pair = own.shape[0]
    fields = (own, par)

    def build(half, pair, carry):
        spread(dup, half * n_pair + pair, fields[half][pair], dof)
        return carry

    over_pairs(fields, build, 0)
    for copy in copies:
        copy.wait()

    def put(pair, values):
        for block in range(out.shape[0]):
            out[block, pair] = values

    apply_rows(held, pos, dup, terms, dof, put)


def second_kernel(count, dof, terms, ids, pos, b_own, b_par, z_own, z_par, *rest):
    ops, (out, basis, mine, coeffs) = rest[:count], rest[count : count + 4]
    rest = rest[count + 4 :]
    held, sems, dup = rest[:count], rest[count], rest[count + 1]
    copies = start_copies(ops, held, sems)
    n_pair = b_own.shape[0]
    b_ref, z_ref = (b_own, b_par), (z_own, z_par)
    shape = b_own.shape[1:]
    zero = jnp.zeros(shape, F32)

    def dots(half, pair, carry):
        b, z = b_ref[half][pair], z_ref[half][pair]
        return carry[0] + b * b, carry[1] + b * z

    norm, cross = over_pairs(b_ref, dots, (zero, zero))
    beta_sq = lane_sum(norm)
    beta = jnp.sqrt(beta_sq)
    scale = 1.0 / beta
    h00 = lane_sum(cross) * scale * scale

    def remove(half, pair, carry):
        w = z_ref[half][pair] * scale - (h00 * scale) * b_ref[half][pair]
        basis[half * n_pair + pair] = w
        return carry + w * w

    h10 = jnp.sqrt(lane_sum(over_pairs(b_ref, remove, zero)))
    unit = 1.0 / h10

    def build(half, pair, carry):
        v = basis[half * n_pair + pair] * unit
        basis[half * n_pair + pair] = v
        spread(dup, half * n_pair + pair, v, dof)
        return carry

    over_pairs(b_ref, build, 0)
    coeffs[...] = place([beta, h00, h10], shape)
    n_mine = mine.shape[0]
    mine[...] = basis[pl.ds(ids[0] * n_mine, n_mine)]
    for copy in copies:
        copy.wait()

    def put(pair, values):
        for block in range(out.shape[0]):
            out[block, pair] = values

    apply_rows(held, pos, dup, terms, dof, put)


def third_kernel(
    count, dof, terms, ids, pos, b_own, b_par, basis, z_own, z_par, b_mine, v1_mine, coeffs, *rest
):
    ops, (sums, mine, coeffs_out) = rest[:count], rest[count : count + 3]
    rest = rest[count + 3 :]
    held, sems, dup, work, image = (
        rest[:count],
        rest[count],
        rest[count + 1],
        rest[count + 2],
        rest[count + 3],
    )
    copies = start_copies(ops, held, sems)
    n_pair = b_own.shape[0]
    b_ref, z_ref = (b_own, b_par), (z_own, z_par)
    shape = b_own.shape[1:]
    zero = jnp.zeros(shape, F32)
    known = coeffs[...]
    scale = 1.0 / known[:, 0:1]

    def dots(half, pair, carry):
        z = z_ref[half][pair]
        return carry[0] + b_ref[half][pair] * z, carry[1] + basis[half * n_pair + pair] * z

    first, second = over_pairs(b_ref, dots, (zero, zero))
    h01 = lane_sum(first) * scale
    h11 = lane_sum(second)

    def remove(half, pair, carry):
        w = (
            z_ref[half][pair]
            - (h01 * scale) * b_ref[half][pair]
            - h11 * basis[half * n_pair + pair]
        )
        work[half * n_pair + pair] = w
        return carry + w * w

    h21 = jnp.sqrt(lane_sum(over_pairs(b_ref, remove, zero)))
    unit = 1.0 / h21

    def build(half, pair, carry):
        v = work[half * n_pair + pair] * unit
        work[half * n_pair + pair] = v
        spread(dup, half * n_pair + pair, v, dof)
        return carry

    over_pairs(b_ref, build, 0)
    n_mine = mine.shape[0]
    mine[...] = work[pl.ds(ids[0] * n_mine, n_mine)]
    for copy in copies:
        copy.wait()

    def put(pair, values):
        image[pair] = values

    apply_rows(held, pos, dup, terms, dof, put)

    def last(pair, carry):
        u = image[pair]
        return (
            carry[0] + b_mine[pair] * u,
            carry[1] + v1_mine[pair] * u,
            carry[2] + mine[pair] * u,
            carry[3] + u * u,
        )

    parts = lax.fori_loop(0, n_mine, last, (zero, zero, zero, zero), unroll=True)
    packed = place([lane_sum(part) for part in parts], shape)
    for block in range(sums.shape[0]):
        sums[block] = packed
    lane = lax.broadcasted_iota(jnp.int32, shape, 1)
    merged = jnp.where(lane == 3, h01, known)
    merged = jnp.where(lane == 4, h11, merged)
    coeffs_out[...] = jnp.where(lane == 5, h21, merged)


def combine_kernel(ids, sums, coeffs, b_mine, v1_mine, v2_mine, out):
    total = sums[0]
    for block in range(1, sums.shape[0]):
        total = total + sums[block]
    known = coeffs[...]
    beta, h00, h10 = known[:, 0:1], known[:, 1:2], known[:, 2:3]
    h01, h11, h21 = known[:, 3:4], known[:, 4:5], known[:, 5:6]
    scale = 1.0 / beta
    h02, h12, h22, g22 = total[:, 0:1] * scale, total[:, 1:2], total[:, 2:3], total[:, 3:4]
    g00 = h00 * h00 + h10 * h10
    g01 = h00 * h01 + h10 * h11
    g02 = h00 * h02 + h10 * h12
    g11 = h01 * h01 + h11 * h11 + h21 * h21
    g12 = h01 * h02 + h11 * h12 + h21 * h22
    l10 = g01 / g00
    l20 = g02 / g00
    d1 = g11 - l10 * g01
    e21 = g12 - l20 * g01
    l21 = e21 / d1
    d2 = g22 - l20 * g02 - l21 * e21
    r0 = beta * h00
    r1 = beta * h01 - l10 * r0
    r2 = beta * h02 - l20 * r0 - l21 * r1
    y2 = r2 / d2
    y1 = r1 / d1 - l21 * y2
    y0 = r0 / g00 - l10 * y1 - l20 * y2
    c0 = y0 * scale
    parts, per_part = out.shape[0], out.shape[1]
    for part in range(parts):
        target = part ^ ids[2]
        for inner in range(per_part):
            pair = part * per_part + inner
            out[target, inner] = c0 * b_mine[pair] + y1 * v1_mine[pair] + y2 * v2_mine[pair]


def finish_kernel(dof, parts, out):
    for pair in range(parts.shape[1]):
        stacked = jnp.concatenate([parts[q, pair] for q in range(parts.shape[0])], axis=0)
        turned = stacked.T
        out[2 * pair] = turned[:dof]
        out[2 * pair + 1] = turned[dof:]


def per_device(coarse_op, right_side, owner_map, neighbor_table):
    nz = lax.axis_size("z")
    n_sub = lax.axis_size("sub")
    per_dev, dof, width = coarse_op.shape
    terms = width // dof
    hops = terms - 1
    rhs = right_side.shape[2] // n_sub
    n_loc = n_sub * per_dev
    n_own = n_loc // 2
    me_z, me_c, me_s = lax.axis_index("z"), lax.axis_index("core"), lax.axis_index("sub")
    ids = jnp.stack([me_z, me_c, me_s]).astype(jnp.int32)
    even = per_dev % 2 == 0
    lanes = 2 * dof
    field = (n_own, rhs, lanes)

    if n_sub == 4:
        hop_x = [(s, s ^ 1) for s in range(n_sub)]
        hop_y = [(s, s ^ 2) for s in range(n_sub)]
        op_x = lax.ppermute(coarse_op, "sub", hop_x)
        op_y = lax.ppermute(coarse_op, "sub", hop_y)
    order = jnp.arange(n_sub, dtype=jnp.int32) ^ me_s

    positions = pl.pallas_call(
        functools.partial(position_kernel, (per_dev, n_sub, nz, hops)),
        out_shape=jax.ShapeDtypeStruct((n_loc * terms,), jnp.int32),
        in_specs=[SMEM, SMEM, SMEM],
        out_specs=SMEM,
        scratch_shapes=[pltpu.SMEM((owner_map.shape[0],), jnp.int32)],
        name="positions",
    )(ids, owner_map, neighbor_table.reshape(-1))

    turned = right_side.reshape(per_dev, dof, n_sub, rhs).transpose(2, 0, 3, 1)
    if even:
        turned = turned.reshape(n_sub, per_dev // 2, 2, rhs, dof).transpose(0, 1, 3, 2, 4)
        turned = turned.reshape(n_sub, per_dev // 2, rhs, lanes)
    mine = lax.all_to_all(turned, "sub", split_axis=0, concat_axis=0, tiled=True)[order]
    if not even:
        mine = mine.reshape(n_own, 2, rhs, dof).transpose(0, 2, 1, 3)
    b_mine = mine.reshape(field)

    swap = [(c, c ^ 1) for c in range(CORES)]

    def gather(copies):
        own = lax.all_to_all(copies, "z", split_axis=0, concat_axis=0, tiled=True)
        par = lax.ppermute(own, "core", swap)
        return own.reshape((nz * n_own,) + field[1:]), par.reshape((nz * n_own,) + field[1:])

    b_own, b_par = gather(jnp.broadcast_to(b_mine[None], (nz,) + field))

    if n_sub == 4:
        op_x, op_y, b_own, b_par = lax.optimization_barrier((op_x, op_y, b_own, b_par))
        half = per_dev // 2
        op_d0 = lax.ppermute(op_y[:half], "sub", hop_x)
        op_d1 = lax.ppermute(op_x[half:], "sub", hop_y)
        ops = [coarse_op, op_x, op_y, op_d0, op_d1]
    else:
        every = lax.all_gather(coarse_op, "sub", axis=0)[order]
        ops = [every[k] for k in range(n_sub)]
    count = len(ops)
    held = [pltpu.VMEM(op.shape, F32) for op in ops]
    sems = pltpu.SemaphoreType.DMA((count,))
    dup = pltpu.VMEM((CORES * nz * n_loc, rhs, lanes), F32)
    spread_shape = jax.ShapeDtypeStruct((nz,) + field, F32)
    small = jax.ShapeDtypeStruct(field[1:], F32)
    own_shape = jax.ShapeDtypeStruct(field, F32)

    z1 = pl.pallas_call(
        functools.partial(first_kernel, count, dof, terms),
        out_shape=spread_shape,
        in_specs=[SMEM, VMEM, VMEM] + [ANY] * count,
        out_specs=VMEM,
        scratch_shapes=held + [sems, dup],
        compiler_params=PARAMS,
        name="first",
    )(positions, b_own, b_par, *ops)
    z1_own, z1_par = gather(z1)

    z2, basis, v1_mine, coeffs = pl.pallas_call(
        functools.partial(second_kernel, count, dof, terms),
        out_shape=[
            spread_shape,
            jax.ShapeDtypeStruct((CORES * nz * n_own,) + field[1:], F32),
            own_shape,
            small,
        ],
        in_specs=[SMEM, SMEM] + [VMEM] * 4 + [ANY] * count,
        out_specs=[VMEM] * 4,
        scratch_shapes=held + [sems, dup],
        compiler_params=PARAMS,
        name="second",
    )(ids, positions, b_own, b_par, z1_own, z1_par, *ops)
    z2_own, z2_par = gather(z2)

    copies = nz * CORES
    sums, v2_mine, coeffs = pl.pallas_call(
        functools.partial(third_kernel, count, dof, terms),
        out_shape=[jax.ShapeDtypeStruct((copies,) + field[1:], F32), own_shape, small],
        in_specs=[SMEM, SMEM] + [VMEM] * 8 + [ANY] * count,
        out_specs=[VMEM] * 3,
        scratch_shapes=held
        + [
            sems,
            dup,
            pltpu.VMEM((CORES * nz * n_own,) + field[1:], F32),
            pltpu.VMEM(field, F32),
        ],
        compiler_params=PARAMS,
        name="third",
    )(ids, positions, b_own, b_par, basis, z2_own, z2_par, b_mine, v1_mine, coeffs, *ops)
    sums = lax.all_to_all(sums, ("z", "core"), split_axis=0, concat_axis=0, tiled=True)

    blocks = (n_sub, per_dev // 2, rhs, lanes) if even else (1,) + field
    result = pl.pallas_call(
        combine_kernel,
        out_shape=jax.ShapeDtypeStruct(blocks, F32),
        in_specs=[SMEM] + [VMEM] * 5,
        out_specs=VMEM,
        name="combine",
    )(ids if even else ids * 0, sums, coeffs, b_mine, v1_mine, v2_mine)
    if even:
        result = lax.all_to_all(result, "sub", split_axis=0, concat_axis=0, tiled=True)
        return pl.pallas_call(
            functools.partial(finish_kernel, dof),
            out_shape=jax.ShapeDtypeStruct(right_side.shape, F32),
            in_specs=[VMEM],
            out_specs=VMEM,
            name="finish",
        )(result)
    result = result.reshape(n_own, rhs, 2, dof).transpose(0, 2, 1, 3).reshape(n_sub, per_dev, rhs, dof)
    result = lax.all_to_all(result[order], "sub", split_axis=0, concat_axis=0, tiled=True)
    return result.transpose(1, 3, 0, 2).reshape(right_side.shape)


def solution(mesh):
    n_grp, n_sub = mesh.shape["grp"], mesh.shape["sub"]
    inner = Mesh(mesh.devices.reshape(n_grp // CORES, CORES, n_sub), ("z", "core", "sub"))
    split = P(("z", "core", "sub"), None, None)
    return jax.shard_map(
        per_device,
        mesh=inner,
        in_specs=(split, split, P(), P()),
        out_specs=split,
        check_vma=False,
    )
```

time: 309 us -> 151 us (0.49)
  blocking collectives: 135 us -> 52.6 us
  matrix products: 42.5 us -> 0 us
  local copies, waits for them, and re-layouts: 42.9 us -> 9.38 us
  Pallas kernels: 0 us -> 32.9 us
  other arithmetic: 21.1 us -> 0.67 us
  between operations: 13.7 us -> 0.1 us
  starting transfers between devices: 6.36 us -> 13.1 us
  waiting for transfers between devices: 46.8 us -> 41.1 us
    psum x10 -> x0, blocking collectives: 89 us -> none  [reduce_sum(): return lax.psum(values, 'sub')]
    all_gather x1 -> x0, waiting for transfers between devices: 46.1 us -> none  [per_device(): op_rows = lax.all_gather(coarse_op, 'grp', axis=0, tiled=True)]
    all_to_all x1 -> x4, blocking collectives: 9.14 us -> 52.6 us  [the longest x2 33.7 us: gather(): own = lax.all_to_all(copies, 'z', split_axis=0, concat_axis=0, tiled=True)]
    dot_general x7 -> x0, matrix products: 42.5 us -> none  [the longest x3 38.9 us: per_device(): jnp.einsum('sac,scr->sar', op_rows, stacked, precision=lax.Precision.HIGH...]
    all_gather x3 -> x0, blocking collectives: 36.5 us -> none  [per_device(): piece = lax.all_gather(apply_vector, 'sub', axis=0, tiled=True)]
    pallas_call x0 -> x6, Pallas kernels: none -> 32.9 us  [the longest x1 7.87 us: per_device(): pl.pallas_call(functools.partial(third_kernel, count, dof, terms), out_sh...]
    ppermute x0 -> x7, waiting for transfers between devices: none -> 24.3 us  [the longest x1 16 us: per_device(): op_y = lax.ppermute(coarse_op, 'sub', hop_y)]
    all_to_all x1 -> x2, waiting for transfers between devices: 0.01 us -> 16.8 us  [the longest x1 11.8 us: gather(): own = lax.all_to_all(copies, 'z', split_axis=0, concat_axis=0, tiled=True)]
  transfers between devices with their start and end apart: 2 -> 9, of which waited for: 1 -> 8; matrix products, arithmetic and copies ran while one was open for 10% -> 1% of each run, Pallas kernels for 0% -> 5%
where the time goes in v1:
time: 151 us; the launch traced here: 150 us
  blocking collectives  52.6 us (35%)
  waiting for transfers between devices  41.1 us (27%)
  Pallas kernels  32.9 us (22%)
  starting transfers between devices  13.1 us (9%)
  local copies, waits for them, and re-layouts  9.38 us (6%)
    all_to_all x2, blocking collectives, gather(): own = lax.all_to_all(copies, 'z', split_axis=0, concat_axis=0, tiled=True)  33.7 us
    ppermute x1, waiting for transfers between devices, per_device(): op_y = lax.ppermute(coarse_op, 'sub', hop_y)  16 us
    all_to_all x1, waiting for transfers between devices, gather(): own = lax.all_to_all(copies, 'z', split_axis=0, concat_axis=0, tiled=True)  11.8 us
    all_to_all x1, blocking collectives, per_device(): lax.all_to_all(sums, ('z', 'core'), split_axis=0, concat_axis=0, tiled=True)  9.88 us
    all_to_all x1, blocking collectives, per_device(): lax.all_to_all(result, 'sub', split_axis=0, concat_axis=0, tiled=True)  9.02 us
    pallas_call x1, Pallas kernels, per_device(): pl.pallas_call(functools.partial(third_kernel, count, dof, terms), out_sh...  7.87 us
    pallas_call x1, Pallas kernels, per_device(): pl.pallas_call(functools.partial(position_kernel, (per_dev, n_sub, nz, ho...  7.38 us
    pallas_call x1, Pallas kernels, per_device(): pl.pallas_call(functools.partial(second_kernel, count, dof, terms), out_s...  6.91 us
  transfers between devices with their start and end apart: 9, of which 8 were waited for; matrix products, arithmetic and copies ran while one was open for 1% of the time, Pallas kernels for 5%

profile of v1, /device:TPU:0, one launch (start us, length us, event | category | flops | bytes accessed | tf_op | source)
XLA Modules:
  0.0 149.8 jit_solution(7182153373893121171)
XLA Ops:
  0.0 1.1 copy.6
  1.3 0.8 reshape.51
  2.1 5.2 %all-to-all-start = ((f32[4,4,16,128]{3,2,1,0:T(8,128)}), f32[4,4,16,128]{3,2,1,0:T(8,128)S(1)}, u32[]{:S(2)}, u32[]{:S(2)}) async-start(f32[4,4,16,128]{3,2,1,0:T(8,128)} %reshape.51), calls=%async_computation | async-start | bytes 262144 | tf_op jit(solution)/shard_map/all_to_all | solution.py:368
  7.3 5.0 %all-to-all-done = f32[4,4,16,128]{3,2,1,0:T(8,128)S(1)} async-done(((f32[4,4,16,128]{3,2,1,0:T(8,128)}), f32[4,4,16,128]{3,2,1,0:T(8,128)S(1)}, u32[]{:S(2)}, u32[]{:S(2)}) %all-to-all-start) | async-done | bytes 131104 | tf_op jit(solution)/shard_map/all_to_all | solution.py:368
  12.9 0.8 broadcast_in_dim.9
  13.8 4.9 %all-to-all-start.1 = ((f32[4,16,16,128]{3,2,1,0:T(8,128)}), f32[4,16,16,128]{3,2,1,0:T(8,128)S(1)}, u32[]{:S(2)}, u32[]{:S(2)}) async-start(f32[4,16,16,128]{3,2,1,0:T(8,128)} %broadcast_in_dim.9), calls=%async_computation.1 | async-start | bytes 1048576 | tf_op jit(solution)/shard_map/all_to_all | solution.py:376
  18.6 0.9 collective-permute-start.1
  19.9 11.8 %all-to-all-done.1 = f32[4,16,16,128]{3,2,1,0:T(8,128)S(1)} async-done(((f32[4,16,16,128]{3,2,1,0:T(8,128)}), f32[4,16,16,128]{3,2,1,0:T(8,128)S(1)}, u32[]{:S(2)}, u32[]{:S(2)}) %all-to-all-start.1) | async-done | bytes 524320 | tf_op jit(solution)/shard_map/all_to_all | solution.py:376
  31.7 16.0 %collective-permute-done.1.rest_2_ = f32[8,64,576]{2,1,0:T(8,128)S(1)} collective-permute-done((f32[8,64,576]{2,1,0:T(8,128)}, f32[8,64,576]{2,1,0:T(8,128)S(1)}, u32[]{:S(2)}, u32[]{:S(2)}) %collective-permute-start.1) | collective-permute-done | bytes 1179680 | tf_op jit(solution)/shard_map/ppermute | solution.py:352
  47.7 0.9 collective-permute-done.rest_1_
  48.6 0.8 copy-done.4
  49.4 0.9 slice.7
  50.3 0.9 slice.6
  51.6 1.3 collective-permute-start.4
  53.0 0.7 reshape.48.table
  53.8 0.7 pad_add_fusion.ids
  54.4 7.4 %positions.1.pos = s32[288]{0:T(512)} custom-call(s32[3]{0:T(128)} %pad_add_fusion.ids, s32[256]{0:T(256)} %owner.1, s32[2048]{0:T(1024)} %reshape.48.table), custom_call_target="tpu_custom_call" | custom-call | tf_op jit(solution)/shard_map/positions/pallas_call | solution.py:355
  61.8 3.5 %collective-permute-done.3.rest_3_ = f32[4,64,576]{2,1,0:T(8,128)} collective-permute-done((f32[4,64,576]{2,1,0:T(8,128)}, f32[4,64,576]{2,1,0:T(8,128)}, u32[]{:S(2)}, u32[]{:S(2)}) %collective-permute-start.3) | collective-permute-done | bytes 589856 | tf_op jit(solution)/shard_map/ppermute | solution.py:385
  65.4 0.8 copy-done.3
  66.3 6.5 %first.1 = f32[4,16,16,128]{3,2,1,0:T(8,128)} custom-call(s32[288]{0:T(512)} %positions.1.pos, f32[64,16,128]{2,1,0:T(8,128)} %bitcast.20, f32[64,16,128]{2,1,0:T(8,128)} %bitcast.23, f32[8,64,576]{2,1,0:T(8,128)} %rest_0_.5, f32[8,64,576]{2,1,0:T(8,128)} %copy-done.1, f32[8,64,576]{2,1,0:T(8,128)} %copy-done, f32[4,64,576]{2,1,0:T(8,128)} %collective-permute-done.3.rest_3_, ...), custom_call_target="tpu_custom_call" | custom-call | tf_op jit(solution)/shard_map/first/pallas_call | solution.py:399
  72.8 15.2 %all_to_all.30 = f32[4,16,16,128]{3,2,1,0:T(8,128)S(1)} all-to-all(f32[4,16,16,128]{3,2,1,0:T(8,128)} %first.1), channel_id=1, replica_groups=mesh['z'=4,'core'=2,'sub'=4] {'z'}, dimensions={0} | all-to-all | bytes 1048576 | tf_op jit(solution)/shard_map/all_to_all | solution.py:376
  88.0 1.9 %collective-permute-done.5 = f32[4,16,16,128]{3,2,1,0:T(8,128)S(1)} collective-permute-done((f32[4,16,16,128]{3,2,1,0:T(8,128)S(1)}, f32[4,16,16,128]{3,2,1,0:T(8,128)S(1)}, u32[]{:S(2)}, u32[]{:S(2)}) %collective-permute-start.5) | collective-permute-done | bytes 524320 | tf_op jit(solution)/shard_map/ppermute | solution.py:377
  89.9 0.8 copy-done.9
  90.7 6.9 %second.1 = (f32[4,16,16,128]{3,2,1,0:T(8,128)}, f32[128,16,128]{2,1,0:T(8,128)}, f32[16,16,128]{2,1,0:T(8,128)}, f32[16,128]{1,0:T(8,128)}) custom-call(s32[3]{0:T(128)} %pad_add_fusion.ids, s32[288]{0:T(512)} %positions.1.pos, f32[64,16,128]{2,1,0:T(8,128)} %bitcast.21, f32[64,16,128]{2,1,0:T(8,128)} %bitcast.24, f32[64,16,128]{2,1,0:T(8,128)} %bitcast.30, ...), custom_call_target="tpu_custom_call" | custom-call | tf_op jit(solution)/shard_map/second/pallas_call | solution.py:410
  97.6 18.5 %all_to_all.31 = f32[4,16,16,128]{3,2,1,0:T(8,128)S(1)} all-to-all(f32[4,16,16,128]{3,2,1,0:T(8,128)} %get-tuple-element.21), channel_id=1, replica_groups=mesh['z'=4,'core'=2,'sub'=4] {'z'}, dimensions={0} | all-to-all | bytes 1048576 | tf_op jit(solution)/shard_map/all_to_all | solution.py:376
  116.2 1.9 %collective-permute-done.6 = f32[4,16,16,128]{3,2,1,0:T(8,128)S(1)} collective-permute-done((f32[4,16,16,128]{3,2,1,0:T(8,128)S(1)}, f32[4,16,16,128]{3,2,1,0:T(8,128)S(1)}, u32[]{:S(2)}, u32[]{:S(2)}) %collective-permute-start.6) | collective-permute-done | bytes 524320 | tf_op jit(solution)/shard_map/ppermute | solution.py:377
  118.1 0.8 copy-done.8
  118.9 7.9 %third.1 = (f32[8,16,128]{2,1,0:T(8,128)}, f32[16,16,128]{2,1,0:T(8,128)}, f32[16,128]{1,0:T(8,128)}) custom-call(s32[3]{0:T(128)} %pad_add_fusion.ids, s32[288]{0:T(512)} %positions.1.pos, f32[64,16,128]{2,1,0:T(8,128)} %bitcast.22, f32[64,16,128]{2,1,0:T(8,128)} %bitcast.25, f32[128,16,128]{2,1,0:T(8,128)} %get-tuple-element.20.basis, ...), custom_call_target="tpu_custom_call" | custom-call | tf_op jit(solution)/shard_map/third/pallas_call | solution.py:427
  126.8 9.9 %all_to_all.32.sums = f32[8,16,128]{2,1,0:T(8,128)} all-to-all(f32[8,16,128]{2,1,0:T(8,128)} %get-tuple-element.24), channel_id=1, replica_groups=mesh['z'=4,'core'=2,'sub'=4] {'z','core'}, dimensions={0} | all-to-all | bytes 131072 | tf_op jit(solution)/shard_map/all_to_all | solution.py:442
  136.6 2.4 %combine.1 = f32[4,4,16,128]{3,2,1,0:T(8,128)} custom-call(s32[3]{0:T(128)} %pad_add_fusion.ids, f32[8,16,128]{2,1,0:T(8,128)} %all_to_all.32.sums, f32[16,128]{1,0:T(8,128)} %get-tuple-element.25.coeffs, f32[16,16,128]{2,1,0:T(8,128)} %bitcast.28, f32[16,16,128]{2,1,0:T(8,128)} %get-tuple-element.22.v1_mine, f32[16,16,128]{2,1,0:T(8,128)} %get-tuple-element.26.v2_mine), custom_call_target="tpu_custom_call" | custom-call | tf_op jit(solution)/shard_map/combine/pallas_call | solution.py:445
  139.1 9.0 %all_to_all.33.parts = f32[4,4,16,128]{3,2,1,0:T(8,128)} all-to-all(f32[4,4,16,128]{3,2,1,0:T(8,128)} %combine.1), channel_id=1, replica_groups=mesh['z'=4,'core'=2,'sub'=4] {'sub'}, dimensions={0} | all-to-all | bytes 262144 | tf_op jit(solution)/shard_map/all_to_all | solution.py:453
  148.1 1.7 %finish.1 = f32[8,64,64]{2,1,0:T(8,128)} custom-call(f32[4,4,16,128]{3,2,1,0:T(8,128)} %all_to_all.33.parts), custom_call_target="tpu_custom_call" | custom-call | tf_op jit(solution)/shard_map/finish/pallas_call | solution.py:454
  (30 shorter events, 1.8 us)
Async XLA Ops:
  2.1 10.2 %all-to-all-start = ((f32[4,4,16,128]{3,2,1,0:T(8,128)}), f32[4,4,16,128]{3,2,1,0:T(8,128)S(1)}, u32[]{:S(2)}, u32[]{:S(2)}) async-start(f32[4,4,16,128]{3,2,1,0:T(8,128)} %reshape.51), calls=%async_computation | async-start | bytes 262144 | tf_op jit(solution)/shard_map/all_to_all | solution.py:368
  12.9 37.3 %copy-start.5 = (f32[4,4,16,128]{3,2,1,0:T(8,128)}, f32[4,4,16,128]{3,2,1,0:T(8,128)S(1)}, u32[]{:S(2)}) copy-start(f32[4,4,16,128]{3,2,1,0:T(8,128)S(1)} %gather_fusion) | copy-start | bytes 393220
  13.8 17.9 %all-to-all-start.1 = ((f32[4,16,16,128]{3,2,1,0:T(8,128)}), f32[4,16,16,128]{3,2,1,0:T(8,128)S(1)}, u32[]{:S(2)}, u32[]{:S(2)}) async-start(f32[4,16,16,128]{3,2,1,0:T(8,128)} %broadcast_in_dim.9), calls=%async_computation.1 | async-start | bytes 1048576 | tf_op jit(solution)/shard_map/all_to_all | solution.py:376
  18.6 29.0 %collective-permute-start.1 = (f32[8,64,576]{2,1,0:T(8,128)}, f32[8,64,576]{2,1,0:T(8,128)S(1)}, u32[]{:S(2)}, u32[]{:S(2)}) collective-permute-start(f32[8,64,576]{2,1,0:T(8,128)} %rest_0_.5), channel_id=1, source_target_pairs={{0,2},{1,3},{2,0},{3,1},{4,6},{5,7},{6,4},{7,5},{8,10},{9,11},{10,... | collective-permute-start | bytes 3538952 | tf_op jit(solution)/shard_map/ppermute | solution.py:352
  19.6 29.0 %collective-permute-start = (f32[8,64,576]{2,1,0:T(8,128)}, f32[8,64,576]{2,1,0:T(8,128)S(1)}, u32[]{:S(2)}, u32[]{:S(2)}) collective-permute-start(f32[8,64,576]{2,1,0:T(8,128)} %rest_0_.5), channel_id=1, source_target_pairs={{0,1},{1,0},{2,3},{3,2},{4,5},{5,4},{6,7},{7,6},{8,9},{9,8},{10,11... | collective-permute-start | bytes 3538952 | tf_op jit(solution)/shard_map/ppermute | solution.py:351
  31.7 33.7 %copy-start.2 = (f32[4,16,16,128]{3,2,1,0:T(8,128)}, f32[4,16,16,128]{3,2,1,0:T(8,128)S(1)}, u32[]{:S(2)}) copy-start(f32[4,16,16,128]{3,2,1,0:T(8,128)S(1)} %all-to-all-done.1) | copy-start | bytes 1572868
  31.7 16.8 %collective-permute-start.2 = (f32[4,16,16,128]{3,2,1,0:T(8,128)S(1)}, f32[4,16,16,128]{3,2,1,0:T(8,128)S(1)}, u32[]{:S(2)}, u32[]{:S(2)}) collective-permute-start(f32[4,16,16,128]{3,2,1,0:T(8,128)S(1)} %all-to-all-done.1), channel_id=1, source_target_pairs={{0,4},{4,0},{1,5},{5,1},{2,6},{6,2},{3,7},{7,3},{8,12},{12,8},{9,1... | collective-permute-start | bytes 1572872 | tf_op jit(solution)/shard_map/ppermute | solution.py:377
  47.7 3.5 %copy-start = (f32[8,64,576]{2,1,0:T(8,128)}, f32[8,64,576]{2,1,0:T(8,128)S(1)}, u32[]{:S(2)}) copy-start(f32[8,64,576]{2,1,0:T(8,128)S(1)} %collective-permute-done.1.rest_2_) | copy-start | bytes 3538948
  48.5 2.6 %copy-start.1 = (f32[8,64,576]{2,1,0:T(8,128)}, f32[8,64,576]{2,1,0:T(8,128)S(1)}, u32[]{:S(2)}) copy-start(f32[8,64,576]{2,1,0:T(8,128)S(1)} %collective-permute-done.rest_1_) | copy-start | bytes 3538948
  48.5 0.8 copy-start.4
  49.4 3.6 %copy-start.10 = (s32[256,8]{0,1:T(8,128)S(1)}, s32[256,8]{0,1:T(8,128)}, u32[]{:S(2)}) copy-start(s32[256,8]{0,1:T(8,128)} %param.7) | copy-start | bytes 24580
  51.1 14.2 %collective-permute-start.3 = (f32[4,64,576]{2,1,0:T(8,128)}, f32[4,64,576]{2,1,0:T(8,128)}, u32[]{:S(2)}, u32[]{:S(2)}) collective-permute-start(f32[4,64,576]{2,1,0:T(8,128)} %slice.6), channel_id=1, source_target_pairs={{0,1},{1,0},{2,3},{3,2},{4,5},{5,4},{6,7},{7,6},{8,9},{9,8},{10,11... | collective-permute-start | bytes 1769480 | tf_op jit(solution)/shard_map/ppermute | solution.py:385
  51.6 13.8 %collective-permute-start.4 = (f32[4,64,576]{2,1,0:T(8,128)}, f32[4,64,576]{2,1,0:T(8,128)S(1)}, u32[]{:S(2)}, u32[]{:S(2)}) collective-permute-start(f32[4,64,576]{2,1,0:T(8,128)} %slice.7), channel_id=1, source_target_pairs={{0,2},{1,3},{2,0},{3,1},{4,6},{5,7},{6,4},{7,5},{8,10},{9,11},{10,... | collective-permute-start | bytes 1769480 | tf_op jit(solution)/shard_map/ppermute | solution.py:386
  65.4 0.8 copy-start.3
  88.0 1.9 %copy-start.7 = (f32[4,16,16,128]{3,2,1,0:T(8,128)}, f32[4,16,16,128]{3,2,1,0:T(8,128)S(1)}, u32[]{:S(2)}) copy-start(f32[4,16,16,128]{3,2,1,0:T(8,128)S(1)} %all_to_all.30) | copy-start | bytes 1572868
  88.0 1.9 %collective-permute-start.5 = (f32[4,16,16,128]{3,2,1,0:T(8,128)S(1)}, f32[4,16,16,128]{3,2,1,0:T(8,128)S(1)}, u32[]{:S(2)}, u32[]{:S(2)}) collective-permute-start(f32[4,16,16,128]{3,2,1,0:T(8,128)S(1)} %all_to_all.30), channel_id=1, source_target_pairs={{0,4},{4,0},{1,5},{5,1},{2,6},{6,2},{3,7},{7,3},{8,12},{12,8},{9,1... | collective-permute-start | bytes 1572872 | tf_op jit(solution)/shard_map/ppermute | solution.py:377
  89.9 0.8 copy-start.9
  116.2 1.9 %copy-start.6 = (f32[4,16,16,128]{3,2,1,0:T(8,128)}, f32[4,16,16,128]{3,2,1,0:T(8,128)S(1)}, u32[]{:S(2)}) copy-start(f32[4,16,16,128]{3,2,1,0:T(8,128)S(1)} %all_to_all.31) | copy-start | bytes 1572868
  116.2 1.9 %collective-permute-start.6 = (f32[4,16,16,128]{3,2,1,0:T(8,128)S(1)}, f32[4,16,16,128]{3,2,1,0:T(8,128)S(1)}, u32[]{:S(2)}, u32[]{:S(2)}) collective-permute-start(f32[4,16,16,128]{3,2,1,0:T(8,128)S(1)} %all_to_all.31), channel_id=1, source_target_pairs={{0,4},{4,0},{1,5},{5,1},{2,6},{6,2},{3,7},{7,3},{8,12},{12,8},{9,1... | collective-permute-start | bytes 1572872 | tf_op jit(solution)/shard_map/ppermute | solution.py:377
  118.1 0.8 copy-start.8

commit v2 on v1

v2 whole, which is shorter than its diff:
```python
import functools

import jax
import jax.numpy as jnp
from jax import lax
from jax.experimental import pallas as pl
from jax.experimental.pallas import tpu as pltpu
from jax.sharding import Mesh
from jax.sharding import PartitionSpec as P


F32 = jnp.float32
BF16 = jnp.bfloat16
CORES = 2
VMEM = pl.BlockSpec(memory_space=pltpu.VMEM)
SMEM = pl.BlockSpec(memory_space=pltpu.SMEM)
ANY = pl.BlockSpec(memory_space=pl.ANY)
PARAMS = pltpu.CompilerParams(vmem_limit_bytes=20 * 1024 * 1024)
SMALL = pltpu.CompilerParams(vmem_limit_bytes=4 * 1024 * 1024)


def divide(value, size):
    if size & (size - 1):
        return lax.div(value, jnp.int32(size))
    return lax.shift_right_logical(value, jnp.int32(size.bit_length() - 1))


def remain(value, size):
    if size & (size - 1):
        return lax.rem(value, jnp.int32(size))
    return value & (size - 1)


def low_half(shape, dof):
    return lax.broadcasted_iota(jnp.int32, shape, 1) < dof


def lane_sum(values):
    return jnp.sum(values, axis=1, keepdims=True)


def split_bf16(values):
    high = values.astype(BF16)
    return high, (values - high.astype(F32)).astype(BF16)


def place(columns, shape):
    lane = lax.broadcasted_iota(jnp.int32, shape, 1)
    packed = jnp.zeros(shape, F32)
    for index, column in enumerate(columns):
        packed = jnp.where(lane == index, column, packed)
    return packed


def dense_rows(columns, shape, rows):
    size, lanes = shape
    per_row = lanes // size
    flipped = place(columns, shape).T
    lane = lax.broadcasted_iota(jnp.int32, (1, lanes), 1)
    wide = jnp.concatenate([flipped] * per_row, axis=1)
    packed = []
    for row in range(rows):
        line = jnp.zeros((1, lanes), F32)
        for inner in range(per_row):
            index = row * per_row + inner
            if index < len(columns):
                line = jnp.where(divide(lane, size) == inner, wide[index : index + 1], line)
        packed.append(line)
    return jnp.concatenate(packed, axis=0)


def position_kernel(geometry, ids, owner, table, out, where):
    per_dev, n_sub, nz, hops = geometry
    me_z, me_c, me_s = ids[0], ids[1], ids[2]
    sites = owner.shape[0]

    def locate(slot):
        dev = divide(slot, per_dev)
        grp = divide(dev, n_sub)
        block = (remain(grp, CORES) ^ me_c) * nz + divide(grp, CORES)
        return (block * n_sub + (remain(dev, n_sub) ^ me_s)) * per_dev + remain(slot, per_dev)

    def fill(slot, carry):
        where[owner[slot]] = locate(slot)
        return carry

    lax.fori_loop(0, sites, fill, 0, unroll=8)

    def look(local, carry):
        dev = (me_z * CORES + me_c) * n_sub + (divide(local, per_dev) ^ me_s)
        slot = dev * per_dev + remain(local, per_dev)
        base = owner[slot] * hops
        out[local * (hops + 1)] = locate(slot)
        for hop in range(hops):
            out[local * (hops + 1) + 1 + hop] = where[table[base + hop]]
        return carry

    lax.fori_loop(0, n_sub * per_dev, look, 0, unroll=2)


def spread(dup, pair, values, dof):
    mask = low_half(values.shape, dof)
    rolled = pltpu.roll(values, dof, 1)
    dup[2 * pair] = jnp.where(mask, values, rolled)
    dup[2 * pair + 1] = jnp.where(mask, rolled, values)


def site_product(op, local, pos, dup, terms, dof):
    rows = dup.shape[1]
    mask = low_half((rows, 2 * dof), dof)
    tiles = []
    for first in range(0, terms - 1, 2):
        left = dup[pos[local * terms + first]]
        right = dup[pos[local * terms + first + 1]]
        tiles.append(jnp.where(mask, left, right))
    if terms % 2:
        tiles.append(dup[pos[local * terms + terms - 1]][:, :dof])
    high, low = split_bf16(jnp.concatenate(tiles, axis=1))
    op_high, op_low = split_bf16(op)
    product = lax.dot_general(
        jnp.concatenate([high, low], axis=0),
        jnp.concatenate([op_high, op_low], axis=0),
        (((1,), (1,)), ((), ())),
        preferred_element_type=F32,
    )
    total = product[:rows] + product[rows:]
    return total + pltpu.roll(total, dof, 1)


def apply_rows(ops, pos, dup, terms, dof, put, base=0):
    per_part = ops[0].shape[0]
    rows = dup.shape[1]
    mask = low_half((rows, 2 * dof), dof)
    if per_part % 2:
        for pair in range(len(ops) * per_part // 2):
            halves = [
                site_product(ops[i // per_part][i % per_part], i, pos, dup, terms, dof)
                for i in (2 * pair, 2 * pair + 1)
            ]
            put(pair, jnp.where(mask, halves[0], halves[1]))
        return
    for op in ops:

        def body(inner, carry, base=base, op=op):
            first = base + 2 * inner
            even = site_product(op[2 * inner], first, pos, dup, terms, dof)
            odd = site_product(op[2 * inner + 1], first + 1, pos, dup, terms, dof)
            put(base // 2 + inner, jnp.where(mask, even, odd))
            return carry

        lax.fori_loop(0, op.shape[0] // 2, body, 0, unroll=True)
        base += op.shape[0]


def put_copies(out):
    def put(pair, values):
        for block in range(out.shape[0]):
            out[block, pair] = values

    return put


def start_copies(sources, targets, sems):
    copies = [
        pltpu.make_async_copy(source, target, sems.at[index])
        for index, (source, target) in enumerate(zip(sources, targets))
    ]
    for copy in copies:
        copy.start()
    return copies


def over_pairs(fields, step, init):
    n_pair = fields[0].shape[0]
    for half in range(2):
        init = lax.fori_loop(
            0, n_pair, lambda pair, carry, half=half: step(half, pair, carry), init, unroll=8
        )
    return init


def first_kernel(count, base, dof, terms, pos, own, par, *rest):
    ops, rest = rest[:count], rest[count:]
    before = None
    if base:
        before, rest = rest[0], rest[1:]
    out, held, sems, dup = rest[0], rest[1 : count + 1], rest[count + 1], rest[count + 2]
    copies = start_copies(ops, held, sems)
    n_pair = own.shape[0]
    fields = (own, par)

    def build(half, pair, carry):
        spread(dup, half * n_pair + pair, fields[half][pair], dof)
        return carry

    over_pairs(fields, build, 0)
    put = put_copies(out)
    if base:
        for pair in range(base // 2):
            put(pair, before[0, pair])
    for copy in copies:
        copy.wait()
    apply_rows(held, pos, dup, terms, dof, put, base)


def second_kernel(count, sends, dof, terms, ids, pos, b_own, b_par, z_own, z_par, *rest):
    ops, (out, basis, mine, coeffs) = rest[:count], rest[count : count + 4]
    shares, rest = rest[count + 4 : count + 4 + sends], rest[count + 4 + sends :]
    held, sems, dup = rest[:count], rest[count], rest[count + 1]
    copies = start_copies(ops, held, sems)
    n_pair = b_own.shape[0]
    b_ref, z_ref = (b_own, b_par), (z_own, z_par)
    shape = b_own.shape[1:]
    zero = jnp.zeros(shape, F32)

    def dots(half, pair, carry):
        b, z = b_ref[half][pair], z_ref[half][pair]
        return carry[0] + b * b, carry[1] + b * z

    norm, cross = over_pairs(b_ref, dots, (zero, zero))
    beta_sq = lane_sum(norm)
    beta = jnp.sqrt(beta_sq)
    scale = 1.0 / beta
    h00 = lane_sum(cross) * scale * scale

    def remove(half, pair, carry):
        w = z_ref[half][pair] * scale - (h00 * scale) * b_ref[half][pair]
        basis[half * n_pair + pair] = w
        return carry + w * w

    h10 = jnp.sqrt(lane_sum(over_pairs(b_ref, remove, zero)))
    unit = 1.0 / h10

    def build(half, pair, carry):
        v = basis[half * n_pair + pair] * unit
        basis[half * n_pair + pair] = v
        spread(dup, half * n_pair + pair, v, dof)
        return carry

    over_pairs(b_ref, build, 0)
    coeffs[...] = place([beta, h00, h10], shape)
    n_mine = mine.shape[0]
    mine[...] = basis[pl.ds(ids[0] * n_mine, n_mine)]
    for copy in copies:
        copy.wait()

    apply_rows(held, pos, dup, terms, dof, put_copies(out))
    for index, share in enumerate(shares):
        start = index * share.shape[1]
        for inner in range(share.shape[1]):
            share[0, inner] = z_own[ids[0] * n_mine + start + inner]
            share[1, inner] = out[0, start + inner]


def third_kernel(
    count, dof, terms, ids, pos, b_own, b_par, basis, z_own, z_par, b_mine, v1_mine, coeffs, *rest
):
    ops, (sums, mine) = rest[:count], rest[count : count + 2]
    rest = rest[count + 2 :]
    held, sems, dup, work, image = (
        rest[:count],
        rest[count],
        rest[count + 1],
        rest[count + 2],
        rest[count + 3],
    )
    copies = start_copies(ops, held, sems)
    n_pair = b_own.shape[0]
    b_ref, z_ref = (b_own, b_par), (z_own, z_par)
    shape = b_own.shape[1:]
    zero = jnp.zeros(shape, F32)
    known = coeffs[...]
    scale = 1.0 / known[:, 0:1]

    def dots(half, pair, carry):
        z = z_ref[half][pair]
        return carry[0] + b_ref[half][pair] * z, carry[1] + basis[half * n_pair + pair] * z

    first, second = over_pairs(b_ref, dots, (zero, zero))
    h01 = lane_sum(first) * scale
    h11 = lane_sum(second)

    def remove(half, pair, carry):
        w = (
            z_ref[half][pair]
            - (h01 * scale) * b_ref[half][pair]
            - h11 * basis[half * n_pair + pair]
        )
        work[half * n_pair + pair] = w
        return carry + w * w

    h21 = jnp.sqrt(lane_sum(over_pairs(b_ref, remove, zero)))
    unit = 1.0 / h21

    def build(half, pair, carry):
        v = work[half * n_pair + pair] * unit
        work[half * n_pair + pair] = v
        spread(dup, half * n_pair + pair, v, dof)
        return carry

    over_pairs(b_ref, build, 0)
    n_mine = mine.shape[0]
    mine[...] = work[pl.ds(ids[0] * n_mine, n_mine)]
    for copy in copies:
        copy.wait()

    def put(pair, values):
        image[pair] = values

    apply_rows(held, pos, dup, terms, dof, put)

    def last(pair, carry):
        u = image[pair]
        return (
            carry[0] + b_mine[pair] * u,
            carry[1] + v1_mine[pair] * u,
            carry[2] + mine[pair] * u,
            carry[3] + u * u,
        )

    parts = lax.fori_loop(0, n_mine, last, (zero, zero, zero, zero), unroll=True)
    solved = [known[:, 0:1], known[:, 1:2], known[:, 2:3], h01, h11, h21]
    columns = [lane_sum(part) for part in parts] + solved
    if len(sums.shape) == 3 and sums.shape[1:] == shape:
        packed = place(columns, shape)
    else:
        packed = dense_rows(columns, shape, sums.shape[1])
    for block in range(sums.shape[0]):
        sums[block] = packed


def weigh(values):
    d02, h12, h22, g22, beta, h00, h10, h01, h11, h21 = values
    scale = 1.0 / beta
    h02 = d02 * scale
    g00 = h00 * h00 + h10 * h10
    g01 = h00 * h01 + h10 * h11
    g02 = h00 * h02 + h10 * h12
    g11 = h01 * h01 + h11 * h11 + h21 * h21
    g12 = h01 * h02 + h11 * h12 + h21 * h22
    inv0 = 1.0 / g00
    l10 = g01 * inv0
    l20 = g02 * inv0
    d1 = g11 - l10 * g01
    e21 = g12 - l20 * g01
    inv1 = 1.0 / d1
    l21 = e21 * inv1
    d2 = g22 - l20 * g02 - l21 * e21
    r0 = beta * h00
    r1 = beta * h01 - l10 * r0
    r2 = beta * h02 - l20 * r0 - l21 * r1
    y2 = r2 / d2
    y1 = r1 * inv1 - l21 * y2
    y0 = r0 * inv0 - l10 * y1 - l20 * y2
    return scale, y0, y1, y2


def combine_kernel(sums, b_mine, v1_mine, v2_mine, out):
    total = sums[0]
    for block in range(1, sums.shape[0]):
        total = total + sums[block]
    known = sums[0]
    values = [(total if i < 4 else known)[:, i : i + 1] for i in range(10)]
    scale, y0, y1, y2 = weigh(values)
    for pair in range(b_mine.shape[0]):
        out[pair] = (y0 * scale) * b_mine[pair] + y1 * v1_mine[pair] + y2 * v2_mine[pair]


def finish_kernel(dof, ids, info, turned, *rest):
    shares, out, stack, factor = rest[:-3], rest[-3], rest[-2], rest[-1]
    n_sub, per_part, rhs, lanes = turned.shape
    per_row = lanes // rhs
    n_rows = info.shape[1]
    first = [info[quarter] for quarter in range(n_sub)]
    total = list(first)
    for block in range(1, info.shape[0] // n_sub):
        for quarter in range(n_sub):
            total[quarter] = total[quarter] + info[block * n_sub + quarter]
    known = [jnp.concatenate([f[r : r + 1] for f in first], axis=0) for r in range(n_rows)]
    added = [jnp.concatenate([t[r : r + 1] for t in total], axis=0) for r in range(n_rows)]
    values = []
    for index in range(10):
        source = (added if index < 4 else known)[index // per_row]
        shift = rhs * (index % per_row)
        values.append(pltpu.roll(source, lanes - shift, 1) if shift else source)
    scale, y0, y1, y2 = weigh(values)
    h00, h10, h01, h11, h21 = values[5:]
    gamma = y2 / h21
    both = (y1 - gamma * h11) / h10
    coeffs = [(y0 - both * h00 - gamma * h01) * scale, both * scale, gamma]
    flipped = jnp.concatenate(coeffs, axis=0)
    spare = -flipped.shape[0] % 8
    if spare:
        flipped = jnp.concatenate([flipped, jnp.zeros((spare, lanes), F32)], axis=0)
    flipped = flipped.T
    for index in range(3 * n_sub):
        factor[index] = jnp.broadcast_to(flipped[:rhs, index : index + 1], (rhs, lanes))
    for k in range(n_sub):
        quarter = ids[2] ^ k
        alpha, beta, gamma = (factor[part * n_sub + quarter] for part in range(3))
        start = pl.multiple_of(quarter * rhs, 8)
        for pair in range(per_part):
            mixed = alpha * turned[quarter, pair] + beta * shares[k][0, pair]
            stack[pair, pl.ds(start, rhs), :] = mixed + gamma * shares[k][1, pair]
    for pair in range(per_part):
        both = stack[pair].T
        out[2 * pair] = both[:dof]
        out[2 * pair + 1] = both[dof:]


def per_device(coarse_op, right_side, owner_map, neighbor_table):
    nz = lax.axis_size("z")
    n_sub = lax.axis_size("sub")
    per_dev, dof, width = coarse_op.shape
    terms = width // dof
    hops = terms - 1
    rhs = right_side.shape[2] // n_sub
    n_loc = n_sub * per_dev
    n_own = n_loc // 2
    me_z, me_c, me_s = lax.axis_index("z"), lax.axis_index("core"), lax.axis_index("sub")
    ids = jnp.stack([me_z, me_c, me_s]).astype(jnp.int32)
    even = per_dev % 2 == 0
    lanes = 2 * dof
    field = (n_own, rhs, lanes)

    relay = n_sub == 4 and even
    order = jnp.arange(n_sub, dtype=jnp.int32) ^ me_s
    hops_to = [[(s, s ^ k) for s in range(n_sub)] for k in range(n_sub)]
    half = per_dev // 2
    if relay:
        op_low, op_high = coarse_op[:half], coarse_op[half:]
        x_high = lax.ppermute(op_high, "sub", hops_to[1])
        y_low = lax.ppermute(op_low, "sub", hops_to[2])
        x_low = lax.ppermute(op_low, "sub", hops_to[1])
        y_high = lax.ppermute(op_high, "sub", hops_to[2])

    positions = pl.pallas_call(
        functools.partial(position_kernel, (per_dev, n_sub, nz, hops)),
        out_shape=jax.ShapeDtypeStruct((n_loc * terms,), jnp.int32),
        in_specs=[SMEM, SMEM, SMEM],
        out_specs=SMEM,
        scratch_shapes=[pltpu.SMEM((owner_map.shape[0],), jnp.int32)],
        compiler_params=SMALL,
        name="positions",
    )(ids, owner_map, neighbor_table.reshape(-1))

    turned = right_side.reshape(per_dev, dof, n_sub, rhs).transpose(2, 0, 3, 1)
    if even:
        turned = turned.reshape(n_sub, per_dev // 2, 2, rhs, dof).transpose(0, 1, 3, 2, 4)
        turned = turned.reshape(n_sub, per_dev // 2, rhs, lanes)
    mine = lax.all_to_all(turned, "sub", split_axis=0, concat_axis=0, tiled=True)
    mine = mine[order]
    if not even:
        mine = mine.reshape(n_own, 2, rhs, dof).transpose(0, 2, 1, 3)
    b_mine = mine.reshape(field)

    swap = [(c, c ^ 1) for c in range(CORES)]

    def over_z(copies):
        return lax.all_to_all(copies, "z", split_axis=0, concat_axis=0, tiled=True)

    def partner(own):
        par = lax.ppermute(own, "core", swap)
        return own.reshape((nz * n_own,) + field[1:]), par.reshape((nz * n_own,) + field[1:])

    if relay:
        d_low = lax.ppermute(y_low, "sub", hops_to[1])
        d_high = lax.ppermute(x_high, "sub", hops_to[2])
        stages = [[coarse_op, x_low, x_high, y_low, y_high], [d_low, d_high]]
    b_own = over_z(jnp.broadcast_to(b_mine[None], (nz,) + field))
    if not relay:
        every = lax.all_gather(coarse_op, "sub", axis=0)[order]
        stages = [[every[k] for k in range(n_sub)]]
    b_own, b_par = partner(b_own)
    ops = [op for stage in stages for op in stage]
    count = len(ops)

    def held(parts):
        return [pltpu.VMEM(op.shape, F32) for op in parts] + [
            pltpu.SemaphoreType.DMA((len(parts),)),
            pltpu.VMEM((CORES * nz * n_loc, rhs, lanes), F32),
        ]

    full = (CORES * nz * n_own,) + field[1:]
    small = jax.ShapeDtypeStruct(field[1:], F32)
    own_shape = jax.ShapeDtypeStruct(field, F32)

    z1, base = [], 0
    for index, stage in enumerate(stages):
        rows = base + sum(op.shape[0] for op in stage)
        blocks = nz if index + 1 == len(stages) else 1
        z1 = [
            pl.pallas_call(
                functools.partial(first_kernel, len(stage), base, dof, terms),
                out_shape=jax.ShapeDtypeStruct((blocks, rows // 2) + field[1:], F32),
                in_specs=[SMEM, VMEM, VMEM] + [ANY] * len(stage) + [VMEM] * len(z1),
                out_specs=VMEM,
                scratch_shapes=held(stage),
                compiler_params=PARAMS,
                name="first",
            )(positions, b_own, b_par, *stage, *z1)
        ]
        base = rows
    z1 = z1[0]
    z1_own, z1_par = partner(over_z(z1))

    sends = n_sub if even else 0
    share = jax.ShapeDtypeStruct((2, per_dev // 2, rhs, lanes), F32)
    z2, basis, v1_mine, coeffs, *shares = pl.pallas_call(
        functools.partial(second_kernel, count, sends, dof, terms),
        out_shape=[
            jax.ShapeDtypeStruct((nz,) + field, F32),
            jax.ShapeDtypeStruct(full, F32),
            own_shape,
            small,
        ]
        + [share] * sends,
        in_specs=[SMEM, SMEM] + [VMEM] * 4 + [ANY] * count,
        out_specs=[VMEM] * (4 + sends),
        scratch_shapes=held(ops),
        compiler_params=PARAMS,
        name="second",
    )(ids, positions, b_own, b_par, z1_own, z1_par, *ops)
    z2_own = over_z(z2)
    shares[1:] = [lax.ppermute(shares[k], "sub", hops_to[k]) for k in range(1, sends)]
    z2_own, z2_par = partner(z2_own)

    axes = ("z", "core", "sub") if even else ("z", "core")
    copies = nz * CORES * (n_sub if even else 1)
    note = (pl.cdiv(10 * rhs, lanes), lanes) if even else field[1:]
    sums, v2_mine = pl.pallas_call(
        functools.partial(third_kernel, count, dof, terms),
        out_shape=[jax.ShapeDtypeStruct((copies,) + note, F32), own_shape],
        in_specs=[SMEM, SMEM] + [VMEM] * 8 + [ANY] * count,
        out_specs=[VMEM] * 2,
        scratch_shapes=held(ops) + [pltpu.VMEM(full, F32), pltpu.VMEM(field, F32)],
        compiler_params=PARAMS,
        name="third",
    )(ids, positions, b_own, b_par, basis, z2_own, z2_par, b_mine, v1_mine, coeffs, *ops)
    sums = lax.all_to_all(sums, axes, split_axis=0, concat_axis=0, tiled=True)

    if even:
        return pl.pallas_call(
            functools.partial(finish_kernel, dof),
            out_shape=jax.ShapeDtypeStruct(right_side.shape, F32),
            in_specs=[SMEM] + [VMEM] * (2 + sends),
            out_specs=VMEM,
            scratch_shapes=[
                pltpu.VMEM((per_dev // 2, n_sub * rhs, lanes), F32),
                pltpu.VMEM((3 * n_sub, rhs, lanes), F32),
            ],
            compiler_params=SMALL,
            name="finish",
        )(ids, sums, turned, *shares)
    result = pl.pallas_call(
        combine_kernel,
        out_shape=own_shape,
        in_specs=[VMEM] * 4,
        out_specs=VMEM,
        compiler_params=SMALL,
            name="combine",
    )(sums, b_mine, v1_mine, v2_mine)
    result = result.reshape(n_own, rhs, 2, dof).transpose(0, 2, 1, 3)
    result = result.reshape(n_sub, per_dev, rhs, dof)[order]
    result = lax.all_to_all(result, "sub", split_axis=0, concat_axis=0, tiled=True)
    return result.transpose(1, 3, 0, 2).reshape(right_side.shape)


def solution(mesh):
    n_grp, n_sub = mesh.shape["grp"], mesh.shape["sub"]
    inner = Mesh(mesh.devices.reshape(n_grp // CORES, CORES, n_sub), ("z", "core", "sub"))
    split = P(("z", "core", "sub"), None, None)

    return jax.shard_map(
        per_device,
        mesh=inner,
        in_specs=(split, split, P(), P()),
        out_specs=split,
        check_vma=False,
    )
```

time: 151 us -> 131 us (0.87)
  blocking collectives: 52.6 us -> 33.4 us
  starting transfers between devices: 13.1 us -> 22.9 us
  Pallas kernels: 32.9 us -> 24.5 us
  local copies, waits for them, and re-layouts: 9.38 us -> 4.94 us
  waiting for transfers between devices: 41.1 us -> 44.4 us
    all_to_all x4 -> x2, blocking collectives: 52.6 us -> 33.4 us  [over_z(): return lax.all_to_all(copies, 'z', split_axis=0, concat_axis=0, tiled=True)]
    ppermute x7 -> x12, waiting for transfers between devices: 24.3 us -> 32.1 us  [the longest x1 13.8 us: per_device(): x_high = lax.ppermute(op_high, 'sub', hops_to[1])]
    ppermute x7 -> x12, starting transfers between devices: 3.05 us -> 9.57 us  [the longest x3 3.49 us: per_device(): lax.ppermute(shares[k], 'sub', hops_to[k])]
    all_to_all x1 -> x2, waiting for transfers between devices: 11.8 us -> 7.27 us  [the longest x1 7.27 us: per_device(): sums = lax.all_to_all(sums, axes, split_axis=0, concat_axis=0, tiled=True)]
    pallas_call x1, Pallas kernels: 7.38 us -> 3.33 us  [per_device(): pl.pallas_call(functools.partial(position_kernel, (per_dev, n_sub, nz, ho...]
    pallas_call x3, Pallas kernels: 15.9 us -> 12 us  [the longest x2 6.43 us: per_device(): pl.pallas_call(functools.partial(first_kernel, len(stage), base, dof, ter...]
    unnamed x24 -> x8, local copies, waits for them, and re-layouts: 4.46 us -> 1.21 us
    all_to_all x1 -> x2, starting transfers between devices: 4.87 us -> 8.1 us  [the longest x1 4.87 us: over_z(): return lax.all_to_all(copies, 'z', split_axis=0, concat_axis=0, tiled=True)]
  transfers between devices with their start and end apart: 9 -> 15, of which waited for: 8 -> 7; matrix products, arithmetic and copies ran while one was open for 1% -> 1% of each run, Pallas kernels for 5% -> 11%
where the time goes in v2:
time: 131 us; the launch traced here: 130 us
  waiting for transfers between devices  44.4 us (34%)
  blocking collectives  33.4 us (25%)
  Pallas kernels  24.5 us (19%)
  starting transfers between devices  22.9 us (17%)
  local copies, waits for them, and re-layouts  4.94 us (4%)
    all_to_all x2, blocking collectives, over_z(): return lax.all_to_all(copies, 'z', split_axis=0, concat_axis=0, tiled=True)  33.4 us
    ppermute x1, waiting for transfers between devices, per_device(): x_high = lax.ppermute(op_high, 'sub', hops_to[1])  13.8 us
    ppermute x1, waiting for transfers between devices, per_device(): y_high = lax.ppermute(op_high, 'sub', hops_to[2])  9.26 us
    all_to_all x1, waiting for transfers between devices, per_device(): sums = lax.all_to_all(sums, axes, split_axis=0, concat_axis=0, tiled=True)  7.27 us
    ppermute x1, waiting for transfers between devices, per_device(): d_high = lax.ppermute(x_high, 'sub', hops_to[2])  7.08 us
    pallas_call x1, Pallas kernels, per_device(): pl.pallas_call(functools.partial(third_kernel, count, dof, terms), out_sh...  7.07 us
    pallas_call x2, Pallas kernels, per_device(): pl.pallas_call(functools.partial(first_kernel, len(stage), base, dof, ter...  6.43 us
    pallas_call x1, Pallas kernels, per_device(): pl.pallas_call(functools.partial(second_kernel, count, sends, dof, terms)...  5.57 us
  transfers between devices with their start and end apart: 15, of which 7 were waited for; matrix products, arithmetic and copies ran while one was open for 1% of the time, Pallas kernels for 11%

profile of v2, /device:TPU:0, one launch (start us, length us, event | category | flops | bytes accessed | tf_op | source)
XLA Modules:
  0.0 130.4 jit_solution(14796622966398926704)
XLA Ops:
  0.0 1.1 copy.6
  1.1 0.2 copy.8
  1.3 0.9 reshape.51.turned
  2.2 5.2 %all-to-all-start = ((f32[4,4,16,128]{3,2,1,0:T(8,128)}), f32[4,4,16,128]{3,2,1,0:T(8,128)S(1)}, u32[]{:S(2)}, u32[]{:S(2)}) async-start(f32[4,4,16,128]{3,2,1,0:T(8,128)} %reshape.51.turned), calls=%async_computation | async-start | bytes 262144 | tf_op jit(solution)/shard_map/all_to_all | solution.py:451
  7.4 5.0 %all-to-all-done = f32[4,4,16,128]{3,2,1,0:T(8,128)S(1)} async-done(((f32[4,4,16,128]{3,2,1,0:T(8,128)}), f32[4,4,16,128]{3,2,1,0:T(8,128)S(1)}, u32[]{:S(2)}, u32[]{:S(2)}) %all-to-all-start) | async-done | bytes 131104 | tf_op jit(solution)/shard_map/all_to_all | solution.py:451
  12.4 0.6 gather_fusion
  12.9 0.8 broadcast_in_dim.9
  13.8 4.9 %all-to-all-start.1 = ((f32[4,16,16,128]{3,2,1,0:T(8,128)}), f32[4,16,16,128]{3,2,1,0:T(8,128)S(1)}, u32[]{:S(2)}, u32[]{:S(2)}) async-start(f32[4,16,16,128]{3,2,1,0:T(8,128)} %broadcast_in_dim.9), calls=%async_computation.1 | async-start | bytes 1048576 | tf_op jit(solution)/shard_map/all_to_all | solution.py:460
  18.7 1.2 fusion.1
  19.8 0.9 collective-permute-start.3
  20.7 0.4 collective-permute-start.1
  21.1 1.7 %collective-permute-start.6 = (f32[4,64,576]{2,1,0:T(8,128)}, f32[4,64,576]{2,1,0:T(8,128)}, u32[]{:S(2)}, u32[]{:S(2)}) collective-permute-start(f32[4,64,576]{2,1,0:T(8,128)} %get-tuple-element.23), channel_id=1, source_target_pairs={{0,2},{1,3},{2,0},{3,1},{4,6},{5,7},{6,4},{7,5},{8,10},{9,11},{10,... | collective-permute-start | bytes 1769480 | tf_op jit(solution)/shard_map/ppermute | solution.py:435
  22.8 1.1 collective-permute-start.5
  23.9 13.8 %collective-permute-done.3.rest_2_ = f32[4,64,576]{2,1,0:T(8,128)S(1)} collective-permute-done((f32[4,64,576]{2,1,0:T(8,128)}, f32[4,64,576]{2,1,0:T(8,128)S(1)}, u32[]{:S(2)}, u32[]{:S(2)}) %collective-permute-start.3) | collective-permute-done | bytes 589856 | tf_op jit(solution)/shard_map/ppermute | solution.py:432
  37.6 0.9 collective-permute-start.4
  38.7 1.1 collective-permute-start.2
  40.1 3.3 %positions.1.pos = s32[288]{0:T(512)S(1)} custom-call(s32[3]{0:T(128)S(1)} %pad_add_fusion.ids, s32[256]{0:T(256)S(1)} %copy-done.1, s32[2048]{0:T(1024)S(1)} %reshape.48.table), custom_call_target="tpu_custom_call" | custom-call | tf_op jit(solution)/shard_map/positions/pallas_call | solution.py:437
  43.5 9.3 %collective-permute-done.6.rest_4_ = f32[4,64,576]{2,1,0:T(8,128)} collective-permute-done((f32[4,64,576]{2,1,0:T(8,128)}, f32[4,64,576]{2,1,0:T(8,128)}, u32[]{:S(2)}, u32[]{:S(2)}) %collective-permute-start.6) | collective-permute-done | bytes 589856 | tf_op jit(solution)/shard_map/ppermute | solution.py:435
  52.7 3.8 %first.2.rest_2_ = f32[1,12,16,128]{3,2,1,0:T(8,128)S(1)} custom-call(s32[288]{0:T(512)S(1)} %positions.1.pos, f32[64,16,128]{2,1,0:T(8,128)S(1)} %bitcast.19, f32[64,16,128]{2,1,0:T(8,128)S(1)} %bitcast.23, f32[8,64,576]{2,1,0:T(8,128)S(1)} %copy-done, f32[4,64,576]{2,1,0:T(8,128)} %collective-permute-done.5.rest_1_, ...), custom_call_target="tpu_custom_call" | custom-call | tf_op jit(solution)/shard_map/first/pallas_call | solution.py:493
  56.6 7.1 %collective-permute-done.4.rest_1_.rest_6_ = f32[4,64,576]{2,1,0:T(8,128)} collective-permute-done((f32[4,64,576]{2,1,0:T(8,128)S(1)}, f32[4,64,576]{2,1,0:T(8,128)}, u32[]{:S(2)}, u32[]{:S(2)}) %collective-permute-start.4) | collective-permute-done | bytes 589856 | tf_op jit(solution)/shard_map/ppermute | solution.py:468
  63.6 2.6 %first.3 = f32[4,16,16,128]{3,2,1,0:T(8,128)S(1)} custom-call(s32[288]{0:T(512)S(1)} %positions.1.pos, f32[64,16,128]{2,1,0:T(8,128)S(1)} %bitcast.20, f32[64,16,128]{2,1,0:T(8,128)S(1)} %bitcast.24, f32[4,64,576]{2,1,0:T(8,128)} %collective-permute-done.2.rest_0_.rest_5_, f32[4,64,576]{2,1,0:T(8,128)} %collective-permute-done.4.rest_1_.rest_6_, ...), custom_call_target="tpu_custom_call" | custom-call | tf_op jit(solution)/shard_map/first/pallas_call | solution.py:493
  66.2 16.0 %all_to_all.25 = f32[4,16,16,128]{3,2,1,0:T(8,128)S(1)} all-to-all(f32[4,16,16,128]{3,2,1,0:T(8,128)S(1)} %first.3), channel_id=1, replica_groups=mesh['z'=4,'core'=2,'sub'=4] {'z'}, dimensions={0} | all-to-all | bytes 1048576 | tf_op jit(solution)/shard_map/all_to_all | solution.py:460
  82.2 1.9 %collective-permute-done.7 = f32[4,16,16,128]{3,2,1,0:T(8,128)S(1)} collective-permute-done((f32[4,16,16,128]{3,2,1,0:T(8,128)S(1)}, f32[4,16,16,128]{3,2,1,0:T(8,128)S(1)}, u32[]{:S(2)}, u32[]{:S(2)}) %collective-permute-start.7) | collective-permute-done | bytes 524320 | tf_op jit(solution)/shard_map/ppermute | solution.py:463
  84.1 5.6 %second.1 = (f32[4,16,16,128]{3,2,1,0:T(8,128)S(1)}, f32[128,16,128]{2,1,0:T(8,128)S(1)}, f32[16,16,128]{2,1,0:T(8,128)S(1)}, f32[16,128]{1,0:T(8,128)S(1)}, f32...) custom-call(s32[3]{0:T(128)S(1)} %pad_add_fusion.ids, ...), custom_call_target="tpu_custom_call" | custom-call | tf_op jit(solution)/shard_map/second/pallas_call | solution.py:509
  89.7 17.5 %all_to_all.26 = f32[4,16,16,128]{3,2,1,0:T(8,128)S(1)} all-to-all(f32[4,16,16,128]{3,2,1,0:T(8,128)S(1)} %get-tuple-element.15), channel_id=1, replica_groups=mesh['z'=4,'core'=2,'sub'=4] {'z'}, dimensions={0} | all-to-all | bytes 1048576 | tf_op jit(solution)/shard_map/all_to_all | solution.py:460
  107.2 1.1 collective-permute-start.9
  108.3 1.4 %collective-permute-start.10 = (f32[2,4,16,128]{3,2,1,0:T(8,128)S(1)}, f32[2,4,16,128]{3,2,1,0:T(8,128)S(1)}, u32[]{:S(2)}, u32[]{:S(2)}) collective-permute-start(f32[2,4,16,128]{3,2,1,0:T(8,128)S(1)} %get-tuple-element.21), channel_id=1, source_target_pairs={{0,2},{1,3},{2,0},{3,1},{4,6},{5,7},{6,4},{7,5},{8,10},{9,11},{10,... | collective-permute-start | bytes 196616 | tf_op jit(solution)/shard_map/ppermute | solution.py:525
  109.7 1.0 collective-permute-start.11
  110.7 7.1 %third.1 = (f32[32,2,128]{2,1,0:T(2,128)}, f32[16,16,128]{2,1,0:T(8,128)}) custom-call(s32[3]{0:T(128)S(1)} %pad_add_fusion.ids, s32[288]{0:T(512)S(1)} %positions.1.pos, f32[64,16,128]{2,1,0:T(8,128)S(1)} %bitcast.22, f32[64,16,128]{2,1,0:T(8,128)S(1)} %bitcast.26, f32[128,16,128]{2,1,0:T(8,128)S(1)} %get-tuple-element.14.basis, ...), custom_call_target="tpu_custom_call" | custom-call | tf_op jit(solution)/shard_map/third/pallas_call | solution.py:531
  117.8 3.2 %all-to-all-start.4 = ((f32[32,2,128]{2,1,0:T(2,128)}), f32[32,2,128]{2,1,0:T(2,128)S(1)}, u32[]{:S(2)}, u32[]{:S(2)}) async-start(f32[32,2,128]{2,1,0:T(2,128)} %get-tuple-element.18), calls=%async_computation.4 | async-start | bytes 65536 | tf_op jit(solution)/shard_map/all_to_all | solution.py:540
  121.0 7.3 %all-to-all-done.4.info = f32[32,2,128]{2,1,0:T(2,128)S(1)} async-done(((f32[32,2,128]{2,1,0:T(2,128)}), f32[32,2,128]{2,1,0:T(2,128)S(1)}, u32[]{:S(2)}, u32[]{:S(2)}) %all-to-all-start.4) | async-done | bytes 32800 | tf_op jit(solution)/shard_map/all_to_all | solution.py:540
  128.3 2.1 %finish.1 = f32[8,64,64]{2,1,0:T(8,128)} custom-call(s32[3]{0:T(128)S(1)} %pad_add_fusion.ids, f32[32,2,128]{2,1,0:T(2,128)S(1)} %all-to-all-done.4.info, f32[4,4,16,128]{3,2,1,0:T(8,128)} %reshape.51.turned, f32[2,4,16,128]{3,2,1,0:T(8,128)S(1)} %get-tuple-element.19.rest_0_, f32[2,4,16,128]{3,2,1,0:T(8,128)S(1)} %collective-permute-done.9.rest_1_, ...), custom_call_target="tpu_custom_call" | custom-call | tf_op jit(solution)/shard_map/finish/pallas_call | solution.py:543
  (23 shorter events, 0.5 us)
Async XLA Ops:
  1.3 17.4 %copy-start = (f32[8,64,576]{2,1,0:T(8,128)S(1)}, f32[8,64,576]{2,1,0:T(8,128)}, u32[]{:S(2)}) copy-start(f32[8,64,576]{2,1,0:T(8,128)} %rest_0_.5) | copy-start | bytes 3538948
  2.2 10.2 %all-to-all-start = ((f32[4,4,16,128]{3,2,1,0:T(8,128)}), f32[4,4,16,128]{3,2,1,0:T(8,128)S(1)}, u32[]{:S(2)}, u32[]{:S(2)}) async-start(f32[4,4,16,128]{3,2,1,0:T(8,128)} %reshape.51.turned), calls=%async_computation | async-start | bytes 262144 | tf_op jit(solution)/shard_map/all_to_all | solution.py:451
  13.8 26.0 %all-to-all-start.1 = ((f32[4,16,16,128]{3,2,1,0:T(8,128)}), f32[4,16,16,128]{3,2,1,0:T(8,128)S(1)}, u32[]{:S(2)}, u32[]{:S(2)}) async-start(f32[4,16,16,128]{3,2,1,0:T(8,128)} %broadcast_in_dim.9), calls=%async_computation.1 | async-start | bytes 1048576 | tf_op jit(solution)/shard_map/all_to_all | solution.py:460
  18.7 21.1 %copy-start.2 = (s32[256,8]{0,1:T(8,128)S(1)}, s32[256,8]{0,1:T(8,128)}, u32[]{:S(2)}) copy-start(s32[256,8]{0,1:T(8,128)} %param.7) | copy-start | bytes 24580
  18.7 21.5 %copy-start.1 = (s32[256]{0:T(256)S(1)}, s32[256]{0:T(256)}, u32[]{:S(2)}) copy-start(s32[256]{0:T(256)} %owner.1) | copy-start | bytes 3076
  19.8 17.8 %collective-permute-start.3 = (f32[4,64,576]{2,1,0:T(8,128)}, f32[4,64,576]{2,1,0:T(8,128)S(1)}, u32[]{:S(2)}, u32[]{:S(2)}) collective-permute-start(f32[4,64,576]{2,1,0:T(8,128)} %get-tuple-element.23), channel_id=1, source_target_pairs={{0,1},{1,0},{2,3},{3,2},{4,5},{5,4},{6,7},{7,6},{8,9},{9,8},{10,11... | collective-permute-start | bytes 1769480 | tf_op jit(solution)/shard_map/ppermute | solution.py:432
  20.7 17.9 %collective-permute-start.1 = (f32[4,64,576]{2,1,0:T(8,128)}, f32[4,64,576]{2,1,0:T(8,128)}, u32[]{:S(2)}, u32[]{:S(2)}) collective-permute-start(f32[4,64,576]{2,1,0:T(8,128)} %get-tuple-element.24), channel_id=1, source_target_pairs={{0,2},{1,3},{2,0},{3,1},{4,6},{5,7},{6,4},{7,5},{8,10},{9,11},{10,... | collective-permute-start | bytes 1769480 | tf_op jit(solution)/shard_map/ppermute | solution.py:433
  21.1 31.6 %collective-permute-start.6 = (f32[4,64,576]{2,1,0:T(8,128)}, f32[4,64,576]{2,1,0:T(8,128)}, u32[]{:S(2)}, u32[]{:S(2)}) collective-permute-start(f32[4,64,576]{2,1,0:T(8,128)} %get-tuple-element.23), channel_id=1, source_target_pairs={{0,2},{1,3},{2,0},{3,1},{4,6},{5,7},{6,4},{7,5},{8,10},{9,11},{10,... | collective-permute-start | bytes 1769480 | tf_op jit(solution)/shard_map/ppermute | solution.py:435
  22.8 29.9 %collective-permute-start.5 = (f32[4,64,576]{2,1,0:T(8,128)}, f32[4,64,576]{2,1,0:T(8,128)}, u32[]{:S(2)}, u32[]{:S(2)}) collective-permute-start(f32[4,64,576]{2,1,0:T(8,128)} %get-tuple-element.24), channel_id=1, source_target_pairs={{0,1},{1,0},{2,3},{3,2},{4,5},{5,4},{6,7},{7,6},{8,9},{9,8},{10,11... | collective-permute-start | bytes 1769480 | tf_op jit(solution)/shard_map/ppermute | solution.py:434
  37.6 26.0 %collective-permute-start.4 = (f32[4,64,576]{2,1,0:T(8,128)S(1)}, f32[4,64,576]{2,1,0:T(8,128)}, u32[]{:S(2)}, u32[]{:S(2)}) collective-permute-start(f32[4,64,576]{2,1,0:T(8,128)S(1)} %collective-permute-done.3.rest_2_), channel_id=1, source_target_pairs={{0,2},{1,3},{2,0},{3,1},{4,6},{5,7},{6,4},{7,5},{8,10},{9,11},{10,... | collective-permute-start | bytes 1769480 | tf_op jit(solution)/shard_map/ppermute | solution.py:468
  38.7 25.0 %collective-permute-start.2 = (f32[4,64,576]{2,1,0:T(8,128)}, f32[4,64,576]{2,1,0:T(8,128)}, u32[]{:S(2)}, u32[]{:S(2)}) collective-permute-start(f32[4,64,576]{2,1,0:T(8,128)} %collective-permute-done.1.rest_3_), channel_id=1, source_target_pairs={{0,1},{1,0},{2,3},{3,2},{4,5},{5,4},{6,7},{7,6},{8,9},{9,8},{10,11... | collective-permute-start | bytes 1769480 | tf_op jit(solution)/shard_map/ppermute | solution.py:467
  39.8 12.9 %collective-permute-start = (f32[4,16,16,128]{3,2,1,0:T(8,128)S(1)}, f32[4,16,16,128]{3,2,1,0:T(8,128)S(1)}, u32[]{:S(2)}, u32[]{:S(2)}) collective-permute-start(f32[4,16,16,128]{3,2,1,0:T(8,128)S(1)} %all-to-all-done.1), channel_id=1, source_target_pairs={{0,4},{4,0},{1,5},{5,1},{2,6},{6,2},{3,7},{7,3},{8,12},{12,8},{9,1... | collective-permute-start | bytes 1572872 | tf_op jit(solution)/shard_map/ppermute | solution.py:463
  82.2 1.9 %collective-permute-start.7 = (f32[4,16,16,128]{3,2,1,0:T(8,128)S(1)}, f32[4,16,16,128]{3,2,1,0:T(8,128)S(1)}, u32[]{:S(2)}, u32[]{:S(2)}) collective-permute-start(f32[4,16,16,128]{3,2,1,0:T(8,128)S(1)} %all_to_all.25), channel_id=1, source_target_pairs={{0,4},{4,0},{1,5},{5,1},{2,6},{6,2},{3,7},{7,3},{8,12},{12,8},{9,1... | collective-permute-start | bytes 1572872 | tf_op jit(solution)/shard_map/ppermute | solution.py:463
  107.2 3.5 %collective-permute-start.8 = (f32[4,16,16,128]{3,2,1,0:T(8,128)S(1)}, f32[4,16,16,128]{3,2,1,0:T(8,128)S(1)}, u32[]{:S(2)}, u32[]{:S(2)}) collective-permute-start(f32[4,16,16,128]{3,2,1,0:T(8,128)S(1)} %all_to_all.26), channel_id=1, source_target_pairs={{0,4},{4,0},{1,5},{5,1},{2,6},{6,2},{3,7},{7,3},{8,12},{12,8},{9,1... | collective-permute-start | bytes 1572872 | tf_op jit(solution)/shard_map/ppermute | solution.py:463
  107.2 13.8 %collective-permute-start.9 = (f32[2,4,16,128]{3,2,1,0:T(8,128)}, f32[2,4,16,128]{3,2,1,0:T(8,128)S(1)}, u32[]{:S(2)}, u32[]{:S(2)}) collective-permute-start(f32[2,4,16,128]{3,2,1,0:T(8,128)} %get-tuple-element.20), channel_id=1, source_target_pairs={{0,1},{1,0},{2,3},{3,2},{4,5},{5,4},{6,7},{7,6},{8,9},{9,8},{10,11... | collective-permute-start | bytes 196616 | tf_op jit(solution)/shard_map/ppermute | solution.py:525
  108.3 12.7 %collective-permute-start.10 = (f32[2,4,16,128]{3,2,1,0:T(8,128)S(1)}, f32[2,4,16,128]{3,2,1,0:T(8,128)S(1)}, u32[]{:S(2)}, u32[]{:S(2)}) collective-permute-start(f32[2,4,16,128]{3,2,1,0:T(8,128)S(1)} %get-tuple-element.21), channel_id=1, source_target_pairs={{0,2},{1,3},{2,0},{3,1},{4,6},{5,7},{6,4},{7,5},{8,10},{9,11},{10,... | collective-permute-start | bytes 196616 | tf_op jit(solution)/shard_map/ppermute | solution.py:525
  109.7 11.3 %collective-permute-start.11 = (f32[2,4,16,128]{3,2,1,0:T(8,128)S(1)}, f32[2,4,16,128]{3,2,1,0:T(8,128)S(1)}, u32[]{:S(2)}, u32[]{:S(2)}) collective-permute-start(f32[2,4,16,128]{3,2,1,0:T(8,128)S(1)} %get-tuple-element.22), channel_id=1, source_target_pairs={{0,3},{1,2},{2,1},{3,0},{4,7},{5,6},{6,5},{7,4},{8,11},{9,10},{10,... | collective-permute-start | bytes 196616 | tf_op jit(solution)/shard_map/ppermute | solution.py:525
  117.8 10.5 %all-to-all-start.4 = ((f32[32,2,128]{2,1,0:T(2,128)}), f32[32,2,128]{2,1,0:T(2,128)S(1)}, u32[]{:S(2)}, u32[]{:S(2)}) async-start(f32[32,2,128]{2,1,0:T(2,128)} %get-tuple-element.18), calls=%async_computation.4 | async-start | bytes 65536 | tf_op jit(solution)/shard_map/all_to_all | solution.py:540

commit v3 on v2

v3 whole, which is shorter than its diff:
```python
import functools

import jax
import jax.numpy as jnp
from jax import lax
from jax.experimental import pallas as pl
from jax.experimental.pallas import tpu as pltpu
from jax.sharding import Mesh
from jax.sharding import PartitionSpec as P


F32 = jnp.float32
BF16 = jnp.bfloat16
CORES = 2
VMEM = pl.BlockSpec(memory_space=pltpu.VMEM)
SMEM = pl.BlockSpec(memory_space=pltpu.SMEM)
HBM = pl.BlockSpec(memory_space=pltpu.HBM)
ANY = pl.BlockSpec(memory_space=pl.ANY)
PARAMS = pltpu.CompilerParams(vmem_limit_bytes=20 * 1024 * 1024)
SMALL = pltpu.CompilerParams(vmem_limit_bytes=4 * 1024 * 1024)


def divide(value, size):
    if size & (size - 1):
        return lax.div(value, jnp.int32(size))
    return lax.shift_right_logical(value, jnp.int32(size.bit_length() - 1))


def remain(value, size):
    if size & (size - 1):
        return lax.rem(value, jnp.int32(size))
    return value & (size - 1)


def low_half(shape, dof):
    return lax.broadcasted_iota(jnp.int32, shape, 1) < dof


def lane_sum(values):
    return jnp.sum(values, axis=1, keepdims=True)


def split_bf16(values):
    high = values.astype(BF16)
    return high, (values - high.astype(F32)).astype(BF16)


def place(columns, shape):
    lane = lax.broadcasted_iota(jnp.int32, shape, 1)
    packed = jnp.zeros(shape, F32)
    for index, column in enumerate(columns):
        packed = jnp.where(lane == index, column, packed)
    return packed


def dense_rows(columns, shape, rows):
    size, lanes = shape
    per_row = lanes // size
    flipped = place(columns, shape).T
    lane = lax.broadcasted_iota(jnp.int32, (1, lanes), 1)
    wide = jnp.concatenate([flipped] * per_row, axis=1)
    packed = []
    for row in range(rows):
        line = jnp.zeros((1, lanes), F32)
        for inner in range(per_row):
            index = row * per_row + inner
            if index < len(columns):
                line = jnp.where(divide(lane, size) == inner, wide[index : index + 1], line)
        packed.append(line)
    return jnp.concatenate(packed, axis=0)


def position_kernel(geometry, ids, owner, table, out, where):
    per_dev, n_sub, nz, hops = geometry
    me_z, me_c, me_s = ids[0], ids[1], ids[2]
    sites = owner.shape[0]

    def locate(slot):
        dev = divide(slot, per_dev)
        grp = divide(dev, n_sub)
        block = (remain(grp, CORES) ^ me_c) * nz + (divide(grp, CORES) ^ me_z)
        return (block * n_sub + (remain(dev, n_sub) ^ me_s)) * per_dev + remain(slot, per_dev)

    def fill(slot, carry):
        where[owner[slot]] = locate(slot)
        return carry

    lax.fori_loop(0, sites, fill, 0, unroll=8)

    def look(local, carry):
        dev = (me_z * CORES + me_c) * n_sub + (divide(local, per_dev) ^ me_s)
        slot = dev * per_dev + remain(local, per_dev)
        base = owner[slot] * hops
        out[local * (hops + 1)] = locate(slot)
        for hop in range(hops):
            out[local * (hops + 1) + 1 + hop] = where[table[base + hop]]
        return carry

    lax.fori_loop(0, n_sub * per_dev, look, 0, unroll=2)


def pack_kernel(dof, op, right, low, high, turned, held, op_held, sems):
    half = op.shape[0] // 2
    sources = [right, op.at[pl.ds(0, half)], op.at[pl.ds(half, half)]]
    copies = start_copies(sources, [held, op_held.at[0], op_held.at[1]], sems)
    n_sub, per_part, rhs = turned.shape[0], turned.shape[1], turned.shape[2]
    copies[0].wait()
    for pair in range(per_part):
        both = jnp.concatenate([held[2 * pair], held[2 * pair + 1]], axis=0).T
        for quarter in range(n_sub):
            turned[quarter, pair] = both[quarter * rhs : (quarter + 1) * rhs]
    main = op.shape[2] - dof
    for index, target in enumerate((low, high)):
        copies[index + 1].wait()
        for pair in range(half // 2):
            even, odd = op_held[index, 2 * pair], op_held[index, 2 * pair + 1]
            target[pair, :, :main] = even[:, :main]
            target[pair, :, main : 2 * main] = odd[:, :main]
            target[pair, :, 2 * main :] = jnp.concatenate([even[:, main:], odd[:, main:]], axis=1)


def spread(dup, pair, values, dof):
    mask = low_half(values.shape, dof)
    rolled = pltpu.roll(values, dof, 1)
    dup[2 * pair] = jnp.where(mask, values, rolled)
    dup[2 * pair + 1] = jnp.where(mask, rolled, values)


def site_product(stacked, local, pos, dup, terms, dof):
    rows = dup.shape[1]
    mask = low_half((rows, 2 * dof), dof)
    tiles = []
    for first in range(0, terms - 1, 2):
        left = dup[pos[local * terms + first]]
        right = dup[pos[local * terms + first + 1]]
        tiles.append(jnp.where(mask, left, right))
    if terms % 2:
        tiles.append(dup[pos[local * terms + terms - 1]][:, :dof])
    high, low = split_bf16(jnp.concatenate(tiles, axis=1))
    product = lax.dot_general(
        jnp.concatenate([high, low], axis=0),
        stacked,
        (((1,), (1,)), ((), ())),
        preferred_element_type=F32,
    )
    total = product[:rows] + product[rows:]
    return total + pltpu.roll(total, dof, 1)


def stack_split(op):
    high, low = split_bf16(op)
    return jnp.concatenate([high, low], axis=0)


def pair_product(stacks, local, pos, dup, terms, dof):
    even, odd = (
        site_product(stack, local + i, pos, dup, terms, dof) for i, stack in enumerate(stacks)
    )
    return jnp.where(low_half(even.shape, dof), even, odd)


def apply_rows(stages, pos, dup, terms, dof, put):
    base = 0
    for stage in stages:

        def body(pair, carry, base=base, stage=stage):
            stacks = [stage[2 * pair], stage[2 * pair + 1]]
            put(base // 2 + pair, pair_product(stacks, base + 2 * pair, pos, dup, terms, dof))
            return carry

        lax.fori_loop(0, stage.shape[0] // 2, body, 0, unroll=4)
        base += stage.shape[0]


def split_rows(ops, split, base, pos, dup, terms, dof, put):
    offset = 0
    if ops[0].shape[2] == terms * dof:
        flat = [(op, i) for op in ops for i in range(op.shape[0])]
        for pair in range(len(flat) // 2):
            stacks = [stack_split(op[i]) for op, i in flat[2 * pair : 2 * pair + 2]]
            split[2 * pair], split[2 * pair + 1] = stacks
            put((base + 2 * pair) // 2, pair_product(stacks, base + 2 * pair, pos, dup, terms, dof))
        return
    for op in ops:
        main = op.shape[2] // 2 - dof

        def body(pair, carry, offset=offset, op=op, main=main):
            rows = op[pair]
            tail = rows[:, 2 * main :]
            even = jnp.concatenate([rows[:, :main], tail[:, :dof]], axis=1)
            odd = jnp.concatenate([rows[:, main : 2 * main], tail[:, dof:]], axis=1)
            stacks = [stack_split(even), stack_split(odd)]
            split[offset + 2 * pair], split[offset + 2 * pair + 1] = stacks
            local = base + offset + 2 * pair
            put(divide(local, 2), pair_product(stacks, local, pos, dup, terms, dof))
            return carry

        lax.fori_loop(0, op.shape[0], body, 0, unroll=True)
        offset += 2 * op.shape[0]


def start_copies(sources, targets, sems):
    copies = [
        pltpu.make_async_copy(source, target, sems.at[index])
        for index, (source, target) in enumerate(zip(sources, targets))
    ]
    for copy in copies:
        copy.start()
    return copies


def over_pairs(fields, step, init):
    n_pair = fields[0].shape[0]
    for block in range(len(fields)):
        init = lax.fori_loop(
            0, n_pair, lambda pair, carry, block=block: step(block, pair, carry), init, unroll=8
        )
    return init


def share_out(values, shares):
    for index, share in enumerate(shares):
        for inner in range(share.shape[0]):
            share[inner] = values[index * share.shape[0] + inner]


def first_kernel(n_field, count, dof, terms, pos, *rest):
    fields, ops, rest = rest[:n_field], rest[n_field : n_field + count], rest[n_field + count :]
    out, split, dup = rest[:3]
    held, sems = rest[3 : count + 3], rest[count + 3]
    copies = start_copies(ops, held, sems)
    n_pair = fields[0].shape[0]

    def build(block, pair, carry):
        spread(dup, block * n_pair + pair, fields[block][pair], dof)
        return carry

    over_pairs(fields, build, 0)
    for copy in copies:
        copy.wait()

    def put(pair, values):
        out[pair] = values

    split_rows(held, split, 0, pos, dup, terms, dof, put)


def more_kernel(count, dof, terms, pos, dup, before, *rest):
    ops, out, split, shares = rest[:count], rest[count], rest[count + 1], rest[count + 2 :]
    base = 2 * before.shape[0]
    for pair in range(before.shape[0]):
        out[pair] = before[pair]

    def put(pair, values):
        out[pair] = values

    split_rows(ops, split, base, pos, dup, terms, dof, put)
    share_out(out, shares)


def second_kernel(n_field, count, sends, dof, terms, pos, *rest):
    b_ref, z_ref, rest = rest[:n_field], rest[n_field : 2 * n_field], rest[2 * n_field :]
    stages, (out, basis, mine, coeffs) = rest[:count], rest[count : count + 4]
    shares, dup = rest[count + 4 : count + 4 + sends], rest[count + 4 + sends]
    n_pair = b_ref[0].shape[0]
    shape = b_ref[0].shape[1:]
    zero = jnp.zeros(shape, F32)

    def dots(block, pair, carry):
        b, z = b_ref[block][pair], z_ref[block][pair]
        return carry[0] + b * b, carry[1] + b * z

    norm, cross = over_pairs(b_ref, dots, (zero, zero))
    beta = jnp.sqrt(lane_sum(norm))
    scale = 1.0 / beta
    h00 = lane_sum(cross) * scale * scale

    def remove(block, pair, carry):
        w = z_ref[block][pair] * scale - (h00 * scale) * b_ref[block][pair]
        basis[block * n_pair + pair] = w
        return carry + w * w

    h10 = jnp.sqrt(lane_sum(over_pairs(b_ref, remove, zero)))
    unit = 1.0 / h10

    def build(block, pair, carry):
        v = basis[block * n_pair + pair] * unit
        basis[block * n_pair + pair] = v
        spread(dup, block * n_pair + pair, v, dof)
        return carry

    over_pairs(b_ref, build, 0)
    coeffs[...] = place([beta, h00, h10], shape)
    mine[...] = basis[:n_pair]

    def put(pair, values):
        out[pair] = values

    apply_rows(stages, pos, dup, terms, dof, put)
    share_out(out, shares)


def third_kernel(n_field, count, dof, terms, pos, basis, v1_mine, coeffs, *rest):
    b_ref, z_ref, rest = rest[:n_field], rest[n_field : 2 * n_field], rest[2 * n_field :]
    stages, (sums, mine, dup, work, image) = rest[:count], rest[count:]
    b_mine = b_ref[0]
    n_pair = b_mine.shape[0]
    shape = b_mine.shape[1:]
    zero = jnp.zeros(shape, F32)
    known = coeffs[...]
    scale = 1.0 / known[:, 0:1]

    def dots(block, pair, carry):
        z = z_ref[block][pair]
        return carry[0] + b_ref[block][pair] * z, carry[1] + basis[block * n_pair + pair] * z

    first, second = over_pairs(b_ref, dots, (zero, zero))
    h01 = lane_sum(first) * scale
    h11 = lane_sum(second)

    def remove(block, pair, carry):
        w = (
            z_ref[block][pair]
            - (h01 * scale) * b_ref[block][pair]
            - h11 * basis[block * n_pair + pair]
        )
        work[block * n_pair + pair] = w
        return carry + w * w

    h21 = jnp.sqrt(lane_sum(over_pairs(b_ref, remove, zero)))
    unit = 1.0 / h21

    def build(block, pair, carry):
        v = work[block * n_pair + pair] * unit
        work[block * n_pair + pair] = v
        spread(dup, block * n_pair + pair, v, dof)
        return carry

    over_pairs(b_ref, build, 0)
    mine[...] = work[:n_pair]

    def put(pair, values):
        image[pair] = values

    apply_rows(stages, pos, dup, terms, dof, put)

    def last(pair, carry):
        u = image[pair]
        return (
            carry[0] + b_mine[pair] * u,
            carry[1] + v1_mine[pair] * u,
            carry[2] + mine[pair] * u,
            carry[3] + u * u,
        )

    parts = lax.fori_loop(0, n_pair, last, (zero, zero, zero, zero), unroll=True)
    solved = [known[:, 0:1], known[:, 1:2], known[:, 2:3], h01, h11, h21]
    columns = [lane_sum(part) for part in parts] + solved
    if len(sums.shape) == 3 and sums.shape[1:] == shape:
        packed = place(columns, shape)
    else:
        packed = dense_rows(columns, shape, sums.shape[1])
    for block in range(sums.shape[0]):
        sums[block] = packed


def weigh(values):
    d02, h12, h22, g22, beta, h00, h10, h01, h11, h21 = values
    scale = 1.0 / beta
    h02 = d02 * scale
    g00 = h00 * h00 + h10 * h10
    g01 = h00 * h01 + h10 * h11
    g02 = h00 * h02 + h10 * h12
    g11 = h01 * h01 + h11 * h11 + h21 * h21
    g12 = h01 * h02 + h11 * h12 + h21 * h22
    inv0 = 1.0 / g00
    l10 = g01 * inv0
    l20 = g02 * inv0
    d1 = g11 - l10 * g01
    e21 = g12 - l20 * g01
    inv1 = 1.0 / d1
    l21 = e21 * inv1
    d2 = g22 - l20 * g02 - l21 * e21
    r0 = beta * h00
    r1 = beta * h01 - l10 * r0
    r2 = beta * h02 - l20 * r0 - l21 * r1
    y2 = r2 / d2
    y1 = r1 * inv1 - l21 * y2
    y0 = r0 * inv0 - l10 * y1 - l20 * y2
    return scale, y0, y1, y2


def combine_kernel(sums, b_mine, v1_mine, v2_mine, out):
    total = sums[0]
    for block in range(1, sums.shape[0]):
        total = total + sums[block]
    known = sums[0]
    values = [(total if i < 4 else known)[:, i : i + 1] for i in range(10)]
    scale, y0, y1, y2 = weigh(values)
    for pair in range(b_mine.shape[0]):
        out[pair] = (y0 * scale) * b_mine[pair] + y1 * v1_mine[pair] + y2 * v2_mine[pair]


def finish_kernel(dof, ids, info, turned, *rest):
    out, stack, factor = rest[-3:]
    n_sub, per_part, rhs, lanes = turned.shape
    z1, z2 = rest[:n_sub], rest[n_sub : 2 * n_sub]
    per_row = lanes // rhs
    n_rows = info.shape[1]
    first = [info[quarter] for quarter in range(n_sub)]
    total = list(first)
    for block in range(1, info.shape[0] // n_sub):
        for quarter in range(n_sub):
            total[quarter] = total[quarter] + info[block * n_sub + quarter]
    known = [jnp.concatenate([f[r : r + 1] for f in first], axis=0) for r in range(n_rows)]
    added = [jnp.concatenate([t[r : r + 1] for t in total], axis=0) for r in range(n_rows)]
    values = []
    for index in range(10):
        source = (added if index < 4 else known)[index // per_row]
        shift = rhs * (index % per_row)
        values.append(pltpu.roll(source, lanes - shift, 1) if shift else source)
    scale, y0, y1, y2 = weigh(values)
    h00, h10, h01, h11, h21 = values[5:]
    gamma = y2 / h21
    both = (y1 - gamma * h11) / h10
    coeffs = [(y0 - both * h00 - gamma * h01) * scale, both * scale, gamma]
    flipped = jnp.concatenate(coeffs, axis=0)
    spare = -flipped.shape[0] % 8
    if spare:
        flipped = jnp.concatenate([flipped, jnp.zeros((spare, lanes), F32)], axis=0)
    flipped = flipped.T
    for index in range(3 * n_sub):
        factor[index] = jnp.broadcast_to(flipped[:rhs, index : index + 1], (rhs, lanes))
    for k in range(n_sub):
        quarter = ids[2] ^ k
        alpha, beta, gamma = (factor[part * n_sub + quarter] for part in range(3))
        start = pl.multiple_of(quarter * rhs, 8)
        for pair in range(per_part):
            mixed = alpha * turned[quarter, pair] + beta * z1[k][pair]
            stack[pair, pl.ds(start, rhs), :] = mixed + gamma * z2[k][pair]
    for pair in range(per_part):
        both = stack[pair].T
        out[2 * pair] = both[:dof]
        out[2 * pair + 1] = both[dof:]


def per_device(coarse_op, right_side, owner_map, neighbor_table):
    nz = lax.axis_size("z")
    n_sub = lax.axis_size("sub")
    per_dev, dof, width = coarse_op.shape
    terms = width // dof
    hops = terms - 1
    rhs = right_side.shape[2] // n_sub
    n_loc = n_sub * per_dev
    n_own = n_loc // 2
    me_z, me_c, me_s = lax.axis_index("z"), lax.axis_index("core"), lax.axis_index("sub")
    ids = jnp.stack([me_z, me_c, me_s]).astype(jnp.int32)
    even = per_dev % 2 == 0
    lanes = 2 * dof
    field = (n_own, rhs, lanes)

    relay = n_sub == 4 and per_dev % 4 == 0 and terms % 2 == 1
    order = jnp.arange(n_sub, dtype=jnp.int32) ^ me_s
    hops_to = [[(s, s ^ k) for s in range(n_sub)] for k in range(n_sub)]
    half = per_dev // 2
    if relay:
        halves = [jax.ShapeDtypeStruct((half // 2, dof, 2 * width), F32)] * 2
        op_low, op_high, turned = pl.pallas_call(
            functools.partial(pack_kernel, dof),
            out_shape=halves + [jax.ShapeDtypeStruct((n_sub, half, rhs, lanes), F32)],
            in_specs=[HBM, HBM],
            out_specs=[VMEM] * 3,
            scratch_shapes=[
                pltpu.VMEM(right_side.shape, F32),
                pltpu.VMEM((2, half, dof, width), F32),
                pltpu.SemaphoreType.DMA((3,)),
            ],
            compiler_params=SMALL,
            name="pack",
        )(coarse_op, right_side)
        x_high = lax.ppermute(op_high, "sub", hops_to[1])
        y_low = lax.ppermute(op_low, "sub", hops_to[2])
        x_low = lax.ppermute(op_low, "sub", hops_to[1])
        y_high = lax.ppermute(op_high, "sub", hops_to[2])

    positions = pl.pallas_call(
        functools.partial(position_kernel, (per_dev, n_sub, nz, hops)),
        out_shape=jax.ShapeDtypeStruct((n_loc * terms,), jnp.int32),
        in_specs=[SMEM, SMEM, SMEM],
        out_specs=SMEM,
        scratch_shapes=[pltpu.SMEM((owner_map.shape[0],), jnp.int32)],
        compiler_params=SMALL,
        name="positions",
    )(ids, owner_map, neighbor_table.reshape(-1))

    if not relay:
        turned = right_side.reshape(per_dev, dof, n_sub, rhs).transpose(2, 0, 3, 1)
    if even and not relay:
        turned = turned.reshape(n_sub, per_dev // 2, 2, rhs, dof).transpose(0, 1, 3, 2, 4)
        turned = turned.reshape(n_sub, per_dev // 2, rhs, lanes)
    mine = lax.all_to_all(turned, "sub", split_axis=0, concat_axis=0, tiled=True)
    mine = mine[order]
    if not even:
        mine = mine.reshape(n_own, 2, rhs, dof).transpose(0, 2, 1, 3)
    b_mine = mine.reshape(field)

    swap = [(c, c ^ 1) for c in range(CORES)]

    def step_z(own, offset):
        return lax.ppermute(own, "z", [(z, z ^ offset) for z in range(nz)])

    def gather(own):
        direct = (2, 1) if nz == 4 else range(1, nz)
        found = {offset: step_z(own, offset) for offset in direct}
        if nz == 4:
            found[3] = step_z(found[2], 1)
        parts = [own] + [found[offset] for offset in range(1, nz)]
        return parts + [lax.ppermute(part, "core", swap) for part in parts]

    if relay:
        d_low = lax.ppermute(y_low, "sub", hops_to[1])
        d_high = lax.ppermute(x_high, "sub", hops_to[2])
        stages = [[op_low, op_high, x_low, x_high, y_low, y_high], [d_low, d_high]]
    if not relay:
        every = lax.all_gather(coarse_op, "sub", axis=0)[order]
        stages = [[every[k] for k in range(n_sub)]]
    b_parts = gather(b_mine)
    n_field = len(b_parts)
    dup = (CORES * nz * n_loc, rhs, lanes)
    full = (CORES * nz * n_own,) + field[1:]
    small = jax.ShapeDtypeStruct(field[1:], F32)
    own_shape = jax.ShapeDtypeStruct(field, F32)
    sends = n_sub if even else 0
    share = [jax.ShapeDtypeStruct((per_dev // 2, rhs, lanes), F32)] * sends

    def split_shape(sites):
        return jax.ShapeDtypeStruct((sites, 2 * dof, width), BF16)

    ops = stages[0]
    rows = sum(op.shape[0] * op.shape[2] // width for op in ops)
    z1, split, spread_b = pl.pallas_call(
        functools.partial(first_kernel, n_field, len(ops), dof, terms),
        out_shape=[
            jax.ShapeDtypeStruct((rows // 2,) + field[1:], F32),
            split_shape(rows),
            jax.ShapeDtypeStruct(dup, F32),
        ],
        in_specs=[SMEM] + [VMEM] * n_field + [ANY] * len(ops),
        out_specs=[VMEM] * 3,
        scratch_shapes=[pltpu.VMEM(op.shape, F32) for op in ops]
        + [pltpu.SemaphoreType.DMA((len(ops),))],
        compiler_params=PARAMS,
        name="first",
    )(positions, *b_parts, *ops)
    splits, shares1 = [split], []
    if relay:
        ops = stages[1]
        z1, split, *shares1 = pl.pallas_call(
            functools.partial(more_kernel, len(ops), dof, terms),
            out_shape=[own_shape, split_shape(n_loc - rows)] + share,
            in_specs=[SMEM, VMEM, VMEM] + [VMEM] * len(ops),
            out_specs=[VMEM] * (2 + sends),
            compiler_params=PARAMS,
            name="more",
        )(positions, spread_b, z1, *ops)
        splits.append(split)
    elif even:
        shares1 = [z1[k * per_dev // 2 : (k + 1) * per_dev // 2] for k in range(n_sub)]
    count = len(splits)

    def send(shares):
        return shares[:1] + [lax.ppermute(shares[k], "sub", hops_to[k]) for k in range(1, sends)]

    z1_parts = gather(z1)
    shares1 = send(shares1)

    z2, basis, v1_mine, coeffs, *shares2 = pl.pallas_call(
        functools.partial(second_kernel, n_field, count, sends, dof, terms),
        out_shape=[own_shape, jax.ShapeDtypeStruct(full, F32), own_shape, small] + share,
        in_specs=[SMEM] + [VMEM] * (2 * n_field + count),
        out_specs=[VMEM] * (4 + sends),
        scratch_shapes=[pltpu.VMEM(dup, F32)],
        compiler_params=PARAMS,
        name="second",
    )(positions, *b_parts, *z1_parts, *splits)
    z2_parts = gather(z2)
    shares2 = send(shares2)
    z2_parts, shares1, shares2 = lax.optimization_barrier((z2_parts, shares1, shares2))

    axes = ("z", "core", "sub") if even else ("z", "core")
    copies = nz * CORES * (n_sub if even else 1)
    note = (pl.cdiv(10 * rhs, lanes), lanes) if even else field[1:]
    sums, v2_mine = pl.pallas_call(
        functools.partial(third_kernel, n_field, count, dof, terms),
        out_shape=[jax.ShapeDtypeStruct((copies,) + note, F32), own_shape],
        in_specs=[SMEM] + [VMEM] * (3 + 2 * n_field + count),
        out_specs=[VMEM] * 2,
        scratch_shapes=[pltpu.VMEM(dup, F32), pltpu.VMEM(full, F32), pltpu.VMEM(field, F32)],
        compiler_params=PARAMS,
        name="third",
    )(positions, basis, v1_mine, coeffs, *b_parts, *z2_parts, *splits)
    sums = lax.all_to_all(sums, axes, split_axis=0, concat_axis=0, tiled=True)

    if even:
        return pl.pallas_call(
            functools.partial(finish_kernel, dof),
            out_shape=jax.ShapeDtypeStruct(right_side.shape, F32),
            in_specs=[SMEM] + [VMEM] * (2 + 2 * sends),
            out_specs=VMEM,
            scratch_shapes=[
                pltpu.VMEM((per_dev // 2, n_sub * rhs, lanes), F32),
                pltpu.VMEM((3 * n_sub, rhs, lanes), F32),
            ],
            compiler_params=SMALL,
            name="finish",
        )(ids, sums, turned, *shares1, *shares2)
    result = pl.pallas_call(
        combine_kernel,
        out_shape=own_shape,
        in_specs=[VMEM] * 4,
        out_specs=VMEM,
        compiler_params=SMALL,
            name="combine",
    )(sums, b_mine, v1_mine, v2_mine)
    result = result.reshape(n_own, rhs, 2, dof).transpose(0, 2, 1, 3)
    result = result.reshape(n_sub, per_dev, rhs, dof)[order]
    result = lax.all_to_all(result, "sub", split_axis=0, concat_axis=0, tiled=True)
    return result.transpose(1, 3, 0, 2).reshape(right_side.shape)


def solution(mesh):
    n_grp, n_sub = mesh.shape["grp"], mesh.shape["sub"]
    inner = Mesh(mesh.devices.reshape(n_grp // CORES, CORES, n_sub), ("z", "core", "sub"))
    split = P(("z", "core", "sub"), None, None)

    return jax.shard_map(
        per_device,
        mesh=inner,
        in_specs=(split, split, P(), P()),
        out_specs=split,
        check_vma=False,
    )
```

time: 131 us -> 129 us (0.985)
  blocking collectives: 33.4 us -> 11.3 us
  starting transfers between devices: 22.9 us -> 35.3 us
  waiting for transfers between devices: 44.4 us -> 53.5 us
  local copies, waits for them, and re-layouts: 4.94 us -> 3.06 us
    ppermute x6 -> x27, waiting for transfers between devices: 1.92 us -> 35.7 us  [the longest x9 17 us: step_z(): return lax.ppermute(own, 'z', [(z, z ^ offset) for z in range(nz)])]
    all_to_all x2 -> x1, blocking collectives: 33.4 us -> 11.3 us  [per_device(): sums = lax.all_to_all(sums, axes, split_axis=0, concat_axis=0, tiled=True)]
    ppermute x6 -> x27, starting transfers between devices: 3.5 us -> 23.4 us  [the longest x9 16.9 us: step_z(): return lax.ppermute(own, 'z', [(z, z ^ offset) for z in range(nz)])]
    ppermute x1, waiting for transfers between devices: 13.8 us -> 0.01 us  [per_device(): x_high = lax.ppermute(op_high, 'sub', hops_to[1])]
    ppermute x1, waiting for transfers between devices: 9.26 us -> 0.56 us  [per_device(): y_high = lax.ppermute(op_high, 'sub', hops_to[2])]
    all_to_all x2 -> x0, starting transfers between devices: 8.1 us -> none  [the longest x1 4.87 us: over_z(): return lax.all_to_all(copies, 'z', split_axis=0, concat_axis=0, tiled=True)]
    all_to_all x2 -> x0, waiting for transfers between devices: 7.27 us -> none  [the longest x1 7.27 us: per_device(): sums = lax.all_to_all(sums, axes, split_axis=0, concat_axis=0, tiled=True)]
    ppermute x1, waiting for transfers between devices: 7.08 us -> 0.01 us  [per_device(): d_high = lax.ppermute(x_high, 'sub', hops_to[2])]
  transfers between devices with their start and end apart: 15 -> 34, of which waited for: 7 -> 19; matrix products, arithmetic and copies ran while one was open for 1% -> 1% of each run, Pallas kernels for 11% -> 6%
where the time goes in v3:
time: 129 us
  waiting for transfers between devices  53.5 us (41%)
  starting transfers between devices  35.3 us (27%)
  Pallas kernels  25.4 us (20%)
  blocking collectives  11.3 us (9%)
  local copies, waits for them, and re-layouts  3.06 us (2%)
    ppermute x9, waiting for transfers between devices, step_z(): return lax.ppermute(own, 'z', [(z, z ^ offset) for z in range(nz)])  17 us
    ppermute x9, starting transfers between devices, step_z(): return lax.ppermute(own, 'z', [(z, z ^ offset) for z in range(nz)])  16.9 us
    ppermute x6, waiting for transfers between devices, send(): lax.ppermute(shares[k], 'sub', hops_to[k])  14.9 us
    all_to_all x1, waiting for transfers between devices, per_device(): lax.all_to_all(turned, 'sub', split_axis=0, concat_axis=0, tiled=True)  11.3 us
    all_to_all x1, blocking collectives, per_device(): sums = lax.all_to_all(sums, axes, split_axis=0, concat_axis=0, tiled=True)  11.3 us
    pallas_call x1, Pallas kernels, per_device(): pl.pallas_call(functools.partial(third_kernel, n_field, count, dof, terms...  7.28 us
    ppermute x1, waiting for transfers between devices, per_device(): d_low = lax.ppermute(y_low, 'sub', hops_to[1])  5.18 us
    pallas_call x1, Pallas kernels, per_device(): pl.pallas_call(functools.partial(second_kernel, n_field, count, sends, do...  5.15 us
  transfers between devices with their start and end apart: 34, of which 19 were waited for; matrix products, arithmetic and copies ran while one was open for 1% of the time, Pallas kernels for 6%

profile of v3, /device:TPU:0, one launch (start us, length us, event | category | flops | bytes accessed | tf_op | source)
XLA Modules:
  0.0 128.8 jit_solution(15605091851587505607)
XLA Ops:
  2.3 1.4 %pack.1 = (f32[2,64,1152]{2,1,0:T(8,128)S(1)}, f32[2,64,1152]{2,1,0:T(8,128)S(1)}, f32[4,4,16,128]{3,2,1,0:T(8,128)}) custom-call(f32[8,64,576]{2,1,0:T(8,128)S(1)} %copy-done, f32[8,64,64]{2,1,0:T(8,128)S(1)} %copy-done.1), custom_call_target="tpu_custom_call" | custom-call | tf_op jit(solution)/shard_map/pack/pallas_call | solution.py:468
  3.7 3.1 %collective-permute-start.9 = (f32[2,64,1152]{2,1,0:T(8,128)S(1)}, f32[2,64,1152]{2,1,0:T(8,128)S(1)}, u32[]{:S(2)}, u32[]{:S(2)}) collective-permute-start(f32[2,64,1152]{2,1,0:T(8,128)S(1)} %get-tuple-element.43.rest_8_), channel_id=1, source_target_pairs={{0,2},{1,3},{2,0},{3,1},{4,6},{5,7},{6,4},{7,5},{8,10},{9,11},{10,... | collective-permute-start | bytes 1769480 | tf_op jit(solution)/shard_map/ppermute | solution.py:482
  6.7 1.5 %collective-permute-start.8 = (f32[2,64,1152]{2,1,0:T(8,128)S(1)}, f32[2,64,1152]{2,1,0:T(8,128)S(1)}, u32[]{:S(2)}, u32[]{:S(2)}) collective-permute-start(f32[2,64,1152]{2,1,0:T(8,128)S(1)} %get-tuple-element.44.rest_9_), channel_id=1, source_target_pairs={{0,1},{1,0},{2,3},{3,2},{4,5},{5,4},{6,7},{7,6},{8,9},{9,8},{10,11... | collective-permute-start | bytes 1769480 | tf_op jit(solution)/shard_map/ppermute | solution.py:481
  8.2 3.3 %all-to-all-start = ((f32[4,4,16,128]{3,2,1,0:T(8,128)}), f32[4,4,16,128]{3,2,1,0:T(8,128)S(1)}, u32[]{:S(2)}, u32[]{:S(2)}) async-start(f32[4,4,16,128]{3,2,1,0:T(8,128)} %get-tuple-element.42.turned), calls=%async_computation | async-start | bytes 262144 | tf_op jit(solution)/shard_map/all_to_all | solution.py:501
  11.6 11.3 %all-to-all-done = f32[4,4,16,128]{3,2,1,0:T(8,128)S(1)} async-done(((f32[4,4,16,128]{3,2,1,0:T(8,128)}), f32[4,4,16,128]{3,2,1,0:T(8,128)S(1)}, u32[]{:S(2)}, u32[]{:S(2)}) %all-to-all-start) | async-done | bytes 131104 | tf_op jit(solution)/shard_map/all_to_all | solution.py:501
  23.5 2.7 %collective-permute-start.1 = (f32[16,16,128]{2,1,0:T(8,128)S(1)}, f32[16,16,128]{2,1,0:T(8,128)S(1)}, u32[]{:S(2)}, u32[]{:S(2)}) collective-permute-start(f32[16,16,128]{2,1,0:T(8,128)S(1)} %bitcast.6), channel_id=1, source_target_pairs={{0,16},{8,24},{16,0},{24,8},{1,17},{9,25},{17,1},{25,9},{2,18},{10... | collective-permute-start | bytes 393224 | tf_op jit(solution)/shard_map/ppermute | solution.py:510
  26.1 1.6 %collective-permute-start = (f32[16,16,128]{2,1,0:T(8,128)S(1)}, f32[16,16,128]{2,1,0:T(8,128)S(1)}, u32[]{:S(2)}, u32[]{:S(2)}) collective-permute-start(f32[16,16,128]{2,1,0:T(8,128)S(1)} %bitcast.7), channel_id=1, source_target_pairs={{0,8},{8,0},{16,24},{24,16},{1,9},{9,1},{17,25},{25,17},{2,10},{10... | collective-permute-start | bytes 393224 | tf_op jit(solution)/shard_map/ppermute | solution.py:510
  27.7 3.7 %collective-permute-done.1.rest_2_ = f32[16,16,128]{2,1,0:T(8,128)S(1)} collective-permute-done((f32[16,16,128]{2,1,0:T(8,128)S(1)}, f32[16,16,128]{2,1,0:T(8,128)S(1)}, u32[]{:S(2)}, u32[]{:S(2)}) %collective-permute-start.1) | collective-permute-done | bytes 131104 | tf_op jit(solution)/shard_map/ppermute | solution.py:510
  32.1 2.0 %collective-permute-start.7 = (f32[2,64,1152]{2,1,0:T(8,128)S(1)}, f32[2,64,1152]{2,1,0:T(8,128)}, u32[]{:S(2)}, u32[]{:S(2)}) collective-permute-start(f32[2,64,1152]{2,1,0:T(8,128)S(1)} %get-tuple-element.43.rest_8_), channel_id=1, source_target_pairs={{0,1},{1,0},{2,3},{3,2},{4,5},{5,4},{6,7},{7,6},{8,9},{9,8},{10,11... | collective-permute-start | bytes 1769480 | tf_op jit(solution)/shard_map/ppermute | solution.py:483
  36.1 4.4 %collective-permute-done.2.rest_3_ = f32[16,16,128]{2,1,0:T(8,128)S(1)} collective-permute-done((f32[16,16,128]{2,1,0:T(8,128)S(1)}, f32[16,16,128]{2,1,0:T(8,128)S(1)}, u32[]{:S(2)}, u32[]{:S(2)}) %collective-permute-start.2) | collective-permute-done | bytes 131104 | tf_op jit(solution)/shard_map/ppermute | solution.py:510
  40.5 1.3 %collective-permute-done.5.rest_6_ = f32[16,16,128]{2,1,0:T(8,128)S(1)} collective-permute-done((f32[16,16,128]{2,1,0:T(8,128)S(1)}, f32[16,16,128]{2,1,0:T(8,128)S(1)}, u32[]{:S(2)}, u32[]{:S(2)}) %collective-permute-start.5) | collective-permute-done | bytes 131104 | tf_op jit(solution)/shard_map/ppermute | solution.py:518
  43.7 3.5 %positions.1.pos = s32[288]{0:T(512)S(1)} custom-call(s32[3]{0:T(128)S(1)} %pad_add_fusion.ids, s32[256]{0:T(256)S(1)} %copy-done.2, s32[2048]{0:T(1024)S(1)} %reshape.22.table), custom_call_target="tpu_custom_call" | custom-call | tf_op jit(solution)/shard_map/positions/pallas_call | solution.py:486
  48.4 4.1 %first.1 = (f32[12,16,128]{2,1,0:T(8,128)S(1)}, bf16[24,128,576]{2,1,0:T(8,128)(2,1)S(1)}, f32[256,16,128]{2,1,0:T(8,128)S(1)}) custom-call(s32[288]{0:T(512)S(1)} %positions.1.pos, f32[16,16,128]{2,1,0:T(8,128)S(1)} %bitcast.9, f32[16,16,128]{2,1,0:T(8,128)S(1)} %collective-permute-done.rest_1_, f32[16,16,128]{2,1,0:T(8,128)S(1)} %collective-permute-done.1.rest_2_, ...), custom_call_target="tpu_custom_call" | custom-call | tf_op jit(solution)/shard_map/first/pallas_call | solution.py:541
  52.5 5.2 %collective-permute-done.11.rest_0_ = f32[2,64,1152]{2,1,0:T(8,128)} collective-permute-done((f32[2,64,1152]{2,1,0:T(8,128)S(1)}, f32[2,64,1152]{2,1,0:T(8,128)}, u32[]{:S(2)}, u32[]{:S(2)}) %collective-permute-start.11) | collective-permute-done | bytes 589856 | tf_op jit(solution)/shard_map/ppermute | solution.py:521
  57.7 1.9 %more.1 = (f32[16,16,128]{2,1,0:T(8,128)S(1)}, bf16[8,128,576]{2,1,0:T(8,128)(2,1)S(1)}, f32[4,16,128]{2,1,0:T(8,128)S(1)}, f32[4,16,128]{2,1,0:T(8,128)S(1)}, f...) custom-call(s32[288]{0:T(512)S(1)} %positions.1.pos, f32[256,16,128]{2,1,0:T(8,128)S(1)} %get-tuple-element.45.dup, ...), custom_call_target="tpu_custom_call" | custom-call | tf_op jit(solution)/shard_map/more/pallas_call | solution.py:558
  60.8 4.1 %collective-permute-start.13 = (f32[16,16,128]{2,1,0:T(8,128)S(1)}, f32[16,16,128]{2,1,0:T(8,128)S(1)}, u32[]{:S(2)}, u32[]{:S(2)}) collective-permute-start(f32[16,16,128]{2,1,0:T(8,128)S(1)} %get-tuple-element.47.rest_8_), channel_id=1, source_target_pairs={{0,8},{8,0},{16,24},{24,16},{1,9},{9,1},{17,25},{25,17},{2,10},{10... | collective-permute-start | bytes 393224 | tf_op jit(solution)/shard_map/ppermute | solution.py:510
  64.8 1.3 %collective-permute-done.14.rest_10_ = f32[16,16,128]{2,1,0:T(8,128)S(1)} collective-permute-done((f32[16,16,128]{2,1,0:T(8,128)S(1)}, f32[16,16,128]{2,1,0:T(8,128)S(1)}, u32[]{:S(2)}, u32[]{:S(2)}) %collective-permute-start.14) | collective-permute-done | bytes 131104 | tf_op jit(solution)/shard_map/ppermute | solution.py:510
  66.2 1.8 %collective-permute-start.15 = (f32[16,16,128]{2,1,0:T(8,128)S(1)}, f32[16,16,128]{2,1,0:T(8,128)S(1)}, u32[]{:S(2)}, u32[]{:S(2)}) collective-permute-start(f32[16,16,128]{2,1,0:T(8,128)S(1)} %collective-permute-done.14.rest_10_), channel_id=1, source_target_pairs={{0,8},{8,0},{16,24},{24,16},{1,9},{9,1},{17,25},{25,17},{2,10},{10... | collective-permute-start | bytes 393224 | tf_op jit(solution)/shard_map/ppermute | solution.py:510
  68.8 2.3 %collective-permute-done.15.rest_11_ = f32[16,16,128]{2,1,0:T(8,128)S(1)} collective-permute-done((f32[16,16,128]{2,1,0:T(8,128)S(1)}, f32[16,16,128]{2,1,0:T(8,128)S(1)}, u32[]{:S(2)}, u32[]{:S(2)}) %collective-permute-start.15) | collective-permute-done | bytes 131104 | tf_op jit(solution)/shard_map/ppermute | solution.py:510
  72.5 5.2 %second.1 = (f32[16,16,128]{2,1,0:T(8,128)S(1)}, f32[128,16,128]{2,1,0:T(8,128)S(1)}, f32[16,16,128]{2,1,0:T(8,128)S(1)}, f32[16,128]{1,0:T(8,128)S(1)}, f32[4,1...) custom-call(s32[288]{0:T(512)S(1)} %positions.1.pos, ...), custom_call_target="tpu_custom_call" | custom-call | tf_op jit(solution)/shard_map/second/pallas_call | solution.py:577
  77.7 2.5 %collective-permute-start.21 = (f32[16,16,128]{2,1,0:T(8,128)S(1)}, f32[16,16,128]{2,1,0:T(8,128)S(1)}, u32[]{:S(2)}, u32[]{:S(2)}) collective-permute-start(f32[16,16,128]{2,1,0:T(8,128)S(1)} %get-tuple-element.62.rest_8_), channel_id=1, source_target_pairs={{0,16},{8,24},{16,0},{24,8},{1,17},{9,25},{17,1},{25,9},{2,18},{10... | collective-permute-start | bytes 393224 | tf_op jit(solution)/shard_map/ppermute | solution.py:510
  80.2 2.0 %collective-permute-start.20 = (f32[16,16,128]{2,1,0:T(8,128)S(1)}, f32[16,16,128]{2,1,0:T(8,128)S(1)}, u32[]{:S(2)}, u32[]{:S(2)}) collective-permute-start(f32[16,16,128]{2,1,0:T(8,128)S(1)} %get-tuple-element.62.rest_8_), channel_id=1, source_target_pairs={{0,8},{8,0},{16,24},{24,16},{1,9},{9,1},{17,25},{25,17},{2,10},{10... | collective-permute-start | bytes 393224 | tf_op jit(solution)/shard_map/ppermute | solution.py:510
  82.2 4.8 %collective-permute-done.21.rest_10_ = f32[16,16,128]{2,1,0:T(8,128)S(1)} collective-permute-done((f32[16,16,128]{2,1,0:T(8,128)S(1)}, f32[16,16,128]{2,1,0:T(8,128)S(1)}, u32[]{:S(2)}, u32[]{:S(2)}) %collective-permute-start.21) | collective-permute-done | bytes 131104 | tf_op jit(solution)/shard_map/ppermute | solution.py:510
  87.5 1.7 %collective-permute-start.27 = (f32[4,16,128]{2,1,0:T(8,128)S(1)}, f32[4,16,128]{2,1,0:T(8,128)S(1)}, u32[]{:S(2)}, u32[]{:S(2)}) collective-permute-start(f32[4,16,128]{2,1,0:T(8,128)S(1)} %get-tuple-element.55), channel_id=1, source_target_pairs={{0,1},{1,0},{2,3},{3,2},{4,5},{5,4},{6,7},{7,6},{8,9},{9,8},{10,11... | collective-permute-start | bytes 98312 | tf_op jit(solution)/shard_map/ppermute | solution.py:572
  91.5 1.7 %collective-permute-done.28.rest_2_ = f32[4,16,128]{2,1,0:T(8,128)S(1)} collective-permute-done((f32[4,16,128]{2,1,0:T(8,128)S(1)}, f32[4,16,128]{2,1,0:T(8,128)S(1)}, u32[]{:S(2)}, u32[]{:S(2)}) %collective-permute-start.28) | collective-permute-done | bytes 32800 | tf_op jit(solution)/shard_map/ppermute | solution.py:572
  93.8 1.6 %collective-permute-done.29.rest_3_ = f32[4,16,128]{2,1,0:T(8,128)S(1)} collective-permute-done((f32[4,16,128]{2,1,0:T(8,128)S(1)}, f32[4,16,128]{2,1,0:T(8,128)S(1)}, u32[]{:S(2)}, u32[]{:S(2)}) %collective-permute-start.29) | collective-permute-done | bytes 32800 | tf_op jit(solution)/shard_map/ppermute | solution.py:572
  95.9 3.5 %collective-permute-done.30.rest_5_ = f32[4,16,128]{2,1,0:T(8,128)S(1)} collective-permute-done((f32[4,16,128]{2,1,0:T(8,128)S(1)}, f32[4,16,128]{2,1,0:T(8,128)S(1)}, u32[]{:S(2)}, u32[]{:S(2)}) %collective-permute-start.30) | collective-permute-done | bytes 32800 | tf_op jit(solution)/shard_map/ppermute | solution.py:572
  100.0 3.2 %collective-permute-done.31.rest_6_ = f32[4,16,128]{2,1,0:T(8,128)S(1)} collective-permute-done((f32[4,16,128]{2,1,0:T(8,128)S(1)}, f32[4,16,128]{2,1,0:T(8,128)S(1)}, u32[]{:S(2)}, u32[]{:S(2)}) %collective-permute-start.31) | collective-permute-done | bytes 32800 | tf_op jit(solution)/shard_map/ppermute | solution.py:572
  103.7 4.4 %collective-permute-done.32.rest_7_ = f32[4,16,128]{2,1,0:T(8,128)S(1)} collective-permute-done((f32[4,16,128]{2,1,0:T(8,128)S(1)}, f32[4,16,128]{2,1,0:T(8,128)S(1)}, u32[]{:S(2)}, u32[]{:S(2)}) %collective-permute-start.32) | collective-permute-done | bytes 32800 | tf_op jit(solution)/shard_map/ppermute | solution.py:572
  108.1 7.3 %third.1 = (f32[32,2,128]{2,1,0:T(2,128)S(1)}, f32[16,16,128]{2,1,0:T(8,128)}) custom-call(s32[288]{0:T(512)S(1)} %positions.1.pos, f32[128,16,128]{2,1,0:T(8,128)S(1)} %get-tuple-element.50.basis, f32[16,16,128]{2,1,0:T(8,128)S(1)} %get-tuple-element.51.v1_mine, f32[16,128]{1,0:T(8,128)S(1)} %get-tuple-element.52.coeffs, f32[16,16,128]{2,1,0:T(8,128)S(1)} %bitcast.11, ...), custom_call_target="tpu_custom_call" | custom-call | tf_op jit(solution)/shard_map/third/pallas_call | solution.py:593
  115.4 11.3 %all_to_all.10.info = f32[32,2,128]{2,1,0:T(2,128)S(1)} all-to-all(f32[32,2,128]{2,1,0:T(2,128)S(1)} %get-tuple-element.70), channel_id=1, replica_groups=mesh['z'=4,'core'=2,'sub'=4] {'z','core','sub'}, dimensions={0} | all-to-all | bytes 65536 | tf_op jit(solution)/shard_map/all_to_all | solution.py:602
  126.7 2.1 %finish.1 = f32[8,64,64]{2,1,0:T(8,128)} custom-call(s32[3]{0:T(128)S(1)} %pad_add_fusion.ids, f32[32,2,128]{2,1,0:T(2,128)S(1)} %all_to_all.10.info, f32[4,4,16,128]{3,2,1,0:T(8,128)} %get-tuple-element.42.turned, f32[4,16,128]{2,1,0:T(8,128)S(1)} %get-tuple-element.71.rest_0_, f32[4,16,128]{2,1,0:T(8,128)S(1)} %collective-permute-done.27.rest_1_, ...), custom_call_target="tpu_custom_call" | custom-call | tf_op jit(solution)/shard_map/finish/pallas_call | solution.py:605
  (58 shorter events, 16.7 us)
Async XLA Ops:
  3.7 30.5 %collective-permute-start.9 = (f32[2,64,1152]{2,1,0:T(8,128)S(1)}, f32[2,64,1152]{2,1,0:T(8,128)S(1)}, u32[]{:S(2)}, u32[]{:S(2)}) collective-permute-start(f32[2,64,1152]{2,1,0:T(8,128)S(1)} %get-tuple-element.43.rest_8_), channel_id=1, source_target_pairs={{0,2},{1,3},{2,0},{3,1},{4,6},{5,7},{6,4},{7,5},{8,10},{9,11},{10,... | collective-permute-start | bytes 1769480 | tf_op jit(solution)/shard_map/ppermute | solution.py:482
  6.7 27.5 %collective-permute-start.8 = (f32[2,64,1152]{2,1,0:T(8,128)S(1)}, f32[2,64,1152]{2,1,0:T(8,128)S(1)}, u32[]{:S(2)}, u32[]{:S(2)}) collective-permute-start(f32[2,64,1152]{2,1,0:T(8,128)S(1)} %get-tuple-element.44.rest_9_), channel_id=1, source_target_pairs={{0,1},{1,0},{2,3},{3,2},{4,5},{5,4},{6,7},{7,6},{8,9},{9,8},{10,11... | collective-permute-start | bytes 1769480 | tf_op jit(solution)/shard_map/ppermute | solution.py:481
  8.2 14.7 %all-to-all-start = ((f32[4,4,16,128]{3,2,1,0:T(8,128)}), f32[4,4,16,128]{3,2,1,0:T(8,128)S(1)}, u32[]{:S(2)}, u32[]{:S(2)}) async-start(f32[4,4,16,128]{3,2,1,0:T(8,128)} %get-tuple-element.42.turned), calls=%async_computation | async-start | bytes 262144 | tf_op jit(solution)/shard_map/all_to_all | solution.py:501
  23.5 8.0 %collective-permute-start.1 = (f32[16,16,128]{2,1,0:T(8,128)S(1)}, f32[16,16,128]{2,1,0:T(8,128)S(1)}, u32[]{:S(2)}, u32[]{:S(2)}) collective-permute-start(f32[16,16,128]{2,1,0:T(8,128)S(1)} %bitcast.6), channel_id=1, source_target_pairs={{0,16},{8,24},{16,0},{24,8},{1,17},{9,25},{17,1},{25,9},{2,18},{10... | collective-permute-start | bytes 393224 | tf_op jit(solution)/shard_map/ppermute | solution.py:510
  26.1 6.0 %collective-permute-start = (f32[16,16,128]{2,1,0:T(8,128)S(1)}, f32[16,16,128]{2,1,0:T(8,128)S(1)}, u32[]{:S(2)}, u32[]{:S(2)}) collective-permute-start(f32[16,16,128]{2,1,0:T(8,128)S(1)} %bitcast.7), channel_id=1, source_target_pairs={{0,8},{8,0},{16,24},{24,16},{1,9},{9,1},{17,25},{25,17},{2,10},{10... | collective-permute-start | bytes 393224 | tf_op jit(solution)/shard_map/ppermute | solution.py:510
  27.7 7.8 %collective-permute-start.3 = (f32[16,16,128]{2,1,0:T(8,128)S(1)}, f32[16,16,128]{2,1,0:T(8,128)S(1)}, u32[]{:S(2)}, u32[]{:S(2)}) collective-permute-start(f32[16,16,128]{2,1,0:T(8,128)S(1)} %bitcast.8), channel_id=1, source_target_pairs={{0,4},{4,0},{1,5},{5,1},{2,6},{6,2},{3,7},{7,3},{8,12},{12,8},{9,1... | collective-permute-start | bytes 393224 | tf_op jit(solution)/shard_map/ppermute | solution.py:518
  31.4 16.3 %collective-permute-start.10 = (f32[2,64,1152]{2,1,0:T(8,128)S(1)}, f32[2,64,1152]{2,1,0:T(8,128)}, u32[]{:S(2)}, u32[]{:S(2)}) collective-permute-start(f32[2,64,1152]{2,1,0:T(8,128)S(1)} %get-tuple-element.44.rest_9_), channel_id=1, source_target_pairs={{0,2},{1,3},{2,0},{3,1},{4,6},{5,7},{6,4},{7,5},{8,10},{9,11},{10,... | collective-permute-start | bytes 1769480 | tf_op jit(solution)/shard_map/ppermute | solution.py:484
  32.1 16.3 %collective-permute-start.7 = (f32[2,64,1152]{2,1,0:T(8,128)S(1)}, f32[2,64,1152]{2,1,0:T(8,128)}, u32[]{:S(2)}, u32[]{:S(2)}) collective-permute-start(f32[2,64,1152]{2,1,0:T(8,128)S(1)} %get-tuple-element.43.rest_8_), channel_id=1, source_target_pairs={{0,1},{1,0},{2,3},{3,2},{4,5},{5,4},{6,7},{7,6},{8,9},{9,8},{10,11... | collective-permute-start | bytes 1769480 | tf_op jit(solution)/shard_map/ppermute | solution.py:483
  34.2 23.5 %collective-permute-start.11 = (f32[2,64,1152]{2,1,0:T(8,128)S(1)}, f32[2,64,1152]{2,1,0:T(8,128)}, u32[]{:S(2)}, u32[]{:S(2)}) collective-permute-start(f32[2,64,1152]{2,1,0:T(8,128)S(1)} %collective-permute-done.9.rest_12_), channel_id=1, source_target_pairs={{0,1},{1,0},{2,3},{3,2},{4,5},{5,4},{6,7},{7,6},{8,9},{9,8},{10,11... | collective-permute-start | bytes 1769480 | tf_op jit(solution)/shard_map/ppermute | solution.py:521
  34.2 23.5 %collective-permute-start.12 = (f32[2,64,1152]{2,1,0:T(8,128)S(1)}, f32[2,64,1152]{2,1,0:T(8,128)}, u32[]{:S(2)}, u32[]{:S(2)}) collective-permute-start(f32[2,64,1152]{2,1,0:T(8,128)S(1)} %collective-permute-done.8.rest_11_), channel_id=1, source_target_pairs={{0,2},{1,3},{2,0},{3,1},{4,6},{5,7},{6,4},{7,5},{8,10},{9,11},{10,... | collective-permute-start | bytes 1769480 | tf_op jit(solution)/shard_map/ppermute | solution.py:522
  35.5 5.0 %collective-permute-start.2 = (f32[16,16,128]{2,1,0:T(8,128)S(1)}, f32[16,16,128]{2,1,0:T(8,128)S(1)}, u32[]{:S(2)}, u32[]{:S(2)}) collective-permute-start(f32[16,16,128]{2,1,0:T(8,128)S(1)} %collective-permute-done.1.rest_2_), channel_id=1, source_target_pairs={{0,8},{8,0},{16,24},{24,16},{1,9},{9,1},{17,25},{25,17},{2,10},{10... | collective-permute-start | bytes 393224 | tf_op jit(solution)/shard_map/ppermute | solution.py:510
  40.5 1.3 %collective-permute-start.5 = (f32[16,16,128]{2,1,0:T(8,128)S(1)}, f32[16,16,128]{2,1,0:T(8,128)S(1)}, u32[]{:S(2)}, u32[]{:S(2)}) collective-permute-start(f32[16,16,128]{2,1,0:T(8,128)S(1)} %collective-permute-done.1.rest_2_), channel_id=1, source_target_pairs={{0,4},{4,0},{1,5},{5,1},{2,6},{6,2},{3,7},{7,3},{8,12},{12,8},{9,1... | collective-permute-start | bytes 393224 | tf_op jit(solution)/shard_map/ppermute | solution.py:518
  43.2 4.0 %collective-permute-start.6 = (f32[16,16,128]{2,1,0:T(8,128)S(1)}, f32[16,16,128]{2,1,0:T(8,128)S(1)}, u32[]{:S(2)}, u32[]{:S(2)}) collective-permute-start(f32[16,16,128]{2,1,0:T(8,128)S(1)} %collective-permute-done.2.rest_3_), channel_id=1, source_target_pairs={{0,4},{4,0},{1,5},{5,1},{2,6},{6,2},{3,7},{7,3},{8,12},{12,8},{9,1... | collective-permute-start | bytes 393224 | tf_op jit(solution)/shard_map/ppermute | solution.py:518
  59.6 6.6 %collective-permute-start.14 = (f32[16,16,128]{2,1,0:T(8,128)S(1)}, f32[16,16,128]{2,1,0:T(8,128)S(1)}, u32[]{:S(2)}, u32[]{:S(2)}) collective-permute-start(f32[16,16,128]{2,1,0:T(8,128)S(1)} %get-tuple-element.47.rest_8_), channel_id=1, source_target_pairs={{0,16},{8,24},{16,0},{24,8},{1,17},{9,25},{17,1},{25,9},{2,18},{10... | collective-permute-start | bytes 393224 | tf_op jit(solution)/shard_map/ppermute | solution.py:510
  60.8 8.0 %collective-permute-start.13 = (f32[16,16,128]{2,1,0:T(8,128)S(1)}, f32[16,16,128]{2,1,0:T(8,128)S(1)}, u32[]{:S(2)}, u32[]{:S(2)}) collective-permute-start(f32[16,16,128]{2,1,0:T(8,128)S(1)} %get-tuple-element.47.rest_8_), channel_id=1, source_target_pairs={{0,8},{8,0},{16,24},{24,16},{1,9},{9,1},{17,25},{25,17},{2,10},{10... | collective-permute-start | bytes 393224 | tf_op jit(solution)/shard_map/ppermute | solution.py:510
  66.2 5.0 %collective-permute-start.15 = (f32[16,16,128]{2,1,0:T(8,128)S(1)}, f32[16,16,128]{2,1,0:T(8,128)S(1)}, u32[]{:S(2)}, u32[]{:S(2)}) collective-permute-start(f32[16,16,128]{2,1,0:T(8,128)S(1)} %collective-permute-done.14.rest_10_), channel_id=1, source_target_pairs={{0,8},{8,0},{16,24},{24,16},{1,9},{9,1},{17,25},{25,17},{2,10},{10... | collective-permute-start | bytes 393224 | tf_op jit(solution)/shard_map/ppermute | solution.py:510
  68.0 3.2 %collective-permute-start.16 = (f32[16,16,128]{2,1,0:T(8,128)S(1)}, f32[16,16,128]{2,1,0:T(8,128)S(1)}, u32[]{:S(2)}, u32[]{:S(2)}) collective-permute-start(f32[16,16,128]{2,1,0:T(8,128)S(1)} %get-tuple-element.47.rest_8_), channel_id=1, source_target_pairs={{0,4},{4,0},{1,5},{5,1},{2,6},{6,2},{3,7},{7,3},{8,12},{12,8},{9,1... | collective-permute-start | bytes 393224 | tf_op jit(solution)/shard_map/ppermute | solution.py:518
  68.0 3.2 %collective-permute-start.18 = (f32[16,16,128]{2,1,0:T(8,128)S(1)}, f32[16,16,128]{2,1,0:T(8,128)S(1)}, u32[]{:S(2)}, u32[]{:S(2)}) collective-permute-start(f32[16,16,128]{2,1,0:T(8,128)S(1)} %collective-permute-done.14.rest_10_), channel_id=1, source_target_pairs={{0,4},{4,0},{1,5},{5,1},{2,6},{6,2},{3,7},{7,3},{8,12},{12,8},{9,1... | collective-permute-start | bytes 393224 | tf_op jit(solution)/shard_map/ppermute | solution.py:518
  68.8 2.4 %collective-permute-start.17 = (f32[16,16,128]{2,1,0:T(8,128)S(1)}, f32[16,16,128]{2,1,0:T(8,128)S(1)}, u32[]{:S(2)}, u32[]{:S(2)}) collective-permute-start(f32[16,16,128]{2,1,0:T(8,128)S(1)} %collective-permute-done.13.rest_9_), channel_id=1, source_target_pairs={{0,4},{4,0},{1,5},{5,1},{2,6},{6,2},{3,7},{7,3},{8,12},{12,8},{9,1... | collective-permute-start | bytes 393224 | tf_op jit(solution)/shard_map/ppermute | solution.py:518
  77.7 9.4 %collective-permute-start.21 = (f32[16,16,128]{2,1,0:T(8,128)S(1)}, f32[16,16,128]{2,1,0:T(8,128)S(1)}, u32[]{:S(2)}, u32[]{:S(2)}) collective-permute-start(f32[16,16,128]{2,1,0:T(8,128)S(1)} %get-tuple-element.62.rest_8_), channel_id=1, source_target_pairs={{0,16},{8,24},{16,0},{24,8},{1,17},{9,25},{17,1},{25,9},{2,18},{10... | collective-permute-start | bytes 393224 | tf_op jit(solution)/shard_map/ppermute | solution.py:510
  80.2 13.0 %collective-permute-start.20 = (f32[16,16,128]{2,1,0:T(8,128)S(1)}, f32[16,16,128]{2,1,0:T(8,128)S(1)}, u32[]{:S(2)}, u32[]{:S(2)}) collective-permute-start(f32[16,16,128]{2,1,0:T(8,128)S(1)} %get-tuple-element.62.rest_8_), channel_id=1, source_target_pairs={{0,8},{8,0},{16,24},{24,16},{1,9},{9,1},{17,25},{25,17},{2,10},{10... | collective-permute-start | bytes 393224 | tf_op jit(solution)/shard_map/ppermute | solution.py:510
  87.0 6.7 %collective-permute-start.22 = (f32[16,16,128]{2,1,0:T(8,128)S(1)}, f32[16,16,128]{2,1,0:T(8,128)S(1)}, u32[]{:S(2)}, u32[]{:S(2)}) collective-permute-start(f32[16,16,128]{2,1,0:T(8,128)S(1)} %collective-permute-done.21.rest_10_), channel_id=1, source_target_pairs={{0,8},{8,0},{16,24},{24,16},{1,9},{9,1},{17,25},{25,17},{2,10},{10... | collective-permute-start | bytes 393224 | tf_op jit(solution)/shard_map/ppermute | solution.py:510
  87.5 3.9 %collective-permute-start.27 = (f32[4,16,128]{2,1,0:T(8,128)S(1)}, f32[4,16,128]{2,1,0:T(8,128)S(1)}, u32[]{:S(2)}, u32[]{:S(2)}) collective-permute-start(f32[4,16,128]{2,1,0:T(8,128)S(1)} %get-tuple-element.55), channel_id=1, source_target_pairs={{0,1},{1,0},{2,3},{3,2},{4,5},{5,4},{6,7},{7,6},{8,9},{9,8},{10,11... | collective-permute-start | bytes 98312 | tf_op jit(solution)/shard_map/ppermute | solution.py:572
  89.3 3.9 %collective-permute-start.28 = (f32[4,16,128]{2,1,0:T(8,128)S(1)}, f32[4,16,128]{2,1,0:T(8,128)S(1)}, u32[]{:S(2)}, u32[]{:S(2)}) collective-permute-start(f32[4,16,128]{2,1,0:T(8,128)S(1)} %get-tuple-element.56), channel_id=1, source_target_pairs={{0,2},{1,3},{2,0},{3,1},{4,6},{5,7},{6,4},{7,5},{8,10},{9,11},{10,... | collective-permute-start | bytes 98312 | tf_op jit(solution)/shard_map/ppermute | solution.py:572
  90.6 4.8 %collective-permute-start.29 = (f32[4,16,128]{2,1,0:T(8,128)S(1)}, f32[4,16,128]{2,1,0:T(8,128)S(1)}, u32[]{:S(2)}, u32[]{:S(2)}) collective-permute-start(f32[4,16,128]{2,1,0:T(8,128)S(1)} %get-tuple-element.57), channel_id=1, source_target_pairs={{0,3},{1,2},{2,1},{3,0},{4,7},{5,6},{6,5},{7,4},{8,11},{9,10},{10,... | collective-permute-start | bytes 98312 | tf_op jit(solution)/shard_map/ppermute | solution.py:572
  91.5 16.6 %collective-permute-start.23 = (f32[16,16,128]{2,1,0:T(8,128)S(1)}, f32[16,16,128]{2,1,0:T(8,128)S(1)}, u32[]{:S(2)}, u32[]{:S(2)}) collective-permute-start(f32[16,16,128]{2,1,0:T(8,128)S(1)} %get-tuple-element.62.rest_8_), channel_id=1, source_target_pairs={{0,4},{4,0},{1,5},{5,1},{2,6},{6,2},{3,7},{7,3},{8,12},{12,8},{9,1... | collective-permute-start | bytes 393224 | tf_op jit(solution)/shard_map/ppermute | solution.py:518
  93.2 14.9 %collective-permute-start.25 = (f32[16,16,128]{2,1,0:T(8,128)S(1)}, f32[16,16,128]{2,1,0:T(8,128)S(1)}, u32[]{:S(2)}, u32[]{:S(2)}) collective-permute-start(f32[16,16,128]{2,1,0:T(8,128)S(1)} %collective-permute-done.21.rest_10_), channel_id=1, source_target_pairs={{0,4},{4,0},{1,5},{5,1},{2,6},{6,2},{3,7},{7,3},{8,12},{12,8},{9,1... | collective-permute-start | bytes 393224 | tf_op jit(solution)/shard_map/ppermute | solution.py:518
  93.2 14.9 %collective-permute-start.24 = (f32[16,16,128]{2,1,0:T(8,128)S(1)}, f32[16,16,128]{2,1,0:T(8,128)S(1)}, u32[]{:S(2)}, u32[]{:S(2)}) collective-permute-start(f32[16,16,128]{2,1,0:T(8,128)S(1)} %collective-permute-done.20.rest_9_), channel_id=1, source_target_pairs={{0,4},{4,0},{1,5},{5,1},{2,6},{6,2},{3,7},{7,3},{8,12},{12,8},{9,1... | collective-permute-start | bytes 393224 | tf_op jit(solution)/shard_map/ppermute | solution.py:518
  93.7 14.4 %collective-permute-start.26 = (f32[16,16,128]{2,1,0:T(8,128)S(1)}, f32[16,16,128]{2,1,0:T(8,128)S(1)}, u32[]{:S(2)}, u32[]{:S(2)}) collective-permute-start(f32[16,16,128]{2,1,0:T(8,128)S(1)} %collective-permute-done.22.rest_11_), channel_id=1, source_target_pairs={{0,4},{4,0},{1,5},{5,1},{2,6},{6,2},{3,7},{7,3},{8,12},{12,8},{9,1... | collective-permute-start | bytes 393224 | tf_op jit(solution)/shard_map/ppermute | solution.py:518
  95.4 3.9 %collective-permute-start.30 = (f32[4,16,128]{2,1,0:T(8,128)S(1)}, f32[4,16,128]{2,1,0:T(8,128)S(1)}, u32[]{:S(2)}, u32[]{:S(2)}) collective-permute-start(f32[4,16,128]{2,1,0:T(8,128)S(1)} %get-tuple-element.59), channel_id=1, source_target_pairs={{0,1},{1,0},{2,3},{3,2},{4,5},{5,4},{6,7},{7,6},{8,9},{9,8},{10,11... | collective-permute-start | bytes 98312 | tf_op jit(solution)/shard_map/ppermute | solution.py:572
  99.3 3.9 %collective-permute-start.31 = (f32[4,16,128]{2,1,0:T(8,128)S(1)}, f32[4,16,128]{2,1,0:T(8,128)S(1)}, u32[]{:S(2)}, u32[]{:S(2)}) collective-permute-start(f32[4,16,128]{2,1,0:T(8,128)S(1)} %get-tuple-element.60), channel_id=1, source_target_pairs={{0,2},{1,3},{2,0},{3,1},{4,6},{5,7},{6,4},{7,5},{8,10},{9,11},{10,... | collective-permute-start | bytes 98312 | tf_op jit(solution)/shard_map/ppermute | solution.py:572
  103.3 4.8 %collective-permute-start.32 = (f32[4,16,128]{2,1,0:T(8,128)S(1)}, f32[4,16,128]{2,1,0:T(8,128)S(1)}, u32[]{:S(2)}, u32[]{:S(2)}) collective-permute-start(f32[4,16,128]{2,1,0:T(8,128)S(1)} %get-tuple-element.61), channel_id=1, source_target_pairs={{0,3},{1,2},{2,1},{3,0},{4,7},{5,6},{6,5},{7,4},{8,11},{9,10},{10,... | collective-permute-start | bytes 98312 | tf_op jit(solution)/shard_map/ppermute | solution.py:572
  (6 other events, 87.4 us)

commit v4 on v3

--- a/solution.py
+++ b/solution.py
@@ -99,7 +99,7 @@
     lax.fori_loop(0, n_sub * per_dev, look, 0, unroll=2)
 
 
-def pack_kernel(dof, op, right, low, high, turned, held, op_held, sems):
+def pack_kernel(dof, op, right, low, high, turned, kept, held, op_held, sems):
     half = op.shape[0] // 2
     sources = [right, op.at[pl.ds(0, half)], op.at[pl.ds(half, half)]]
     copies = start_copies(sources, [held, op_held.at[0], op_held.at[1]], sems)
@@ -109,6 +109,7 @@
         both = jnp.concatenate([held[2 * pair], held[2 * pair + 1]], axis=0).T
         for quarter in range(n_sub):
             turned[quarter, pair] = both[quarter * rhs : (quarter + 1) * rhs]
+            kept[quarter, pair] = both[quarter * rhs : (quarter + 1) * rhs]
     main = op.shape[2] - dof
     for index, target in enumerate((low, high)):
         copies[index + 1].wait()
@@ -126,9 +127,8 @@
     dup[2 * pair + 1] = jnp.where(mask, rolled, values)
 
 
-def site_product(stacked, local, pos, dup, terms, dof):
-    rows = dup.shape[1]
-    mask = low_half((rows, 2 * dof), dof)
+def site_vector(local, pos, dup, terms, dof):
+    mask = low_half((dup.shape[1], 2 * dof), dof)
     tiles = []
     for first in range(0, terms - 1, 2):
         left = dup[pos[local * terms + first]]
@@ -136,67 +136,66 @@
         tiles.append(jnp.where(mask, left, right))
     if terms % 2:
         tiles.append(dup[pos[local * terms + terms - 1]][:, :dof])
-    high, low = split_bf16(jnp.concatenate(tiles, axis=1))
+    return list(split_bf16(jnp.concatenate(tiles, axis=1)))
+
+
+def row_pairs(op, pair, dof):
+    if op.shape[1] == 2 * dof:
+        return op[pair, :dof], op[pair, dof:]
+    main = op.shape[2] // 2 - dof
+    rows = op[pair]
+    tail = rows[:, 2 * main :]
+    even = jnp.concatenate([rows[:, :main], tail[:, :dof]], axis=1)
+    odd = jnp.concatenate([rows[:, main : 2 * main], tail[:, dof:]], axis=1)
+    return even, odd
+
+
+def to_columns(even, odd):
+    width, lanes = even.shape[1], 2 * even.shape[0]
+    pieces = []
+    for start in range(0, width, lanes):
+        stop = min(start + lanes, width)
+        pieces.append(jnp.concatenate([even[:, start:stop], odd[:, start:stop]], axis=0).T)
+    return jnp.concatenate(split_bf16(jnp.concatenate(pieces, axis=0)), axis=1)
+
+
+def pair_product(columns, local, pos, dup, terms, dof):
+    rows, lanes = dup.shape[1], 2 * dof
+    vectors = [v for i in range(2) for v in site_vector(local + i, pos, dup, terms, dof)]
     product = lax.dot_general(
-        jnp.concatenate([high, low], axis=0),
-        stacked,
-        (((1,), (1,)), ((), ())),
+        jnp.concatenate(vectors, axis=0),
+        columns,
+        (((1,), (0,)), ((), ())),
         preferred_element_type=F32,
     )
-    total = product[:rows] + product[rows:]
-    return total + pltpu.roll(total, dof, 1)
-
-
-def stack_split(op):
-    high, low = split_bf16(op)
-    return jnp.concatenate([high, low], axis=0)
-
-
-def pair_product(stacks, local, pos, dup, terms, dof):
-    even, odd = (
-        site_product(stack, local + i, pos, dup, terms, dof) for i, stack in enumerate(stacks)
-    )
+    product = product[:, :lanes] + product[:, lanes:]
+    even = product[:rows] + product[rows : 2 * rows]
+    odd = product[2 * rows : 3 * rows] + product[3 * rows :]
     return jnp.where(low_half(even.shape, dof), even, odd)
+
+
+def rows_product(pair_rows, local, pos, dup, terms, dof):
+    rows = dup.shape[1]
+    halves = []
+    for i, op in enumerate(pair_rows):
+        product = lax.dot_general(
+            jnp.concatenate(site_vector(local + i, pos, dup, terms, dof), axis=0),
+            jnp.concatenate(split_bf16(op), axis=0),
+            (((1,), (1,)), ((), ())),
+            preferred_element_type=F32,
+        )
+        total = product[:rows] + product[rows:]
+        halves.append(total + pltpu.roll(total, dof, 1))
+    return jnp.where(low_half(halves[0].shape, dof), halves[0], halves[1])
 
 
 def apply_rows(stages, pos, dup, terms, dof, put):
     base = 0
     for stage in stages:
-
-        def body(pair, carry, base=base, stage=stage):
-            stacks = [stage[2 * pair], stage[2 * pair + 1]]
-            put(base // 2 + pair, pair_product(stacks, base + 2 * pair, pos, dup, terms, dof))
-            return carry
-
-        lax.fori_loop(0, stage.shape[0] // 2, body, 0, unroll=4)
+        for pair in range(stage.shape[0]):
+            columns = stage[pair]
+            put(base + pair, pair_product(columns, 2 * (base + pair), pos, dup, terms, dof))
         base += stage.shape[0]
-
-
-def split_rows(ops, split, base, pos, dup, terms, dof, put):
-    offset = 0
-    if ops[0].shape[2] == terms * dof:
-        flat = [(op, i) for op in ops for i in range(op.shape[0])]
-        for pair in range(len(flat) // 2):
-            stacks = [stack_split(op[i]) for op, i in flat[2 * pair : 2 * pair + 2]]
-            split[2 * pair], split[2 * pair + 1] = stacks
-            put((base + 2 * pair) // 2, pair_product(stacks, base + 2 * pair, pos, dup, terms, dof))
-        return
-    for op in ops:
-        main = op.shape[2] // 2 - dof
-
-        def body(pair, carry, offset=offset, op=op, main=main):
-            rows = op[pair]
-            tail = rows[:, 2 * main :]
-            even = jnp.concatenate([rows[:, :main], tail[:, :dof]], axis=1)
-            odd = jnp.concatenate([rows[:, main : 2 * main], tail[:, dof:]], axis=1)
-            stacks = [stack_split(even), stack_split(odd)]
-            split[offset + 2 * pair], split[offset + 2 * pair + 1] = stacks
-            local = base + offset + 2 * pair
-            put(divide(local, 2), pair_product(stacks, local, pos, dup, terms, dof))
-            return carry
-
-        lax.fori_loop(0, op.shape[0], body, 0, unroll=True)
-        offset += 2 * op.shape[0]
 
 
 def start_copies(sources, targets, sems):
@@ -213,7 +212,7 @@
     n_pair = fields[0].shape[0]
     for block in range(len(fields)):
         init = lax.fori_loop(
-            0, n_pair, lambda pair, carry, block=block: step(block, pair, carry), init, unroll=8
+            0, n_pair, lambda pair, carry, block=block: step(block, pair, carry), init, unroll=16
         )
     return init
 
@@ -242,26 +241,40 @@
     def put(pair, values):
         out[pair] = values
 
-    split_rows(held, split, 0, pos, dup, terms, dof, put)
+    base = 0
+    for op in held:
+        for inner in range(op.shape[0]):
+            columns = to_columns(*row_pairs(op, inner, dof))
+            split[base] = columns
+            put(base, pair_product(columns, 2 * base, pos, dup, terms, dof))
+            base += 1
 
 
 def more_kernel(count, dof, terms, pos, dup, before, *rest):
-    ops, out, split, shares = rest[:count], rest[count], rest[count + 1], rest[count + 2 :]
-    base = 2 * before.shape[0]
-    for pair in range(before.shape[0]):
+    ops, out, shares = rest[:count], rest[count], rest[count + 1 :]
+    base = before.shape[0]
+    for pair in range(base):
         out[pair] = before[pair]
-
-    def put(pair, values):
-        out[pair] = values
-
-    split_rows(ops, split, base, pos, dup, terms, dof, put)
+    for op in ops:
+        for inner in range(op.shape[0]):
+            out[base] = rows_product(row_pairs(op, inner, dof), 2 * base, pos, dup, terms, dof)
+            base += 1
     share_out(out, shares)
+
+
+def turn_kernel(count, dof, *rest):
+    ops, split = rest[:count], rest[count]
+    base = 0
+    for op in ops:
+        for inner in range(op.shape[0]):
+            split[base] = to_columns(*row_pairs(op, inner, dof))
+            base += 1
 
 
 def second_kernel(n_field, count, sends, dof, terms, pos, *rest):
     b_ref, z_ref, rest = rest[:n_field], rest[n_field : 2 * n_field], rest[2 * n_field :]
-    stages, (out, basis, mine, coeffs) = rest[:count], rest[count : count + 4]
-    shares, dup = rest[count + 4 : count + 4 + sends], rest[count + 4 + sends]
+    stages, (out, basis, coeffs) = rest[:count], rest[count : count + 3]
+    shares, dup = rest[count + 3 : count + 3 + sends], rest[count + 3 + sends]
     n_pair = b_ref[0].shape[0]
     shape = b_ref[0].shape[1:]
     zero = jnp.zeros(shape, F32)
@@ -291,7 +304,6 @@
 
     over_pairs(b_ref, build, 0)
     coeffs[...] = place([beta, h00, h10], shape)
-    mine[...] = basis[:n_pair]
 
     def put(pair, values):
         out[pair] = values
@@ -300,9 +312,9 @@
     share_out(out, shares)
 
 
-def third_kernel(n_field, count, dof, terms, pos, basis, v1_mine, coeffs, *rest):
+def third_kernel(n_field, count, dof, terms, pos, basis, coeffs, *rest):
     b_ref, z_ref, rest = rest[:n_field], rest[n_field : 2 * n_field], rest[2 * n_field :]
-    stages, (sums, mine, dup, work, image) = rest[:count], rest[count:]
+    stages, (sums, work, dup, image) = rest[:count], rest[count:]
     b_mine = b_ref[0]
     n_pair = b_mine.shape[0]
     shape = b_mine.shape[1:]
@@ -337,7 +349,6 @@
         return carry
 
     over_pairs(b_ref, build, 0)
-    mine[...] = work[:n_pair]
 
     def put(pair, values):
         image[pair] = values
@@ -348,8 +359,8 @@
         u = image[pair]
         return (
             carry[0] + b_mine[pair] * u,
-            carry[1] + v1_mine[pair] * u,
-            carry[2] + mine[pair] * u,
+            carry[1] + basis[pair] * u,
+            carry[2] + work[pair] * u,
             carry[3] + u * u,
         )
 
@@ -465,11 +476,11 @@
     half = per_dev // 2
     if relay:
         halves = [jax.ShapeDtypeStruct((half // 2, dof, 2 * width), F32)] * 2
-        op_low, op_high, turned = pl.pallas_call(
+        op_low, op_high, turned, kept = pl.pallas_call(
             functools.partial(pack_kernel, dof),
-            out_shape=halves + [jax.ShapeDtypeStruct((n_sub, half, rhs, lanes), F32)],
+            out_shape=halves + [jax.ShapeDtypeStruct((n_sub, half, rhs, lanes), F32)] * 2,
             in_specs=[HBM, HBM],
-            out_specs=[VMEM] * 3,
+            out_specs=[VMEM] * 4,
             scratch_shapes=[
                 pltpu.VMEM(right_side.shape, F32),
                 pltpu.VMEM((2, half, dof, width), F32),
@@ -498,6 +509,8 @@
     if even and not relay:
         turned = turned.reshape(n_sub, per_dev // 2, 2, rhs, dof).transpose(0, 1, 3, 2, 4)
         turned = turned.reshape(n_sub, per_dev // 2, rhs, lanes)
+    if not relay:
+        kept = turned
     mine = lax.all_to_all(turned, "sub", split_axis=0, concat_axis=0, tiled=True)
     mine = mine[order]
     if not even:
@@ -523,7 +536,7 @@
         stages = [[op_low, op_high, x_low, x_high, y_low, y_high], [d_low, d_high]]
     if not relay:
         every = lax.all_gather(coarse_op, "sub", axis=0)[order]
-        stages = [[every[k] for k in range(n_sub)]]
+        stages = [[every.reshape(n_own, 2 * dof, width)]]
     b_parts = gather(b_mine)
     n_field = len(b_parts)
     dup = (CORES * nz * n_loc, rhs, lanes)
@@ -533,16 +546,16 @@
     sends = n_sub if even else 0
     share = [jax.ShapeDtypeStruct((per_dev // 2, rhs, lanes), F32)] * sends
 
-    def split_shape(sites):
-        return jax.ShapeDtypeStruct((sites, 2 * dof, width), BF16)
+    def split_shape(pairs):
+        return jax.ShapeDtypeStruct((pairs, width, 4 * dof), BF16)
 
     ops = stages[0]
-    rows = sum(op.shape[0] * op.shape[2] // width for op in ops)
+    done = sum(op.shape[0] for op in ops)
     z1, split, spread_b = pl.pallas_call(
         functools.partial(first_kernel, n_field, len(ops), dof, terms),
         out_shape=[
-            jax.ShapeDtypeStruct((rows // 2,) + field[1:], F32),
-            split_shape(rows),
+            jax.ShapeDtypeStruct((done,) + field[1:], F32),
+            split_shape(done),
             jax.ShapeDtypeStruct(dup, F32),
         ],
         in_specs=[SMEM] + [VMEM] * n_field + [ANY] * len(ops),
@@ -555,14 +568,22 @@
     splits, shares1 = [split], []
     if relay:
         ops = stages[1]
-        z1, split, *shares1 = pl.pallas_call(
+        z1, *shares1 = pl.pallas_call(
             functools.partial(more_kernel, len(ops), dof, terms),
-            out_shape=[own_shape, split_shape(n_loc - rows)] + share,
+            out_shape=[own_shape] + share,
             in_specs=[SMEM, VMEM, VMEM] + [VMEM] * len(ops),
-            out_specs=[VMEM] * (2 + sends),
+            out_specs=[VMEM] * (1 + sends),
             compiler_params=PARAMS,
             name="more",
         )(positions, spread_b, z1, *ops)
+        split = pl.pallas_call(
+            functools.partial(turn_kernel, len(ops), dof),
+            out_shape=split_shape(n_own - done),
+            in_specs=[VMEM] * len(ops),
+            out_specs=VMEM,
+            compiler_params=PARAMS,
+            name="turn",
+        )(*ops)
         splits.append(split)
     elif even:
         shares1 = [z1[k * per_dev // 2 : (k + 1) * per_dev // 2] for k in range(n_sub)]
@@ -574,11 +595,11 @@
     z1_parts = gather(z1)
     shares1 = send(shares1)
 
-    z2, basis, v1_mine, coeffs, *shares2 = pl.pallas_call(
+    z2, basis, coeffs, *shares2 = pl.pallas_call(
         functools.partial(second_kernel, n_field, count, sends, dof, terms),
-        out_shape=[own_shape, jax.ShapeDtypeStruct(full, F32), own_shape, small] + share,
+        out_shape=[own_shape, jax.ShapeDtypeStruct(full, F32), small] + share,
         in_specs=[SMEM] + [VMEM] * (2 * n_field + count),
-        out_specs=[VMEM] * (4 + sends),
+        out_specs=[VMEM] * (3 + sends),
         scratch_shapes=[pltpu.VMEM(dup, F32)],
         compiler_params=PARAMS,
         name="second",
@@ -590,15 +611,17 @@
     axes = ("z", "core", "sub") if even else ("z", "core")
     copies = nz * CORES * (n_sub if even else 1)
     note = (pl.cdiv(10 * rhs, lanes), lanes) if even else field[1:]
-    sums, v2_mine = pl.pallas_call(
+    keep = [] if even else [jax.ShapeDtypeStruct(full, F32)]
+    sums, *work = pl.pallas_call(
         functools.partial(third_kernel, n_field, count, dof, terms),
-        out_shape=[jax.ShapeDtypeStruct((copies,) + note, F32), own_shape],
-        in_specs=[SMEM] + [VMEM] * (3 + 2 * n_field + count),
-        out_specs=[VMEM] * 2,
-        scratch_shapes=[pltpu.VMEM(dup, F32), pltpu.VMEM(full, F32), pltpu.VMEM(field, F32)],
+        out_shape=[jax.ShapeDtypeStruct((copies,) + note, F32)] + keep,
+        in_specs=[SMEM] + [VMEM] * (2 + 2 * n_field + count),
+        out_specs=[VMEM] * (1 + len(keep)),
+        scratch_shapes=[pltpu.VMEM(full, F32)] * (1 - len(keep))
+        + [pltpu.VMEM(dup, F32), pltpu.VMEM(field, F32)],
         compiler_params=PARAMS,
         name="third",
-    )(positions, basis, v1_mine, coeffs, *b_parts, *z2_parts, *splits)
+    )(positions, basis, coeffs, *b_parts, *z2_parts, *splits)
     sums = lax.all_to_all(sums, axes, split_axis=0, concat_axis=0, tiled=True)
 
     if even:
@@ -613,7 +636,7 @@
             ],
             compiler_params=SMALL,
             name="finish",
-        )(ids, sums, turned, *shares1, *shares2)
+        )(ids, sums, kept, *shares1, *shares2)
     result = pl.pallas_call(
         combine_kernel,
         out_shape=own_shape,
@@ -621,7 +644,7 @@
         out_specs=VMEM,
         compiler_params=SMALL,
             name="combine",
-    )(sums, b_mine, v1_mine, v2_mine)
+    )(sums, b_mine, basis[:n_own], work[0][:n_own])
     result = result.reshape(n_own, rhs, 2, dof).transpose(0, 2, 1, 3)
     result = result.reshape(n_sub, per_dev, rhs, dof)[order]
     result = lax.all_to_all(result, "sub", split_axis=0, concat_axis=0, tiled=True)

time: 129 us -> 121 us (0.938)
  Pallas kernels: 25.4 us -> 17.8 us
  waiting for transfers between devices: 53.5 us -> 51.7 us
  local copies, waits for them, and re-layouts: 3.06 us -> 4.62 us
    pallas_call x1, Pallas kernels: 7.28 us -> 2.97 us  [per_device(): pl.pallas_call(functools.partial(third_kernel, n_field, count, dof, terms...]
    pallas_call x1, Pallas kernels: 5.15 us -> 2.48 us  [per_device(): pl.pallas_call(functools.partial(second_kernel, n_field, count, sends, do...]
  transfers between devices with their start and end apart: 34 -> 34, of which waited for: 19 -> 17; matrix products, arithmetic and copies ran while one was open for 1% -> 2% of each run, Pallas kernels for 6% -> 7%
where the time goes in v4:
time: 121 us
  waiting for transfers between devices  51.7 us (43%)
  starting transfers between devices  35 us (29%)
  Pallas kernels  17.8 us (15%)
  blocking collectives  11.3 us (9%)
  local copies, waits for them, and re-layouts  4.62 us (4%)
    ppermute x9, waiting for transfers between devices, step_z(): return lax.ppermute(own, 'z', [(z, z ^ offset) for z in range(nz)])  18.1 us
    ppermute x9, starting transfers between devices, step_z(): return lax.ppermute(own, 'z', [(z, z ^ offset) for z in range(nz)])  16.2 us
    ppermute x6, waiting for transfers between devices, send(): lax.ppermute(shares[k], 'sub', hops_to[k])  14.2 us
    all_to_all x1, waiting for transfers between devices, per_device(): lax.all_to_all(turned, 'sub', split_axis=0, concat_axis=0, tiled=True)  11.3 us
    all_to_all x1, blocking collectives, per_device(): sums = lax.all_to_all(sums, axes, split_axis=0, concat_axis=0, tiled=True)  11.3 us
    ppermute x6, starting transfers between devices, send(): lax.ppermute(shares[k], 'sub', hops_to[k])  5.49 us
    ppermute x1, waiting for transfers between devices, per_device(): d_low = lax.ppermute(y_low, 'sub', hops_to[1])  4.64 us
    pallas_call x1, Pallas kernels, per_device(): pl.pallas_call(functools.partial(first_kernel, n_field, len(ops), dof, te...  4.07 us
  transfers between devices with their start and end apart: 34, of which 17 were waited for; matrix products, arithmetic and copies ran while one was open for 2% of the time, Pallas kernels for 7%

profile of v4, /device:TPU:0, one launch (start us, length us, event | category | flops | bytes accessed | tf_op | source)
XLA Modules:
  0.0 120.7 jit_solution(2371006793762339681)
XLA Ops:
  2.3 1.4 %pack.1 = (f32[2,64,1152]{2,1,0:T(8,128)S(1)}, f32[2,64,1152]{2,1,0:T(8,128)S(1)}, f32[4,4,16,128]{3,2,1,0:T(8,128)}, f32[4,4,16,128]{3,2,1,0:T(8,128)S(1)}) custom-call(f32[8,64,576]{2,1,0:T(8,128)S(1)} %copy-done, f32[8,64,64]{2,1,0:T(8,128)S(1)} %copy-done.1), custom_call_target="tpu_custom_call" | custom-call | tf_op jit(solution)/shard_map/pack/pallas_call | solution.py:479
  3.7 3.1 %collective-permute-start.9 = (f32[2,64,1152]{2,1,0:T(8,128)S(1)}, f32[2,64,1152]{2,1,0:T(8,128)}, u32[]{:S(2)}, u32[]{:S(2)}) collective-permute-start(f32[2,64,1152]{2,1,0:T(8,128)S(1)} %get-tuple-element.41.rest_8_), channel_id=1, source_target_pairs={{0,2},{1,3},{2,0},{3,1},{4,6},{5,7},{6,4},{7,5},{8,10},{9,11},{10,... | collective-permute-start | bytes 1769480 | tf_op jit(solution)/shard_map/ppermute | solution.py:493
  6.7 1.5 %collective-permute-start.8 = (f32[2,64,1152]{2,1,0:T(8,128)S(1)}, f32[2,64,1152]{2,1,0:T(8,128)}, u32[]{:S(2)}, u32[]{:S(2)}) collective-permute-start(f32[2,64,1152]{2,1,0:T(8,128)S(1)} %get-tuple-element.42.rest_9_), channel_id=1, source_target_pairs={{0,1},{1,0},{2,3},{3,2},{4,5},{5,4},{6,7},{7,6},{8,9},{9,8},{10,11... | collective-permute-start | bytes 1769480 | tf_op jit(solution)/shard_map/ppermute | solution.py:492
  8.2 3.3 %all-to-all-start = ((f32[4,4,16,128]{3,2,1,0:T(8,128)}), f32[4,4,16,128]{3,2,1,0:T(8,128)S(1)}, u32[]{:S(2)}, u32[]{:S(2)}) async-start(f32[4,4,16,128]{3,2,1,0:T(8,128)} %get-tuple-element.40), calls=%async_computation | async-start | bytes 262144 | tf_op jit(solution)/shard_map/all_to_all | solution.py:514
  11.6 11.3 %all-to-all-done = f32[4,4,16,128]{3,2,1,0:T(8,128)S(1)} async-done(((f32[4,4,16,128]{3,2,1,0:T(8,128)}), f32[4,4,16,128]{3,2,1,0:T(8,128)S(1)}, u32[]{:S(2)}, u32[]{:S(2)}) %all-to-all-start) | async-done | bytes 131104 | tf_op jit(solution)/shard_map/all_to_all | solution.py:514
  23.5 2.7 %collective-permute-start.1 = (f32[16,16,128]{2,1,0:T(8,128)S(1)}, f32[16,16,128]{2,1,0:T(8,128)S(1)}, u32[]{:S(2)}, u32[]{:S(2)}) collective-permute-start(f32[16,16,128]{2,1,0:T(8,128)S(1)} %bitcast.6), channel_id=1, source_target_pairs={{0,16},{8,24},{16,0},{24,8},{1,17},{9,25},{17,1},{25,9},{2,18},{10... | collective-permute-start | bytes 393224 | tf_op jit(solution)/shard_map/ppermute | solution.py:523
  26.1 1.6 %collective-permute-start = (f32[16,16,128]{2,1,0:T(8,128)S(1)}, f32[16,16,128]{2,1,0:T(8,128)S(1)}, u32[]{:S(2)}, u32[]{:S(2)}) collective-permute-start(f32[16,16,128]{2,1,0:T(8,128)S(1)} %bitcast.7), channel_id=1, source_target_pairs={{0,8},{8,0},{16,24},{24,16},{1,9},{9,1},{17,25},{25,17},{2,10},{10... | collective-permute-start | bytes 393224 | tf_op jit(solution)/shard_map/ppermute | solution.py:523
  27.7 3.8 %collective-permute-done.1.rest_2_ = f32[16,16,128]{2,1,0:T(8,128)S(1)} collective-permute-done((f32[16,16,128]{2,1,0:T(8,128)S(1)}, f32[16,16,128]{2,1,0:T(8,128)S(1)}, u32[]{:S(2)}, u32[]{:S(2)}) %collective-permute-start.1) | collective-permute-done | bytes 131104 | tf_op jit(solution)/shard_map/ppermute | solution.py:523
  32.2 1.9 %collective-permute-start.7 = (f32[2,64,1152]{2,1,0:T(8,128)S(1)}, f32[2,64,1152]{2,1,0:T(8,128)}, u32[]{:S(2)}, u32[]{:S(2)}) collective-permute-start(f32[2,64,1152]{2,1,0:T(8,128)S(1)} %get-tuple-element.41.rest_8_), channel_id=1, source_target_pairs={{0,1},{1,0},{2,3},{3,2},{4,5},{5,4},{6,7},{7,6},{8,9},{9,8},{10,11... | collective-permute-start | bytes 1769480 | tf_op jit(solution)/shard_map/ppermute | solution.py:494
  36.2 4.4 %collective-permute-done.2.rest_3_ = f32[16,16,128]{2,1,0:T(8,128)S(1)} collective-permute-done((f32[16,16,128]{2,1,0:T(8,128)S(1)}, f32[16,16,128]{2,1,0:T(8,128)S(1)}, u32[]{:S(2)}, u32[]{:S(2)}) %collective-permute-start.2) | collective-permute-done | bytes 131104 | tf_op jit(solution)/shard_map/ppermute | solution.py:523
  40.6 1.3 %collective-permute-done.5.rest_6_ = f32[16,16,128]{2,1,0:T(8,128)S(1)} collective-permute-done((f32[16,16,128]{2,1,0:T(8,128)S(1)}, f32[16,16,128]{2,1,0:T(8,128)S(1)}, u32[]{:S(2)}, u32[]{:S(2)}) %collective-permute-start.5) | collective-permute-done | bytes 131104 | tf_op jit(solution)/shard_map/ppermute | solution.py:531
  45.3 3.5 %positions.1.pos = s32[288]{0:T(512)S(1)} custom-call(s32[3]{0:T(128)S(1)} %pad_add_fusion.ids, s32[256]{0:T(256)S(1)} %copy-done.2, s32[2048]{0:T(1024)S(1)} %reshape.22.table), custom_call_target="tpu_custom_call" | custom-call | tf_op jit(solution)/shard_map/positions/pallas_call | solution.py:497
  48.9 4.1 %first.1 = (f32[12,16,128]{2,1,0:T(8,128)S(1)}, bf16[12,576,256]{2,1,0:T(8,128)(2,1)S(1)}, f32[256,16,128]{2,1,0:T(8,128)S(1)}) custom-call(s32[288]{0:T(512)S(1)} %positions.1.pos, f32[16,16,128]{2,1,0:T(8,128)S(1)} %bitcast.9, f32[16,16,128]{2,1,0:T(8,128)S(1)} %collective-permute-done.rest_1_, f32[16,16,128]{2,1,0:T(8,128)S(1)} %collective-permute-done.1.rest_2_, ...), custom_call_target="tpu_custom_call" | custom-call | tf_op jit(solution)/shard_map/first/pallas_call | solution.py:554
  53.0 4.6 %collective-permute-done.11.rest_0_ = f32[2,64,1152]{2,1,0:T(8,128)S(1)} collective-permute-done((f32[2,64,1152]{2,1,0:T(8,128)}, f32[2,64,1152]{2,1,0:T(8,128)S(1)}, u32[]{:S(2)}, u32[]{:S(2)}) %collective-permute-start.11) | collective-permute-done | bytes 589856 | tf_op jit(solution)/shard_map/ppermute | solution.py:534
  58.8 1.4 %collective-permute-start.14 = (f32[16,16,128]{2,1,0:T(8,128)S(1)}, f32[16,16,128]{2,1,0:T(8,128)S(1)}, u32[]{:S(2)}, u32[]{:S(2)}) collective-permute-start(f32[16,16,128]{2,1,0:T(8,128)S(1)} %get-tuple-element.45.rest_8_), channel_id=1, source_target_pairs={{0,16},{8,24},{16,0},{24,8},{1,17},{9,25},{17,1},{25,9},{2,18},{10... | collective-permute-start | bytes 393224 | tf_op jit(solution)/shard_map/ppermute | solution.py:523
  60.2 3.9 %collective-permute-start.13 = (f32[16,16,128]{2,1,0:T(8,128)S(1)}, f32[16,16,128]{2,1,0:T(8,128)S(1)}, u32[]{:S(2)}, u32[]{:S(2)}) collective-permute-start(f32[16,16,128]{2,1,0:T(8,128)S(1)} %get-tuple-element.45.rest_8_), channel_id=1, source_target_pairs={{0,8},{8,0},{16,24},{24,16},{1,9},{9,1},{17,25},{25,17},{2,10},{10... | collective-permute-start | bytes 393224 | tf_op jit(solution)/shard_map/ppermute | solution.py:523
  64.0 1.8 %collective-permute-done.14.rest_10_ = f32[16,16,128]{2,1,0:T(8,128)S(1)} collective-permute-done((f32[16,16,128]{2,1,0:T(8,128)S(1)}, f32[16,16,128]{2,1,0:T(8,128)S(1)}, u32[]{:S(2)}, u32[]{:S(2)}) %collective-permute-start.14) | collective-permute-done | bytes 131104 | tf_op jit(solution)/shard_map/ppermute | solution.py:523
  65.9 1.5 %collective-permute-start.15 = (f32[16,16,128]{2,1,0:T(8,128)S(1)}, f32[16,16,128]{2,1,0:T(8,128)S(1)}, u32[]{:S(2)}, u32[]{:S(2)}) collective-permute-start(f32[16,16,128]{2,1,0:T(8,128)S(1)} %collective-permute-done.14.rest_10_), channel_id=1, source_target_pairs={{0,8},{8,0},{16,24},{24,16},{1,9},{9,1},{17,25},{25,17},{2,10},{10... | collective-permute-start | bytes 393224 | tf_op jit(solution)/shard_map/ppermute | solution.py:523
  68.0 2.8 %collective-permute-done.15.rest_11_ = f32[16,16,128]{2,1,0:T(8,128)S(1)} collective-permute-done((f32[16,16,128]{2,1,0:T(8,128)S(1)}, f32[16,16,128]{2,1,0:T(8,128)S(1)}, u32[]{:S(2)}, u32[]{:S(2)}) %collective-permute-start.15) | collective-permute-done | bytes 131104 | tf_op jit(solution)/shard_map/ppermute | solution.py:523
  72.2 2.5 %second.1 = (f32[16,16,128]{2,1,0:T(8,128)S(1)}, f32[128,16,128]{2,1,0:T(8,128)S(1)}, f32[16,128]{1,0:T(8,128)S(1)}, f32[4,16,128]{2,1,0:T(8,128)S(1)}, f32[4,16...) custom-call(s32[288]{0:T(512)S(1)} %positions.1.pos, f32[16,16,128]{2,1,0:T(8,128)S(1)} %bitcast.10, ...), custom_call_target="tpu_custom_call" | custom-call | tf_op jit(solution)/shard_map/second/pallas_call | solution.py:598
  74.7 2.3 %collective-permute-start.21 = (f32[16,16,128]{2,1,0:T(8,128)S(1)}, f32[16,16,128]{2,1,0:T(8,128)S(1)}, u32[]{:S(2)}, u32[]{:S(2)}) collective-permute-start(f32[16,16,128]{2,1,0:T(8,128)S(1)} %get-tuple-element.58.rest_8_), channel_id=1, source_target_pairs={{0,16},{8,24},{16,0},{24,8},{1,17},{9,25},{17,1},{25,9},{2,18},{10... | collective-permute-start | bytes 393224 | tf_op jit(solution)/shard_map/ppermute | solution.py:523
  77.0 2.0 %collective-permute-start.20 = (f32[16,16,128]{2,1,0:T(8,128)S(1)}, f32[16,16,128]{2,1,0:T(8,128)S(1)}, u32[]{:S(2)}, u32[]{:S(2)}) collective-permute-start(f32[16,16,128]{2,1,0:T(8,128)S(1)} %get-tuple-element.58.rest_8_), channel_id=1, source_target_pairs={{0,8},{8,0},{16,24},{24,16},{1,9},{9,1},{17,25},{25,17},{2,10},{10... | collective-permute-start | bytes 393224 | tf_op jit(solution)/shard_map/ppermute | solution.py:523
  79.0 5.1 %collective-permute-done.21.rest_10_ = f32[16,16,128]{2,1,0:T(8,128)S(1)} collective-permute-done((f32[16,16,128]{2,1,0:T(8,128)S(1)}, f32[16,16,128]{2,1,0:T(8,128)S(1)}, u32[]{:S(2)}, u32[]{:S(2)}) %collective-permute-start.21) | collective-permute-done | bytes 131104 | tf_op jit(solution)/shard_map/ppermute | solution.py:523
  84.3 1.5 %collective-permute-start.27 = (f32[4,16,128]{2,1,0:T(8,128)S(1)}, f32[4,16,128]{2,1,0:T(8,128)S(1)}, u32[]{:S(2)}, u32[]{:S(2)}) collective-permute-start(f32[4,16,128]{2,1,0:T(8,128)S(1)} %get-tuple-element.51), channel_id=1, source_target_pairs={{0,1},{1,0},{2,3},{3,2},{4,5},{5,4},{6,7},{7,6},{8,9},{9,8},{10,11... | collective-permute-start | bytes 98312 | tf_op jit(solution)/shard_map/ppermute | solution.py:593
  88.2 1.5 %collective-permute-done.28.rest_2_ = f32[4,16,128]{2,1,0:T(8,128)S(1)} collective-permute-done((f32[4,16,128]{2,1,0:T(8,128)S(1)}, f32[4,16,128]{2,1,0:T(8,128)S(1)}, u32[]{:S(2)}, u32[]{:S(2)}) %collective-permute-start.28) | collective-permute-done | bytes 32800 | tf_op jit(solution)/shard_map/ppermute | solution.py:593
  90.3 1.6 %collective-permute-done.29.rest_3_ = f32[4,16,128]{2,1,0:T(8,128)S(1)} collective-permute-done((f32[4,16,128]{2,1,0:T(8,128)S(1)}, f32[4,16,128]{2,1,0:T(8,128)S(1)}, u32[]{:S(2)}, u32[]{:S(2)}) %collective-permute-start.29) | collective-permute-done | bytes 32800 | tf_op jit(solution)/shard_map/ppermute | solution.py:593
  92.6 3.3 %collective-permute-done.30.rest_5_ = f32[4,16,128]{2,1,0:T(8,128)S(1)} collective-permute-done((f32[4,16,128]{2,1,0:T(8,128)S(1)}, f32[4,16,128]{2,1,0:T(8,128)S(1)}, u32[]{:S(2)}, u32[]{:S(2)}) %collective-permute-start.30) | collective-permute-done | bytes 32800 | tf_op jit(solution)/shard_map/ppermute | solution.py:593
  96.6 3.2 %collective-permute-done.31.rest_6_ = f32[4,16,128]{2,1,0:T(8,128)S(1)} collective-permute-done((f32[4,16,128]{2,1,0:T(8,128)S(1)}, f32[4,16,128]{2,1,0:T(8,128)S(1)}, u32[]{:S(2)}, u32[]{:S(2)}) %collective-permute-start.31) | collective-permute-done | bytes 32800 | tf_op jit(solution)/shard_map/ppermute | solution.py:593
  100.5 4.2 %collective-permute-done.32.rest_7_ = f32[4,16,128]{2,1,0:T(8,128)S(1)} collective-permute-done((f32[4,16,128]{2,1,0:T(8,128)S(1)}, f32[4,16,128]{2,1,0:T(8,128)S(1)}, u32[]{:S(2)}, u32[]{:S(2)}) %collective-permute-start.32) | collective-permute-done | bytes 32800 | tf_op jit(solution)/shard_map/ppermute | solution.py:593
  104.7 3.0 %third.1 = f32[32,2,128]{2,1,0:T(2,128)S(1)} custom-call(s32[288]{0:T(512)S(1)} %positions.1.pos, f32[128,16,128]{2,1,0:T(8,128)S(1)} %get-tuple-element.47.basis, f32[16,128]{1,0:T(8,128)S(1)} %get-tuple-element.48.coeffs, f32[16,16,128]{2,1,0:T(8,128)S(1)} %bitcast.11, f32[16,16,128]{2,1,0:T(8,128)S(1)} %collective-permute-done.rest_1_, ...), custom_call_target="tpu_custom_call" | custom-call | tf_op jit(solution)/shard_map/third/pallas_call | solution.py:615
  107.6 11.3 %all_to_all.10.info = f32[32,2,128]{2,1,0:T(2,128)S(1)} all-to-all(f32[32,2,128]{2,1,0:T(2,128)S(1)} %third.1), channel_id=1, replica_groups=mesh['z'=4,'core'=2,'sub'=4] {'z','core','sub'}, dimensions={0} | all-to-all | bytes 65536 | tf_op jit(solution)/shard_map/all_to_all | solution.py:625
  119.0 1.7 %finish.1 = f32[8,64,64]{2,1,0:T(8,128)} custom-call(s32[3]{0:T(128)S(1)} %pad_add_fusion.ids, f32[32,2,128]{2,1,0:T(2,128)S(1)} %all_to_all.10.info, f32[4,4,16,128]{3,2,1,0:T(8,128)S(1)} %get-tuple-element.66.turned, f32[4,16,128]{2,1,0:T(8,128)S(1)} %get-tuple-element.67.rest_0_, f32[4,16,128]{2,1,0:T(8,128)S(1)} %collective-permute-done.27.rest_1_, ...), custom_call_target="tpu_custom_call" | custom-call | tf_op jit(solution)/shard_map/finish/pallas_call | solution.py:628
  (59 shorter events, 17.3 us)
Async XLA Ops:
  3.7 30.5 %collective-permute-start.9 = (f32[2,64,1152]{2,1,0:T(8,128)S(1)}, f32[2,64,1152]{2,1,0:T(8,128)}, u32[]{:S(2)}, u32[]{:S(2)}) collective-permute-start(f32[2,64,1152]{2,1,0:T(8,128)S(1)} %get-tuple-element.41.rest_8_), channel_id=1, source_target_pairs={{0,2},{1,3},{2,0},{3,1},{4,6},{5,7},{6,4},{7,5},{8,10},{9,11},{10,... | collective-permute-start | bytes 1769480 | tf_op jit(solution)/shard_map/ppermute | solution.py:493
  6.7 27.6 %collective-permute-start.8 = (f32[2,64,1152]{2,1,0:T(8,128)S(1)}, f32[2,64,1152]{2,1,0:T(8,128)}, u32[]{:S(2)}, u32[]{:S(2)}) collective-permute-start(f32[2,64,1152]{2,1,0:T(8,128)S(1)} %get-tuple-element.42.rest_9_), channel_id=1, source_target_pairs={{0,1},{1,0},{2,3},{3,2},{4,5},{5,4},{6,7},{7,6},{8,9},{9,8},{10,11... | collective-permute-start | bytes 1769480 | tf_op jit(solution)/shard_map/ppermute | solution.py:492
  8.2 14.7 %all-to-all-start = ((f32[4,4,16,128]{3,2,1,0:T(8,128)}), f32[4,4,16,128]{3,2,1,0:T(8,128)S(1)}, u32[]{:S(2)}, u32[]{:S(2)}) async-start(f32[4,4,16,128]{3,2,1,0:T(8,128)} %get-tuple-element.40), calls=%async_computation | async-start | bytes 262144 | tf_op jit(solution)/shard_map/all_to_all | solution.py:514
  23.5 8.1 %collective-permute-start.1 = (f32[16,16,128]{2,1,0:T(8,128)S(1)}, f32[16,16,128]{2,1,0:T(8,128)S(1)}, u32[]{:S(2)}, u32[]{:S(2)}) collective-permute-start(f32[16,16,128]{2,1,0:T(8,128)S(1)} %bitcast.6), channel_id=1, source_target_pairs={{0,16},{8,24},{16,0},{24,8},{1,17},{9,25},{17,1},{25,9},{2,18},{10... | collective-permute-start | bytes 393224 | tf_op jit(solution)/shard_map/ppermute | solution.py:523
  26.1 6.1 %collective-permute-start = (f32[16,16,128]{2,1,0:T(8,128)S(1)}, f32[16,16,128]{2,1,0:T(8,128)S(1)}, u32[]{:S(2)}, u32[]{:S(2)}) collective-permute-start(f32[16,16,128]{2,1,0:T(8,128)S(1)} %bitcast.7), channel_id=1, source_target_pairs={{0,8},{8,0},{16,24},{24,16},{1,9},{9,1},{17,25},{25,17},{2,10},{10... | collective-permute-start | bytes 393224 | tf_op jit(solution)/shard_map/ppermute | solution.py:523
  27.7 7.9 %collective-permute-start.3 = (f32[16,16,128]{2,1,0:T(8,128)S(1)}, f32[16,16,128]{2,1,0:T(8,128)S(1)}, u32[]{:S(2)}, u32[]{:S(2)}) collective-permute-start(f32[16,16,128]{2,1,0:T(8,128)S(1)} %bitcast.8), channel_id=1, source_target_pairs={{0,4},{4,0},{1,5},{5,1},{2,6},{6,2},{3,7},{7,3},{8,12},{12,8},{9,1... | collective-permute-start | bytes 393224 | tf_op jit(solution)/shard_map/ppermute | solution.py:531
  31.6 17.3 %collective-permute-start.10 = (f32[2,64,1152]{2,1,0:T(8,128)S(1)}, f32[2,64,1152]{2,1,0:T(8,128)}, u32[]{:S(2)}, u32[]{:S(2)}) collective-permute-start(f32[2,64,1152]{2,1,0:T(8,128)S(1)} %get-tuple-element.42.rest_9_), channel_id=1, source_target_pairs={{0,2},{1,3},{2,0},{3,1},{4,6},{5,7},{6,4},{7,5},{8,10},{9,11},{10,... | collective-permute-start | bytes 1769480 | tf_op jit(solution)/shard_map/ppermute | solution.py:495
  32.2 16.6 %collective-permute-start.7 = (f32[2,64,1152]{2,1,0:T(8,128)S(1)}, f32[2,64,1152]{2,1,0:T(8,128)}, u32[]{:S(2)}, u32[]{:S(2)}) collective-permute-start(f32[2,64,1152]{2,1,0:T(8,128)S(1)} %get-tuple-element.41.rest_8_), channel_id=1, source_target_pairs={{0,1},{1,0},{2,3},{3,2},{4,5},{5,4},{6,7},{7,6},{8,9},{9,8},{10,11... | collective-permute-start | bytes 1769480 | tf_op jit(solution)/shard_map/ppermute | solution.py:494
  34.2 23.4 %collective-permute-start.11 = (f32[2,64,1152]{2,1,0:T(8,128)}, f32[2,64,1152]{2,1,0:T(8,128)S(1)}, u32[]{:S(2)}, u32[]{:S(2)}) collective-permute-start(f32[2,64,1152]{2,1,0:T(8,128)} %collective-permute-done.9.rest_12_), channel_id=1, source_target_pairs={{0,1},{1,0},{2,3},{3,2},{4,5},{5,4},{6,7},{7,6},{8,9},{9,8},{10,11... | collective-permute-start | bytes 1769480 | tf_op jit(solution)/shard_map/ppermute | solution.py:534
  34.3 23.3 %collective-permute-start.12 = (f32[2,64,1152]{2,1,0:T(8,128)}, f32[2,64,1152]{2,1,0:T(8,128)S(1)}, u32[]{:S(2)}, u32[]{:S(2)}) collective-permute-start(f32[2,64,1152]{2,1,0:T(8,128)} %collective-permute-done.8.rest_11_), channel_id=1, source_target_pairs={{0,2},{1,3},{2,0},{3,1},{4,6},{5,7},{6,4},{7,5},{8,10},{9,11},{10,... | collective-permute-start | bytes 1769480 | tf_op jit(solution)/shard_map/ppermute | solution.py:535
  35.6 5.0 %collective-permute-start.2 = (f32[16,16,128]{2,1,0:T(8,128)S(1)}, f32[16,16,128]{2,1,0:T(8,128)S(1)}, u32[]{:S(2)}, u32[]{:S(2)}) collective-permute-start(f32[16,16,128]{2,1,0:T(8,128)S(1)} %collective-permute-done.1.rest_2_), channel_id=1, source_target_pairs={{0,8},{8,0},{16,24},{24,16},{1,9},{9,1},{17,25},{25,17},{2,10},{10... | collective-permute-start | bytes 393224 | tf_op jit(solution)/shard_map/ppermute | solution.py:523
  43.3 5.6 %collective-permute-start.6 = (f32[16,16,128]{2,1,0:T(8,128)S(1)}, f32[16,16,128]{2,1,0:T(8,128)S(1)}, u32[]{:S(2)}, u32[]{:S(2)}) collective-permute-start(f32[16,16,128]{2,1,0:T(8,128)S(1)} %collective-permute-done.2.rest_3_), channel_id=1, source_target_pairs={{0,4},{4,0},{1,5},{5,1},{2,6},{6,2},{3,7},{7,3},{8,12},{12,8},{9,1... | collective-permute-start | bytes 393224 | tf_op jit(solution)/shard_map/ppermute | solution.py:531
  58.8 7.1 %collective-permute-start.14 = (f32[16,16,128]{2,1,0:T(8,128)S(1)}, f32[16,16,128]{2,1,0:T(8,128)S(1)}, u32[]{:S(2)}, u32[]{:S(2)}) collective-permute-start(f32[16,16,128]{2,1,0:T(8,128)S(1)} %get-tuple-element.45.rest_8_), channel_id=1, source_target_pairs={{0,16},{8,24},{16,0},{24,8},{1,17},{9,25},{17,1},{25,9},{2,18},{10... | collective-permute-start | bytes 393224 | tf_op jit(solution)/shard_map/ppermute | solution.py:523
  60.2 7.9 %collective-permute-start.13 = (f32[16,16,128]{2,1,0:T(8,128)S(1)}, f32[16,16,128]{2,1,0:T(8,128)S(1)}, u32[]{:S(2)}, u32[]{:S(2)}) collective-permute-start(f32[16,16,128]{2,1,0:T(8,128)S(1)} %get-tuple-element.45.rest_8_), channel_id=1, source_target_pairs={{0,8},{8,0},{16,24},{24,16},{1,9},{9,1},{17,25},{25,17},{2,10},{10... | collective-permute-start | bytes 393224 | tf_op jit(solution)/shard_map/ppermute | solution.py:523
  65.9 5.0 %collective-permute-start.15 = (f32[16,16,128]{2,1,0:T(8,128)S(1)}, f32[16,16,128]{2,1,0:T(8,128)S(1)}, u32[]{:S(2)}, u32[]{:S(2)}) collective-permute-start(f32[16,16,128]{2,1,0:T(8,128)S(1)} %collective-permute-done.14.rest_10_), channel_id=1, source_target_pairs={{0,8},{8,0},{16,24},{24,16},{1,9},{9,1},{17,25},{25,17},{2,10},{10... | collective-permute-start | bytes 393224 | tf_op jit(solution)/shard_map/ppermute | solution.py:523
  67.4 3.9 %collective-permute-start.16 = (f32[16,16,128]{2,1,0:T(8,128)S(1)}, f32[16,16,128]{2,1,0:T(8,128)S(1)}, u32[]{:S(2)}, u32[]{:S(2)}) collective-permute-start(f32[16,16,128]{2,1,0:T(8,128)S(1)} %get-tuple-element.45.rest_8_), channel_id=1, source_target_pairs={{0,4},{4,0},{1,5},{5,1},{2,6},{6,2},{3,7},{7,3},{8,12},{12,8},{9,1... | collective-permute-start | bytes 393224 | tf_op jit(solution)/shard_map/ppermute | solution.py:531
  67.4 3.9 %collective-permute-start.18 = (f32[16,16,128]{2,1,0:T(8,128)S(1)}, f32[16,16,128]{2,1,0:T(8,128)S(1)}, u32[]{:S(2)}, u32[]{:S(2)}) collective-permute-start(f32[16,16,128]{2,1,0:T(8,128)S(1)} %collective-permute-done.14.rest_10_), channel_id=1, source_target_pairs={{0,4},{4,0},{1,5},{5,1},{2,6},{6,2},{3,7},{7,3},{8,12},{12,8},{9,1... | collective-permute-start | bytes 393224 | tf_op jit(solution)/shard_map/ppermute | solution.py:531
  68.0 3.3 %collective-permute-start.17 = (f32[16,16,128]{2,1,0:T(8,128)S(1)}, f32[16,16,128]{2,1,0:T(8,128)S(1)}, u32[]{:S(2)}, u32[]{:S(2)}) collective-permute-start(f32[16,16,128]{2,1,0:T(8,128)S(1)} %collective-permute-done.13.rest_9_), channel_id=1, source_target_pairs={{0,4},{4,0},{1,5},{5,1},{2,6},{6,2},{3,7},{7,3},{8,12},{12,8},{9,1... | collective-permute-start | bytes 393224 | tf_op jit(solution)/shard_map/ppermute | solution.py:531
  70.8 1.3 %collective-permute-start.19 = (f32[16,16,128]{2,1,0:T(8,128)S(1)}, f32[16,16,128]{2,1,0:T(8,128)S(1)}, u32[]{:S(2)}, u32[]{:S(2)}) collective-permute-start(f32[16,16,128]{2,1,0:T(8,128)S(1)} %collective-permute-done.15.rest_11_), channel_id=1, source_target_pairs={{0,4},{4,0},{1,5},{5,1},{2,6},{6,2},{3,7},{7,3},{8,12},{12,8},{9,1... | collective-permute-start | bytes 393224 | tf_op jit(solution)/shard_map/ppermute | solution.py:531
  74.7 9.4 %collective-permute-start.21 = (f32[16,16,128]{2,1,0:T(8,128)S(1)}, f32[16,16,128]{2,1,0:T(8,128)S(1)}, u32[]{:S(2)}, u32[]{:S(2)}) collective-permute-start(f32[16,16,128]{2,1,0:T(8,128)S(1)} %get-tuple-element.58.rest_8_), channel_id=1, source_target_pairs={{0,16},{8,24},{16,0},{24,8},{1,17},{9,25},{17,1},{25,9},{2,18},{10... | collective-permute-start | bytes 393224 | tf_op jit(solution)/shard_map/ppermute | solution.py:523
  77.0 12.8 %collective-permute-start.20 = (f32[16,16,128]{2,1,0:T(8,128)S(1)}, f32[16,16,128]{2,1,0:T(8,128)S(1)}, u32[]{:S(2)}, u32[]{:S(2)}) collective-permute-start(f32[16,16,128]{2,1,0:T(8,128)S(1)} %get-tuple-element.58.rest_8_), channel_id=1, source_target_pairs={{0,8},{8,0},{16,24},{24,16},{1,9},{9,1},{17,25},{25,17},{2,10},{10... | collective-permute-start | bytes 393224 | tf_op jit(solution)/shard_map/ppermute | solution.py:523
  84.1 6.2 %collective-permute-start.22 = (f32[16,16,128]{2,1,0:T(8,128)S(1)}, f32[16,16,128]{2,1,0:T(8,128)S(1)}, u32[]{:S(2)}, u32[]{:S(2)}) collective-permute-start(f32[16,16,128]{2,1,0:T(8,128)S(1)} %collective-permute-done.21.rest_10_), channel_id=1, source_target_pairs={{0,8},{8,0},{16,24},{24,16},{1,9},{9,1},{17,25},{25,17},{2,10},{10... | collective-permute-start | bytes 393224 | tf_op jit(solution)/shard_map/ppermute | solution.py:523
  84.3 3.9 %collective-permute-start.27 = (f32[4,16,128]{2,1,0:T(8,128)S(1)}, f32[4,16,128]{2,1,0:T(8,128)S(1)}, u32[]{:S(2)}, u32[]{:S(2)}) collective-permute-start(f32[4,16,128]{2,1,0:T(8,128)S(1)} %get-tuple-element.51), channel_id=1, source_target_pairs={{0,1},{1,0},{2,3},{3,2},{4,5},{5,4},{6,7},{7,6},{8,9},{9,8},{10,11... | collective-permute-start | bytes 98312 | tf_op jit(solution)/shard_map/ppermute | solution.py:593
  85.8 3.9 %collective-permute-start.28 = (f32[4,16,128]{2,1,0:T(8,128)S(1)}, f32[4,16,128]{2,1,0:T(8,128)S(1)}, u32[]{:S(2)}, u32[]{:S(2)}) collective-permute-start(f32[4,16,128]{2,1,0:T(8,128)S(1)} %get-tuple-element.52), channel_id=1, source_target_pairs={{0,2},{1,3},{2,0},{3,1},{4,6},{5,7},{6,4},{7,5},{8,10},{9,11},{10,... | collective-permute-start | bytes 98312 | tf_op jit(solution)/shard_map/ppermute | solution.py:593
  87.2 4.8 %collective-permute-start.29 = (f32[4,16,128]{2,1,0:T(8,128)S(1)}, f32[4,16,128]{2,1,0:T(8,128)S(1)}, u32[]{:S(2)}, u32[]{:S(2)}) collective-permute-start(f32[4,16,128]{2,1,0:T(8,128)S(1)} %get-tuple-element.53), channel_id=1, source_target_pairs={{0,3},{1,2},{2,1},{3,0},{4,7},{5,6},{6,5},{7,4},{8,11},{9,10},{10,... | collective-permute-start | bytes 98312 | tf_op jit(solution)/shard_map/ppermute | solution.py:593
  88.2 16.4 %collective-permute-start.23 = (f32[16,16,128]{2,1,0:T(8,128)S(1)}, f32[16,16,128]{2,1,0:T(8,128)S(1)}, u32[]{:S(2)}, u32[]{:S(2)}) collective-permute-start(f32[16,16,128]{2,1,0:T(8,128)S(1)} %get-tuple-element.58.rest_8_), channel_id=1, source_target_pairs={{0,4},{4,0},{1,5},{5,1},{2,6},{6,2},{3,7},{7,3},{8,12},{12,8},{9,1... | collective-permute-start | bytes 393224 | tf_op jit(solution)/shard_map/ppermute | solution.py:531
  89.8 14.9 %collective-permute-start.25 = (f32[16,16,128]{2,1,0:T(8,128)S(1)}, f32[16,16,128]{2,1,0:T(8,128)S(1)}, u32[]{:S(2)}, u32[]{:S(2)}) collective-permute-start(f32[16,16,128]{2,1,0:T(8,128)S(1)} %collective-permute-done.21.rest_10_), channel_id=1, source_target_pairs={{0,4},{4,0},{1,5},{5,1},{2,6},{6,2},{3,7},{7,3},{8,12},{12,8},{9,1... | collective-permute-start | bytes 393224 | tf_op jit(solution)/shard_map/ppermute | solution.py:531
  89.8 14.9 %collective-permute-start.24 = (f32[16,16,128]{2,1,0:T(8,128)S(1)}, f32[16,16,128]{2,1,0:T(8,128)S(1)}, u32[]{:S(2)}, u32[]{:S(2)}) collective-permute-start(f32[16,16,128]{2,1,0:T(8,128)S(1)} %collective-permute-done.20.rest_9_), channel_id=1, source_target_pairs={{0,4},{4,0},{1,5},{5,1},{2,6},{6,2},{3,7},{7,3},{8,12},{12,8},{9,1... | collective-permute-start | bytes 393224 | tf_op jit(solution)/shard_map/ppermute | solution.py:531
  90.3 14.4 %collective-permute-start.26 = (f32[16,16,128]{2,1,0:T(8,128)S(1)}, f32[16,16,128]{2,1,0:T(8,128)S(1)}, u32[]{:S(2)}, u32[]{:S(2)}) collective-permute-start(f32[16,16,128]{2,1,0:T(8,128)S(1)} %collective-permute-done.22.rest_11_), channel_id=1, source_target_pairs={{0,4},{4,0},{1,5},{5,1},{2,6},{6,2},{3,7},{7,3},{8,12},{12,8},{9,1... | collective-permute-start | bytes 393224 | tf_op jit(solution)/shard_map/ppermute | solution.py:531
  92.0 3.9 %collective-permute-start.30 = (f32[4,16,128]{2,1,0:T(8,128)S(1)}, f32[4,16,128]{2,1,0:T(8,128)S(1)}, u32[]{:S(2)}, u32[]{:S(2)}) collective-permute-start(f32[4,16,128]{2,1,0:T(8,128)S(1)} %get-tuple-element.55), channel_id=1, source_target_pairs={{0,1},{1,0},{2,3},{3,2},{4,5},{5,4},{6,7},{7,6},{8,9},{9,8},{10,11... | collective-permute-start | bytes 98312 | tf_op jit(solution)/shard_map/ppermute | solution.py:593
  95.9 3.9 %collective-permute-start.31 = (f32[4,16,128]{2,1,0:T(8,128)S(1)}, f32[4,16,128]{2,1,0:T(8,128)S(1)}, u32[]{:S(2)}, u32[]{:S(2)}) collective-permute-start(f32[4,16,128]{2,1,0:T(8,128)S(1)} %get-tuple-element.56), channel_id=1, source_target_pairs={{0,2},{1,3},{2,0},{3,1},{4,6},{5,7},{6,4},{7,5},{8,10},{9,11},{10,... | collective-permute-start | bytes 98312 | tf_op jit(solution)/shard_map/ppermute | solution.py:593
  99.8 4.8 %collective-permute-start.32 = (f32[4,16,128]{2,1,0:T(8,128)S(1)}, f32[4,16,128]{2,1,0:T(8,128)S(1)}, u32[]{:S(2)}, u32[]{:S(2)}) collective-permute-start(f32[4,16,128]{2,1,0:T(8,128)S(1)} %get-tuple-element.57), channel_id=1, source_target_pairs={{0,3},{1,2},{2,1},{3,0},{4,7},{5,6},{6,5},{7,4},{8,11},{9,10},{10,... | collective-permute-start | bytes 98312 | tf_op jit(solution)/shard_map/ppermute | solution.py:593
  (6 other events, 89.2 us)

commit v5 on v4

--- a/solution.py
+++ b/solution.py
@@ -208,33 +208,47 @@
     return copies
 
 
-def over_pairs(fields, step, init):
-    n_pair = fields[0].shape[0]
-    for block in range(len(fields)):
-        init = lax.fori_loop(
-            0, n_pair, lambda pair, carry, block=block: step(block, pair, carry), init, unroll=16
-        )
+def over_pairs(blocks, step, init):
+    spot = 0
+    for block, chunks in enumerate(blocks):
+        start = 0
+        for chunk in chunks:
+
+            def body(pair, carry, block=block, chunk=chunk, start=start, spot=spot):
+                return step(block, chunk[pair], start + pair, spot + pair, carry)
+
+            init = lax.fori_loop(0, chunk.shape[0], body, init, unroll=True)
+            start += chunk.shape[0]
+            spot += chunk.shape[0]
     return init
 
 
-def share_out(values, shares):
+def in_blocks(refs, chunks):
+    size = len(refs) // chunks
+    return [[refs[chunk * size + block] for chunk in range(chunks)] for block in range(size)]
+
+
+def share_out(chunks, values, shares):
+    first = [(chunk, pair) for chunk in chunks for pair in range(chunk.shape[0])]
     for index, share in enumerate(shares):
-        for inner in range(share.shape[0]):
-            share[inner] = values[index * share.shape[0] + inner]
+        for inner in range(share.shape[1]):
+            spot = index * share.shape[1] + inner
+            chunk, pair = first[spot]
+            share[0, inner] = chunk[pair]
+            share[1, inner] = values[spot]
 
 
 def first_kernel(n_field, count, dof, terms, pos, *rest):
     fields, ops, rest = rest[:n_field], rest[n_field : n_field + count], rest[n_field + count :]
     out, split, dup = rest[:3]
-    held, sems = rest[3 : count + 3], rest[count + 3]
+    held, sems = rest[3 : 3 + count], rest[3 + count]
     copies = start_copies(ops, held, sems)
-    n_pair = fields[0].shape[0]
-
-    def build(block, pair, carry):
-        spread(dup, block * n_pair + pair, fields[block][pair], dof)
+
+    def build(block, value, pair, spot, carry):
+        spread(dup, spot, value, dof)
         return carry
 
-    over_pairs(fields, build, 0)
+    over_pairs(in_blocks(fields, 1), build, 0)
     for copy in copies:
         copy.wait()
 
@@ -250,16 +264,14 @@
             base += 1
 
 
-def more_kernel(count, dof, terms, pos, dup, before, *rest):
-    ops, out, shares = rest[:count], rest[count], rest[count + 1 :]
-    base = before.shape[0]
-    for pair in range(base):
-        out[pair] = before[pair]
+def more_kernel(base, dof, terms, pos, dup, *rest):
+    ops, out = rest[:-1], rest[-1]
+    done = 0
     for op in ops:
         for inner in range(op.shape[0]):
-            out[base] = rows_product(row_pairs(op, inner, dof), 2 * base, pos, dup, terms, dof)
-            base += 1
-    share_out(out, shares)
+            local = 2 * (base + done)
+            out[done] = rows_product(row_pairs(op, inner, dof), local, pos, dup, terms, dof)
+            done += 1
 
 
 def turn_kernel(count, dof, *rest):
@@ -271,49 +283,50 @@
             base += 1
 
 
-def second_kernel(n_field, count, sends, dof, terms, pos, *rest):
-    b_ref, z_ref, rest = rest[:n_field], rest[n_field : 2 * n_field], rest[2 * n_field :]
+def second_kernel(n_field, chunks, count, sends, dof, terms, pos, *rest):
+    b_ref, rest = rest[:n_field], rest[n_field:]
+    z_blocks, rest = in_blocks(rest[: chunks * n_field], chunks), rest[chunks * n_field :]
     stages, (out, basis, coeffs) = rest[:count], rest[count : count + 3]
     shares, dup = rest[count + 3 : count + 3 + sends], rest[count + 3 + sends]
-    n_pair = b_ref[0].shape[0]
     shape = b_ref[0].shape[1:]
     zero = jnp.zeros(shape, F32)
 
-    def dots(block, pair, carry):
-        b, z = b_ref[block][pair], z_ref[block][pair]
+    def dots(block, z, pair, spot, carry):
+        b = b_ref[block][pair]
         return carry[0] + b * b, carry[1] + b * z
 
-    norm, cross = over_pairs(b_ref, dots, (zero, zero))
+    norm, cross = over_pairs(z_blocks, dots, (zero, zero))
     beta = jnp.sqrt(lane_sum(norm))
     scale = 1.0 / beta
     h00 = lane_sum(cross) * scale * scale
 
-    def remove(block, pair, carry):
-        w = z_ref[block][pair] * scale - (h00 * scale) * b_ref[block][pair]
-        basis[block * n_pair + pair] = w
+    def remove(block, z, pair, spot, carry):
+        w = z * scale - (h00 * scale) * b_ref[block][pair]
+        basis[spot] = w
         return carry + w * w
 
-    h10 = jnp.sqrt(lane_sum(over_pairs(b_ref, remove, zero)))
+    h10 = jnp.sqrt(lane_sum(over_pairs(z_blocks, remove, zero)))
     unit = 1.0 / h10
 
-    def build(block, pair, carry):
-        v = basis[block * n_pair + pair] * unit
-        basis[block * n_pair + pair] = v
-        spread(dup, block * n_pair + pair, v, dof)
+    def build(block, w, pair, spot, carry):
+        v = w * unit
+        basis[spot] = v
+        spread(dup, spot, v, dof)
         return carry
 
-    over_pairs(b_ref, build, 0)
+    over_pairs([[basis]], build, 0)
     coeffs[...] = place([beta, h00, h10], shape)
 
     def put(pair, values):
         out[pair] = values
 
     apply_rows(stages, pos, dup, terms, dof, put)
-    share_out(out, shares)
+    share_out(z_blocks[0], out, shares)
 
 
 def third_kernel(n_field, count, dof, terms, pos, basis, coeffs, *rest):
-    b_ref, z_ref, rest = rest[:n_field], rest[n_field : 2 * n_field], rest[2 * n_field :]
+    b_ref, rest = rest[:n_field], rest[n_field:]
+    z_blocks, rest = in_blocks(rest[:n_field], 1), rest[n_field:]
     stages, (sums, work, dup, image) = rest[:count], rest[count:]
     b_mine = b_ref[0]
     n_pair = b_mine.shape[0]
@@ -322,33 +335,28 @@
     known = coeffs[...]
     scale = 1.0 / known[:, 0:1]
 
-    def dots(block, pair, carry):
-        z = z_ref[block][pair]
-        return carry[0] + b_ref[block][pair] * z, carry[1] + basis[block * n_pair + pair] * z
-
-    first, second = over_pairs(b_ref, dots, (zero, zero))
+    def dots(block, z, pair, spot, carry):
+        return carry[0] + b_ref[block][pair] * z, carry[1] + basis[spot] * z
+
+    first, second = over_pairs(z_blocks, dots, (zero, zero))
     h01 = lane_sum(first) * scale
     h11 = lane_sum(second)
 
-    def remove(block, pair, carry):
-        w = (
-            z_ref[block][pair]
-            - (h01 * scale) * b_ref[block][pair]
-            - h11 * basis[block * n_pair + pair]
-        )
-        work[block * n_pair + pair] = w
+    def remove(block, z, pair, spot, carry):
+        w = z - (h01 * scale) * b_ref[block][pair] - h11 * basis[spot]
+        work[spot] = w
         return carry + w * w
 
-    h21 = jnp.sqrt(lane_sum(over_pairs(b_ref, remove, zero)))
+    h21 = jnp.sqrt(lane_sum(over_pairs(z_blocks, remove, zero)))
     unit = 1.0 / h21
 
-    def build(block, pair, carry):
-        v = work[block * n_pair + pair] * unit
-        work[block * n_pair + pair] = v
-        spread(dup, block * n_pair + pair, v, dof)
+    def build(block, w, pair, spot, carry):
+        v = w * unit
+        work[spot] = v
+        spread(dup, spot, v, dof)
         return carry
 
-    over_pairs(b_ref, build, 0)
+    over_pairs([[work]], build, 0)
 
     def put(pair, values):
         image[pair] = values
@@ -415,7 +423,7 @@
 def finish_kernel(dof, ids, info, turned, *rest):
     out, stack, factor = rest[-3:]
     n_sub, per_part, rhs, lanes = turned.shape
-    z1, z2 = rest[:n_sub], rest[n_sub : 2 * n_sub]
+    shares = rest[:n_sub]
     per_row = lanes // rhs
     n_rows = info.shape[1]
     first = [info[quarter] for quarter in range(n_sub)]
@@ -447,8 +455,8 @@
         alpha, beta, gamma = (factor[part * n_sub + quarter] for part in range(3))
         start = pl.multiple_of(quarter * rhs, 8)
         for pair in range(per_part):
-            mixed = alpha * turned[quarter, pair] + beta * z1[k][pair]
-            stack[pair, pl.ds(start, rhs), :] = mixed + gamma * z2[k][pair]
+            mixed = alpha * turned[quarter, pair] + beta * shares[k][0, pair]
+            stack[pair, pl.ds(start, rhs), :] = mixed + gamma * shares[k][1, pair]
     for pair in range(per_part):
         both = stack[pair].T
         out[2 * pair] = both[:dof]
@@ -523,12 +531,14 @@
         return lax.ppermute(own, "z", [(z, z ^ offset) for z in range(nz)])
 
     def gather(own):
-        direct = (2, 1) if nz == 4 else range(1, nz)
-        found = {offset: step_z(own, offset) for offset in direct}
         if nz == 4:
-            found[3] = step_z(found[2], 1)
-        parts = [own] + [found[offset] for offset in range(1, nz)]
-        return parts + [lax.ppermute(part, "core", swap) for part in parts]
+            cross, near = step_z(own, 2), step_z(own, 1)
+            parts = [own, near, cross, step_z(cross, 1)]
+        else:
+            parts = [own] + [step_z(own, offset) for offset in range(1, nz)]
+        for index in range(nz):
+            parts.append(lax.ppermute(parts[index], "core", swap))
+        return parts
 
     if relay:
         d_low = lax.ppermute(y_low, "sub", hops_to[1])
@@ -544,7 +554,7 @@
     small = jax.ShapeDtypeStruct(field[1:], F32)
     own_shape = jax.ShapeDtypeStruct(field, F32)
     sends = n_sub if even else 0
-    share = [jax.ShapeDtypeStruct((per_dev // 2, rhs, lanes), F32)] * sends
+    share = [jax.ShapeDtypeStruct((2, per_dev // 2, rhs, lanes), F32)] * sends
 
     def split_shape(pairs):
         return jax.ShapeDtypeStruct((pairs, width, 4 * dof), BF16)
@@ -565,17 +575,19 @@
         compiler_params=PARAMS,
         name="first",
     )(positions, *b_parts, *ops)
-    splits, shares1 = [split], []
+    splits, chunks = [split], 1
+    z1_parts = gather(z1)
     if relay:
-        ops = stages[1]
-        z1, *shares1 = pl.pallas_call(
-            functools.partial(more_kernel, len(ops), dof, terms),
-            out_shape=[own_shape] + share,
-            in_specs=[SMEM, VMEM, VMEM] + [VMEM] * len(ops),
-            out_specs=[VMEM] * (1 + sends),
+        ops, chunks = stages[1], 2
+        late = pl.pallas_call(
+            functools.partial(more_kernel, done, dof, terms),
+            out_shape=jax.ShapeDtypeStruct((n_own - done,) + field[1:], F32),
+            in_specs=[SMEM, VMEM] + [VMEM] * len(ops),
+            out_specs=VMEM,
             compiler_params=PARAMS,
             name="more",
-        )(positions, spread_b, z1, *ops)
+        )(positions, spread_b, *ops)
+        z1_parts = z1_parts + gather(late)
         split = pl.pallas_call(
             functools.partial(turn_kernel, len(ops), dof),
             out_shape=split_shape(n_own - done),
@@ -585,28 +597,20 @@
             name="turn",
         )(*ops)
         splits.append(split)
-    elif even:
-        shares1 = [z1[k * per_dev // 2 : (k + 1) * per_dev // 2] for k in range(n_sub)]
     count = len(splits)
 
-    def send(shares):
-        return shares[:1] + [lax.ppermute(shares[k], "sub", hops_to[k]) for k in range(1, sends)]
-
-    z1_parts = gather(z1)
-    shares1 = send(shares1)
-
-    z2, basis, coeffs, *shares2 = pl.pallas_call(
-        functools.partial(second_kernel, n_field, count, sends, dof, terms),
+    z2, basis, coeffs, *shares = pl.pallas_call(
+        functools.partial(second_kernel, n_field, chunks, count, sends, dof, terms),
         out_shape=[own_shape, jax.ShapeDtypeStruct(full, F32), small] + share,
-        in_specs=[SMEM] + [VMEM] * (2 * n_field + count),
+        in_specs=[SMEM] + [VMEM] * ((1 + chunks) * n_field + count),
         out_specs=[VMEM] * (3 + sends),
         scratch_shapes=[pltpu.VMEM(dup, F32)],
         compiler_params=PARAMS,
         name="second",
     )(positions, *b_parts, *z1_parts, *splits)
     z2_parts = gather(z2)
-    shares2 = send(shares2)
-    z2_parts, shares1, shares2 = lax.optimization_barrier((z2_parts, shares1, shares2))
+    shares[1:] = [lax.ppermute(shares[k], "sub", hops_to[k]) for k in range(1, sends)]
+    z2_parts, shares = lax.optimization_barrier((z2_parts, shares))
 
     axes = ("z", "core", "sub") if even else ("z", "core")
     copies = nz * CORES * (n_sub if even else 1)
@@ -628,7 +632,7 @@
         return pl.pallas_call(
             functools.partial(finish_kernel, dof),
             out_shape=jax.ShapeDtypeStruct(right_side.shape, F32),
-            in_specs=[SMEM] + [VMEM] * (2 + 2 * sends),
+            in_specs=[SMEM] + [VMEM] * (2 + sends),
             out_specs=VMEM,
             scratch_shapes=[
                 pltpu.VMEM((per_dev // 2, n_sub * rhs, lanes), F32),
@@ -636,7 +640,7 @@
             ],
             compiler_params=SMALL,
             name="finish",
-        )(ids, sums, kept, *shares1, *shares2)
+        )(ids, sums, kept, *shares)
     result = pl.pallas_call(
         combine_kernel,
         out_shape=own_shape,

time: 121 us -> 116 us (0.959)
  waiting for transfers between devices: 51.7 us -> 45.5 us
    ppermute x18 -> x19, waiting for transfers between devices: 17.6 us -> 6.89 us  [the longest x3 4.93 us: per_device(): lax.ppermute(shares[k], 'sub', hops_to[k])]
    ppermute x9 -> x12, waiting for transfers between devices: 18.1 us -> 26.3 us  [step_z(): return lax.ppermute(own, 'z', [(z, z ^ offset) for z in range(nz)])]
    ppermute x1, waiting for transfers between devices: 4.64 us -> 0.01 us  [per_device(): d_low = lax.ppermute(y_low, 'sub', hops_to[1])]
    ppermute x9 -> x12, starting transfers between devices: 16.2 us -> 16.6 us  [step_z(): return lax.ppermute(own, 'z', [(z, z ^ offset) for z in range(nz)])]
    ppermute x18 -> x19, starting transfers between devices: 6.89 us -> 7.14 us  [the longest x3 4.74 us: per_device(): lax.ppermute(shares[k], 'sub', hops_to[k])]
  transfers between devices with their start and end apart: 34 -> 38, of which waited for: 17 -> 14; matrix products, arithmetic and copies ran while one was open for 2% -> 2% of each run, Pallas kernels for 7% -> 8%
where the time goes in v5:
time: 116 us; the launch traced here: 115 us
  waiting for transfers between devices  45.5 us (39%)
  starting transfers between devices  35.7 us (31%)
  Pallas kernels  17.8 us (15%)
  blocking collectives  11.2 us (10%)
  local copies, waits for them, and re-layouts  4.62 us (4%)
    ppermute x12, waiting for transfers between devices, step_z(): return lax.ppermute(own, 'z', [(z, z ^ offset) for z in range(nz)])  26.3 us
    ppermute x12, starting transfers between devices, step_z(): return lax.ppermute(own, 'z', [(z, z ^ offset) for z in range(nz)])  16.6 us
    all_to_all x1, waiting for transfers between devices, per_device(): lax.all_to_all(turned, 'sub', split_axis=0, concat_axis=0, tiled=True)  11.5 us
    all_to_all x1, blocking collectives, per_device(): sums = lax.all_to_all(sums, axes, split_axis=0, concat_axis=0, tiled=True)  11.2 us
    ppermute x3, waiting for transfers between devices, per_device(): lax.ppermute(shares[k], 'sub', hops_to[k])  4.93 us
    ppermute x3, starting transfers between devices, per_device(): lax.ppermute(shares[k], 'sub', hops_to[k])  4.74 us
    pallas_call x1, Pallas kernels, per_device(): pl.pallas_call(functools.partial(first_kernel, n_field, len(ops), dof, te...  3.73 us
    pallas_call x1, Pallas kernels, per_device(): pl.pallas_call(functools.partial(position_kernel, (per_dev, n_sub, nz, ho...  3.51 us
  transfers between devices with their start and end apart: 38, of which 14 were waited for; matrix products, arithmetic and copies ran while one was open for 2% of the time, Pallas kernels for 8%

profile of v5, /device:TPU:0, one launch (start us, length us, event | category | flops | bytes accessed | tf_op | source)
XLA Modules:
  0.0 115.2 jit_solution(13199752276277719496)
XLA Ops:
  0.0 1.3 %copy-done = f32[8,64,576]{2,1,0:T(8,128)S(1)} copy-done((f32[8,64,576]{2,1,0:T(8,128)S(1)}, f32[8,64,576]{2,1,0:T(8,128)}, u32[]{:S(2)}) %copy-start) | copy-done | bytes 1179672
  2.3 1.7 %pack.1 = (f32[2,64,1152]{2,1,0:T(8,128)}, f32[2,64,1152]{2,1,0:T(8,128)}, f32[4,4,16,128]{3,2,1,0:T(8,128)}, f32[4,4,16,128]{3,2,1,0:T(8,128)S(1)}) custom-call(f32[8,64,576]{2,1,0:T(8,128)S(1)} %copy-done, f32[8,64,64]{2,1,0:T(8,128)S(1)} %copy-done.1), custom_call_target="tpu_custom_call" | custom-call | tf_op jit(solution)/shard_map/pack/pallas_call | solution.py:487
  4.0 3.1 %collective-permute-start.9 = (f32[2,64,1152]{2,1,0:T(8,128)}, f32[2,64,1152]{2,1,0:T(8,128)S(1)}, u32[]{:S(2)}, u32[]{:S(2)}) collective-permute-start(f32[2,64,1152]{2,1,0:T(8,128)} %get-tuple-element.32.rest_8_), channel_id=1, source_target_pairs={{0,2},{1,3},{2,0},{3,1},{4,6},{5,7},{6,4},{7,5},{8,10},{9,11},{10,... | collective-permute-start | bytes 1769480 | tf_op jit(solution)/shard_map/ppermute | solution.py:501
  7.1 1.5 %collective-permute-start.8 = (f32[2,64,1152]{2,1,0:T(8,128)}, f32[2,64,1152]{2,1,0:T(8,128)S(1)}, u32[]{:S(2)}, u32[]{:S(2)}) collective-permute-start(f32[2,64,1152]{2,1,0:T(8,128)} %get-tuple-element.33.rest_9_), channel_id=1, source_target_pairs={{0,1},{1,0},{2,3},{3,2},{4,5},{5,4},{6,7},{7,6},{8,9},{9,8},{10,11... | collective-permute-start | bytes 1769480 | tf_op jit(solution)/shard_map/ppermute | solution.py:500
  8.6 3.3 %all-to-all-start = ((f32[4,4,16,128]{3,2,1,0:T(8,128)}), f32[4,4,16,128]{3,2,1,0:T(8,128)S(1)}, u32[]{:S(2)}, u32[]{:S(2)}) async-start(f32[4,4,16,128]{3,2,1,0:T(8,128)} %get-tuple-element.31), calls=%async_computation | async-start | bytes 262144 | tf_op jit(solution)/shard_map/all_to_all | solution.py:522
  11.9 11.5 %all-to-all-done = f32[4,4,16,128]{3,2,1,0:T(8,128)S(1)} async-done(((f32[4,4,16,128]{3,2,1,0:T(8,128)}), f32[4,4,16,128]{3,2,1,0:T(8,128)S(1)}, u32[]{:S(2)}, u32[]{:S(2)}) %all-to-all-start) | async-done | bytes 131104 | tf_op jit(solution)/shard_map/all_to_all | solution.py:522
  24.0 2.7 %collective-permute-start.1 = (f32[16,16,128]{2,1,0:T(8,128)S(1)}, f32[16,16,128]{2,1,0:T(8,128)S(1)}, u32[]{:S(2)}, u32[]{:S(2)}) collective-permute-start(f32[16,16,128]{2,1,0:T(8,128)S(1)} %bitcast.6), channel_id=1, source_target_pairs={{0,16},{8,24},{16,0},{24,8},{1,17},{9,25},{17,1},{25,9},{2,18},{10... | collective-permute-start | bytes 393224 | tf_op jit(solution)/shard_map/ppermute | solution.py:531
  26.7 1.6 %collective-permute-start = (f32[16,16,128]{2,1,0:T(8,128)S(1)}, f32[16,16,128]{2,1,0:T(8,128)S(1)}, u32[]{:S(2)}, u32[]{:S(2)}) collective-permute-start(f32[16,16,128]{2,1,0:T(8,128)S(1)} %bitcast.7), channel_id=1, source_target_pairs={{0,8},{8,0},{16,24},{24,16},{1,9},{9,1},{17,25},{25,17},{2,10},{10... | collective-permute-start | bytes 393224 | tf_op jit(solution)/shard_map/ppermute | solution.py:531
  28.3 3.7 %collective-permute-done.1.rest_2_ = f32[16,16,128]{2,1,0:T(8,128)S(1)} collective-permute-done((f32[16,16,128]{2,1,0:T(8,128)S(1)}, f32[16,16,128]{2,1,0:T(8,128)S(1)}, u32[]{:S(2)}, u32[]{:S(2)}) %collective-permute-start.1) | collective-permute-done | bytes 131104 | tf_op jit(solution)/shard_map/ppermute | solution.py:531
  32.7 2.0 %collective-permute-start.7 = (f32[2,64,1152]{2,1,0:T(8,128)}, f32[2,64,1152]{2,1,0:T(8,128)}, u32[]{:S(2)}, u32[]{:S(2)}) collective-permute-start(f32[2,64,1152]{2,1,0:T(8,128)} %get-tuple-element.32.rest_8_), channel_id=1, source_target_pairs={{0,1},{1,0},{2,3},{3,2},{4,5},{5,4},{6,7},{7,6},{8,9},{9,8},{10,11... | collective-permute-start | bytes 1769480 | tf_op jit(solution)/shard_map/ppermute | solution.py:502
  35.3 4.4 %collective-permute-done.2.rest_3_ = f32[16,16,128]{2,1,0:T(8,128)S(1)} collective-permute-done((f32[16,16,128]{2,1,0:T(8,128)S(1)}, f32[16,16,128]{2,1,0:T(8,128)S(1)}, u32[]{:S(2)}, u32[]{:S(2)}) %collective-permute-start.2) | collective-permute-done | bytes 131104 | tf_op jit(solution)/shard_map/ppermute | solution.py:531
  39.8 1.3 %collective-permute-start.19 = (f32[2,64,1152]{2,1,0:T(8,128)S(1)}, f32[2,64,1152]{2,1,0:T(8,128)S(1)}, u32[]{:S(2)}, u32[]{:S(2)}) collective-permute-start(f32[2,64,1152]{2,1,0:T(8,128)S(1)} %collective-permute-done.8.rest_11_), channel_id=1, source_target_pairs={{0,2},{1,3},{2,0},{3,1},{4,6},{5,7},{6,4},{7,5},{8,10},{9,11},{10,... | collective-permute-start | bytes 1769480 | tf_op jit(solution)/shard_map/ppermute | solution.py:545
  44.4 3.5 %positions.1.pos = s32[288]{0:T(512)S(1)} custom-call(s32[3]{0:T(128)S(1)} %pad_add_fusion.ids, s32[256]{0:T(256)S(1)} %copy-done.2, s32[2048]{0:T(1024)S(1)} %reshape.22.table), custom_call_target="tpu_custom_call" | custom-call | tf_op jit(solution)/shard_map/positions/pallas_call | solution.py:505
  48.8 3.7 %first.1 = (f32[12,16,128]{2,1,0:T(8,128)S(1)}, bf16[12,576,256]{2,1,0:T(8,128)(2,1)S(1)}, f32[256,16,128]{2,1,0:T(8,128)S(1)}) custom-call(s32[288]{0:T(512)S(1)} %positions.1.pos, f32[16,16,128]{2,1,0:T(8,128)S(1)} %bitcast.9, f32[16,16,128]{2,1,0:T(8,128)S(1)} %collective-permute-done.rest_1_, f32[16,16,128]{2,1,0:T(8,128)S(1)} %collective-permute-done.1.rest_2_, ...), custom_call_target="tpu_custom_call" | custom-call | tf_op jit(solution)/shard_map/first/pallas_call | solution.py:564
  53.7 3.2 %collective-permute-start.11 = (f32[12,16,128]{2,1,0:T(8,128)S(1)}, f32[12,16,128]{2,1,0:T(8,128)S(1)}, u32[]{:S(2)}, u32[]{:S(2)}) collective-permute-start(f32[12,16,128]{2,1,0:T(8,128)S(1)} %get-tuple-element.34.rest_8_), channel_id=1, source_target_pairs={{0,8},{8,0},{16,24},{24,16},{1,9},{9,1},{17,25},{25,17},{2,10},{10... | collective-permute-start | bytes 294920 | tf_op jit(solution)/shard_map/ppermute | solution.py:531
  56.9 2.9 %collective-permute-done.12.rest_10_ = f32[12,16,128]{2,1,0:T(8,128)S(1)} collective-permute-done((f32[12,16,128]{2,1,0:T(8,128)S(1)}, f32[12,16,128]{2,1,0:T(8,128)S(1)}, u32[]{:S(2)}, u32[]{:S(2)}) %collective-permute-start.12) | collective-permute-done | bytes 98336 | tf_op jit(solution)/shard_map/ppermute | solution.py:531
  60.7 3.8 %collective-permute-done.13.rest_11_ = f32[12,16,128]{2,1,0:T(8,128)S(1)} collective-permute-done((f32[12,16,128]{2,1,0:T(8,128)S(1)}, f32[12,16,128]{2,1,0:T(8,128)S(1)}, u32[]{:S(2)}, u32[]{:S(2)}) %collective-permute-start.13) | collective-permute-done | bytes 98336 | tf_op jit(solution)/shard_map/ppermute | solution.py:531
  66.2 1.6 %collective-permute-start.21 = (f32[4,16,128]{2,1,0:T(8,128)S(1)}, f32[4,16,128]{2,1,0:T(8,128)S(1)}, u32[]{:S(2)}, u32[]{:S(2)}) collective-permute-start(f32[4,16,128]{2,1,0:T(8,128)S(1)} %more.1.rest_16_), channel_id=1, source_target_pairs={{0,16},{8,24},{16,0},{24,8},{1,17},{9,25},{17,1},{25,9},{2,18},{10... | collective-permute-start | bytes 98312 | tf_op jit(solution)/shard_map/ppermute | solution.py:531
  67.8 1.9 %collective-permute-start.20 = (f32[4,16,128]{2,1,0:T(8,128)S(1)}, f32[4,16,128]{2,1,0:T(8,128)S(1)}, u32[]{:S(2)}, u32[]{:S(2)}) collective-permute-start(f32[4,16,128]{2,1,0:T(8,128)S(1)} %more.1.rest_16_), channel_id=1, source_target_pairs={{0,8},{8,0},{16,24},{24,16},{1,9},{9,1},{17,25},{25,17},{2,10},{10... | collective-permute-start | bytes 98312 | tf_op jit(solution)/shard_map/ppermute | solution.py:531
  69.7 1.7 %collective-permute-done.21.rest_18_ = f32[4,16,128]{2,1,0:T(8,128)S(1)} collective-permute-done((f32[4,16,128]{2,1,0:T(8,128)S(1)}, f32[4,16,128]{2,1,0:T(8,128)S(1)}, u32[]{:S(2)}, u32[]{:S(2)}) %collective-permute-start.21) | collective-permute-done | bytes 32800 | tf_op jit(solution)/shard_map/ppermute | solution.py:531
  72.3 3.0 %collective-permute-done.22.rest_19_ = f32[4,16,128]{2,1,0:T(8,128)S(1)} collective-permute-done((f32[4,16,128]{2,1,0:T(8,128)S(1)}, f32[4,16,128]{2,1,0:T(8,128)S(1)}, u32[]{:S(2)}, u32[]{:S(2)}) %collective-permute-start.22) | collective-permute-done | bytes 32800 | tf_op jit(solution)/shard_map/ppermute | solution.py:531
  76.5 2.5 %second.1 = (f32[16,16,128]{2,1,0:T(8,128)S(1)}, f32[128,16,128]{2,1,0:T(8,128)S(1)}, f32[16,128]{1,0:T(8,128)S(1)}, f32[2,4,16,128]{3,2,1,0:T(8,128)S(1)}, f32[...) custom-call(s32[288]{0:T(512)S(1)} %positions.1.pos, ...), custom_call_target="tpu_custom_call" | custom-call | tf_op jit(solution)/shard_map/second/pallas_call | solution.py:602
  79.0 1.3 %collective-permute-start.28 = (f32[16,16,128]{2,1,0:T(8,128)S(1)}, f32[16,16,128]{2,1,0:T(8,128)S(1)}, u32[]{:S(2)}, u32[]{:S(2)}) collective-permute-start(f32[16,16,128]{2,1,0:T(8,128)S(1)} %get-tuple-element.44.rest_8_), channel_id=1, source_target_pairs={{0,16},{8,24},{16,0},{24,8},{1,17},{9,25},{17,1},{25,9},{2,18},{10... | collective-permute-start | bytes 393224 | tf_op jit(solution)/shard_map/ppermute | solution.py:531
  80.4 1.9 %collective-permute-start.27 = (f32[16,16,128]{2,1,0:T(8,128)S(1)}, f32[16,16,128]{2,1,0:T(8,128)S(1)}, u32[]{:S(2)}, u32[]{:S(2)}) collective-permute-start(f32[16,16,128]{2,1,0:T(8,128)S(1)} %get-tuple-element.44.rest_8_), channel_id=1, source_target_pairs={{0,8},{8,0},{16,24},{24,16},{1,9},{9,1},{17,25},{25,17},{2,10},{10... | collective-permute-start | bytes 393224 | tf_op jit(solution)/shard_map/ppermute | solution.py:531
  82.3 6.2 %collective-permute-done.28.rest_10_ = f32[16,16,128]{2,1,0:T(8,128)S(1)} collective-permute-done((f32[16,16,128]{2,1,0:T(8,128)S(1)}, f32[16,16,128]{2,1,0:T(8,128)S(1)}, u32[]{:S(2)}, u32[]{:S(2)}) %collective-permute-start.28) | collective-permute-done | bytes 131104 | tf_op jit(solution)/shard_map/ppermute | solution.py:531
  89.6 1.5 %collective-permute-start.35 = (f32[2,4,16,128]{3,2,1,0:T(8,128)S(1)}, f32[2,4,16,128]{3,2,1,0:T(8,128)S(1)}, u32[]{:S(2)}, u32[]{:S(2)}) collective-permute-start(f32[2,4,16,128]{3,2,1,0:T(8,128)S(1)} %get-tuple-element.42), channel_id=1, source_target_pairs={{0,2},{1,3},{2,0},{3,1},{4,6},{5,7},{6,4},{7,5},{8,10},{9,11},{10,... | collective-permute-start | bytes 196616 | tf_op jit(solution)/shard_map/ppermute | solution.py:612
  91.1 1.6 %collective-permute-done.34.rest_1_ = f32[2,4,16,128]{3,2,1,0:T(8,128)S(1)} collective-permute-done((f32[2,4,16,128]{3,2,1,0:T(8,128)S(1)}, f32[2,4,16,128]{3,2,1,0:T(8,128)S(1)}, u32[]{:S(2)}, u32[]{:S(2)}) %collective-permute-start.34) | collective-permute-done | bytes 65568 | tf_op jit(solution)/shard_map/ppermute | solution.py:612
  93.8 2.1 %collective-permute-start.36 = (f32[2,4,16,128]{3,2,1,0:T(8,128)S(1)}, f32[2,4,16,128]{3,2,1,0:T(8,128)S(1)}, u32[]{:S(2)}, u32[]{:S(2)}) collective-permute-start(f32[2,4,16,128]{3,2,1,0:T(8,128)S(1)} %get-tuple-element.43), channel_id=1, source_target_pairs={{0,3},{1,2},{2,1},{3,0},{4,7},{5,6},{6,5},{7,4},{8,11},{9,10},{10,... | collective-permute-start | bytes 196616 | tf_op jit(solution)/shard_map/ppermute | solution.py:612
  95.9 3.3 %collective-permute-done.36.rest_3_ = f32[2,4,16,128]{3,2,1,0:T(8,128)S(1)} collective-permute-done((f32[2,4,16,128]{3,2,1,0:T(8,128)S(1)}, f32[2,4,16,128]{3,2,1,0:T(8,128)S(1)}, u32[]{:S(2)}, u32[]{:S(2)}) %collective-permute-start.36) | collective-permute-done | bytes 65568 | tf_op jit(solution)/shard_map/ppermute | solution.py:612
  99.2 3.0 %third.1 = f32[32,2,128]{2,1,0:T(2,128)S(1)} custom-call(s32[288]{0:T(512)S(1)} %positions.1.pos, f32[128,16,128]{2,1,0:T(8,128)S(1)} %get-tuple-element.37.basis, f32[16,128]{1,0:T(8,128)S(1)} %get-tuple-element.38.coeffs, f32[16,16,128]{2,1,0:T(8,128)S(1)} %bitcast.11, f32[16,16,128]{2,1,0:T(8,128)S(1)} %collective-permute-done.rest_1_, ...), custom_call_target="tpu_custom_call" | custom-call | tf_op jit(solution)/shard_map/third/pallas_call | solution.py:619
  102.2 11.2 %all_to_all.10.info = f32[32,2,128]{2,1,0:T(2,128)S(1)} all-to-all(f32[32,2,128]{2,1,0:T(2,128)S(1)} %third.1), channel_id=1, replica_groups=mesh['z'=4,'core'=2,'sub'=4] {'z','core','sub'}, dimensions={0} | all-to-all | bytes 65536 | tf_op jit(solution)/shard_map/all_to_all | solution.py:629
  113.5 1.7 %finish.1 = f32[8,64,64]{2,1,0:T(8,128)} custom-call(s32[3]{0:T(128)S(1)} %pad_add_fusion.ids, f32[32,2,128]{2,1,0:T(2,128)S(1)} %all_to_all.10.info, f32[4,4,16,128]{3,2,1,0:T(8,128)S(1)} %get-tuple-element.52.turned, f32[2,4,16,128]{3,2,1,0:T(8,128)S(1)} %get-tuple-element.53.rest_0_, f32[2,4,16,128]{3,2,1,0:T(8,128)S(1)} %collective-permute-done.34.rest_1_, ...), custom_call_target="tpu_custom_call" | custom-call | tf_op jit(solution)/shard_map/finish/pallas_call | solution.py:632
  (67 shorter events, 15.1 us)
Async XLA Ops:
  4.0 35.7 %collective-permute-start.9 = (f32[2,64,1152]{2,1,0:T(8,128)}, f32[2,64,1152]{2,1,0:T(8,128)S(1)}, u32[]{:S(2)}, u32[]{:S(2)}) collective-permute-start(f32[2,64,1152]{2,1,0:T(8,128)} %get-tuple-element.32.rest_8_), channel_id=1, source_target_pairs={{0,2},{1,3},{2,0},{3,1},{4,6},{5,7},{6,4},{7,5},{8,10},{9,11},{10,... | collective-permute-start | bytes 1769480 | tf_op jit(solution)/shard_map/ppermute | solution.py:501
  7.1 32.7 %collective-permute-start.8 = (f32[2,64,1152]{2,1,0:T(8,128)}, f32[2,64,1152]{2,1,0:T(8,128)S(1)}, u32[]{:S(2)}, u32[]{:S(2)}) collective-permute-start(f32[2,64,1152]{2,1,0:T(8,128)} %get-tuple-element.33.rest_9_), channel_id=1, source_target_pairs={{0,1},{1,0},{2,3},{3,2},{4,5},{5,4},{6,7},{7,6},{8,9},{9,8},{10,11... | collective-permute-start | bytes 1769480 | tf_op jit(solution)/shard_map/ppermute | solution.py:500
  8.6 14.9 %all-to-all-start = ((f32[4,4,16,128]{3,2,1,0:T(8,128)}), f32[4,4,16,128]{3,2,1,0:T(8,128)S(1)}, u32[]{:S(2)}, u32[]{:S(2)}) async-start(f32[4,4,16,128]{3,2,1,0:T(8,128)} %get-tuple-element.31), calls=%async_computation | async-start | bytes 262144 | tf_op jit(solution)/shard_map/all_to_all | solution.py:522
  24.0 8.0 %collective-permute-start.1 = (f32[16,16,128]{2,1,0:T(8,128)S(1)}, f32[16,16,128]{2,1,0:T(8,128)S(1)}, u32[]{:S(2)}, u32[]{:S(2)}) collective-permute-start(f32[16,16,128]{2,1,0:T(8,128)S(1)} %bitcast.6), channel_id=1, source_target_pairs={{0,16},{8,24},{16,0},{24,8},{1,17},{9,25},{17,1},{25,9},{2,18},{10... | collective-permute-start | bytes 393224 | tf_op jit(solution)/shard_map/ppermute | solution.py:531
  26.7 6.0 %collective-permute-start = (f32[16,16,128]{2,1,0:T(8,128)S(1)}, f32[16,16,128]{2,1,0:T(8,128)S(1)}, u32[]{:S(2)}, u32[]{:S(2)}) collective-permute-start(f32[16,16,128]{2,1,0:T(8,128)S(1)} %bitcast.7), channel_id=1, source_target_pairs={{0,8},{8,0},{16,24},{24,16},{1,9},{9,1},{17,25},{25,17},{2,10},{10... | collective-permute-start | bytes 393224 | tf_op jit(solution)/shard_map/ppermute | solution.py:531
  28.3 6.5 %collective-permute-start.3 = (f32[16,16,128]{2,1,0:T(8,128)S(1)}, f32[16,16,128]{2,1,0:T(8,128)S(1)}, u32[]{:S(2)}, u32[]{:S(2)}) collective-permute-start(f32[16,16,128]{2,1,0:T(8,128)S(1)} %bitcast.8), channel_id=1, source_target_pairs={{0,4},{4,0},{1,5},{5,1},{2,6},{6,2},{3,7},{7,3},{8,12},{12,8},{9,1... | collective-permute-start | bytes 393224 | tf_op jit(solution)/shard_map/ppermute | solution.py:540
  32.0 16.0 %collective-permute-start.10 = (f32[2,64,1152]{2,1,0:T(8,128)}, f32[2,64,1152]{2,1,0:T(8,128)}, u32[]{:S(2)}, u32[]{:S(2)}) collective-permute-start(f32[2,64,1152]{2,1,0:T(8,128)} %get-tuple-element.33.rest_9_), channel_id=1, source_target_pairs={{0,2},{1,3},{2,0},{3,1},{4,6},{5,7},{6,4},{7,5},{8,10},{9,11},{10,... | collective-permute-start | bytes 1769480 | tf_op jit(solution)/shard_map/ppermute | solution.py:503
  32.7 16.1 %collective-permute-start.7 = (f32[2,64,1152]{2,1,0:T(8,128)}, f32[2,64,1152]{2,1,0:T(8,128)}, u32[]{:S(2)}, u32[]{:S(2)}) collective-permute-start(f32[2,64,1152]{2,1,0:T(8,128)} %get-tuple-element.32.rest_8_), channel_id=1, source_target_pairs={{0,1},{1,0},{2,3},{3,2},{4,5},{5,4},{6,7},{7,6},{8,9},{9,8},{10,11... | collective-permute-start | bytes 1769480 | tf_op jit(solution)/shard_map/ppermute | solution.py:502
  34.7 5.0 %collective-permute-start.2 = (f32[16,16,128]{2,1,0:T(8,128)S(1)}, f32[16,16,128]{2,1,0:T(8,128)S(1)}, u32[]{:S(2)}, u32[]{:S(2)}) collective-permute-start(f32[16,16,128]{2,1,0:T(8,128)S(1)} %collective-permute-done.1.rest_2_), channel_id=1, source_target_pairs={{0,8},{8,0},{16,24},{24,16},{1,9},{9,1},{17,25},{25,17},{2,10},{10... | collective-permute-start | bytes 393224 | tf_op jit(solution)/shard_map/ppermute | solution.py:531
  39.7 24.8 %collective-permute-start.18 = (f32[2,64,1152]{2,1,0:T(8,128)S(1)}, f32[2,64,1152]{2,1,0:T(8,128)S(1)}, u32[]{:S(2)}, u32[]{:S(2)}) collective-permute-start(f32[2,64,1152]{2,1,0:T(8,128)S(1)} %collective-permute-done.9.rest_12_), channel_id=1, source_target_pairs={{0,1},{1,0},{2,3},{3,2},{4,5},{5,4},{6,7},{7,6},{8,9},{9,8},{10,11... | collective-permute-start | bytes 1769480 | tf_op jit(solution)/shard_map/ppermute | solution.py:544
  39.8 25.2 %collective-permute-start.19 = (f32[2,64,1152]{2,1,0:T(8,128)S(1)}, f32[2,64,1152]{2,1,0:T(8,128)S(1)}, u32[]{:S(2)}, u32[]{:S(2)}) collective-permute-start(f32[2,64,1152]{2,1,0:T(8,128)S(1)} %collective-permute-done.8.rest_11_), channel_id=1, source_target_pairs={{0,2},{1,3},{2,0},{3,1},{4,6},{5,7},{6,4},{7,5},{8,10},{9,11},{10,... | collective-permute-start | bytes 1769480 | tf_op jit(solution)/shard_map/ppermute | solution.py:545
  42.4 5.6 %collective-permute-start.6 = (f32[16,16,128]{2,1,0:T(8,128)S(1)}, f32[16,16,128]{2,1,0:T(8,128)S(1)}, u32[]{:S(2)}, u32[]{:S(2)}) collective-permute-start(f32[16,16,128]{2,1,0:T(8,128)S(1)} %collective-permute-done.2.rest_3_), channel_id=1, source_target_pairs={{0,4},{4,0},{1,5},{5,1},{2,6},{6,2},{3,7},{7,3},{8,12},{12,8},{9,1... | collective-permute-start | bytes 393224 | tf_op jit(solution)/shard_map/ppermute | solution.py:540
  52.5 7.4 %collective-permute-start.12 = (f32[12,16,128]{2,1,0:T(8,128)S(1)}, f32[12,16,128]{2,1,0:T(8,128)S(1)}, u32[]{:S(2)}, u32[]{:S(2)}) collective-permute-start(f32[12,16,128]{2,1,0:T(8,128)S(1)} %get-tuple-element.34.rest_8_), channel_id=1, source_target_pairs={{0,16},{8,24},{16,0},{24,8},{1,17},{9,25},{17,1},{25,9},{2,18},{10... | collective-permute-start | bytes 294920 | tf_op jit(solution)/shard_map/ppermute | solution.py:531
  53.7 6.4 %collective-permute-start.11 = (f32[12,16,128]{2,1,0:T(8,128)S(1)}, f32[12,16,128]{2,1,0:T(8,128)S(1)}, u32[]{:S(2)}, u32[]{:S(2)}) collective-permute-start(f32[12,16,128]{2,1,0:T(8,128)S(1)} %get-tuple-element.34.rest_8_), channel_id=1, source_target_pairs={{0,8},{8,0},{16,24},{24,16},{1,9},{9,1},{17,25},{25,17},{2,10},{10... | collective-permute-start | bytes 294920 | tf_op jit(solution)/shard_map/ppermute | solution.py:531
  59.9 4.6 %collective-permute-start.13 = (f32[12,16,128]{2,1,0:T(8,128)S(1)}, f32[12,16,128]{2,1,0:T(8,128)S(1)}, u32[]{:S(2)}, u32[]{:S(2)}) collective-permute-start(f32[12,16,128]{2,1,0:T(8,128)S(1)} %collective-permute-done.12.rest_10_), channel_id=1, source_target_pairs={{0,8},{8,0},{16,24},{24,16},{1,9},{9,1},{17,25},{25,17},{2,10},{10... | collective-permute-start | bytes 294920 | tf_op jit(solution)/shard_map/ppermute | solution.py:531
  60.2 7.6 %collective-permute-start.14 = (f32[12,16,128]{2,1,0:T(8,128)S(1)}, f32[12,16,128]{2,1,0:T(8,128)S(1)}, u32[]{:S(2)}, u32[]{:S(2)}) collective-permute-start(f32[12,16,128]{2,1,0:T(8,128)S(1)} %get-tuple-element.34.rest_8_), channel_id=1, source_target_pairs={{0,4},{4,0},{1,5},{5,1},{2,6},{6,2},{3,7},{7,3},{8,12},{12,8},{9,1... | collective-permute-start | bytes 294920 | tf_op jit(solution)/shard_map/ppermute | solution.py:540
  60.2 11.6 %collective-permute-start.15 = (f32[12,16,128]{2,1,0:T(8,128)S(1)}, f32[12,16,128]{2,1,0:T(8,128)S(1)}, u32[]{:S(2)}, u32[]{:S(2)}) collective-permute-start(f32[12,16,128]{2,1,0:T(8,128)S(1)} %collective-permute-done.11.rest_9_), channel_id=1, source_target_pairs={{0,4},{4,0},{1,5},{5,1},{2,6},{6,2},{3,7},{7,3},{8,12},{12,8},{9,1... | collective-permute-start | bytes 294920 | tf_op jit(solution)/shard_map/ppermute | solution.py:540
  64.5 7.3 %collective-permute-start.16 = (f32[12,16,128]{2,1,0:T(8,128)S(1)}, f32[12,16,128]{2,1,0:T(8,128)S(1)}, u32[]{:S(2)}, u32[]{:S(2)}) collective-permute-start(f32[12,16,128]{2,1,0:T(8,128)S(1)} %collective-permute-done.12.rest_10_), channel_id=1, source_target_pairs={{0,4},{4,0},{1,5},{5,1},{2,6},{6,2},{3,7},{7,3},{8,12},{12,8},{9,1... | collective-permute-start | bytes 294920 | tf_op jit(solution)/shard_map/ppermute | solution.py:540
  64.5 11.3 %collective-permute-start.17 = (f32[12,16,128]{2,1,0:T(8,128)S(1)}, f32[12,16,128]{2,1,0:T(8,128)S(1)}, u32[]{:S(2)}, u32[]{:S(2)}) collective-permute-start(f32[12,16,128]{2,1,0:T(8,128)S(1)} %collective-permute-done.13.rest_11_), channel_id=1, source_target_pairs={{0,4},{4,0},{1,5},{5,1},{2,6},{6,2},{3,7},{7,3},{8,12},{12,8},{9,1... | collective-permute-start | bytes 294920 | tf_op jit(solution)/shard_map/ppermute | solution.py:540
  66.2 5.2 %collective-permute-start.21 = (f32[4,16,128]{2,1,0:T(8,128)S(1)}, f32[4,16,128]{2,1,0:T(8,128)S(1)}, u32[]{:S(2)}, u32[]{:S(2)}) collective-permute-start(f32[4,16,128]{2,1,0:T(8,128)S(1)} %more.1.rest_16_), channel_id=1, source_target_pairs={{0,16},{8,24},{16,0},{24,8},{1,17},{9,25},{17,1},{25,9},{2,18},{10... | collective-permute-start | bytes 98312 | tf_op jit(solution)/shard_map/ppermute | solution.py:531
  67.8 4.4 %collective-permute-start.20 = (f32[4,16,128]{2,1,0:T(8,128)S(1)}, f32[4,16,128]{2,1,0:T(8,128)S(1)}, u32[]{:S(2)}, u32[]{:S(2)}) collective-permute-start(f32[4,16,128]{2,1,0:T(8,128)S(1)} %more.1.rest_16_), channel_id=1, source_target_pairs={{0,8},{8,0},{16,24},{24,16},{1,9},{9,1},{17,25},{25,17},{2,10},{10... | collective-permute-start | bytes 98312 | tf_op jit(solution)/shard_map/ppermute | solution.py:531
  71.8 4.0 %collective-permute-start.25 = (f32[4,16,128]{2,1,0:T(8,128)S(1)}, f32[4,16,128]{2,1,0:T(8,128)S(1)}, u32[]{:S(2)}, u32[]{:S(2)}) collective-permute-start(f32[4,16,128]{2,1,0:T(8,128)S(1)} %collective-permute-done.21.rest_18_), channel_id=1, source_target_pairs={{0,4},{4,0},{1,5},{5,1},{2,6},{6,2},{3,7},{7,3},{8,12},{12,8},{9,1... | collective-permute-start | bytes 98312 | tf_op jit(solution)/shard_map/ppermute | solution.py:540
  79.0 9.4 %collective-permute-start.28 = (f32[16,16,128]{2,1,0:T(8,128)S(1)}, f32[16,16,128]{2,1,0:T(8,128)S(1)}, u32[]{:S(2)}, u32[]{:S(2)}) collective-permute-start(f32[16,16,128]{2,1,0:T(8,128)S(1)} %get-tuple-element.44.rest_8_), channel_id=1, source_target_pairs={{0,16},{8,24},{16,0},{24,8},{1,17},{9,25},{17,1},{25,9},{2,18},{10... | collective-permute-start | bytes 393224 | tf_op jit(solution)/shard_map/ppermute | solution.py:531
  80.4 12.3 %collective-permute-start.27 = (f32[16,16,128]{2,1,0:T(8,128)S(1)}, f32[16,16,128]{2,1,0:T(8,128)S(1)}, u32[]{:S(2)}, u32[]{:S(2)}) collective-permute-start(f32[16,16,128]{2,1,0:T(8,128)S(1)} %get-tuple-element.44.rest_8_), channel_id=1, source_target_pairs={{0,8},{8,0},{16,24},{24,16},{1,9},{9,1},{17,25},{25,17},{2,10},{10... | collective-permute-start | bytes 393224 | tf_op jit(solution)/shard_map/ppermute | solution.py:531
  88.4 5.4 %collective-permute-start.29 = (f32[16,16,128]{2,1,0:T(8,128)S(1)}, f32[16,16,128]{2,1,0:T(8,128)S(1)}, u32[]{:S(2)}, u32[]{:S(2)}) collective-permute-start(f32[16,16,128]{2,1,0:T(8,128)S(1)} %collective-permute-done.28.rest_10_), channel_id=1, source_target_pairs={{0,8},{8,0},{16,24},{24,16},{1,9},{9,1},{17,25},{25,17},{2,10},{10... | collective-permute-start | bytes 393224 | tf_op jit(solution)/shard_map/ppermute | solution.py:531
  88.4 4.3 %collective-permute-start.34 = (f32[2,4,16,128]{3,2,1,0:T(8,128)S(1)}, f32[2,4,16,128]{3,2,1,0:T(8,128)S(1)}, u32[]{:S(2)}, u32[]{:S(2)}) collective-permute-start(f32[2,4,16,128]{3,2,1,0:T(8,128)S(1)} %get-tuple-element.41), channel_id=1, source_target_pairs={{0,1},{1,0},{2,3},{3,2},{4,5},{5,4},{6,7},{7,6},{8,9},{9,8},{10,11... | collective-permute-start | bytes 196616 | tf_op jit(solution)/shard_map/ppermute | solution.py:612
  89.6 4.3 %collective-permute-start.35 = (f32[2,4,16,128]{3,2,1,0:T(8,128)S(1)}, f32[2,4,16,128]{3,2,1,0:T(8,128)S(1)}, u32[]{:S(2)}, u32[]{:S(2)}) collective-permute-start(f32[2,4,16,128]{3,2,1,0:T(8,128)S(1)} %get-tuple-element.42), channel_id=1, source_target_pairs={{0,2},{1,3},{2,0},{3,1},{4,6},{5,7},{6,4},{7,5},{8,10},{9,11},{10,... | collective-permute-start | bytes 196616 | tf_op jit(solution)/shard_map/ppermute | solution.py:612
  91.1 8.1 %collective-permute-start.30 = (f32[16,16,128]{2,1,0:T(8,128)S(1)}, f32[16,16,128]{2,1,0:T(8,128)S(1)}, u32[]{:S(2)}, u32[]{:S(2)}) collective-permute-start(f32[16,16,128]{2,1,0:T(8,128)S(1)} %get-tuple-element.44.rest_8_), channel_id=1, source_target_pairs={{0,4},{4,0},{1,5},{5,1},{2,6},{6,2},{3,7},{7,3},{8,12},{12,8},{9,1... | collective-permute-start | bytes 393224 | tf_op jit(solution)/shard_map/ppermute | solution.py:540
  92.7 6.5 %collective-permute-start.32 = (f32[16,16,128]{2,1,0:T(8,128)S(1)}, f32[16,16,128]{2,1,0:T(8,128)S(1)}, u32[]{:S(2)}, u32[]{:S(2)}) collective-permute-start(f32[16,16,128]{2,1,0:T(8,128)S(1)} %collective-permute-done.28.rest_10_), channel_id=1, source_target_pairs={{0,4},{4,0},{1,5},{5,1},{2,6},{6,2},{3,7},{7,3},{8,12},{12,8},{9,1... | collective-permute-start | bytes 393224 | tf_op jit(solution)/shard_map/ppermute | solution.py:540
  92.7 6.5 %collective-permute-start.31 = (f32[16,16,128]{2,1,0:T(8,128)S(1)}, f32[16,16,128]{2,1,0:T(8,128)S(1)}, u32[]{:S(2)}, u32[]{:S(2)}) collective-permute-start(f32[16,16,128]{2,1,0:T(8,128)S(1)} %collective-permute-done.27.rest_9_), channel_id=1, source_target_pairs={{0,4},{4,0},{1,5},{5,1},{2,6},{6,2},{3,7},{7,3},{8,12},{12,8},{9,1... | collective-permute-start | bytes 393224 | tf_op jit(solution)/shard_map/ppermute | solution.py:540
  93.8 5.4 %collective-permute-start.33 = (f32[16,16,128]{2,1,0:T(8,128)S(1)}, f32[16,16,128]{2,1,0:T(8,128)S(1)}, u32[]{:S(2)}, u32[]{:S(2)}) collective-permute-start(f32[16,16,128]{2,1,0:T(8,128)S(1)} %collective-permute-done.29.rest_11_), channel_id=1, source_target_pairs={{0,4},{4,0},{1,5},{5,1},{2,6},{6,2},{3,7},{7,3},{8,12},{12,8},{9,1... | collective-permute-start | bytes 393224 | tf_op jit(solution)/shard_map/ppermute | solution.py:540
  93.8 5.4 %collective-permute-start.36 = (f32[2,4,16,128]{3,2,1,0:T(8,128)S(1)}, f32[2,4,16,128]{3,2,1,0:T(8,128)S(1)}, u32[]{:S(2)}, u32[]{:S(2)}) collective-permute-start(f32[2,4,16,128]{3,2,1,0:T(8,128)S(1)} %get-tuple-element.43), channel_id=1, source_target_pairs={{0,3},{1,2},{2,1},{3,0},{4,7},{5,6},{6,5},{7,4},{8,11},{9,10},{10,... | collective-permute-start | bytes 196616 | tf_op jit(solution)/shard_map/ppermute | solution.py:612
  (10 other events, 100.1 us)

commit v6 on v5

--- a/solution.py
+++ b/solution.py
@@ -99,25 +99,31 @@
     lax.fori_loop(0, n_sub * per_dev, look, 0, unroll=2)
 
 
-def pack_kernel(dof, op, right, low, high, turned, kept, held, op_held, sems):
+def pack_kernel(dof, op, low, high, held, sems):
     half = op.shape[0] // 2
-    sources = [right, op.at[pl.ds(0, half)], op.at[pl.ds(half, half)]]
-    copies = start_copies(sources, [held, op_held.at[0], op_held.at[1]], sems)
+    count = sems.shape[0]
+    size = op.shape[0] // count
+    sources = [op.at[pl.ds(size * index, size)] for index in range(count)]
+    copies = start_copies(sources, [held.at[index] for index in range(count)], sems)
+    main = op.shape[2] - dof
+    for index in range(count):
+        copies[index].wait()
+        for inner in range(size // 2):
+            even, odd = held[index, 2 * inner], held[index, 2 * inner + 1]
+            pair = (size * index) // 2 + inner
+            target, pair = (low, pair) if pair < half // 2 else (high, pair - half // 2)
+            target[pair, :, :main] = even[:, :main]
+            target[pair, :, main : 2 * main] = odd[:, :main]
+            target[pair, :, 2 * main :] = jnp.concatenate([even[:, main:], odd[:, main:]], axis=1)
+
+
+def turn_right_kernel(right, turned, kept):
     n_sub, per_part, rhs = turned.shape[0], turned.shape[1], turned.shape[2]
-    copies[0].wait()
     for pair in range(per_part):
-        both = jnp.concatenate([held[2 * pair], held[2 * pair + 1]], axis=0).T
+        both = jnp.concatenate([right[2 * pair], right[2 * pair + 1]], axis=0).T
         for quarter in range(n_sub):
             turned[quarter, pair] = both[quarter * rhs : (quarter + 1) * rhs]
             kept[quarter, pair] = both[quarter * rhs : (quarter + 1) * rhs]
-    main = op.shape[2] - dof
-    for index, target in enumerate((low, high)):
-        copies[index + 1].wait()
-        for pair in range(half // 2):
-            even, odd = op_held[index, 2 * pair], op_held[index, 2 * pair + 1]
-            target[pair, :, :main] = even[:, :main]
-            target[pair, :, main : 2 * main] = odd[:, :main]
-            target[pair, :, 2 * main :] = jnp.concatenate([even[:, main:], odd[:, main:]], axis=1)
 
 
 def spread(dup, pair, values, dof):
@@ -484,19 +490,27 @@
     half = per_dev // 2
     if relay:
         halves = [jax.ShapeDtypeStruct((half // 2, dof, 2 * width), F32)] * 2
-        op_low, op_high, turned, kept = pl.pallas_call(
+        parts = per_dev // 2
+        op_low, op_high = pl.pallas_call(
             functools.partial(pack_kernel, dof),
-            out_shape=halves + [jax.ShapeDtypeStruct((n_sub, half, rhs, lanes), F32)] * 2,
-            in_specs=[HBM, HBM],
-            out_specs=[VMEM] * 4,
+            out_shape=halves,
+            in_specs=[HBM],
+            out_specs=[VMEM] * 2,
             scratch_shapes=[
-                pltpu.VMEM(right_side.shape, F32),
-                pltpu.VMEM((2, half, dof, width), F32),
-                pltpu.SemaphoreType.DMA((3,)),
+                pltpu.VMEM((parts, 2, dof, width), F32),
+                pltpu.SemaphoreType.DMA((parts,)),
             ],
             compiler_params=SMALL,
             name="pack",
-        )(coarse_op, right_side)
+        )(pltpu.with_memory_space_constraint(coarse_op, pltpu.HBM))
+        turned, kept = pl.pallas_call(
+            turn_right_kernel,
+            out_shape=[jax.ShapeDtypeStruct((n_sub, half, rhs, lanes), F32)] * 2,
+            in_specs=[VMEM],
+            out_specs=[VMEM] * 2,
+            compiler_params=SMALL,
+            name="pack_right",
+        )(right_side)
         x_high = lax.ppermute(op_high, "sub", hops_to[1])
         y_low = lax.ppermute(op_low, "sub", hops_to[2])
         x_low = lax.ppermute(op_low, "sub", hops_to[1])
@@ -532,7 +546,8 @@
 
     def gather(own):
         if nz == 4:
-            cross, near = step_z(own, 2), step_z(own, 1)
+            cross = step_z(own, 2)
+            near = step_z(own, 1)
             parts = [own, near, cross, step_z(cross, 1)]
         else:
             parts = [own] + [step_z(own, offset) for offset in range(1, nz)]

time: 116 us -> 114 us (0.983)
  waiting for transfers between devices: 45.5 us -> 43.8 us
  Pallas kernels: 17.8 us -> 19.2 us
  local copies, waits for them, and re-layouts: 4.62 us -> 3.31 us
    all_to_all x1, waiting for transfers between devices: 11.5 us -> 9.83 us  [per_device(): lax.all_to_all(turned, 'sub', split_axis=0, concat_axis=0, tiled=True)]
    pallas_call x1 -> x2, Pallas kernels: 1.73 us -> 3.14 us  [the longest x1 2.37 us: per_device(): pl.pallas_call(functools.partial(pack_kernel, dof), out_shape=halves, in_...]
    unnamed x9 -> x7, local copies, waits for them, and re-layouts: 3.06 us -> 1.75 us
where the time goes in v6:
time: 114 us
  waiting for transfers between devices  43.8 us (38%)
  starting transfers between devices  35.7 us (31%)
  Pallas kernels  19.2 us (17%)
  blocking collectives  11.2 us (10%)
  local copies, waits for them, and re-layouts  3.31 us (3%)
    ppermute x12, waiting for transfers between devices, step_z(): return lax.ppermute(own, 'z', [(z, z ^ offset) for z in range(nz)])  26.3 us
    ppermute x12, starting transfers between devices, step_z(): return lax.ppermute(own, 'z', [(z, z ^ offset) for z in range(nz)])  16.6 us
    all_to_all x1, blocking collectives, per_device(): sums = lax.all_to_all(sums, axes, split_axis=0, concat_axis=0, tiled=True)  11.2 us
    all_to_all x1, waiting for transfers between devices, per_device(): lax.all_to_all(turned, 'sub', split_axis=0, concat_axis=0, tiled=True)  9.83 us
    ppermute x3, waiting for transfers between devices, per_device(): lax.ppermute(shares[k], 'sub', hops_to[k])  4.93 us
    ppermute x3, starting transfers between devices, per_device(): lax.ppermute(shares[k], 'sub', hops_to[k])  4.74 us
    pallas_call x1, Pallas kernels, per_device(): pl.pallas_call(functools.partial(first_kernel, n_field, len(ops), dof, te...  3.73 us
    pallas_call x1, Pallas kernels, per_device(): pl.pallas_call(functools.partial(position_kernel, (per_dev, n_sub, nz, ho...  3.51 us
  transfers between devices with their start and end apart: 38, of which 14 were waited for; matrix products, arithmetic and copies ran while one was open for 2% of the time, Pallas kernels for 8%

profile of v6, /device:TPU:0, one launch (start us, length us, event | category | flops | bytes accessed | tf_op | source)
XLA Modules:
  0.0 113.5 jit_solution(11829676046043505288)
XLA Ops:
  0.0 2.4 %pack.1 = (f32[2,64,1152]{2,1,0:T(8,128)}, f32[2,64,1152]{2,1,0:T(8,128)}) custom-call(f32[8,64,576]{2,1,0:T(8,128)} %op.1), custom_call_target="tpu_custom_call" | custom-call | tf_op jit(solution)/shard_map/pack/pallas_call | solution.py:494
  2.4 3.1 %collective-permute-start.9 = (f32[2,64,1152]{2,1,0:T(8,128)}, f32[2,64,1152]{2,1,0:T(8,128)S(1)}, u32[]{:S(2)}, u32[]{:S(2)}) collective-permute-start(f32[2,64,1152]{2,1,0:T(8,128)} %get-tuple-element.32.rest_8_), channel_id=1, source_target_pairs={{0,2},{1,3},{2,0},{3,1},{4,6},{5,7},{6,4},{7,5},{8,10},{9,11},{10,... | collective-permute-start | bytes 1769480 | tf_op jit(solution)/shard_map/ppermute | solution.py:515
  5.4 1.5 %collective-permute-start.8 = (f32[2,64,1152]{2,1,0:T(8,128)}, f32[2,64,1152]{2,1,0:T(8,128)S(1)}, u32[]{:S(2)}, u32[]{:S(2)}) collective-permute-start(f32[2,64,1152]{2,1,0:T(8,128)} %get-tuple-element.33.rest_9_), channel_id=1, source_target_pairs={{0,1},{1,0},{2,3},{3,2},{4,5},{5,4},{6,7},{7,6},{8,9},{9,8},{10,11... | collective-permute-start | bytes 1769480 | tf_op jit(solution)/shard_map/ppermute | solution.py:514
  8.7 3.3 %all-to-all-start = ((f32[4,4,16,128]{3,2,1,0:T(8,128)}), f32[4,4,16,128]{3,2,1,0:T(8,128)S(1)}, u32[]{:S(2)}, u32[]{:S(2)}) async-start(f32[4,4,16,128]{3,2,1,0:T(8,128)} %get-tuple-element.31), calls=%async_computation | async-start | bytes 262144 | tf_op jit(solution)/shard_map/all_to_all | solution.py:536
  12.0 9.8 %all-to-all-done = f32[4,4,16,128]{3,2,1,0:T(8,128)S(1)} async-done(((f32[4,4,16,128]{3,2,1,0:T(8,128)}), f32[4,4,16,128]{3,2,1,0:T(8,128)S(1)}, u32[]{:S(2)}, u32[]{:S(2)}) %all-to-all-start) | async-done | bytes 131104 | tf_op jit(solution)/shard_map/all_to_all | solution.py:536
  22.4 2.7 %collective-permute-start.1 = (f32[16,16,128]{2,1,0:T(8,128)S(1)}, f32[16,16,128]{2,1,0:T(8,128)S(1)}, u32[]{:S(2)}, u32[]{:S(2)}) collective-permute-start(f32[16,16,128]{2,1,0:T(8,128)S(1)} %bitcast.6), channel_id=1, source_target_pairs={{0,16},{8,24},{16,0},{24,8},{1,17},{9,25},{17,1},{25,9},{2,18},{10... | collective-permute-start | bytes 393224 | tf_op jit(solution)/shard_map/ppermute | solution.py:545
  25.1 1.6 %collective-permute-start = (f32[16,16,128]{2,1,0:T(8,128)S(1)}, f32[16,16,128]{2,1,0:T(8,128)S(1)}, u32[]{:S(2)}, u32[]{:S(2)}) collective-permute-start(f32[16,16,128]{2,1,0:T(8,128)S(1)} %bitcast.7), channel_id=1, source_target_pairs={{0,8},{8,0},{16,24},{24,16},{1,9},{9,1},{17,25},{25,17},{2,10},{10... | collective-permute-start | bytes 393224 | tf_op jit(solution)/shard_map/ppermute | solution.py:545
  26.6 3.7 %collective-permute-done.1.rest_2_ = f32[16,16,128]{2,1,0:T(8,128)S(1)} collective-permute-done((f32[16,16,128]{2,1,0:T(8,128)S(1)}, f32[16,16,128]{2,1,0:T(8,128)S(1)}, u32[]{:S(2)}, u32[]{:S(2)}) %collective-permute-start.1) | collective-permute-done | bytes 131104 | tf_op jit(solution)/shard_map/ppermute | solution.py:545
  31.1 2.0 %collective-permute-start.7 = (f32[2,64,1152]{2,1,0:T(8,128)}, f32[2,64,1152]{2,1,0:T(8,128)}, u32[]{:S(2)}, u32[]{:S(2)}) collective-permute-start(f32[2,64,1152]{2,1,0:T(8,128)} %get-tuple-element.32.rest_8_), channel_id=1, source_target_pairs={{0,1},{1,0},{2,3},{3,2},{4,5},{5,4},{6,7},{7,6},{8,9},{9,8},{10,11... | collective-permute-start | bytes 1769480 | tf_op jit(solution)/shard_map/ppermute | solution.py:516
  33.6 4.4 %collective-permute-done.2.rest_3_ = f32[16,16,128]{2,1,0:T(8,128)S(1)} collective-permute-done((f32[16,16,128]{2,1,0:T(8,128)S(1)}, f32[16,16,128]{2,1,0:T(8,128)S(1)}, u32[]{:S(2)}, u32[]{:S(2)}) %collective-permute-start.2) | collective-permute-done | bytes 131104 | tf_op jit(solution)/shard_map/ppermute | solution.py:545
  38.1 1.3 %collective-permute-start.19 = (f32[2,64,1152]{2,1,0:T(8,128)S(1)}, f32[2,64,1152]{2,1,0:T(8,128)S(1)}, u32[]{:S(2)}, u32[]{:S(2)}) collective-permute-start(f32[2,64,1152]{2,1,0:T(8,128)S(1)} %collective-permute-done.8.rest_11_), channel_id=1, source_target_pairs={{0,2},{1,3},{2,0},{3,1},{4,6},{5,7},{6,4},{7,5},{8,10},{9,11},{10,... | collective-permute-start | bytes 1769480 | tf_op jit(solution)/shard_map/ppermute | solution.py:560
  42.8 3.5 %positions.1.pos = s32[288]{0:T(512)S(1)} custom-call(s32[3]{0:T(128)S(1)} %pad_add_fusion.ids, s32[256]{0:T(256)S(1)} %copy-done.1, s32[2048]{0:T(1024)S(1)} %reshape.22.table), custom_call_target="tpu_custom_call" | custom-call | tf_op jit(solution)/shard_map/positions/pallas_call | solution.py:519
  47.1 3.7 %first.1 = (f32[12,16,128]{2,1,0:T(8,128)S(1)}, bf16[12,576,256]{2,1,0:T(8,128)(2,1)S(1)}, f32[256,16,128]{2,1,0:T(8,128)S(1)}) custom-call(s32[288]{0:T(512)S(1)} %positions.1.pos, f32[16,16,128]{2,1,0:T(8,128)S(1)} %bitcast.9, f32[16,16,128]{2,1,0:T(8,128)S(1)} %collective-permute-done.rest_1_, f32[16,16,128]{2,1,0:T(8,128)S(1)} %collective-permute-done.1.rest_2_, ...), custom_call_target="tpu_custom_call" | custom-call | tf_op jit(solution)/shard_map/first/pallas_call | solution.py:579
  50.9 1.2 %collective-permute-start.12 = (f32[12,16,128]{2,1,0:T(8,128)S(1)}, f32[12,16,128]{2,1,0:T(8,128)S(1)}, u32[]{:S(2)}, u32[]{:S(2)}) collective-permute-start(f32[12,16,128]{2,1,0:T(8,128)S(1)} %get-tuple-element.34.rest_8_), channel_id=1, source_target_pairs={{0,16},{8,24},{16,0},{24,8},{1,17},{9,25},{17,1},{25,9},{2,18},{10... | collective-permute-start | bytes 294920 | tf_op jit(solution)/shard_map/ppermute | solution.py:545
  52.1 3.2 %collective-permute-start.11 = (f32[12,16,128]{2,1,0:T(8,128)S(1)}, f32[12,16,128]{2,1,0:T(8,128)S(1)}, u32[]{:S(2)}, u32[]{:S(2)}) collective-permute-start(f32[12,16,128]{2,1,0:T(8,128)S(1)} %get-tuple-element.34.rest_8_), channel_id=1, source_target_pairs={{0,8},{8,0},{16,24},{24,16},{1,9},{9,1},{17,25},{25,17},{2,10},{10... | collective-permute-start | bytes 294920 | tf_op jit(solution)/shard_map/ppermute | solution.py:545
  55.3 2.9 %collective-permute-done.12.rest_10_ = f32[12,16,128]{2,1,0:T(8,128)S(1)} collective-permute-done((f32[12,16,128]{2,1,0:T(8,128)S(1)}, f32[12,16,128]{2,1,0:T(8,128)S(1)}, u32[]{:S(2)}, u32[]{:S(2)}) %collective-permute-start.12) | collective-permute-done | bytes 98336 | tf_op jit(solution)/shard_map/ppermute | solution.py:545
  59.1 3.8 %collective-permute-done.13.rest_11_ = f32[12,16,128]{2,1,0:T(8,128)S(1)} collective-permute-done((f32[12,16,128]{2,1,0:T(8,128)S(1)}, f32[12,16,128]{2,1,0:T(8,128)S(1)}, u32[]{:S(2)}, u32[]{:S(2)}) %collective-permute-start.13) | collective-permute-done | bytes 98336 | tf_op jit(solution)/shard_map/ppermute | solution.py:545
  64.5 1.6 %collective-permute-start.21 = (f32[4,16,128]{2,1,0:T(8,128)S(1)}, f32[4,16,128]{2,1,0:T(8,128)S(1)}, u32[]{:S(2)}, u32[]{:S(2)}) collective-permute-start(f32[4,16,128]{2,1,0:T(8,128)S(1)} %more.1.rest_16_), channel_id=1, source_target_pairs={{0,16},{8,24},{16,0},{24,8},{1,17},{9,25},{17,1},{25,9},{2,18},{10... | collective-permute-start | bytes 98312 | tf_op jit(solution)/shard_map/ppermute | solution.py:545
  66.2 1.9 %collective-permute-start.20 = (f32[4,16,128]{2,1,0:T(8,128)S(1)}, f32[4,16,128]{2,1,0:T(8,128)S(1)}, u32[]{:S(2)}, u32[]{:S(2)}) collective-permute-start(f32[4,16,128]{2,1,0:T(8,128)S(1)} %more.1.rest_16_), channel_id=1, source_target_pairs={{0,8},{8,0},{16,24},{24,16},{1,9},{9,1},{17,25},{25,17},{2,10},{10... | collective-permute-start | bytes 98312 | tf_op jit(solution)/shard_map/ppermute | solution.py:545
  68.1 1.7 %collective-permute-done.21.rest_18_ = f32[4,16,128]{2,1,0:T(8,128)S(1)} collective-permute-done((f32[4,16,128]{2,1,0:T(8,128)S(1)}, f32[4,16,128]{2,1,0:T(8,128)S(1)}, u32[]{:S(2)}, u32[]{:S(2)}) %collective-permute-start.21) | collective-permute-done | bytes 32800 | tf_op jit(solution)/shard_map/ppermute | solution.py:545
  70.7 3.0 %collective-permute-done.22.rest_19_ = f32[4,16,128]{2,1,0:T(8,128)S(1)} collective-permute-done((f32[4,16,128]{2,1,0:T(8,128)S(1)}, f32[4,16,128]{2,1,0:T(8,128)S(1)}, u32[]{:S(2)}, u32[]{:S(2)}) %collective-permute-start.22) | collective-permute-done | bytes 32800 | tf_op jit(solution)/shard_map/ppermute | solution.py:545
  74.9 2.5 %second.1 = (f32[16,16,128]{2,1,0:T(8,128)S(1)}, f32[128,16,128]{2,1,0:T(8,128)S(1)}, f32[16,128]{1,0:T(8,128)S(1)}, f32[2,4,16,128]{3,2,1,0:T(8,128)S(1)}, f32[...) custom-call(s32[288]{0:T(512)S(1)} %positions.1.pos, ...), custom_call_target="tpu_custom_call" | custom-call | tf_op jit(solution)/shard_map/second/pallas_call | solution.py:617
  77.4 1.3 %collective-permute-start.28 = (f32[16,16,128]{2,1,0:T(8,128)S(1)}, f32[16,16,128]{2,1,0:T(8,128)S(1)}, u32[]{:S(2)}, u32[]{:S(2)}) collective-permute-start(f32[16,16,128]{2,1,0:T(8,128)S(1)} %get-tuple-element.44.rest_8_), channel_id=1, source_target_pairs={{0,16},{8,24},{16,0},{24,8},{1,17},{9,25},{17,1},{25,9},{2,18},{10... | collective-permute-start | bytes 393224 | tf_op jit(solution)/shard_map/ppermute | solution.py:545
  78.7 1.9 %collective-permute-start.27 = (f32[16,16,128]{2,1,0:T(8,128)S(1)}, f32[16,16,128]{2,1,0:T(8,128)S(1)}, u32[]{:S(2)}, u32[]{:S(2)}) collective-permute-start(f32[16,16,128]{2,1,0:T(8,128)S(1)} %get-tuple-element.44.rest_8_), channel_id=1, source_target_pairs={{0,8},{8,0},{16,24},{24,16},{1,9},{9,1},{17,25},{25,17},{2,10},{10... | collective-permute-start | bytes 393224 | tf_op jit(solution)/shard_map/ppermute | solution.py:545
  80.6 6.2 %collective-permute-done.28.rest_10_ = f32[16,16,128]{2,1,0:T(8,128)S(1)} collective-permute-done((f32[16,16,128]{2,1,0:T(8,128)S(1)}, f32[16,16,128]{2,1,0:T(8,128)S(1)}, u32[]{:S(2)}, u32[]{:S(2)}) %collective-permute-start.28) | collective-permute-done | bytes 131104 | tf_op jit(solution)/shard_map/ppermute | solution.py:545
  87.9 1.5 %collective-permute-start.35 = (f32[2,4,16,128]{3,2,1,0:T(8,128)S(1)}, f32[2,4,16,128]{3,2,1,0:T(8,128)S(1)}, u32[]{:S(2)}, u32[]{:S(2)}) collective-permute-start(f32[2,4,16,128]{3,2,1,0:T(8,128)S(1)} %get-tuple-element.42), channel_id=1, source_target_pairs={{0,2},{1,3},{2,0},{3,1},{4,6},{5,7},{6,4},{7,5},{8,10},{9,11},{10,... | collective-permute-start | bytes 196616 | tf_op jit(solution)/shard_map/ppermute | solution.py:627
  89.5 1.6 %collective-permute-done.34.rest_1_ = f32[2,4,16,128]{3,2,1,0:T(8,128)S(1)} collective-permute-done((f32[2,4,16,128]{3,2,1,0:T(8,128)S(1)}, f32[2,4,16,128]{3,2,1,0:T(8,128)S(1)}, u32[]{:S(2)}, u32[]{:S(2)}) %collective-permute-start.34) | collective-permute-done | bytes 65568 | tf_op jit(solution)/shard_map/ppermute | solution.py:627
  92.2 2.1 %collective-permute-start.36 = (f32[2,4,16,128]{3,2,1,0:T(8,128)S(1)}, f32[2,4,16,128]{3,2,1,0:T(8,128)S(1)}, u32[]{:S(2)}, u32[]{:S(2)}) collective-permute-start(f32[2,4,16,128]{3,2,1,0:T(8,128)S(1)} %get-tuple-element.43), channel_id=1, source_target_pairs={{0,3},{1,2},{2,1},{3,0},{4,7},{5,6},{6,5},{7,4},{8,11},{9,10},{10,... | collective-permute-start | bytes 196616 | tf_op jit(solution)/shard_map/ppermute | solution.py:627
  94.3 3.3 %collective-permute-done.36.rest_3_ = f32[2,4,16,128]{3,2,1,0:T(8,128)S(1)} collective-permute-done((f32[2,4,16,128]{3,2,1,0:T(8,128)S(1)}, f32[2,4,16,128]{3,2,1,0:T(8,128)S(1)}, u32[]{:S(2)}, u32[]{:S(2)}) %collective-permute-start.36) | collective-permute-done | bytes 65568 | tf_op jit(solution)/shard_map/ppermute | solution.py:627
  97.6 3.0 %third.1 = f32[32,2,128]{2,1,0:T(2,128)S(1)} custom-call(s32[288]{0:T(512)S(1)} %positions.1.pos, f32[128,16,128]{2,1,0:T(8,128)S(1)} %get-tuple-element.37.basis, f32[16,128]{1,0:T(8,128)S(1)} %get-tuple-element.38.coeffs, f32[16,16,128]{2,1,0:T(8,128)S(1)} %bitcast.11, f32[16,16,128]{2,1,0:T(8,128)S(1)} %collective-permute-done.rest_1_, ...), custom_call_target="tpu_custom_call" | custom-call | tf_op jit(solution)/shard_map/third/pallas_call | solution.py:634
  100.6 11.2 %all_to_all.10.info = f32[32,2,128]{2,1,0:T(2,128)S(1)} all-to-all(f32[32,2,128]{2,1,0:T(2,128)S(1)} %third.1), channel_id=1, replica_groups=mesh['z'=4,'core'=2,'sub'=4] {'z','core','sub'}, dimensions={0} | all-to-all | bytes 65536 | tf_op jit(solution)/shard_map/all_to_all | solution.py:644
  111.8 1.7 %finish.1 = f32[8,64,64]{2,1,0:T(8,128)} custom-call(s32[3]{0:T(128)S(1)} %pad_add_fusion.ids, f32[32,2,128]{2,1,0:T(2,128)S(1)} %all_to_all.10.info, f32[4,4,16,128]{3,2,1,0:T(8,128)S(1)} %get-tuple-element.52.turned, f32[2,4,16,128]{3,2,1,0:T(8,128)S(1)} %get-tuple-element.53.rest_0_, f32[2,4,16,128]{3,2,1,0:T(8,128)S(1)} %collective-permute-done.34.rest_1_, ...), custom_call_target="tpu_custom_call" | custom-call | tf_op jit(solution)/shard_map/finish/pallas_call | solution.py:647
  (66 shorter events, 14.7 us)
Async XLA Ops:
  2.4 35.7 %collective-permute-start.9 = (f32[2,64,1152]{2,1,0:T(8,128)}, f32[2,64,1152]{2,1,0:T(8,128)S(1)}, u32[]{:S(2)}, u32[]{:S(2)}) collective-permute-start(f32[2,64,1152]{2,1,0:T(8,128)} %get-tuple-element.32.rest_8_), channel_id=1, source_target_pairs={{0,2},{1,3},{2,0},{3,1},{4,6},{5,7},{6,4},{7,5},{8,10},{9,11},{10,... | collective-permute-start | bytes 1769480 | tf_op jit(solution)/shard_map/ppermute | solution.py:515
  5.4 32.7 %collective-permute-start.8 = (f32[2,64,1152]{2,1,0:T(8,128)}, f32[2,64,1152]{2,1,0:T(8,128)S(1)}, u32[]{:S(2)}, u32[]{:S(2)}) collective-permute-start(f32[2,64,1152]{2,1,0:T(8,128)} %get-tuple-element.33.rest_9_), channel_id=1, source_target_pairs={{0,1},{1,0},{2,3},{3,2},{4,5},{5,4},{6,7},{7,6},{8,9},{9,8},{10,11... | collective-permute-start | bytes 1769480 | tf_op jit(solution)/shard_map/ppermute | solution.py:514
  8.7 13.2 %all-to-all-start = ((f32[4,4,16,128]{3,2,1,0:T(8,128)}), f32[4,4,16,128]{3,2,1,0:T(8,128)S(1)}, u32[]{:S(2)}, u32[]{:S(2)}) async-start(f32[4,4,16,128]{3,2,1,0:T(8,128)} %get-tuple-element.31), calls=%async_computation | async-start | bytes 262144 | tf_op jit(solution)/shard_map/all_to_all | solution.py:536
  22.4 8.0 %collective-permute-start.1 = (f32[16,16,128]{2,1,0:T(8,128)S(1)}, f32[16,16,128]{2,1,0:T(8,128)S(1)}, u32[]{:S(2)}, u32[]{:S(2)}) collective-permute-start(f32[16,16,128]{2,1,0:T(8,128)S(1)} %bitcast.6), channel_id=1, source_target_pairs={{0,16},{8,24},{16,0},{24,8},{1,17},{9,25},{17,1},{25,9},{2,18},{10... | collective-permute-start | bytes 393224 | tf_op jit(solution)/shard_map/ppermute | solution.py:545
  25.1 6.0 %collective-permute-start = (f32[16,16,128]{2,1,0:T(8,128)S(1)}, f32[16,16,128]{2,1,0:T(8,128)S(1)}, u32[]{:S(2)}, u32[]{:S(2)}) collective-permute-start(f32[16,16,128]{2,1,0:T(8,128)S(1)} %bitcast.7), channel_id=1, source_target_pairs={{0,8},{8,0},{16,24},{24,16},{1,9},{9,1},{17,25},{25,17},{2,10},{10... | collective-permute-start | bytes 393224 | tf_op jit(solution)/shard_map/ppermute | solution.py:545
  26.6 6.5 %collective-permute-start.3 = (f32[16,16,128]{2,1,0:T(8,128)S(1)}, f32[16,16,128]{2,1,0:T(8,128)S(1)}, u32[]{:S(2)}, u32[]{:S(2)}) collective-permute-start(f32[16,16,128]{2,1,0:T(8,128)S(1)} %bitcast.8), channel_id=1, source_target_pairs={{0,4},{4,0},{1,5},{5,1},{2,6},{6,2},{3,7},{7,3},{8,12},{12,8},{9,1... | collective-permute-start | bytes 393224 | tf_op jit(solution)/shard_map/ppermute | solution.py:555
  30.4 16.0 %collective-permute-start.10 = (f32[2,64,1152]{2,1,0:T(8,128)}, f32[2,64,1152]{2,1,0:T(8,128)}, u32[]{:S(2)}, u32[]{:S(2)}) collective-permute-start(f32[2,64,1152]{2,1,0:T(8,128)} %get-tuple-element.33.rest_9_), channel_id=1, source_target_pairs={{0,2},{1,3},{2,0},{3,1},{4,6},{5,7},{6,4},{7,5},{8,10},{9,11},{10,... | collective-permute-start | bytes 1769480 | tf_op jit(solution)/shard_map/ppermute | solution.py:517
  31.1 16.1 %collective-permute-start.7 = (f32[2,64,1152]{2,1,0:T(8,128)}, f32[2,64,1152]{2,1,0:T(8,128)}, u32[]{:S(2)}, u32[]{:S(2)}) collective-permute-start(f32[2,64,1152]{2,1,0:T(8,128)} %get-tuple-element.32.rest_8_), channel_id=1, source_target_pairs={{0,1},{1,0},{2,3},{3,2},{4,5},{5,4},{6,7},{7,6},{8,9},{9,8},{10,11... | collective-permute-start | bytes 1769480 | tf_op jit(solution)/shard_map/ppermute | solution.py:516
  33.1 5.0 %collective-permute-start.2 = (f32[16,16,128]{2,1,0:T(8,128)S(1)}, f32[16,16,128]{2,1,0:T(8,128)S(1)}, u32[]{:S(2)}, u32[]{:S(2)}) collective-permute-start(f32[16,16,128]{2,1,0:T(8,128)S(1)} %collective-permute-done.1.rest_2_), channel_id=1, source_target_pairs={{0,8},{8,0},{16,24},{24,16},{1,9},{9,1},{17,25},{25,17},{2,10},{10... | collective-permute-start | bytes 393224 | tf_op jit(solution)/shard_map/ppermute | solution.py:545
  38.1 24.8 %collective-permute-start.18 = (f32[2,64,1152]{2,1,0:T(8,128)S(1)}, f32[2,64,1152]{2,1,0:T(8,128)S(1)}, u32[]{:S(2)}, u32[]{:S(2)}) collective-permute-start(f32[2,64,1152]{2,1,0:T(8,128)S(1)} %collective-permute-done.9.rest_12_), channel_id=1, source_target_pairs={{0,1},{1,0},{2,3},{3,2},{4,5},{5,4},{6,7},{7,6},{8,9},{9,8},{10,11... | collective-permute-start | bytes 1769480 | tf_op jit(solution)/shard_map/ppermute | solution.py:559
  38.1 25.2 %collective-permute-start.19 = (f32[2,64,1152]{2,1,0:T(8,128)S(1)}, f32[2,64,1152]{2,1,0:T(8,128)S(1)}, u32[]{:S(2)}, u32[]{:S(2)}) collective-permute-start(f32[2,64,1152]{2,1,0:T(8,128)S(1)} %collective-permute-done.8.rest_11_), channel_id=1, source_target_pairs={{0,2},{1,3},{2,0},{3,1},{4,6},{5,7},{6,4},{7,5},{8,10},{9,11},{10,... | collective-permute-start | bytes 1769480 | tf_op jit(solution)/shard_map/ppermute | solution.py:560
  40.8 5.6 %collective-permute-start.6 = (f32[16,16,128]{2,1,0:T(8,128)S(1)}, f32[16,16,128]{2,1,0:T(8,128)S(1)}, u32[]{:S(2)}, u32[]{:S(2)}) collective-permute-start(f32[16,16,128]{2,1,0:T(8,128)S(1)} %collective-permute-done.2.rest_3_), channel_id=1, source_target_pairs={{0,4},{4,0},{1,5},{5,1},{2,6},{6,2},{3,7},{7,3},{8,12},{12,8},{9,1... | collective-permute-start | bytes 393224 | tf_op jit(solution)/shard_map/ppermute | solution.py:555
  50.9 7.4 %collective-permute-start.12 = (f32[12,16,128]{2,1,0:T(8,128)S(1)}, f32[12,16,128]{2,1,0:T(8,128)S(1)}, u32[]{:S(2)}, u32[]{:S(2)}) collective-permute-start(f32[12,16,128]{2,1,0:T(8,128)S(1)} %get-tuple-element.34.rest_8_), channel_id=1, source_target_pairs={{0,16},{8,24},{16,0},{24,8},{1,17},{9,25},{17,1},{25,9},{2,18},{10... | collective-permute-start | bytes 294920 | tf_op jit(solution)/shard_map/ppermute | solution.py:545
  52.1 6.4 %collective-permute-start.11 = (f32[12,16,128]{2,1,0:T(8,128)S(1)}, f32[12,16,128]{2,1,0:T(8,128)S(1)}, u32[]{:S(2)}, u32[]{:S(2)}) collective-permute-start(f32[12,16,128]{2,1,0:T(8,128)S(1)} %get-tuple-element.34.rest_8_), channel_id=1, source_target_pairs={{0,8},{8,0},{16,24},{24,16},{1,9},{9,1},{17,25},{25,17},{2,10},{10... | collective-permute-start | bytes 294920 | tf_op jit(solution)/shard_map/ppermute | solution.py:545
  58.2 4.6 %collective-permute-start.13 = (f32[12,16,128]{2,1,0:T(8,128)S(1)}, f32[12,16,128]{2,1,0:T(8,128)S(1)}, u32[]{:S(2)}, u32[]{:S(2)}) collective-permute-start(f32[12,16,128]{2,1,0:T(8,128)S(1)} %collective-permute-done.12.rest_10_), channel_id=1, source_target_pairs={{0,8},{8,0},{16,24},{24,16},{1,9},{9,1},{17,25},{25,17},{2,10},{10... | collective-permute-start | bytes 294920 | tf_op jit(solution)/shard_map/ppermute | solution.py:545
  58.5 7.6 %collective-permute-start.14 = (f32[12,16,128]{2,1,0:T(8,128)S(1)}, f32[12,16,128]{2,1,0:T(8,128)S(1)}, u32[]{:S(2)}, u32[]{:S(2)}) collective-permute-start(f32[12,16,128]{2,1,0:T(8,128)S(1)} %get-tuple-element.34.rest_8_), channel_id=1, source_target_pairs={{0,4},{4,0},{1,5},{5,1},{2,6},{6,2},{3,7},{7,3},{8,12},{12,8},{9,1... | collective-permute-start | bytes 294920 | tf_op jit(solution)/shard_map/ppermute | solution.py:555
  58.5 11.6 %collective-permute-start.15 = (f32[12,16,128]{2,1,0:T(8,128)S(1)}, f32[12,16,128]{2,1,0:T(8,128)S(1)}, u32[]{:S(2)}, u32[]{:S(2)}) collective-permute-start(f32[12,16,128]{2,1,0:T(8,128)S(1)} %collective-permute-done.11.rest_9_), channel_id=1, source_target_pairs={{0,4},{4,0},{1,5},{5,1},{2,6},{6,2},{3,7},{7,3},{8,12},{12,8},{9,1... | collective-permute-start | bytes 294920 | tf_op jit(solution)/shard_map/ppermute | solution.py:555
  62.9 7.3 %collective-permute-start.16 = (f32[12,16,128]{2,1,0:T(8,128)S(1)}, f32[12,16,128]{2,1,0:T(8,128)S(1)}, u32[]{:S(2)}, u32[]{:S(2)}) collective-permute-start(f32[12,16,128]{2,1,0:T(8,128)S(1)} %collective-permute-done.12.rest_10_), channel_id=1, source_target_pairs={{0,4},{4,0},{1,5},{5,1},{2,6},{6,2},{3,7},{7,3},{8,12},{12,8},{9,1... | collective-permute-start | bytes 294920 | tf_op jit(solution)/shard_map/ppermute | solution.py:555
  62.9 11.3 %collective-permute-start.17 = (f32[12,16,128]{2,1,0:T(8,128)S(1)}, f32[12,16,128]{2,1,0:T(8,128)S(1)}, u32[]{:S(2)}, u32[]{:S(2)}) collective-permute-start(f32[12,16,128]{2,1,0:T(8,128)S(1)} %collective-permute-done.13.rest_11_), channel_id=1, source_target_pairs={{0,4},{4,0},{1,5},{5,1},{2,6},{6,2},{3,7},{7,3},{8,12},{12,8},{9,1... | collective-permute-start | bytes 294920 | tf_op jit(solution)/shard_map/ppermute | solution.py:555
  64.5 5.2 %collective-permute-start.21 = (f32[4,16,128]{2,1,0:T(8,128)S(1)}, f32[4,16,128]{2,1,0:T(8,128)S(1)}, u32[]{:S(2)}, u32[]{:S(2)}) collective-permute-start(f32[4,16,128]{2,1,0:T(8,128)S(1)} %more.1.rest_16_), channel_id=1, source_target_pairs={{0,16},{8,24},{16,0},{24,8},{1,17},{9,25},{17,1},{25,9},{2,18},{10... | collective-permute-start | bytes 98312 | tf_op jit(solution)/shard_map/ppermute | solution.py:545
  66.2 4.4 %collective-permute-start.20 = (f32[4,16,128]{2,1,0:T(8,128)S(1)}, f32[4,16,128]{2,1,0:T(8,128)S(1)}, u32[]{:S(2)}, u32[]{:S(2)}) collective-permute-start(f32[4,16,128]{2,1,0:T(8,128)S(1)} %more.1.rest_16_), channel_id=1, source_target_pairs={{0,8},{8,0},{16,24},{24,16},{1,9},{9,1},{17,25},{25,17},{2,10},{10... | collective-permute-start | bytes 98312 | tf_op jit(solution)/shard_map/ppermute | solution.py:545
  70.1 4.0 %collective-permute-start.25 = (f32[4,16,128]{2,1,0:T(8,128)S(1)}, f32[4,16,128]{2,1,0:T(8,128)S(1)}, u32[]{:S(2)}, u32[]{:S(2)}) collective-permute-start(f32[4,16,128]{2,1,0:T(8,128)S(1)} %collective-permute-done.21.rest_18_), channel_id=1, source_target_pairs={{0,4},{4,0},{1,5},{5,1},{2,6},{6,2},{3,7},{7,3},{8,12},{12,8},{9,1... | collective-permute-start | bytes 98312 | tf_op jit(solution)/shard_map/ppermute | solution.py:555
  77.4 9.4 %collective-permute-start.28 = (f32[16,16,128]{2,1,0:T(8,128)S(1)}, f32[16,16,128]{2,1,0:T(8,128)S(1)}, u32[]{:S(2)}, u32[]{:S(2)}) collective-permute-start(f32[16,16,128]{2,1,0:T(8,128)S(1)} %get-tuple-element.44.rest_8_), channel_id=1, source_target_pairs={{0,16},{8,24},{16,0},{24,8},{1,17},{9,25},{17,1},{25,9},{2,18},{10... | collective-permute-start | bytes 393224 | tf_op jit(solution)/shard_map/ppermute | solution.py:545
  78.7 12.3 %collective-permute-start.27 = (f32[16,16,128]{2,1,0:T(8,128)S(1)}, f32[16,16,128]{2,1,0:T(8,128)S(1)}, u32[]{:S(2)}, u32[]{:S(2)}) collective-permute-start(f32[16,16,128]{2,1,0:T(8,128)S(1)} %get-tuple-element.44.rest_8_), channel_id=1, source_target_pairs={{0,8},{8,0},{16,24},{24,16},{1,9},{9,1},{17,25},{25,17},{2,10},{10... | collective-permute-start | bytes 393224 | tf_op jit(solution)/shard_map/ppermute | solution.py:545
  86.8 5.4 %collective-permute-start.29 = (f32[16,16,128]{2,1,0:T(8,128)S(1)}, f32[16,16,128]{2,1,0:T(8,128)S(1)}, u32[]{:S(2)}, u32[]{:S(2)}) collective-permute-start(f32[16,16,128]{2,1,0:T(8,128)S(1)} %collective-permute-done.28.rest_10_), channel_id=1, source_target_pairs={{0,8},{8,0},{16,24},{24,16},{1,9},{9,1},{17,25},{25,17},{2,10},{10... | collective-permute-start | bytes 393224 | tf_op jit(solution)/shard_map/ppermute | solution.py:545
  86.8 4.3 %collective-permute-start.34 = (f32[2,4,16,128]{3,2,1,0:T(8,128)S(1)}, f32[2,4,16,128]{3,2,1,0:T(8,128)S(1)}, u32[]{:S(2)}, u32[]{:S(2)}) collective-permute-start(f32[2,4,16,128]{3,2,1,0:T(8,128)S(1)} %get-tuple-element.41), channel_id=1, source_target_pairs={{0,1},{1,0},{2,3},{3,2},{4,5},{5,4},{6,7},{7,6},{8,9},{9,8},{10,11... | collective-permute-start | bytes 196616 | tf_op jit(solution)/shard_map/ppermute | solution.py:627
  87.9 4.3 %collective-permute-start.35 = (f32[2,4,16,128]{3,2,1,0:T(8,128)S(1)}, f32[2,4,16,128]{3,2,1,0:T(8,128)S(1)}, u32[]{:S(2)}, u32[]{:S(2)}) collective-permute-start(f32[2,4,16,128]{3,2,1,0:T(8,128)S(1)} %get-tuple-element.42), channel_id=1, source_target_pairs={{0,2},{1,3},{2,0},{3,1},{4,6},{5,7},{6,4},{7,5},{8,10},{9,11},{10,... | collective-permute-start | bytes 196616 | tf_op jit(solution)/shard_map/ppermute | solution.py:627
  89.4 8.1 %collective-permute-start.30 = (f32[16,16,128]{2,1,0:T(8,128)S(1)}, f32[16,16,128]{2,1,0:T(8,128)S(1)}, u32[]{:S(2)}, u32[]{:S(2)}) collective-permute-start(f32[16,16,128]{2,1,0:T(8,128)S(1)} %get-tuple-element.44.rest_8_), channel_id=1, source_target_pairs={{0,4},{4,0},{1,5},{5,1},{2,6},{6,2},{3,7},{7,3},{8,12},{12,8},{9,1... | collective-permute-start | bytes 393224 | tf_op jit(solution)/shard_map/ppermute | solution.py:555
  91.1 6.5 %collective-permute-start.32 = (f32[16,16,128]{2,1,0:T(8,128)S(1)}, f32[16,16,128]{2,1,0:T(8,128)S(1)}, u32[]{:S(2)}, u32[]{:S(2)}) collective-permute-start(f32[16,16,128]{2,1,0:T(8,128)S(1)} %collective-permute-done.28.rest_10_), channel_id=1, source_target_pairs={{0,4},{4,0},{1,5},{5,1},{2,6},{6,2},{3,7},{7,3},{8,12},{12,8},{9,1... | collective-permute-start | bytes 393224 | tf_op jit(solution)/shard_map/ppermute | solution.py:555
  91.1 6.5 %collective-permute-start.31 = (f32[16,16,128]{2,1,0:T(8,128)S(1)}, f32[16,16,128]{2,1,0:T(8,128)S(1)}, u32[]{:S(2)}, u32[]{:S(2)}) collective-permute-start(f32[16,16,128]{2,1,0:T(8,128)S(1)} %collective-permute-done.27.rest_9_), channel_id=1, source_target_pairs={{0,4},{4,0},{1,5},{5,1},{2,6},{6,2},{3,7},{7,3},{8,12},{12,8},{9,1... | collective-permute-start | bytes 393224 | tf_op jit(solution)/shard_map/ppermute | solution.py:555
  92.2 5.4 %collective-permute-start.33 = (f32[16,16,128]{2,1,0:T(8,128)S(1)}, f32[16,16,128]{2,1,0:T(8,128)S(1)}, u32[]{:S(2)}, u32[]{:S(2)}) collective-permute-start(f32[16,16,128]{2,1,0:T(8,128)S(1)} %collective-permute-done.29.rest_11_), channel_id=1, source_target_pairs={{0,4},{4,0},{1,5},{5,1},{2,6},{6,2},{3,7},{7,3},{8,12},{12,8},{9,1... | collective-permute-start | bytes 393224 | tf_op jit(solution)/shard_map/ppermute | solution.py:555
  92.2 5.4 %collective-permute-start.36 = (f32[2,4,16,128]{3,2,1,0:T(8,128)S(1)}, f32[2,4,16,128]{3,2,1,0:T(8,128)S(1)}, u32[]{:S(2)}, u32[]{:S(2)}) collective-permute-start(f32[2,4,16,128]{3,2,1,0:T(8,128)S(1)} %get-tuple-element.43), channel_id=1, source_target_pairs={{0,3},{1,2},{2,1},{3,0},{4,7},{5,6},{6,5},{7,4},{8,11},{9,10},{10,... | collective-permute-start | bytes 196616 | tf_op jit(solution)/shard_map/ppermute | solution.py:627
  (9 other events, 100.0 us)

commit v7 on v6

--- a/solution.py
+++ b/solution.py
@@ -289,7 +289,10 @@
             base += 1
 
 
-def second_kernel(n_field, chunks, count, sends, dof, terms, pos, *rest):
+def second_kernel(n_field, chunks, count, sends, dof, terms, links, *rest):
+    rest, (pos, sem) = rest[:-2], rest[-2:]
+    copy = pltpu.make_async_copy(links, pos, sem)
+    copy.start()
     b_ref, rest = rest[:n_field], rest[n_field:]
     z_blocks, rest = in_blocks(rest[: chunks * n_field], chunks), rest[chunks * n_field :]
     stages, (out, basis, coeffs) = rest[:count], rest[count : count + 3]
@@ -326,11 +329,15 @@
     def put(pair, values):
         out[pair] = values
 
+    copy.wait()
     apply_rows(stages, pos, dup, terms, dof, put)
     share_out(z_blocks[0], out, shares)
 
 
-def third_kernel(n_field, count, dof, terms, pos, basis, coeffs, *rest):
+def third_kernel(n_field, count, dof, terms, links, basis, coeffs, *rest):
+    rest, (pos, sem) = rest[:-2], rest[-2:]
+    copy = pltpu.make_async_copy(links, pos, sem)
+    copy.start()
     b_ref, rest = rest[:n_field], rest[n_field:]
     z_blocks, rest = in_blocks(rest[:n_field], 1), rest[n_field:]
     stages, (sums, work, dup, image) = rest[:count], rest[count:]
@@ -367,6 +374,7 @@
     def put(pair, values):
         image[pair] = values
 
+    copy.wait()
     apply_rows(stages, pos, dup, terms, dof, put)
 
     def last(pair, carry):
@@ -426,7 +434,7 @@
         out[pair] = (y0 * scale) * b_mine[pair] + y1 * v1_mine[pair] + y2 * v2_mine[pair]
 
 
-def finish_kernel(dof, ids, info, turned, *rest):
+def finish_kernel(dof, info, turned, *rest):
     out, stack, factor = rest[-3:]
     n_sub, per_part, rhs, lanes = turned.shape
     shares = rest[:n_sub]
@@ -457,7 +465,7 @@
     for index in range(3 * n_sub):
         factor[index] = jnp.broadcast_to(flipped[:rhs, index : index + 1], (rhs, lanes))
     for k in range(n_sub):
-        quarter = ids[2] ^ k
+        quarter = lax.axis_index("sub") ^ k
         alpha, beta, gamma = (factor[part * n_sub + quarter] for part in range(3))
         start = pl.multiple_of(quarter * rhs, 8)
         for pair in range(per_part):
@@ -613,13 +621,14 @@
         )(*ops)
         splits.append(split)
     count = len(splits)
+    links = [pltpu.SMEM(positions.shape, jnp.int32), pltpu.SemaphoreType.DMA]
 
     z2, basis, coeffs, *shares = pl.pallas_call(
         functools.partial(second_kernel, n_field, chunks, count, sends, dof, terms),
         out_shape=[own_shape, jax.ShapeDtypeStruct(full, F32), small] + share,
-        in_specs=[SMEM] + [VMEM] * ((1 + chunks) * n_field + count),
+        in_specs=[ANY] + [VMEM] * ((1 + chunks) * n_field + count),
         out_specs=[VMEM] * (3 + sends),
-        scratch_shapes=[pltpu.VMEM(dup, F32)],
+        scratch_shapes=[pltpu.VMEM(dup, F32)] + links,
         compiler_params=PARAMS,
         name="second",
     )(positions, *b_parts, *z1_parts, *splits)
@@ -634,10 +643,11 @@
     sums, *work = pl.pallas_call(
         functools.partial(third_kernel, n_field, count, dof, terms),
         out_shape=[jax.ShapeDtypeStruct((copies,) + note, F32)] + keep,
-        in_specs=[SMEM] + [VMEM] * (2 + 2 * n_field + count),
+        in_specs=[ANY] + [VMEM] * (2 + 2 * n_field + count),
         out_specs=[VMEM] * (1 + len(keep)),
         scratch_shapes=[pltpu.VMEM(full, F32)] * (1 - len(keep))
-        + [pltpu.VMEM(dup, F32), pltpu.VMEM(field, F32)],
+        + [pltpu.VMEM(dup, F32), pltpu.VMEM(field, F32)]
+        + links,
         compiler_params=PARAMS,
         name="third",
     )(positions, basis, coeffs, *b_parts, *z2_parts, *splits)
@@ -647,7 +657,7 @@
         return pl.pallas_call(
             functools.partial(finish_kernel, dof),
             out_shape=jax.ShapeDtypeStruct(right_side.shape, F32),
-            in_specs=[SMEM] + [VMEM] * (2 + sends),
+            in_specs=[VMEM] * (2 + sends),
             out_specs=VMEM,
             scratch_shapes=[
                 pltpu.VMEM((per_dev // 2, n_sub * rhs, lanes), F32),
@@ -655,7 +665,7 @@
             ],
             compiler_params=SMALL,
             name="finish",
-        )(ids, sums, kept, *shares)
+        )(sums, kept, *shares)
     result = pl.pallas_call(
         combine_kernel,
         out_shape=own_shape,

time: 114 us -> 113 us (level)
  transfers between devices with their start and end apart: 38 -> 38, of which waited for: 14 -> 14; matrix products, arithmetic and copies ran while one was open for 2% -> 2% of each run, Pallas kernels for 8% -> 9%
where the time goes in v7:
time: 113 us; the launch traced here: 112 us
  waiting for transfers between devices  43.8 us (39%)
  starting transfers between devices  35.7 us (32%)
  Pallas kernels  18.1 us (16%)
  blocking collectives  11.2 us (10%)
  local copies, waits for them, and re-layouts  3.31 us (3%)
    ppermute x12, waiting for transfers between devices, step_z(): return lax.ppermute(own, 'z', [(z, z ^ offset) for z in range(nz)])  26.3 us
    ppermute x12, starting transfers between devices, step_z(): return lax.ppermute(own, 'z', [(z, z ^ offset) for z in range(nz)])  16.6 us
    all_to_all x1, blocking collectives, per_device(): sums = lax.all_to_all(sums, axes, split_axis=0, concat_axis=0, tiled=True)  11.2 us
    all_to_all x1, waiting for transfers between devices, per_device(): lax.all_to_all(turned, 'sub', split_axis=0, concat_axis=0, tiled=True)  9.83 us
    ppermute x3, waiting for transfers between devices, per_device(): lax.ppermute(shares[k], 'sub', hops_to[k])  4.95 us
    ppermute x3, starting transfers between devices, per_device(): lax.ppermute(shares[k], 'sub', hops_to[k])  4.72 us
    pallas_call x1, Pallas kernels, per_device(): pl.pallas_call(functools.partial(first_kernel, n_field, len(ops), dof, te...  3.73 us
    pallas_call x1, Pallas kernels, per_device(): pl.pallas_call(functools.partial(position_kernel, (per_dev, n_sub, nz, ho...  3.51 us
  transfers between devices with their start and end apart: 38, of which 14 were waited for; matrix products, arithmetic and copies ran while one was open for 2% of the time, Pallas kernels for 9%

profile of v7, /device:TPU:0, one launch (start us, length us, event | category | flops | bytes accessed | tf_op | source)
XLA Modules:
  0.0 112.4 jit_solution(5382278433269615746)
XLA Ops:
  0.0 2.4 %pack.1 = (f32[2,64,1152]{2,1,0:T(8,128)}, f32[2,64,1152]{2,1,0:T(8,128)}) custom-call(f32[8,64,576]{2,1,0:T(8,128)} %op.1), custom_call_target="tpu_custom_call" | custom-call | tf_op jit(solution)/shard_map/pack/pallas_call | solution.py:502
  2.4 3.1 %collective-permute-start.9 = (f32[2,64,1152]{2,1,0:T(8,128)}, f32[2,64,1152]{2,1,0:T(8,128)S(1)}, u32[]{:S(2)}, u32[]{:S(2)}) collective-permute-start(f32[2,64,1152]{2,1,0:T(8,128)} %get-tuple-element.32.rest_8_), channel_id=1, source_target_pairs={{0,2},{1,3},{2,0},{3,1},{4,6},{5,7},{6,4},{7,5},{8,10},{9,11},{10,... | collective-permute-start | bytes 1769480 | tf_op jit(solution)/shard_map/ppermute | solution.py:523
  5.4 1.5 %collective-permute-start.8 = (f32[2,64,1152]{2,1,0:T(8,128)}, f32[2,64,1152]{2,1,0:T(8,128)S(1)}, u32[]{:S(2)}, u32[]{:S(2)}) collective-permute-start(f32[2,64,1152]{2,1,0:T(8,128)} %get-tuple-element.33.rest_9_), channel_id=1, source_target_pairs={{0,1},{1,0},{2,3},{3,2},{4,5},{5,4},{6,7},{7,6},{8,9},{9,8},{10,11... | collective-permute-start | bytes 1769480 | tf_op jit(solution)/shard_map/ppermute | solution.py:522
  8.7 3.3 %all-to-all-start = ((f32[4,4,16,128]{3,2,1,0:T(8,128)}), f32[4,4,16,128]{3,2,1,0:T(8,128)S(1)}, u32[]{:S(2)}, u32[]{:S(2)}) async-start(f32[4,4,16,128]{3,2,1,0:T(8,128)} %get-tuple-element.31), calls=%async_computation | async-start | bytes 262144 | tf_op jit(solution)/shard_map/all_to_all | solution.py:544
  12.0 9.8 %all-to-all-done = f32[4,4,16,128]{3,2,1,0:T(8,128)S(1)} async-done(((f32[4,4,16,128]{3,2,1,0:T(8,128)}), f32[4,4,16,128]{3,2,1,0:T(8,128)S(1)}, u32[]{:S(2)}, u32[]{:S(2)}) %all-to-all-start) | async-done | bytes 131104 | tf_op jit(solution)/shard_map/all_to_all | solution.py:544
  22.4 2.7 %collective-permute-start.1 = (f32[16,16,128]{2,1,0:T(8,128)S(1)}, f32[16,16,128]{2,1,0:T(8,128)S(1)}, u32[]{:S(2)}, u32[]{:S(2)}) collective-permute-start(f32[16,16,128]{2,1,0:T(8,128)S(1)} %bitcast.6), channel_id=1, source_target_pairs={{0,16},{8,24},{16,0},{24,8},{1,17},{9,25},{17,1},{25,9},{2,18},{10... | collective-permute-start | bytes 393224 | tf_op jit(solution)/shard_map/ppermute | solution.py:553
  25.1 1.6 %collective-permute-start = (f32[16,16,128]{2,1,0:T(8,128)S(1)}, f32[16,16,128]{2,1,0:T(8,128)S(1)}, u32[]{:S(2)}, u32[]{:S(2)}) collective-permute-start(f32[16,16,128]{2,1,0:T(8,128)S(1)} %bitcast.7), channel_id=1, source_target_pairs={{0,8},{8,0},{16,24},{24,16},{1,9},{9,1},{17,25},{25,17},{2,10},{10... | collective-permute-start | bytes 393224 | tf_op jit(solution)/shard_map/ppermute | solution.py:553
  26.6 3.7 %collective-permute-done.1.rest_2_ = f32[16,16,128]{2,1,0:T(8,128)S(1)} collective-permute-done((f32[16,16,128]{2,1,0:T(8,128)S(1)}, f32[16,16,128]{2,1,0:T(8,128)S(1)}, u32[]{:S(2)}, u32[]{:S(2)}) %collective-permute-start.1) | collective-permute-done | bytes 131104 | tf_op jit(solution)/shard_map/ppermute | solution.py:553
  31.1 2.0 %collective-permute-start.7 = (f32[2,64,1152]{2,1,0:T(8,128)}, f32[2,64,1152]{2,1,0:T(8,128)}, u32[]{:S(2)}, u32[]{:S(2)}) collective-permute-start(f32[2,64,1152]{2,1,0:T(8,128)} %get-tuple-element.32.rest_8_), channel_id=1, source_target_pairs={{0,1},{1,0},{2,3},{3,2},{4,5},{5,4},{6,7},{7,6},{8,9},{9,8},{10,11... | collective-permute-start | bytes 1769480 | tf_op jit(solution)/shard_map/ppermute | solution.py:524
  33.6 4.4 %collective-permute-done.2.rest_3_ = f32[16,16,128]{2,1,0:T(8,128)S(1)} collective-permute-done((f32[16,16,128]{2,1,0:T(8,128)S(1)}, f32[16,16,128]{2,1,0:T(8,128)S(1)}, u32[]{:S(2)}, u32[]{:S(2)}) %collective-permute-start.2) | collective-permute-done | bytes 131104 | tf_op jit(solution)/shard_map/ppermute | solution.py:553
  38.1 1.3 %collective-permute-start.19 = (f32[2,64,1152]{2,1,0:T(8,128)S(1)}, f32[2,64,1152]{2,1,0:T(8,128)S(1)}, u32[]{:S(2)}, u32[]{:S(2)}) collective-permute-start(f32[2,64,1152]{2,1,0:T(8,128)S(1)} %collective-permute-done.8.rest_11_), channel_id=1, source_target_pairs={{0,2},{1,3},{2,0},{3,1},{4,6},{5,7},{6,4},{7,5},{8,10},{9,11},{10,... | collective-permute-start | bytes 1769480 | tf_op jit(solution)/shard_map/ppermute | solution.py:568
  39.6 1.2 %collective-permute-done.4.rest_5_ = f32[16,16,128]{2,1,0:T(8,128)S(1)} collective-permute-done((f32[16,16,128]{2,1,0:T(8,128)S(1)}, f32[16,16,128]{2,1,0:T(8,128)S(1)}, u32[]{:S(2)}, u32[]{:S(2)}) %collective-permute-start.4) | collective-permute-done | bytes 131104 | tf_op jit(solution)/shard_map/ppermute | solution.py:563
  42.8 3.5 %positions.1.pos.links = s32[288]{0:T(512)S(1)} custom-call(s32[3]{0:T(128)S(1)} %pad_add_fusion.ids, s32[256]{0:T(256)S(1)} %copy-done.1, s32[2048]{0:T(1024)S(1)} %reshape.22.table), custom_call_target="tpu_custom_call" | custom-call | tf_op jit(solution)/shard_map/positions/pallas_call | solution.py:527
  47.1 3.7 %first.1 = (f32[12,16,128]{2,1,0:T(8,128)S(1)}, bf16[12,576,256]{2,1,0:T(8,128)(2,1)S(1)}, f32[256,16,128]{2,1,0:T(8,128)S(1)}) custom-call(s32[288]{0:T(512)S(1)} %positions.1.pos.links, f32[16,16,128]{2,1,0:T(8,128)S(1)} %bitcast.9, f32[16,16,128]{2,1,0:T(8,128)S(1)} %collective-permute-done.rest_1_, f32[16,16,128]{2,1,0:T(8,128)S(1)} %collective-permute-done.1.rest_2_, ...), custom_call_target="tpu_custom_call" | custom-call | tf_op jit(solution)/shard_map/first/pallas_call | solution.py:587
  50.9 1.2 %collective-permute-start.12 = (f32[12,16,128]{2,1,0:T(8,128)S(1)}, f32[12,16,128]{2,1,0:T(8,128)S(1)}, u32[]{:S(2)}, u32[]{:S(2)}) collective-permute-start(f32[12,16,128]{2,1,0:T(8,128)S(1)} %get-tuple-element.34.rest_8_), channel_id=1, source_target_pairs={{0,16},{8,24},{16,0},{24,8},{1,17},{9,25},{17,1},{25,9},{2,18},{10... | collective-permute-start | bytes 294920 | tf_op jit(solution)/shard_map/ppermute | solution.py:553
  52.1 3.2 %collective-permute-start.11 = (f32[12,16,128]{2,1,0:T(8,128)S(1)}, f32[12,16,128]{2,1,0:T(8,128)S(1)}, u32[]{:S(2)}, u32[]{:S(2)}) collective-permute-start(f32[12,16,128]{2,1,0:T(8,128)S(1)} %get-tuple-element.34.rest_8_), channel_id=1, source_target_pairs={{0,8},{8,0},{16,24},{24,16},{1,9},{9,1},{17,25},{25,17},{2,10},{10... | collective-permute-start | bytes 294920 | tf_op jit(solution)/shard_map/ppermute | solution.py:553
  55.3 2.9 %collective-permute-done.12.rest_10_ = f32[12,16,128]{2,1,0:T(8,128)S(1)} collective-permute-done((f32[12,16,128]{2,1,0:T(8,128)S(1)}, f32[12,16,128]{2,1,0:T(8,128)S(1)}, u32[]{:S(2)}, u32[]{:S(2)}) %collective-permute-start.12) | collective-permute-done | bytes 98336 | tf_op jit(solution)/shard_map/ppermute | solution.py:553
  59.1 3.8 %collective-permute-done.13.rest_11_ = f32[12,16,128]{2,1,0:T(8,128)S(1)} collective-permute-done((f32[12,16,128]{2,1,0:T(8,128)S(1)}, f32[12,16,128]{2,1,0:T(8,128)S(1)}, u32[]{:S(2)}, u32[]{:S(2)}) %collective-permute-start.13) | collective-permute-done | bytes 98336 | tf_op jit(solution)/shard_map/ppermute | solution.py:553
  64.5 1.6 %collective-permute-start.21 = (f32[4,16,128]{2,1,0:T(8,128)S(1)}, f32[4,16,128]{2,1,0:T(8,128)S(1)}, u32[]{:S(2)}, u32[]{:S(2)}) collective-permute-start(f32[4,16,128]{2,1,0:T(8,128)S(1)} %more.1.rest_16_), channel_id=1, source_target_pairs={{0,16},{8,24},{16,0},{24,8},{1,17},{9,25},{17,1},{25,9},{2,18},{10... | collective-permute-start | bytes 98312 | tf_op jit(solution)/shard_map/ppermute | solution.py:553
  66.2 1.9 %collective-permute-start.20 = (f32[4,16,128]{2,1,0:T(8,128)S(1)}, f32[4,16,128]{2,1,0:T(8,128)S(1)}, u32[]{:S(2)}, u32[]{:S(2)}) collective-permute-start(f32[4,16,128]{2,1,0:T(8,128)S(1)} %more.1.rest_16_), channel_id=1, source_target_pairs={{0,8},{8,0},{16,24},{24,16},{1,9},{9,1},{17,25},{25,17},{2,10},{10... | collective-permute-start | bytes 98312 | tf_op jit(solution)/shard_map/ppermute | solution.py:553
  68.1 1.7 %collective-permute-done.21.rest_18_ = f32[4,16,128]{2,1,0:T(8,128)S(1)} collective-permute-done((f32[4,16,128]{2,1,0:T(8,128)S(1)}, f32[4,16,128]{2,1,0:T(8,128)S(1)}, u32[]{:S(2)}, u32[]{:S(2)}) %collective-permute-start.21) | collective-permute-done | bytes 32800 | tf_op jit(solution)/shard_map/ppermute | solution.py:553
  70.7 3.0 %collective-permute-done.22.rest_19_ = f32[4,16,128]{2,1,0:T(8,128)S(1)} collective-permute-done((f32[4,16,128]{2,1,0:T(8,128)S(1)}, f32[4,16,128]{2,1,0:T(8,128)S(1)}, u32[]{:S(2)}, u32[]{:S(2)}) %collective-permute-start.22) | collective-permute-done | bytes 32800 | tf_op jit(solution)/shard_map/ppermute | solution.py:553
  74.9 2.5 %second.1 = (f32[16,16,128]{2,1,0:T(8,128)S(1)}, f32[128,16,128]{2,1,0:T(8,128)S(1)}, f32[16,128]{1,0:T(8,128)S(1)}, f32[2,4,16,128]{3,2,1,0:T(8,128)S(1)}, f32[...) custom-call(s32[288]{0:T(512)S(1)} %positions.1.pos.links, ...), custom_call_target="tpu_custom_call" | custom-call | tf_op jit(solution)/shard_map/second/pallas_call | solution.py:626
  77.4 1.3 %collective-permute-start.28 = (f32[16,16,128]{2,1,0:T(8,128)S(1)}, f32[16,16,128]{2,1,0:T(8,128)S(1)}, u32[]{:S(2)}, u32[]{:S(2)}) collective-permute-start(f32[16,16,128]{2,1,0:T(8,128)S(1)} %get-tuple-element.44.rest_8_), channel_id=1, source_target_pairs={{0,16},{8,24},{16,0},{24,8},{1,17},{9,25},{17,1},{25,9},{2,18},{10... | collective-permute-start | bytes 393224 | tf_op jit(solution)/shard_map/ppermute | solution.py:553
  78.7 1.9 %collective-permute-start.27 = (f32[16,16,128]{2,1,0:T(8,128)S(1)}, f32[16,16,128]{2,1,0:T(8,128)S(1)}, u32[]{:S(2)}, u32[]{:S(2)}) collective-permute-start(f32[16,16,128]{2,1,0:T(8,128)S(1)} %get-tuple-element.44.rest_8_), channel_id=1, source_target_pairs={{0,8},{8,0},{16,24},{24,16},{1,9},{9,1},{17,25},{25,17},{2,10},{10... | collective-permute-start | bytes 393224 | tf_op jit(solution)/shard_map/ppermute | solution.py:553
  80.6 6.2 %collective-permute-done.28.rest_10_ = f32[16,16,128]{2,1,0:T(8,128)S(1)} collective-permute-done((f32[16,16,128]{2,1,0:T(8,128)S(1)}, f32[16,16,128]{2,1,0:T(8,128)S(1)}, u32[]{:S(2)}, u32[]{:S(2)}) %collective-permute-start.28) | collective-permute-done | bytes 131104 | tf_op jit(solution)/shard_map/ppermute | solution.py:553
  87.9 1.5 %collective-permute-start.35 = (f32[2,4,16,128]{3,2,1,0:T(8,128)S(1)}, f32[2,4,16,128]{3,2,1,0:T(8,128)S(1)}, u32[]{:S(2)}, u32[]{:S(2)}) collective-permute-start(f32[2,4,16,128]{3,2,1,0:T(8,128)S(1)} %get-tuple-element.42), channel_id=1, source_target_pairs={{0,2},{1,3},{2,0},{3,1},{4,6},{5,7},{6,4},{7,5},{8,10},{9,11},{10,... | collective-permute-start | bytes 196616 | tf_op jit(solution)/shard_map/ppermute | solution.py:636
  89.4 1.6 %collective-permute-done.34.rest_1_ = f32[2,4,16,128]{3,2,1,0:T(8,128)S(1)} collective-permute-done((f32[2,4,16,128]{3,2,1,0:T(8,128)S(1)}, f32[2,4,16,128]{3,2,1,0:T(8,128)S(1)}, u32[]{:S(2)}, u32[]{:S(2)}) %collective-permute-start.34) | collective-permute-done | bytes 65568 | tf_op jit(solution)/shard_map/ppermute | solution.py:636
  92.2 2.1 %collective-permute-start.36 = (f32[2,4,16,128]{3,2,1,0:T(8,128)S(1)}, f32[2,4,16,128]{3,2,1,0:T(8,128)S(1)}, u32[]{:S(2)}, u32[]{:S(2)}) collective-permute-start(f32[2,4,16,128]{3,2,1,0:T(8,128)S(1)} %get-tuple-element.43), channel_id=1, source_target_pairs={{0,3},{1,2},{2,1},{3,0},{4,7},{5,6},{6,5},{7,4},{8,11},{9,10},{10,... | collective-permute-start | bytes 196616 | tf_op jit(solution)/shard_map/ppermute | solution.py:636
  94.2 3.3 %collective-permute-done.36.rest_3_ = f32[2,4,16,128]{3,2,1,0:T(8,128)S(1)} collective-permute-done((f32[2,4,16,128]{3,2,1,0:T(8,128)S(1)}, f32[2,4,16,128]{3,2,1,0:T(8,128)S(1)}, u32[]{:S(2)}, u32[]{:S(2)}) %collective-permute-start.36) | collective-permute-done | bytes 65568 | tf_op jit(solution)/shard_map/ppermute | solution.py:636
  97.5 2.5 %third.1 = f32[32,2,128]{2,1,0:T(2,128)S(1)} custom-call(s32[288]{0:T(512)S(1)} %positions.1.pos.links, f32[128,16,128]{2,1,0:T(8,128)S(1)} %get-tuple-element.37.basis, f32[16,128]{1,0:T(8,128)S(1)} %get-tuple-element.38.coeffs, f32[16,16,128]{2,1,0:T(8,128)S(1)} %bitcast.11, f32[16,16,128]{2,1,0:T(8,128)S(1)} %collective-permute-done.rest_1_, ...), custom_call_target="tpu_custom_call" | custom-call | tf_op jit(solution)/shard_map/third/pallas_call | solution.py:643
  100.0 11.2 %all_to_all.10.info = f32[32,2,128]{2,1,0:T(2,128)S(1)} all-to-all(f32[32,2,128]{2,1,0:T(2,128)S(1)} %third.1), channel_id=1, replica_groups=mesh['z'=4,'core'=2,'sub'=4] {'z','core','sub'}, dimensions={0} | all-to-all | bytes 65536 | tf_op jit(solution)/shard_map/all_to_all | solution.py:654
  (66 shorter events, 14.7 us)
Async XLA Ops:
  2.4 35.7 %collective-permute-start.9 = (f32[2,64,1152]{2,1,0:T(8,128)}, f32[2,64,1152]{2,1,0:T(8,128)S(1)}, u32[]{:S(2)}, u32[]{:S(2)}) collective-permute-start(f32[2,64,1152]{2,1,0:T(8,128)} %get-tuple-element.32.rest_8_), channel_id=1, source_target_pairs={{0,2},{1,3},{2,0},{3,1},{4,6},{5,7},{6,4},{7,5},{8,10},{9,11},{10,... | collective-permute-start | bytes 1769480 | tf_op jit(solution)/shard_map/ppermute | solution.py:523
  5.4 32.7 %collective-permute-start.8 = (f32[2,64,1152]{2,1,0:T(8,128)}, f32[2,64,1152]{2,1,0:T(8,128)S(1)}, u32[]{:S(2)}, u32[]{:S(2)}) collective-permute-start(f32[2,64,1152]{2,1,0:T(8,128)} %get-tuple-element.33.rest_9_), channel_id=1, source_target_pairs={{0,1},{1,0},{2,3},{3,2},{4,5},{5,4},{6,7},{7,6},{8,9},{9,8},{10,11... | collective-permute-start | bytes 1769480 | tf_op jit(solution)/shard_map/ppermute | solution.py:522
  8.7 13.2 %all-to-all-start = ((f32[4,4,16,128]{3,2,1,0:T(8,128)}), f32[4,4,16,128]{3,2,1,0:T(8,128)S(1)}, u32[]{:S(2)}, u32[]{:S(2)}) async-start(f32[4,4,16,128]{3,2,1,0:T(8,128)} %get-tuple-element.31), calls=%async_computation | async-start | bytes 262144 | tf_op jit(solution)/shard_map/all_to_all | solution.py:544
  22.4 8.0 %collective-permute-start.1 = (f32[16,16,128]{2,1,0:T(8,128)S(1)}, f32[16,16,128]{2,1,0:T(8,128)S(1)}, u32[]{:S(2)}, u32[]{:S(2)}) collective-permute-start(f32[16,16,128]{2,1,0:T(8,128)S(1)} %bitcast.6), channel_id=1, source_target_pairs={{0,16},{8,24},{16,0},{24,8},{1,17},{9,25},{17,1},{25,9},{2,18},{10... | collective-permute-start | bytes 393224 | tf_op jit(solution)/shard_map/ppermute | solution.py:553
  25.1 6.0 %collective-permute-start = (f32[16,16,128]{2,1,0:T(8,128)S(1)}, f32[16,16,128]{2,1,0:T(8,128)S(1)}, u32[]{:S(2)}, u32[]{:S(2)}) collective-permute-start(f32[16,16,128]{2,1,0:T(8,128)S(1)} %bitcast.7), channel_id=1, source_target_pairs={{0,8},{8,0},{16,24},{24,16},{1,9},{9,1},{17,25},{25,17},{2,10},{10... | collective-permute-start | bytes 393224 | tf_op jit(solution)/shard_map/ppermute | solution.py:553
  26.6 6.5 %collective-permute-start.3 = (f32[16,16,128]{2,1,0:T(8,128)S(1)}, f32[16,16,128]{2,1,0:T(8,128)S(1)}, u32[]{:S(2)}, u32[]{:S(2)}) collective-permute-start(f32[16,16,128]{2,1,0:T(8,128)S(1)} %bitcast.8), channel_id=1, source_target_pairs={{0,4},{4,0},{1,5},{5,1},{2,6},{6,2},{3,7},{7,3},{8,12},{12,8},{9,1... | collective-permute-start | bytes 393224 | tf_op jit(solution)/shard_map/ppermute | solution.py:563
  30.4 16.0 %collective-permute-start.10 = (f32[2,64,1152]{2,1,0:T(8,128)}, f32[2,64,1152]{2,1,0:T(8,128)}, u32[]{:S(2)}, u32[]{:S(2)}) collective-permute-start(f32[2,64,1152]{2,1,0:T(8,128)} %get-tuple-element.33.rest_9_), channel_id=1, source_target_pairs={{0,2},{1,3},{2,0},{3,1},{4,6},{5,7},{6,4},{7,5},{8,10},{9,11},{10,... | collective-permute-start | bytes 1769480 | tf_op jit(solution)/shard_map/ppermute | solution.py:525
  31.1 16.1 %collective-permute-start.7 = (f32[2,64,1152]{2,1,0:T(8,128)}, f32[2,64,1152]{2,1,0:T(8,128)}, u32[]{:S(2)}, u32[]{:S(2)}) collective-permute-start(f32[2,64,1152]{2,1,0:T(8,128)} %get-tuple-element.32.rest_8_), channel_id=1, source_target_pairs={{0,1},{1,0},{2,3},{3,2},{4,5},{5,4},{6,7},{7,6},{8,9},{9,8},{10,11... | collective-permute-start | bytes 1769480 | tf_op jit(solution)/shard_map/ppermute | solution.py:524
  33.1 5.0 %collective-permute-start.2 = (f32[16,16,128]{2,1,0:T(8,128)S(1)}, f32[16,16,128]{2,1,0:T(8,128)S(1)}, u32[]{:S(2)}, u32[]{:S(2)}) collective-permute-start(f32[16,16,128]{2,1,0:T(8,128)S(1)} %collective-permute-done.1.rest_2_), channel_id=1, source_target_pairs={{0,8},{8,0},{16,24},{24,16},{1,9},{9,1},{17,25},{25,17},{2,10},{10... | collective-permute-start | bytes 393224 | tf_op jit(solution)/shard_map/ppermute | solution.py:553
  38.1 24.8 %collective-permute-start.18 = (f32[2,64,1152]{2,1,0:T(8,128)S(1)}, f32[2,64,1152]{2,1,0:T(8,128)S(1)}, u32[]{:S(2)}, u32[]{:S(2)}) collective-permute-start(f32[2,64,1152]{2,1,0:T(8,128)S(1)} %collective-permute-done.9.rest_12_), channel_id=1, source_target_pairs={{0,1},{1,0},{2,3},{3,2},{4,5},{5,4},{6,7},{7,6},{8,9},{9,8},{10,11... | collective-permute-start | bytes 1769480 | tf_op jit(solution)/shard_map/ppermute | solution.py:567
  38.1 25.2 %collective-permute-start.19 = (f32[2,64,1152]{2,1,0:T(8,128)S(1)}, f32[2,64,1152]{2,1,0:T(8,128)S(1)}, u32[]{:S(2)}, u32[]{:S(2)}) collective-permute-start(f32[2,64,1152]{2,1,0:T(8,128)S(1)} %collective-permute-done.8.rest_11_), channel_id=1, source_target_pairs={{0,2},{1,3},{2,0},{3,1},{4,6},{5,7},{6,4},{7,5},{8,10},{9,11},{10,... | collective-permute-start | bytes 1769480 | tf_op jit(solution)/shard_map/ppermute | solution.py:568
  40.8 5.6 %collective-permute-start.6 = (f32[16,16,128]{2,1,0:T(8,128)S(1)}, f32[16,16,128]{2,1,0:T(8,128)S(1)}, u32[]{:S(2)}, u32[]{:S(2)}) collective-permute-start(f32[16,16,128]{2,1,0:T(8,128)S(1)} %collective-permute-done.2.rest_3_), channel_id=1, source_target_pairs={{0,4},{4,0},{1,5},{5,1},{2,6},{6,2},{3,7},{7,3},{8,12},{12,8},{9,1... | collective-permute-start | bytes 393224 | tf_op jit(solution)/shard_map/ppermute | solution.py:563
  50.9 7.4 %collective-permute-start.12 = (f32[12,16,128]{2,1,0:T(8,128)S(1)}, f32[12,16,128]{2,1,0:T(8,128)S(1)}, u32[]{:S(2)}, u32[]{:S(2)}) collective-permute-start(f32[12,16,128]{2,1,0:T(8,128)S(1)} %get-tuple-element.34.rest_8_), channel_id=1, source_target_pairs={{0,16},{8,24},{16,0},{24,8},{1,17},{9,25},{17,1},{25,9},{2,18},{10... | collective-permute-start | bytes 294920 | tf_op jit(solution)/shard_map/ppermute | solution.py:553
  52.1 6.4 %collective-permute-start.11 = (f32[12,16,128]{2,1,0:T(8,128)S(1)}, f32[12,16,128]{2,1,0:T(8,128)S(1)}, u32[]{:S(2)}, u32[]{:S(2)}) collective-permute-start(f32[12,16,128]{2,1,0:T(8,128)S(1)} %get-tuple-element.34.rest_8_), channel_id=1, source_target_pairs={{0,8},{8,0},{16,24},{24,16},{1,9},{9,1},{17,25},{25,17},{2,10},{10... | collective-permute-start | bytes 294920 | tf_op jit(solution)/shard_map/ppermute | solution.py:553
  58.2 4.6 %collective-permute-start.13 = (f32[12,16,128]{2,1,0:T(8,128)S(1)}, f32[12,16,128]{2,1,0:T(8,128)S(1)}, u32[]{:S(2)}, u32[]{:S(2)}) collective-permute-start(f32[12,16,128]{2,1,0:T(8,128)S(1)} %collective-permute-done.12.rest_10_), channel_id=1, source_target_pairs={{0,8},{8,0},{16,24},{24,16},{1,9},{9,1},{17,25},{25,17},{2,10},{10... | collective-permute-start | bytes 294920 | tf_op jit(solution)/shard_map/ppermute | solution.py:553
  58.5 7.6 %collective-permute-start.14 = (f32[12,16,128]{2,1,0:T(8,128)S(1)}, f32[12,16,128]{2,1,0:T(8,128)S(1)}, u32[]{:S(2)}, u32[]{:S(2)}) collective-permute-start(f32[12,16,128]{2,1,0:T(8,128)S(1)} %get-tuple-element.34.rest_8_), channel_id=1, source_target_pairs={{0,4},{4,0},{1,5},{5,1},{2,6},{6,2},{3,7},{7,3},{8,12},{12,8},{9,1... | collective-permute-start | bytes 294920 | tf_op jit(solution)/shard_map/ppermute | solution.py:563
  58.5 11.6 %collective-permute-start.15 = (f32[12,16,128]{2,1,0:T(8,128)S(1)}, f32[12,16,128]{2,1,0:T(8,128)S(1)}, u32[]{:S(2)}, u32[]{:S(2)}) collective-permute-start(f32[12,16,128]{2,1,0:T(8,128)S(1)} %collective-permute-done.11.rest_9_), channel_id=1, source_target_pairs={{0,4},{4,0},{1,5},{5,1},{2,6},{6,2},{3,7},{7,3},{8,12},{12,8},{9,1... | collective-permute-start | bytes 294920 | tf_op jit(solution)/shard_map/ppermute | solution.py:563
  62.9 7.3 %collective-permute-start.16 = (f32[12,16,128]{2,1,0:T(8,128)S(1)}, f32[12,16,128]{2,1,0:T(8,128)S(1)}, u32[]{:S(2)}, u32[]{:S(2)}) collective-permute-start(f32[12,16,128]{2,1,0:T(8,128)S(1)} %collective-permute-done.12.rest_10_), channel_id=1, source_target_pairs={{0,4},{4,0},{1,5},{5,1},{2,6},{6,2},{3,7},{7,3},{8,12},{12,8},{9,1... | collective-permute-start | bytes 294920 | tf_op jit(solution)/shard_map/ppermute | solution.py:563
  62.9 11.3 %collective-permute-start.17 = (f32[12,16,128]{2,1,0:T(8,128)S(1)}, f32[12,16,128]{2,1,0:T(8,128)S(1)}, u32[]{:S(2)}, u32[]{:S(2)}) collective-permute-start(f32[12,16,128]{2,1,0:T(8,128)S(1)} %collective-permute-done.13.rest_11_), channel_id=1, source_target_pairs={{0,4},{4,0},{1,5},{5,1},{2,6},{6,2},{3,7},{7,3},{8,12},{12,8},{9,1... | collective-permute-start | bytes 294920 | tf_op jit(solution)/shard_map/ppermute | solution.py:563
  64.5 5.2 %collective-permute-start.21 = (f32[4,16,128]{2,1,0:T(8,128)S(1)}, f32[4,16,128]{2,1,0:T(8,128)S(1)}, u32[]{:S(2)}, u32[]{:S(2)}) collective-permute-start(f32[4,16,128]{2,1,0:T(8,128)S(1)} %more.1.rest_16_), channel_id=1, source_target_pairs={{0,16},{8,24},{16,0},{24,8},{1,17},{9,25},{17,1},{25,9},{2,18},{10... | collective-permute-start | bytes 98312 | tf_op jit(solution)/shard_map/ppermute | solution.py:553
  66.2 4.4 %collective-permute-start.20 = (f32[4,16,128]{2,1,0:T(8,128)S(1)}, f32[4,16,128]{2,1,0:T(8,128)S(1)}, u32[]{:S(2)}, u32[]{:S(2)}) collective-permute-start(f32[4,16,128]{2,1,0:T(8,128)S(1)} %more.1.rest_16_), channel_id=1, source_target_pairs={{0,8},{8,0},{16,24},{24,16},{1,9},{9,1},{17,25},{25,17},{2,10},{10... | collective-permute-start | bytes 98312 | tf_op jit(solution)/shard_map/ppermute | solution.py:553
  70.1 4.0 %collective-permute-start.25 = (f32[4,16,128]{2,1,0:T(8,128)S(1)}, f32[4,16,128]{2,1,0:T(8,128)S(1)}, u32[]{:S(2)}, u32[]{:S(2)}) collective-permute-start(f32[4,16,128]{2,1,0:T(8,128)S(1)} %collective-permute-done.21.rest_18_), channel_id=1, source_target_pairs={{0,4},{4,0},{1,5},{5,1},{2,6},{6,2},{3,7},{7,3},{8,12},{12,8},{9,1... | collective-permute-start | bytes 98312 | tf_op jit(solution)/shard_map/ppermute | solution.py:563
  77.4 9.4 %collective-permute-start.28 = (f32[16,16,128]{2,1,0:T(8,128)S(1)}, f32[16,16,128]{2,1,0:T(8,128)S(1)}, u32[]{:S(2)}, u32[]{:S(2)}) collective-permute-start(f32[16,16,128]{2,1,0:T(8,128)S(1)} %get-tuple-element.44.rest_8_), channel_id=1, source_target_pairs={{0,16},{8,24},{16,0},{24,8},{1,17},{9,25},{17,1},{25,9},{2,18},{10... | collective-permute-start | bytes 393224 | tf_op jit(solution)/shard_map/ppermute | solution.py:553
  78.7 12.3 %collective-permute-start.27 = (f32[16,16,128]{2,1,0:T(8,128)S(1)}, f32[16,16,128]{2,1,0:T(8,128)S(1)}, u32[]{:S(2)}, u32[]{:S(2)}) collective-permute-start(f32[16,16,128]{2,1,0:T(8,128)S(1)} %get-tuple-element.44.rest_8_), channel_id=1, source_target_pairs={{0,8},{8,0},{16,24},{24,16},{1,9},{9,1},{17,25},{25,17},{2,10},{10... | collective-permute-start | bytes 393224 | tf_op jit(solution)/shard_map/ppermute | solution.py:553
  86.7 5.4 %collective-permute-start.29 = (f32[16,16,128]{2,1,0:T(8,128)S(1)}, f32[16,16,128]{2,1,0:T(8,128)S(1)}, u32[]{:S(2)}, u32[]{:S(2)}) collective-permute-start(f32[16,16,128]{2,1,0:T(8,128)S(1)} %collective-permute-done.28.rest_10_), channel_id=1, source_target_pairs={{0,8},{8,0},{16,24},{24,16},{1,9},{9,1},{17,25},{25,17},{2,10},{10... | collective-permute-start | bytes 393224 | tf_op jit(solution)/shard_map/ppermute | solution.py:553
  86.7 4.3 %collective-permute-start.34 = (f32[2,4,16,128]{3,2,1,0:T(8,128)S(1)}, f32[2,4,16,128]{3,2,1,0:T(8,128)S(1)}, u32[]{:S(2)}, u32[]{:S(2)}) collective-permute-start(f32[2,4,16,128]{3,2,1,0:T(8,128)S(1)} %get-tuple-element.41), channel_id=1, source_target_pairs={{0,1},{1,0},{2,3},{3,2},{4,5},{5,4},{6,7},{7,6},{8,9},{9,8},{10,11... | collective-permute-start | bytes 196616 | tf_op jit(solution)/shard_map/ppermute | solution.py:636
  87.9 4.3 %collective-permute-start.35 = (f32[2,4,16,128]{3,2,1,0:T(8,128)S(1)}, f32[2,4,16,128]{3,2,1,0:T(8,128)S(1)}, u32[]{:S(2)}, u32[]{:S(2)}) collective-permute-start(f32[2,4,16,128]{3,2,1,0:T(8,128)S(1)} %get-tuple-element.42), channel_id=1, source_target_pairs={{0,2},{1,3},{2,0},{3,1},{4,6},{5,7},{6,4},{7,5},{8,10},{9,11},{10,... | collective-permute-start | bytes 196616 | tf_op jit(solution)/shard_map/ppermute | solution.py:636
  89.4 8.1 %collective-permute-start.30 = (f32[16,16,128]{2,1,0:T(8,128)S(1)}, f32[16,16,128]{2,1,0:T(8,128)S(1)}, u32[]{:S(2)}, u32[]{:S(2)}) collective-permute-start(f32[16,16,128]{2,1,0:T(8,128)S(1)} %get-tuple-element.44.rest_8_), channel_id=1, source_target_pairs={{0,4},{4,0},{1,5},{5,1},{2,6},{6,2},{3,7},{7,3},{8,12},{12,8},{9,1... | collective-permute-start | bytes 393224 | tf_op jit(solution)/shard_map/ppermute | solution.py:563
  91.0 6.5 %collective-permute-start.32 = (f32[16,16,128]{2,1,0:T(8,128)S(1)}, f32[16,16,128]{2,1,0:T(8,128)S(1)}, u32[]{:S(2)}, u32[]{:S(2)}) collective-permute-start(f32[16,16,128]{2,1,0:T(8,128)S(1)} %collective-permute-done.28.rest_10_), channel_id=1, source_target_pairs={{0,4},{4,0},{1,5},{5,1},{2,6},{6,2},{3,7},{7,3},{8,12},{12,8},{9,1... | collective-permute-start | bytes 393224 | tf_op jit(solution)/shard_map/ppermute | solution.py:563
  91.0 6.5 %collective-permute-start.31 = (f32[16,16,128]{2,1,0:T(8,128)S(1)}, f32[16,16,128]{2,1,0:T(8,128)S(1)}, u32[]{:S(2)}, u32[]{:S(2)}) collective-permute-start(f32[16,16,128]{2,1,0:T(8,128)S(1)} %collective-permute-done.27.rest_9_), channel_id=1, source_target_pairs={{0,4},{4,0},{1,5},{5,1},{2,6},{6,2},{3,7},{7,3},{8,12},{12,8},{9,1... | collective-permute-start | bytes 393224 | tf_op jit(solution)/shard_map/ppermute | solution.py:563
  92.1 5.4 %collective-permute-start.33 = (f32[16,16,128]{2,1,0:T(8,128)S(1)}, f32[16,16,128]{2,1,0:T(8,128)S(1)}, u32[]{:S(2)}, u32[]{:S(2)}) collective-permute-start(f32[16,16,128]{2,1,0:T(8,128)S(1)} %collective-permute-done.29.rest_11_), channel_id=1, source_target_pairs={{0,4},{4,0},{1,5},{5,1},{2,6},{6,2},{3,7},{7,3},{8,12},{12,8},{9,1... | collective-permute-start | bytes 393224 | tf_op jit(solution)/shard_map/ppermute | solution.py:563
  92.2 5.4 %collective-permute-start.36 = (f32[2,4,16,128]{3,2,1,0:T(8,128)S(1)}, f32[2,4,16,128]{3,2,1,0:T(8,128)S(1)}, u32[]{:S(2)}, u32[]{:S(2)}) collective-permute-start(f32[2,4,16,128]{3,2,1,0:T(8,128)S(1)} %get-tuple-element.43), channel_id=1, source_target_pairs={{0,3},{1,2},{2,1},{3,0},{4,7},{5,6},{6,5},{7,4},{8,11},{9,10},{10,... | collective-permute-start | bytes 196616 | tf_op jit(solution)/shard_map/ppermute | solution.py:636
  (9 other events, 100.0 us)

commit v8 on v7

--- a/solution.py
+++ b/solution.py
@@ -180,21 +180,6 @@
     return jnp.where(low_half(even.shape, dof), even, odd)
 
 
-def rows_product(pair_rows, local, pos, dup, terms, dof):
-    rows = dup.shape[1]
-    halves = []
-    for i, op in enumerate(pair_rows):
-        product = lax.dot_general(
-            jnp.concatenate(site_vector(local + i, pos, dup, terms, dof), axis=0),
-            jnp.concatenate(split_bf16(op), axis=0),
-            (((1,), (1,)), ((), ())),
-            preferred_element_type=F32,
-        )
-        total = product[:rows] + product[rows:]
-        halves.append(total + pltpu.roll(total, dof, 1))
-    return jnp.where(low_half(halves[0].shape, dof), halves[0], halves[1])
-
-
 def apply_rows(stages, pos, dup, terms, dof, put):
     base = 0
     for stage in stages:
@@ -270,23 +255,19 @@
             base += 1
 
 
-def more_kernel(base, dof, terms, pos, dup, *rest):
-    ops, out = rest[:-1], rest[-1]
+def more_kernel(base, dof, terms, links, dup, *rest):
+    ops, (out, split, pos, sem) = rest[:-4], rest[-4:]
+    copy = pltpu.make_async_copy(links, pos, sem)
+    copy.start()
     done = 0
     for op in ops:
         for inner in range(op.shape[0]):
-            local = 2 * (base + done)
-            out[done] = rows_product(row_pairs(op, inner, dof), local, pos, dup, terms, dof)
+            split[done] = to_columns(*row_pairs(op, inner, dof))
             done += 1
-
-
-def turn_kernel(count, dof, *rest):
-    ops, split = rest[:count], rest[count]
-    base = 0
-    for op in ops:
-        for inner in range(op.shape[0]):
-            split[base] = to_columns(*row_pairs(op, inner, dof))
-            base += 1
+    copy.wait()
+    for pair in range(done):
+        local = 2 * (base + pair)
+        out[pair] = pair_product(split[pair], local, pos, dup, terms, dof)
 
 
 def second_kernel(n_field, chunks, count, sends, dof, terms, links, *rest):
@@ -602,23 +583,19 @@
     z1_parts = gather(z1)
     if relay:
         ops, chunks = stages[1], 2
-        late = pl.pallas_call(
+        late, split = pl.pallas_call(
             functools.partial(more_kernel, done, dof, terms),
-            out_shape=jax.ShapeDtypeStruct((n_own - done,) + field[1:], F32),
-            in_specs=[SMEM, VMEM] + [VMEM] * len(ops),
-            out_specs=VMEM,
+            out_shape=[
+                jax.ShapeDtypeStruct((n_own - done,) + field[1:], F32),
+                split_shape(n_own - done),
+            ],
+            in_specs=[ANY, VMEM] + [VMEM] * len(ops),
+            out_specs=[VMEM] * 2,
+            scratch_shapes=[pltpu.SMEM(positions.shape, jnp.int32), pltpu.SemaphoreType.DMA],
             compiler_params=PARAMS,
             name="more",
         )(positions, spread_b, *ops)
         z1_parts = z1_parts + gather(late)
-        split = pl.pallas_call(
-            functools.partial(turn_kernel, len(ops), dof),
-            out_shape=split_shape(n_own - done),
-            in_specs=[VMEM] * len(ops),
-            out_specs=VMEM,
-            compiler_params=PARAMS,
-            name="turn",
-        )(*ops)
         splits.append(split)
     count = len(splits)
     links = [pltpu.SMEM(positions.shape, jnp.int32), pltpu.SemaphoreType.DMA]

time: 113 us -> 113 us (level)
  no operation moved by 1% of the time
where the time goes in v8:
time: 113 us; the launch traced here: 112 us
  waiting for transfers between devices  43.9 us (39%)
  starting transfers between devices  35.9 us (32%)
  Pallas kernels  17.7 us (16%)
  blocking collectives  11.3 us (10%)
  local copies, waits for them, and re-layouts  3.31 us (3%)
    ppermute x12, waiting for transfers between devices, step_z(): return lax.ppermute(own, 'z', [(z, z ^ offset) for z in range(nz)])  26.6 us
    ppermute x12, starting transfers between devices, step_z(): return lax.ppermute(own, 'z', [(z, z ^ offset) for z in range(nz)])  16.7 us
    all_to_all x1, blocking collectives, per_device(): sums = lax.all_to_all(sums, axes, split_axis=0, concat_axis=0, tiled=True)  11.3 us
    all_to_all x1, waiting for transfers between devices, per_device(): lax.all_to_all(turned, 'sub', split_axis=0, concat_axis=0, tiled=True)  9.62 us
    ppermute x3, waiting for transfers between devices, per_device(): lax.ppermute(shares[k], 'sub', hops_to[k])  4.85 us
    ppermute x3, starting transfers between devices, per_device(): lax.ppermute(shares[k], 'sub', hops_to[k])  4.82 us
    pallas_call x1, Pallas kernels, per_device(): pl.pallas_call(functools.partial(first_kernel, n_field, len(ops), dof, te...  3.67 us
    pallas_call x1, Pallas kernels, per_device(): pl.pallas_call(functools.partial(position_kernel, (per_dev, n_sub, nz, ho...  3.51 us
  transfers between devices with their start and end apart: 38, of which 14 were waited for; matrix products, arithmetic and copies ran while one was open for 2% of the time, Pallas kernels for 9%

profile of v8, /device:TPU:0, one launch (start us, length us, event | category | flops | bytes accessed | tf_op | source)
XLA Modules:
  0.0 112.4 jit_solution(7611645648488784060)
XLA Ops:
  0.0 1.4 %pack.1 = (f32[2,64,1152]{2,1,0:T(8,128)S(1)}, f32[2,64,1152]{2,1,0:T(8,128)S(1)}) custom-call(f32[8,64,576]{2,1,0:T(8,128)} %op.1), custom_call_target="tpu_custom_call" | custom-call | tf_op jit(solution)/shard_map/pack/pallas_call | solution.py:483
  1.4 3.1 %collective-permute-start.9 = (f32[2,64,1152]{2,1,0:T(8,128)S(1)}, f32[2,64,1152]{2,1,0:T(8,128)S(1)}, u32[]{:S(2)}, u32[]{:S(2)}) collective-permute-start(f32[2,64,1152]{2,1,0:T(8,128)S(1)} %get-tuple-element.34.rest_8_), channel_id=1, source_target_pairs={{0,2},{1,3},{2,0},{3,1},{4,6},{5,7},{6,4},{7,5},{8,10},{9,11},{10,... | collective-permute-start | bytes 1769480 | tf_op jit(solution)/shard_map/ppermute | solution.py:504
  4.5 1.5 %collective-permute-start.8 = (f32[2,64,1152]{2,1,0:T(8,128)S(1)}, f32[2,64,1152]{2,1,0:T(8,128)S(1)}, u32[]{:S(2)}, u32[]{:S(2)}) collective-permute-start(f32[2,64,1152]{2,1,0:T(8,128)S(1)} %get-tuple-element.35.rest_9_), channel_id=1, source_target_pairs={{0,1},{1,0},{2,3},{3,2},{4,5},{5,4},{6,7},{7,6},{8,9},{9,8},{10,11... | collective-permute-start | bytes 1769480 | tf_op jit(solution)/shard_map/ppermute | solution.py:503
  7.7 3.3 %all-to-all-start = ((f32[4,4,16,128]{3,2,1,0:T(8,128)}), f32[4,4,16,128]{3,2,1,0:T(8,128)S(1)}, u32[]{:S(2)}, u32[]{:S(2)}) async-start(f32[4,4,16,128]{3,2,1,0:T(8,128)} %get-tuple-element.33), calls=%async_computation | async-start | bytes 262144 | tf_op jit(solution)/shard_map/all_to_all | solution.py:525
  11.1 9.6 %all-to-all-done = f32[4,4,16,128]{3,2,1,0:T(8,128)S(1)} async-done(((f32[4,4,16,128]{3,2,1,0:T(8,128)}), f32[4,4,16,128]{3,2,1,0:T(8,128)S(1)}, u32[]{:S(2)}, u32[]{:S(2)}) %all-to-all-start) | async-done | bytes 131104 | tf_op jit(solution)/shard_map/all_to_all | solution.py:525
  21.3 2.7 %collective-permute-start.1 = (f32[16,16,128]{2,1,0:T(8,128)S(1)}, f32[16,16,128]{2,1,0:T(8,128)S(1)}, u32[]{:S(2)}, u32[]{:S(2)}) collective-permute-start(f32[16,16,128]{2,1,0:T(8,128)S(1)} %bitcast.6), channel_id=1, source_target_pairs={{0,16},{8,24},{16,0},{24,8},{1,17},{9,25},{17,1},{25,9},{2,18},{10... | collective-permute-start | bytes 393224 | tf_op jit(solution)/shard_map/ppermute | solution.py:534
  23.9 1.6 %collective-permute-start = (f32[16,16,128]{2,1,0:T(8,128)S(1)}, f32[16,16,128]{2,1,0:T(8,128)S(1)}, u32[]{:S(2)}, u32[]{:S(2)}) collective-permute-start(f32[16,16,128]{2,1,0:T(8,128)S(1)} %bitcast.7), channel_id=1, source_target_pairs={{0,8},{8,0},{16,24},{24,16},{1,9},{9,1},{17,25},{25,17},{2,10},{10... | collective-permute-start | bytes 393224 | tf_op jit(solution)/shard_map/ppermute | solution.py:534
  25.5 3.7 %collective-permute-done.1.rest_2_ = f32[16,16,128]{2,1,0:T(8,128)S(1)} collective-permute-done((f32[16,16,128]{2,1,0:T(8,128)S(1)}, f32[16,16,128]{2,1,0:T(8,128)S(1)}, u32[]{:S(2)}, u32[]{:S(2)}) %collective-permute-start.1) | collective-permute-done | bytes 131104 | tf_op jit(solution)/shard_map/ppermute | solution.py:534
  29.9 2.0 %collective-permute-start.7 = (f32[2,64,1152]{2,1,0:T(8,128)S(1)}, f32[2,64,1152]{2,1,0:T(8,128)}, u32[]{:S(2)}, u32[]{:S(2)}) collective-permute-start(f32[2,64,1152]{2,1,0:T(8,128)S(1)} %get-tuple-element.34.rest_8_), channel_id=1, source_target_pairs={{0,1},{1,0},{2,3},{3,2},{4,5},{5,4},{6,7},{7,6},{8,9},{9,8},{10,11... | collective-permute-start | bytes 1769480 | tf_op jit(solution)/shard_map/ppermute | solution.py:505
  32.5 4.4 %collective-permute-done.2.rest_3_ = f32[16,16,128]{2,1,0:T(8,128)S(1)} collective-permute-done((f32[16,16,128]{2,1,0:T(8,128)S(1)}, f32[16,16,128]{2,1,0:T(8,128)S(1)}, u32[]{:S(2)}, u32[]{:S(2)}) %collective-permute-start.2) | collective-permute-done | bytes 131104 | tf_op jit(solution)/shard_map/ppermute | solution.py:534
  37.0 1.3 %collective-permute-start.19 = (f32[2,64,1152]{2,1,0:T(8,128)S(1)}, f32[2,64,1152]{2,1,0:T(8,128)}, u32[]{:S(2)}, u32[]{:S(2)}) collective-permute-start(f32[2,64,1152]{2,1,0:T(8,128)S(1)} %collective-permute-done.8.rest_11_), channel_id=1, source_target_pairs={{0,2},{1,3},{2,0},{3,1},{4,6},{5,7},{6,4},{7,5},{8,10},{9,11},{10,... | collective-permute-start | bytes 1769480 | tf_op jit(solution)/shard_map/ppermute | solution.py:549
  41.6 3.5 %positions.1.pos.links = s32[288]{0:T(512)S(1)} custom-call(s32[3]{0:T(128)S(1)} %pad_add_fusion.ids, s32[256]{0:T(256)S(1)} %copy-done.1, s32[2048]{0:T(1024)S(1)} %reshape.22.table), custom_call_target="tpu_custom_call" | custom-call | tf_op jit(solution)/shard_map/positions/pallas_call | solution.py:508
  45.7 3.7 %first.1 = (f32[12,16,128]{2,1,0:T(8,128)S(1)}, bf16[12,576,256]{2,1,0:T(8,128)(2,1)S(1)}, f32[256,16,128]{2,1,0:T(8,128)S(1)}) custom-call(s32[288]{0:T(512)S(1)} %positions.1.pos.links, f32[16,16,128]{2,1,0:T(8,128)S(1)} %bitcast.9, f32[16,16,128]{2,1,0:T(8,128)S(1)} %collective-permute-done.rest_1_, f32[16,16,128]{2,1,0:T(8,128)S(1)} %collective-permute-done.1.rest_2_, ...), custom_call_target="tpu_custom_call" | custom-call | tf_op jit(solution)/shard_map/first/pallas_call | solution.py:568
  49.3 1.6 %collective-permute-start.12 = (f32[12,16,128]{2,1,0:T(8,128)S(1)}, f32[12,16,128]{2,1,0:T(8,128)S(1)}, u32[]{:S(2)}, u32[]{:S(2)}) collective-permute-start(f32[12,16,128]{2,1,0:T(8,128)S(1)} %get-tuple-element.36.rest_8_), channel_id=1, source_target_pairs={{0,16},{8,24},{16,0},{24,8},{1,17},{9,25},{17,1},{25,9},{2,18},{10... | collective-permute-start | bytes 294920 | tf_op jit(solution)/shard_map/ppermute | solution.py:534
  50.9 3.0 %collective-permute-start.11 = (f32[12,16,128]{2,1,0:T(8,128)S(1)}, f32[12,16,128]{2,1,0:T(8,128)S(1)}, u32[]{:S(2)}, u32[]{:S(2)}) collective-permute-start(f32[12,16,128]{2,1,0:T(8,128)S(1)} %get-tuple-element.36.rest_8_), channel_id=1, source_target_pairs={{0,8},{8,0},{16,24},{24,16},{1,9},{9,1},{17,25},{25,17},{2,10},{10... | collective-permute-start | bytes 294920 | tf_op jit(solution)/shard_map/ppermute | solution.py:534
  53.9 3.2 %collective-permute-done.12.rest_10_ = f32[12,16,128]{2,1,0:T(8,128)S(1)} collective-permute-done((f32[12,16,128]{2,1,0:T(8,128)S(1)}, f32[12,16,128]{2,1,0:T(8,128)S(1)}, u32[]{:S(2)}, u32[]{:S(2)}) %collective-permute-start.12) | collective-permute-done | bytes 98336 | tf_op jit(solution)/shard_map/ppermute | solution.py:534
  57.8 3.8 %collective-permute-done.13.rest_11_ = f32[12,16,128]{2,1,0:T(8,128)S(1)} collective-permute-done((f32[12,16,128]{2,1,0:T(8,128)S(1)}, f32[12,16,128]{2,1,0:T(8,128)S(1)}, u32[]{:S(2)}, u32[]{:S(2)}) %collective-permute-start.13) | collective-permute-done | bytes 98336 | tf_op jit(solution)/shard_map/ppermute | solution.py:534
  62.2 2.2 %more.1 = (f32[4,16,128]{2,1,0:T(8,128)S(1)}, bf16[4,576,256]{2,1,0:T(8,128)(2,1)S(1)}) custom-call(s32[288]{0:T(512)S(1)} %positions.1.pos.links, f32[256,16,128]{2,1,0:T(8,128)S(1)} %get-tuple-element.37.dup, f32[2,64,1152]{2,1,0:T(8,128)} %collective-permute-done.18.rest_0_, f32[2,64,1152]{2,1,0:T(8,128)} %collective-permute-done.19.rest_1_), custom_call_target="tpu_custom_call" | custom-call | tf_op jit(solution)/shard_map/more/pallas_call | solution.py:586
  64.3 1.8 %collective-permute-start.21 = (f32[4,16,128]{2,1,0:T(8,128)S(1)}, f32[4,16,128]{2,1,0:T(8,128)S(1)}, u32[]{:S(2)}, u32[]{:S(2)}) collective-permute-start(f32[4,16,128]{2,1,0:T(8,128)S(1)} %get-tuple-element.38.rest_16_), channel_id=1, source_target_pairs={{0,16},{8,24},{16,0},{24,8},{1,17},{9,25},{17,1},{25,9},{2,18},{10... | collective-permute-start | bytes 98312 | tf_op jit(solution)/shard_map/ppermute | solution.py:534
  66.1 1.8 %collective-permute-start.20 = (f32[4,16,128]{2,1,0:T(8,128)S(1)}, f32[4,16,128]{2,1,0:T(8,128)S(1)}, u32[]{:S(2)}, u32[]{:S(2)}) collective-permute-start(f32[4,16,128]{2,1,0:T(8,128)S(1)} %get-tuple-element.38.rest_16_), channel_id=1, source_target_pairs={{0,8},{8,0},{16,24},{24,16},{1,9},{9,1},{17,25},{25,17},{2,10},{10... | collective-permute-start | bytes 98312 | tf_op jit(solution)/shard_map/ppermute | solution.py:534
  67.9 1.7 %collective-permute-done.21.rest_18_ = f32[4,16,128]{2,1,0:T(8,128)S(1)} collective-permute-done((f32[4,16,128]{2,1,0:T(8,128)S(1)}, f32[4,16,128]{2,1,0:T(8,128)S(1)}, u32[]{:S(2)}, u32[]{:S(2)}) %collective-permute-start.21) | collective-permute-done | bytes 32800 | tf_op jit(solution)/shard_map/ppermute | solution.py:534
  70.5 3.0 %collective-permute-done.22.rest_19_ = f32[4,16,128]{2,1,0:T(8,128)S(1)} collective-permute-done((f32[4,16,128]{2,1,0:T(8,128)S(1)}, f32[4,16,128]{2,1,0:T(8,128)S(1)}, u32[]{:S(2)}, u32[]{:S(2)}) %collective-permute-start.22) | collective-permute-done | bytes 32800 | tf_op jit(solution)/shard_map/ppermute | solution.py:534
  74.7 2.5 %second.1 = (f32[16,16,128]{2,1,0:T(8,128)S(1)}, f32[128,16,128]{2,1,0:T(8,128)S(1)}, f32[16,128]{1,0:T(8,128)S(1)}, f32[2,4,16,128]{3,2,1,0:T(8,128)S(1)}, f32[...) custom-call(s32[288]{0:T(512)S(1)} %positions.1.pos.links, ...), custom_call_target="tpu_custom_call" | custom-call | tf_op jit(solution)/shard_map/second/pallas_call | solution.py:603
  77.2 1.4 %collective-permute-start.28 = (f32[16,16,128]{2,1,0:T(8,128)S(1)}, f32[16,16,128]{2,1,0:T(8,128)S(1)}, u32[]{:S(2)}, u32[]{:S(2)}) collective-permute-start(f32[16,16,128]{2,1,0:T(8,128)S(1)} %get-tuple-element.48.rest_8_), channel_id=1, source_target_pairs={{0,16},{8,24},{16,0},{24,8},{1,17},{9,25},{17,1},{25,9},{2,18},{10... | collective-permute-start | bytes 393224 | tf_op jit(solution)/shard_map/ppermute | solution.py:534
  78.6 1.8 %collective-permute-start.27 = (f32[16,16,128]{2,1,0:T(8,128)S(1)}, f32[16,16,128]{2,1,0:T(8,128)S(1)}, u32[]{:S(2)}, u32[]{:S(2)}) collective-permute-start(f32[16,16,128]{2,1,0:T(8,128)S(1)} %get-tuple-element.48.rest_8_), channel_id=1, source_target_pairs={{0,8},{8,0},{16,24},{24,16},{1,9},{9,1},{17,25},{25,17},{2,10},{10... | collective-permute-start | bytes 393224 | tf_op jit(solution)/shard_map/ppermute | solution.py:534
  80.4 6.2 %collective-permute-done.28.rest_10_ = f32[16,16,128]{2,1,0:T(8,128)S(1)} collective-permute-done((f32[16,16,128]{2,1,0:T(8,128)S(1)}, f32[16,16,128]{2,1,0:T(8,128)S(1)}, u32[]{:S(2)}, u32[]{:S(2)}) %collective-permute-start.28) | collective-permute-done | bytes 131104 | tf_op jit(solution)/shard_map/ppermute | solution.py:534
  87.7 1.6 %collective-permute-start.35 = (f32[2,4,16,128]{3,2,1,0:T(8,128)S(1)}, f32[2,4,16,128]{3,2,1,0:T(8,128)S(1)}, u32[]{:S(2)}, u32[]{:S(2)}) collective-permute-start(f32[2,4,16,128]{3,2,1,0:T(8,128)S(1)} %get-tuple-element.46), channel_id=1, source_target_pairs={{0,2},{1,3},{2,0},{3,1},{4,6},{5,7},{6,4},{7,5},{8,10},{9,11},{10,... | collective-permute-start | bytes 196616 | tf_op jit(solution)/shard_map/ppermute | solution.py:613
  89.3 1.6 %collective-permute-done.34.rest_1_ = f32[2,4,16,128]{3,2,1,0:T(8,128)S(1)} collective-permute-done((f32[2,4,16,128]{3,2,1,0:T(8,128)S(1)}, f32[2,4,16,128]{3,2,1,0:T(8,128)S(1)}, u32[]{:S(2)}, u32[]{:S(2)}) %collective-permute-start.34) | collective-permute-done | bytes 65568 | tf_op jit(solution)/shard_map/ppermute | solution.py:613
  92.0 2.1 %collective-permute-start.36 = (f32[2,4,16,128]{3,2,1,0:T(8,128)S(1)}, f32[2,4,16,128]{3,2,1,0:T(8,128)S(1)}, u32[]{:S(2)}, u32[]{:S(2)}) collective-permute-start(f32[2,4,16,128]{3,2,1,0:T(8,128)S(1)} %get-tuple-element.47), channel_id=1, source_target_pairs={{0,3},{1,2},{2,1},{3,0},{4,7},{5,6},{6,5},{7,4},{8,11},{9,10},{10,... | collective-permute-start | bytes 196616 | tf_op jit(solution)/shard_map/ppermute | solution.py:613
  94.1 3.3 %collective-permute-done.36.rest_3_ = f32[2,4,16,128]{3,2,1,0:T(8,128)S(1)} collective-permute-done((f32[2,4,16,128]{3,2,1,0:T(8,128)S(1)}, f32[2,4,16,128]{3,2,1,0:T(8,128)S(1)}, u32[]{:S(2)}, u32[]{:S(2)}) %collective-permute-start.36) | collective-permute-done | bytes 65568 | tf_op jit(solution)/shard_map/ppermute | solution.py:613
  97.4 2.5 %third.1 = f32[32,2,128]{2,1,0:T(2,128)S(1)} custom-call(s32[288]{0:T(512)S(1)} %positions.1.pos.links, f32[128,16,128]{2,1,0:T(8,128)S(1)} %get-tuple-element.41.basis, f32[16,128]{1,0:T(8,128)S(1)} %get-tuple-element.42.coeffs, f32[16,16,128]{2,1,0:T(8,128)S(1)} %bitcast.11, f32[16,16,128]{2,1,0:T(8,128)S(1)} %collective-permute-done.rest_1_, ...), custom_call_target="tpu_custom_call" | custom-call | tf_op jit(solution)/shard_map/third/pallas_call | solution.py:620
  99.9 11.3 %all_to_all.10.info = f32[32,2,128]{2,1,0:T(2,128)S(1)} all-to-all(f32[32,2,128]{2,1,0:T(2,128)S(1)} %third.1), channel_id=1, replica_groups=mesh['z'=4,'core'=2,'sub'=4] {'z','core','sub'}, dimensions={0} | all-to-all | bytes 65536 | tf_op jit(solution)/shard_map/all_to_all | solution.py:631
  (65 shorter events, 14.3 us)
Async XLA Ops:
  1.4 35.5 %collective-permute-start.9 = (f32[2,64,1152]{2,1,0:T(8,128)S(1)}, f32[2,64,1152]{2,1,0:T(8,128)S(1)}, u32[]{:S(2)}, u32[]{:S(2)}) collective-permute-start(f32[2,64,1152]{2,1,0:T(8,128)S(1)} %get-tuple-element.34.rest_8_), channel_id=1, source_target_pairs={{0,2},{1,3},{2,0},{3,1},{4,6},{5,7},{6,4},{7,5},{8,10},{9,11},{10,... | collective-permute-start | bytes 1769480 | tf_op jit(solution)/shard_map/ppermute | solution.py:504
  4.5 32.5 %collective-permute-start.8 = (f32[2,64,1152]{2,1,0:T(8,128)S(1)}, f32[2,64,1152]{2,1,0:T(8,128)S(1)}, u32[]{:S(2)}, u32[]{:S(2)}) collective-permute-start(f32[2,64,1152]{2,1,0:T(8,128)S(1)} %get-tuple-element.35.rest_9_), channel_id=1, source_target_pairs={{0,1},{1,0},{2,3},{3,2},{4,5},{5,4},{6,7},{7,6},{8,9},{9,8},{10,11... | collective-permute-start | bytes 1769480 | tf_op jit(solution)/shard_map/ppermute | solution.py:503
  7.7 13.0 %all-to-all-start = ((f32[4,4,16,128]{3,2,1,0:T(8,128)}), f32[4,4,16,128]{3,2,1,0:T(8,128)S(1)}, u32[]{:S(2)}, u32[]{:S(2)}) async-start(f32[4,4,16,128]{3,2,1,0:T(8,128)} %get-tuple-element.33), calls=%async_computation | async-start | bytes 262144 | tf_op jit(solution)/shard_map/all_to_all | solution.py:525
  21.3 8.0 %collective-permute-start.1 = (f32[16,16,128]{2,1,0:T(8,128)S(1)}, f32[16,16,128]{2,1,0:T(8,128)S(1)}, u32[]{:S(2)}, u32[]{:S(2)}) collective-permute-start(f32[16,16,128]{2,1,0:T(8,128)S(1)} %bitcast.6), channel_id=1, source_target_pairs={{0,16},{8,24},{16,0},{24,8},{1,17},{9,25},{17,1},{25,9},{2,18},{10... | collective-permute-start | bytes 393224 | tf_op jit(solution)/shard_map/ppermute | solution.py:534
  23.9 6.0 %collective-permute-start = (f32[16,16,128]{2,1,0:T(8,128)S(1)}, f32[16,16,128]{2,1,0:T(8,128)S(1)}, u32[]{:S(2)}, u32[]{:S(2)}) collective-permute-start(f32[16,16,128]{2,1,0:T(8,128)S(1)} %bitcast.7), channel_id=1, source_target_pairs={{0,8},{8,0},{16,24},{24,16},{1,9},{9,1},{17,25},{25,17},{2,10},{10... | collective-permute-start | bytes 393224 | tf_op jit(solution)/shard_map/ppermute | solution.py:534
  25.5 6.5 %collective-permute-start.3 = (f32[16,16,128]{2,1,0:T(8,128)S(1)}, f32[16,16,128]{2,1,0:T(8,128)S(1)}, u32[]{:S(2)}, u32[]{:S(2)}) collective-permute-start(f32[16,16,128]{2,1,0:T(8,128)S(1)} %bitcast.8), channel_id=1, source_target_pairs={{0,4},{4,0},{1,5},{5,1},{2,6},{6,2},{3,7},{7,3},{8,12},{12,8},{9,1... | collective-permute-start | bytes 393224 | tf_op jit(solution)/shard_map/ppermute | solution.py:544
  29.2 16.0 %collective-permute-start.10 = (f32[2,64,1152]{2,1,0:T(8,128)S(1)}, f32[2,64,1152]{2,1,0:T(8,128)}, u32[]{:S(2)}, u32[]{:S(2)}) collective-permute-start(f32[2,64,1152]{2,1,0:T(8,128)S(1)} %get-tuple-element.35.rest_9_), channel_id=1, source_target_pairs={{0,2},{1,3},{2,0},{3,1},{4,6},{5,7},{6,4},{7,5},{8,10},{9,11},{10,... | collective-permute-start | bytes 1769480 | tf_op jit(solution)/shard_map/ppermute | solution.py:506
  29.9 15.7 %collective-permute-start.7 = (f32[2,64,1152]{2,1,0:T(8,128)S(1)}, f32[2,64,1152]{2,1,0:T(8,128)}, u32[]{:S(2)}, u32[]{:S(2)}) collective-permute-start(f32[2,64,1152]{2,1,0:T(8,128)S(1)} %get-tuple-element.34.rest_8_), channel_id=1, source_target_pairs={{0,1},{1,0},{2,3},{3,2},{4,5},{5,4},{6,7},{7,6},{8,9},{9,8},{10,11... | collective-permute-start | bytes 1769480 | tf_op jit(solution)/shard_map/ppermute | solution.py:505
  31.9 5.0 %collective-permute-start.2 = (f32[16,16,128]{2,1,0:T(8,128)S(1)}, f32[16,16,128]{2,1,0:T(8,128)S(1)}, u32[]{:S(2)}, u32[]{:S(2)}) collective-permute-start(f32[16,16,128]{2,1,0:T(8,128)S(1)} %collective-permute-done.1.rest_2_), channel_id=1, source_target_pairs={{0,8},{8,0},{16,24},{24,16},{1,9},{9,1},{17,25},{25,17},{2,10},{10... | collective-permute-start | bytes 393224 | tf_op jit(solution)/shard_map/ppermute | solution.py:534
  36.9 24.7 %collective-permute-start.18 = (f32[2,64,1152]{2,1,0:T(8,128)S(1)}, f32[2,64,1152]{2,1,0:T(8,128)}, u32[]{:S(2)}, u32[]{:S(2)}) collective-permute-start(f32[2,64,1152]{2,1,0:T(8,128)S(1)} %collective-permute-done.9.rest_12_), channel_id=1, source_target_pairs={{0,1},{1,0},{2,3},{3,2},{4,5},{5,4},{6,7},{7,6},{8,9},{9,8},{10,11... | collective-permute-start | bytes 1769480 | tf_op jit(solution)/shard_map/ppermute | solution.py:548
  37.0 25.2 %collective-permute-start.19 = (f32[2,64,1152]{2,1,0:T(8,128)S(1)}, f32[2,64,1152]{2,1,0:T(8,128)}, u32[]{:S(2)}, u32[]{:S(2)}) collective-permute-start(f32[2,64,1152]{2,1,0:T(8,128)S(1)} %collective-permute-done.8.rest_11_), channel_id=1, source_target_pairs={{0,2},{1,3},{2,0},{3,1},{4,6},{5,7},{6,4},{7,5},{8,10},{9,11},{10,... | collective-permute-start | bytes 1769480 | tf_op jit(solution)/shard_map/ppermute | solution.py:549
  39.6 5.6 %collective-permute-start.6 = (f32[16,16,128]{2,1,0:T(8,128)S(1)}, f32[16,16,128]{2,1,0:T(8,128)S(1)}, u32[]{:S(2)}, u32[]{:S(2)}) collective-permute-start(f32[16,16,128]{2,1,0:T(8,128)S(1)} %collective-permute-done.2.rest_3_), channel_id=1, source_target_pairs={{0,4},{4,0},{1,5},{5,1},{2,6},{6,2},{3,7},{7,3},{8,12},{12,8},{9,1... | collective-permute-start | bytes 393224 | tf_op jit(solution)/shard_map/ppermute | solution.py:544
  49.3 7.7 %collective-permute-start.12 = (f32[12,16,128]{2,1,0:T(8,128)S(1)}, f32[12,16,128]{2,1,0:T(8,128)S(1)}, u32[]{:S(2)}, u32[]{:S(2)}) collective-permute-start(f32[12,16,128]{2,1,0:T(8,128)S(1)} %get-tuple-element.36.rest_8_), channel_id=1, source_target_pairs={{0,16},{8,24},{16,0},{24,8},{1,17},{9,25},{17,1},{25,9},{2,18},{10... | collective-permute-start | bytes 294920 | tf_op jit(solution)/shard_map/ppermute | solution.py:534
  50.9 6.4 %collective-permute-start.11 = (f32[12,16,128]{2,1,0:T(8,128)S(1)}, f32[12,16,128]{2,1,0:T(8,128)S(1)}, u32[]{:S(2)}, u32[]{:S(2)}) collective-permute-start(f32[12,16,128]{2,1,0:T(8,128)S(1)} %get-tuple-element.36.rest_8_), channel_id=1, source_target_pairs={{0,8},{8,0},{16,24},{24,16},{1,9},{9,1},{17,25},{25,17},{2,10},{10... | collective-permute-start | bytes 294920 | tf_op jit(solution)/shard_map/ppermute | solution.py:534
  57.0 4.6 %collective-permute-start.13 = (f32[12,16,128]{2,1,0:T(8,128)S(1)}, f32[12,16,128]{2,1,0:T(8,128)S(1)}, u32[]{:S(2)}, u32[]{:S(2)}) collective-permute-start(f32[12,16,128]{2,1,0:T(8,128)S(1)} %collective-permute-done.12.rest_10_), channel_id=1, source_target_pairs={{0,8},{8,0},{16,24},{24,16},{1,9},{9,1},{17,25},{25,17},{2,10},{10... | collective-permute-start | bytes 294920 | tf_op jit(solution)/shard_map/ppermute | solution.py:534
  57.3 8.8 %collective-permute-start.14 = (f32[12,16,128]{2,1,0:T(8,128)S(1)}, f32[12,16,128]{2,1,0:T(8,128)S(1)}, u32[]{:S(2)}, u32[]{:S(2)}) collective-permute-start(f32[12,16,128]{2,1,0:T(8,128)S(1)} %get-tuple-element.36.rest_8_), channel_id=1, source_target_pairs={{0,4},{4,0},{1,5},{5,1},{2,6},{6,2},{3,7},{7,3},{8,12},{12,8},{9,1... | collective-permute-start | bytes 294920 | tf_op jit(solution)/shard_map/ppermute | solution.py:544
  57.3 12.6 %collective-permute-start.15 = (f32[12,16,128]{2,1,0:T(8,128)S(1)}, f32[12,16,128]{2,1,0:T(8,128)S(1)}, u32[]{:S(2)}, u32[]{:S(2)}) collective-permute-start(f32[12,16,128]{2,1,0:T(8,128)S(1)} %collective-permute-done.11.rest_9_), channel_id=1, source_target_pairs={{0,4},{4,0},{1,5},{5,1},{2,6},{6,2},{3,7},{7,3},{8,12},{12,8},{9,1... | collective-permute-start | bytes 294920 | tf_op jit(solution)/shard_map/ppermute | solution.py:544
  61.6 8.3 %collective-permute-start.16 = (f32[12,16,128]{2,1,0:T(8,128)S(1)}, f32[12,16,128]{2,1,0:T(8,128)S(1)}, u32[]{:S(2)}, u32[]{:S(2)}) collective-permute-start(f32[12,16,128]{2,1,0:T(8,128)S(1)} %collective-permute-done.12.rest_10_), channel_id=1, source_target_pairs={{0,4},{4,0},{1,5},{5,1},{2,6},{6,2},{3,7},{7,3},{8,12},{12,8},{9,1... | collective-permute-start | bytes 294920 | tf_op jit(solution)/shard_map/ppermute | solution.py:544
  61.7 11.8 %collective-permute-start.17 = (f32[12,16,128]{2,1,0:T(8,128)S(1)}, f32[12,16,128]{2,1,0:T(8,128)S(1)}, u32[]{:S(2)}, u32[]{:S(2)}) collective-permute-start(f32[12,16,128]{2,1,0:T(8,128)S(1)} %collective-permute-done.13.rest_11_), channel_id=1, source_target_pairs={{0,4},{4,0},{1,5},{5,1},{2,6},{6,2},{3,7},{7,3},{8,12},{12,8},{9,1... | collective-permute-start | bytes 294920 | tf_op jit(solution)/shard_map/ppermute | solution.py:544
  64.3 5.2 %collective-permute-start.21 = (f32[4,16,128]{2,1,0:T(8,128)S(1)}, f32[4,16,128]{2,1,0:T(8,128)S(1)}, u32[]{:S(2)}, u32[]{:S(2)}) collective-permute-start(f32[4,16,128]{2,1,0:T(8,128)S(1)} %get-tuple-element.38.rest_16_), channel_id=1, source_target_pairs={{0,16},{8,24},{16,0},{24,8},{1,17},{9,25},{17,1},{25,9},{2,18},{10... | collective-permute-start | bytes 98312 | tf_op jit(solution)/shard_map/ppermute | solution.py:534
  66.1 4.3 %collective-permute-start.20 = (f32[4,16,128]{2,1,0:T(8,128)S(1)}, f32[4,16,128]{2,1,0:T(8,128)S(1)}, u32[]{:S(2)}, u32[]{:S(2)}) collective-permute-start(f32[4,16,128]{2,1,0:T(8,128)S(1)} %get-tuple-element.38.rest_16_), channel_id=1, source_target_pairs={{0,8},{8,0},{16,24},{24,16},{1,9},{9,1},{17,25},{25,17},{2,10},{10... | collective-permute-start | bytes 98312 | tf_op jit(solution)/shard_map/ppermute | solution.py:534
  69.6 3.9 %collective-permute-start.22 = (f32[4,16,128]{2,1,0:T(8,128)S(1)}, f32[4,16,128]{2,1,0:T(8,128)S(1)}, u32[]{:S(2)}, u32[]{:S(2)}) collective-permute-start(f32[4,16,128]{2,1,0:T(8,128)S(1)} %collective-permute-done.21.rest_18_), channel_id=1, source_target_pairs={{0,8},{8,0},{16,24},{24,16},{1,9},{9,1},{17,25},{25,17},{2,10},{10... | collective-permute-start | bytes 98312 | tf_op jit(solution)/shard_map/ppermute | solution.py:534
  77.2 9.4 %collective-permute-start.28 = (f32[16,16,128]{2,1,0:T(8,128)S(1)}, f32[16,16,128]{2,1,0:T(8,128)S(1)}, u32[]{:S(2)}, u32[]{:S(2)}) collective-permute-start(f32[16,16,128]{2,1,0:T(8,128)S(1)} %get-tuple-element.48.rest_8_), channel_id=1, source_target_pairs={{0,16},{8,24},{16,0},{24,8},{1,17},{9,25},{17,1},{25,9},{2,18},{10... | collective-permute-start | bytes 393224 | tf_op jit(solution)/shard_map/ppermute | solution.py:534
  78.6 12.3 %collective-permute-start.27 = (f32[16,16,128]{2,1,0:T(8,128)S(1)}, f32[16,16,128]{2,1,0:T(8,128)S(1)}, u32[]{:S(2)}, u32[]{:S(2)}) collective-permute-start(f32[16,16,128]{2,1,0:T(8,128)S(1)} %get-tuple-element.48.rest_8_), channel_id=1, source_target_pairs={{0,8},{8,0},{16,24},{24,16},{1,9},{9,1},{17,25},{25,17},{2,10},{10... | collective-permute-start | bytes 393224 | tf_op jit(solution)/shard_map/ppermute | solution.py:534
  86.6 5.4 %collective-permute-start.29 = (f32[16,16,128]{2,1,0:T(8,128)S(1)}, f32[16,16,128]{2,1,0:T(8,128)S(1)}, u32[]{:S(2)}, u32[]{:S(2)}) collective-permute-start(f32[16,16,128]{2,1,0:T(8,128)S(1)} %collective-permute-done.28.rest_10_), channel_id=1, source_target_pairs={{0,8},{8,0},{16,24},{24,16},{1,9},{9,1},{17,25},{25,17},{2,10},{10... | collective-permute-start | bytes 393224 | tf_op jit(solution)/shard_map/ppermute | solution.py:534
  86.6 4.3 %collective-permute-start.34 = (f32[2,4,16,128]{3,2,1,0:T(8,128)S(1)}, f32[2,4,16,128]{3,2,1,0:T(8,128)S(1)}, u32[]{:S(2)}, u32[]{:S(2)}) collective-permute-start(f32[2,4,16,128]{3,2,1,0:T(8,128)S(1)} %get-tuple-element.45), channel_id=1, source_target_pairs={{0,1},{1,0},{2,3},{3,2},{4,5},{5,4},{6,7},{7,6},{8,9},{9,8},{10,11... | collective-permute-start | bytes 196616 | tf_op jit(solution)/shard_map/ppermute | solution.py:613
  87.7 4.3 %collective-permute-start.35 = (f32[2,4,16,128]{3,2,1,0:T(8,128)S(1)}, f32[2,4,16,128]{3,2,1,0:T(8,128)S(1)}, u32[]{:S(2)}, u32[]{:S(2)}) collective-permute-start(f32[2,4,16,128]{3,2,1,0:T(8,128)S(1)} %get-tuple-element.46), channel_id=1, source_target_pairs={{0,2},{1,3},{2,0},{3,1},{4,6},{5,7},{6,4},{7,5},{8,10},{9,11},{10,... | collective-permute-start | bytes 196616 | tf_op jit(solution)/shard_map/ppermute | solution.py:613
  89.3 8.1 %collective-permute-start.30 = (f32[16,16,128]{2,1,0:T(8,128)S(1)}, f32[16,16,128]{2,1,0:T(8,128)S(1)}, u32[]{:S(2)}, u32[]{:S(2)}) collective-permute-start(f32[16,16,128]{2,1,0:T(8,128)S(1)} %get-tuple-element.48.rest_8_), channel_id=1, source_target_pairs={{0,4},{4,0},{1,5},{5,1},{2,6},{6,2},{3,7},{7,3},{8,12},{12,8},{9,1... | collective-permute-start | bytes 393224 | tf_op jit(solution)/shard_map/ppermute | solution.py:544
  90.9 6.5 %collective-permute-start.32 = (f32[16,16,128]{2,1,0:T(8,128)S(1)}, f32[16,16,128]{2,1,0:T(8,128)S(1)}, u32[]{:S(2)}, u32[]{:S(2)}) collective-permute-start(f32[16,16,128]{2,1,0:T(8,128)S(1)} %collective-permute-done.28.rest_10_), channel_id=1, source_target_pairs={{0,4},{4,0},{1,5},{5,1},{2,6},{6,2},{3,7},{7,3},{8,12},{12,8},{9,1... | collective-permute-start | bytes 393224 | tf_op jit(solution)/shard_map/ppermute | solution.py:544
  90.9 6.5 %collective-permute-start.31 = (f32[16,16,128]{2,1,0:T(8,128)S(1)}, f32[16,16,128]{2,1,0:T(8,128)S(1)}, u32[]{:S(2)}, u32[]{:S(2)}) collective-permute-start(f32[16,16,128]{2,1,0:T(8,128)S(1)} %collective-permute-done.27.rest_9_), channel_id=1, source_target_pairs={{0,4},{4,0},{1,5},{5,1},{2,6},{6,2},{3,7},{7,3},{8,12},{12,8},{9,1... | collective-permute-start | bytes 393224 | tf_op jit(solution)/shard_map/ppermute | solution.py:544
  92.0 5.4 %collective-permute-start.33 = (f32[16,16,128]{2,1,0:T(8,128)S(1)}, f32[16,16,128]{2,1,0:T(8,128)S(1)}, u32[]{:S(2)}, u32[]{:S(2)}) collective-permute-start(f32[16,16,128]{2,1,0:T(8,128)S(1)} %collective-permute-done.29.rest_11_), channel_id=1, source_target_pairs={{0,4},{4,0},{1,5},{5,1},{2,6},{6,2},{3,7},{7,3},{8,12},{12,8},{9,1... | collective-permute-start | bytes 393224 | tf_op jit(solution)/shard_map/ppermute | solution.py:544
  92.0 5.4 %collective-permute-start.36 = (f32[2,4,16,128]{3,2,1,0:T(8,128)S(1)}, f32[2,4,16,128]{3,2,1,0:T(8,128)S(1)}, u32[]{:S(2)}, u32[]{:S(2)}) collective-permute-start(f32[2,4,16,128]{3,2,1,0:T(8,128)S(1)} %get-tuple-element.47), channel_id=1, source_target_pairs={{0,3},{1,2},{2,1},{3,0},{4,7},{5,6},{6,5},{7,4},{8,11},{9,10},{10,... | collective-permute-start | bytes 196616 | tf_op jit(solution)/shard_map/ppermute | solution.py:613
  (9 other events, 96.5 us)

commit v9 on v8

--- a/solution.py
+++ b/solution.py
@@ -232,16 +232,13 @@
 def first_kernel(n_field, count, dof, terms, pos, *rest):
     fields, ops, rest = rest[:n_field], rest[n_field : n_field + count], rest[n_field + count :]
     out, split, dup = rest[:3]
-    held, sems = rest[3 : 3 + count], rest[3 + count]
-    copies = start_copies(ops, held, sems)
+    held = ops
 
     def build(block, value, pair, spot, carry):
         spread(dup, spot, value, dof)
         return carry
 
     over_pairs(in_blocks(fields, 1), build, 0)
-    for copy in copies:
-        copy.wait()
 
     def put(pair, values):
         out[pair] = values
@@ -572,10 +569,8 @@
             split_shape(done),
             jax.ShapeDtypeStruct(dup, F32),
         ],
-        in_specs=[SMEM] + [VMEM] * n_field + [ANY] * len(ops),
+        in_specs=[SMEM] + [VMEM] * n_field + [VMEM] * len(ops),
         out_specs=[VMEM] * 3,
-        scratch_shapes=[pltpu.VMEM(op.shape, F32) for op in ops]
-        + [pltpu.SemaphoreType.DMA((len(ops),))],
         compiler_params=PARAMS,
         name="first",
     )(positions, *b_parts, *ops)

time: 113 us -> 112 us (level)
  transfers between devices with their start and end apart: 38 -> 38, of which waited for: 14 -> 14; matrix products, arithmetic and copies ran while one was open for 2% -> 2% of each run, Pallas kernels for 9% -> 8%
where the time goes in v9:
time: 112 us
  waiting for transfers between devices  43.9 us (39%)
  starting transfers between devices  36 us (32%)
  Pallas kernels  16.9 us (15%)
  blocking collectives  11.3 us (10%)
  local copies, waits for them, and re-layouts  3.31 us (3%)
    ppermute x12, waiting for transfers between devices, step_z(): return lax.ppermute(own, 'z', [(z, z ^ offset) for z in range(nz)])  26.5 us
    ppermute x12, starting transfers between devices, step_z(): return lax.ppermute(own, 'z', [(z, z ^ offset) for z in range(nz)])  16.8 us
    all_to_all x1, blocking collectives, per_device(): sums = lax.all_to_all(sums, axes, split_axis=0, concat_axis=0, tiled=True)  11.3 us
    all_to_all x1, waiting for transfers between devices, per_device(): lax.all_to_all(turned, 'sub', split_axis=0, concat_axis=0, tiled=True)  9.62 us
    ppermute x3, starting transfers between devices, per_device(): lax.ppermute(shares[k], 'sub', hops_to[k])  4.84 us
    ppermute x3, waiting for transfers between devices, per_device(): lax.ppermute(shares[k], 'sub', hops_to[k])  4.83 us
    pallas_call x1, Pallas kernels, per_device(): pl.pallas_call(functools.partial(position_kernel, (per_dev, n_sub, nz, ho...  3.51 us
    all_to_all x1, starting transfers between devices, per_device(): lax.all_to_all(turned, 'sub', split_axis=0, concat_axis=0, tiled=True)  3.33 us
  transfers between devices with their start and end apart: 38, of which 14 were waited for; matrix products, arithmetic and copies ran while one was open for 2% of the time, Pallas kernels for 8%

profile of v9, /device:TPU:0, one launch (start us, length us, event | category | flops | bytes accessed | tf_op | source)
XLA Modules:
  0.0 111.6 jit_solution(11021118474797234879)
XLA Ops:
  0.0 1.4 %pack.1 = (f32[2,64,1152]{2,1,0:T(8,128)S(1)}, f32[2,64,1152]{2,1,0:T(8,128)S(1)}) custom-call(f32[8,64,576]{2,1,0:T(8,128)} %op.1), custom_call_target="tpu_custom_call" | custom-call | tf_op jit(solution)/shard_map/pack/pallas_call | solution.py:480
  1.4 3.1 %collective-permute-start.9 = (f32[2,64,1152]{2,1,0:T(8,128)S(1)}, f32[2,64,1152]{2,1,0:T(8,128)S(1)}, u32[]{:S(2)}, u32[]{:S(2)}) collective-permute-start(f32[2,64,1152]{2,1,0:T(8,128)S(1)} %get-tuple-element.34.rest_8_), channel_id=1, source_target_pairs={{0,2},{1,3},{2,0},{3,1},{4,6},{5,7},{6,4},{7,5},{8,10},{9,11},{10,... | collective-permute-start | bytes 1769480 | tf_op jit(solution)/shard_map/ppermute | solution.py:501
  4.5 1.5 %collective-permute-start.8 = (f32[2,64,1152]{2,1,0:T(8,128)S(1)}, f32[2,64,1152]{2,1,0:T(8,128)S(1)}, u32[]{:S(2)}, u32[]{:S(2)}) collective-permute-start(f32[2,64,1152]{2,1,0:T(8,128)S(1)} %get-tuple-element.35.rest_9_), channel_id=1, source_target_pairs={{0,1},{1,0},{2,3},{3,2},{4,5},{5,4},{6,7},{7,6},{8,9},{9,8},{10,11... | collective-permute-start | bytes 1769480 | tf_op jit(solution)/shard_map/ppermute | solution.py:500
  7.7 3.3 %all-to-all-start = ((f32[4,4,16,128]{3,2,1,0:T(8,128)}), f32[4,4,16,128]{3,2,1,0:T(8,128)S(1)}, u32[]{:S(2)}, u32[]{:S(2)}) async-start(f32[4,4,16,128]{3,2,1,0:T(8,128)} %get-tuple-element.33), calls=%async_computation | async-start | bytes 262144 | tf_op jit(solution)/shard_map/all_to_all | solution.py:522
  11.1 9.6 %all-to-all-done = f32[4,4,16,128]{3,2,1,0:T(8,128)S(1)} async-done(((f32[4,4,16,128]{3,2,1,0:T(8,128)}), f32[4,4,16,128]{3,2,1,0:T(8,128)S(1)}, u32[]{:S(2)}, u32[]{:S(2)}) %all-to-all-start) | async-done | bytes 131104 | tf_op jit(solution)/shard_map/all_to_all | solution.py:522
  21.3 2.7 %collective-permute-start.1 = (f32[16,16,128]{2,1,0:T(8,128)S(1)}, f32[16,16,128]{2,1,0:T(8,128)S(1)}, u32[]{:S(2)}, u32[]{:S(2)}) collective-permute-start(f32[16,16,128]{2,1,0:T(8,128)S(1)} %bitcast.6), channel_id=1, source_target_pairs={{0,16},{8,24},{16,0},{24,8},{1,17},{9,25},{17,1},{25,9},{2,18},{10... | collective-permute-start | bytes 393224 | tf_op jit(solution)/shard_map/ppermute | solution.py:531
  23.9 1.6 %collective-permute-start = (f32[16,16,128]{2,1,0:T(8,128)S(1)}, f32[16,16,128]{2,1,0:T(8,128)S(1)}, u32[]{:S(2)}, u32[]{:S(2)}) collective-permute-start(f32[16,16,128]{2,1,0:T(8,128)S(1)} %bitcast.7), channel_id=1, source_target_pairs={{0,8},{8,0},{16,24},{24,16},{1,9},{9,1},{17,25},{25,17},{2,10},{10... | collective-permute-start | bytes 393224 | tf_op jit(solution)/shard_map/ppermute | solution.py:531
  25.5 3.7 %collective-permute-done.1.rest_2_ = f32[16,16,128]{2,1,0:T(8,128)S(1)} collective-permute-done((f32[16,16,128]{2,1,0:T(8,128)S(1)}, f32[16,16,128]{2,1,0:T(8,128)S(1)}, u32[]{:S(2)}, u32[]{:S(2)}) %collective-permute-start.1) | collective-permute-done | bytes 131104 | tf_op jit(solution)/shard_map/ppermute | solution.py:531
  29.9 2.0 %collective-permute-start.7 = (f32[2,64,1152]{2,1,0:T(8,128)S(1)}, f32[2,64,1152]{2,1,0:T(8,128)}, u32[]{:S(2)}, u32[]{:S(2)}) collective-permute-start(f32[2,64,1152]{2,1,0:T(8,128)S(1)} %get-tuple-element.34.rest_8_), channel_id=1, source_target_pairs={{0,1},{1,0},{2,3},{3,2},{4,5},{5,4},{6,7},{7,6},{8,9},{9,8},{10,11... | collective-permute-start | bytes 1769480 | tf_op jit(solution)/shard_map/ppermute | solution.py:502
  32.5 4.4 %collective-permute-done.2.rest_3_ = f32[16,16,128]{2,1,0:T(8,128)S(1)} collective-permute-done((f32[16,16,128]{2,1,0:T(8,128)S(1)}, f32[16,16,128]{2,1,0:T(8,128)S(1)}, u32[]{:S(2)}, u32[]{:S(2)}) %collective-permute-start.2) | collective-permute-done | bytes 131104 | tf_op jit(solution)/shard_map/ppermute | solution.py:531
  37.0 1.3 %collective-permute-start.19 = (f32[2,64,1152]{2,1,0:T(8,128)S(1)}, f32[2,64,1152]{2,1,0:T(8,128)}, u32[]{:S(2)}, u32[]{:S(2)}) collective-permute-start(f32[2,64,1152]{2,1,0:T(8,128)S(1)} %collective-permute-done.8.rest_11_), channel_id=1, source_target_pairs={{0,2},{1,3},{2,0},{3,1},{4,6},{5,7},{6,4},{7,5},{8,10},{9,11},{10,... | collective-permute-start | bytes 1769480 | tf_op jit(solution)/shard_map/ppermute | solution.py:546
  41.6 3.5 %positions.1.pos.links = s32[288]{0:T(512)S(1)} custom-call(s32[3]{0:T(128)S(1)} %pad_add_fusion.ids, s32[256]{0:T(256)S(1)} %copy-done.1, s32[2048]{0:T(1024)S(1)} %reshape.22.table), custom_call_target="tpu_custom_call" | custom-call | tf_op jit(solution)/shard_map/positions/pallas_call | solution.py:505
  45.7 2.9 %first.1 = (f32[12,16,128]{2,1,0:T(8,128)S(1)}, bf16[12,576,256]{2,1,0:T(8,128)(2,1)S(1)}, f32[256,16,128]{2,1,0:T(8,128)S(1)}) custom-call(s32[288]{0:T(512)S(1)} %positions.1.pos.links, f32[16,16,128]{2,1,0:T(8,128)S(1)} %bitcast.9, f32[16,16,128]{2,1,0:T(8,128)S(1)} %collective-permute-done.rest_1_, f32[16,16,128]{2,1,0:T(8,128)S(1)} %collective-permute-done.1.rest_2_, ...), custom_call_target="tpu_custom_call" | custom-call | tf_op jit(solution)/shard_map/first/pallas_call | solution.py:565
  48.6 1.6 %collective-permute-start.12 = (f32[12,16,128]{2,1,0:T(8,128)S(1)}, f32[12,16,128]{2,1,0:T(8,128)S(1)}, u32[]{:S(2)}, u32[]{:S(2)}) collective-permute-start(f32[12,16,128]{2,1,0:T(8,128)S(1)} %get-tuple-element.36.rest_8_), channel_id=1, source_target_pairs={{0,16},{8,24},{16,0},{24,8},{1,17},{9,25},{17,1},{25,9},{2,18},{10... | collective-permute-start | bytes 294920 | tf_op jit(solution)/shard_map/ppermute | solution.py:531
  50.2 3.0 %collective-permute-start.11 = (f32[12,16,128]{2,1,0:T(8,128)S(1)}, f32[12,16,128]{2,1,0:T(8,128)S(1)}, u32[]{:S(2)}, u32[]{:S(2)}) collective-permute-start(f32[12,16,128]{2,1,0:T(8,128)S(1)} %get-tuple-element.36.rest_8_), channel_id=1, source_target_pairs={{0,8},{8,0},{16,24},{24,16},{1,9},{9,1},{17,25},{25,17},{2,10},{10... | collective-permute-start | bytes 294920 | tf_op jit(solution)/shard_map/ppermute | solution.py:531
  53.2 3.2 %collective-permute-done.12.rest_10_ = f32[12,16,128]{2,1,0:T(8,128)S(1)} collective-permute-done((f32[12,16,128]{2,1,0:T(8,128)S(1)}, f32[12,16,128]{2,1,0:T(8,128)S(1)}, u32[]{:S(2)}, u32[]{:S(2)}) %collective-permute-start.12) | collective-permute-done | bytes 98336 | tf_op jit(solution)/shard_map/ppermute | solution.py:531
  57.1 3.8 %collective-permute-done.13.rest_11_ = f32[12,16,128]{2,1,0:T(8,128)S(1)} collective-permute-done((f32[12,16,128]{2,1,0:T(8,128)S(1)}, f32[12,16,128]{2,1,0:T(8,128)S(1)}, u32[]{:S(2)}, u32[]{:S(2)}) %collective-permute-start.13) | collective-permute-done | bytes 98336 | tf_op jit(solution)/shard_map/ppermute | solution.py:531
  61.4 2.2 %more.1 = (f32[4,16,128]{2,1,0:T(8,128)S(1)}, bf16[4,576,256]{2,1,0:T(8,128)(2,1)S(1)}) custom-call(s32[288]{0:T(512)S(1)} %positions.1.pos.links, f32[256,16,128]{2,1,0:T(8,128)S(1)} %get-tuple-element.37.dup, f32[2,64,1152]{2,1,0:T(8,128)} %collective-permute-done.18.rest_0_, f32[2,64,1152]{2,1,0:T(8,128)} %collective-permute-done.19.rest_1_), custom_call_target="tpu_custom_call" | custom-call | tf_op jit(solution)/shard_map/more/pallas_call | solution.py:581
  63.6 1.8 %collective-permute-start.21 = (f32[4,16,128]{2,1,0:T(8,128)S(1)}, f32[4,16,128]{2,1,0:T(8,128)S(1)}, u32[]{:S(2)}, u32[]{:S(2)}) collective-permute-start(f32[4,16,128]{2,1,0:T(8,128)S(1)} %get-tuple-element.38.rest_16_), channel_id=1, source_target_pairs={{0,16},{8,24},{16,0},{24,8},{1,17},{9,25},{17,1},{25,9},{2,18},{10... | collective-permute-start | bytes 98312 | tf_op jit(solution)/shard_map/ppermute | solution.py:531
  65.4 1.8 %collective-permute-start.20 = (f32[4,16,128]{2,1,0:T(8,128)S(1)}, f32[4,16,128]{2,1,0:T(8,128)S(1)}, u32[]{:S(2)}, u32[]{:S(2)}) collective-permute-start(f32[4,16,128]{2,1,0:T(8,128)S(1)} %get-tuple-element.38.rest_16_), channel_id=1, source_target_pairs={{0,8},{8,0},{16,24},{24,16},{1,9},{9,1},{17,25},{25,17},{2,10},{10... | collective-permute-start | bytes 98312 | tf_op jit(solution)/shard_map/ppermute | solution.py:531
  67.2 1.7 %collective-permute-done.21.rest_18_ = f32[4,16,128]{2,1,0:T(8,128)S(1)} collective-permute-done((f32[4,16,128]{2,1,0:T(8,128)S(1)}, f32[4,16,128]{2,1,0:T(8,128)S(1)}, u32[]{:S(2)}, u32[]{:S(2)}) %collective-permute-start.21) | collective-permute-done | bytes 32800 | tf_op jit(solution)/shard_map/ppermute | solution.py:531
  69.8 3.0 %collective-permute-done.22.rest_19_ = f32[4,16,128]{2,1,0:T(8,128)S(1)} collective-permute-done((f32[4,16,128]{2,1,0:T(8,128)S(1)}, f32[4,16,128]{2,1,0:T(8,128)S(1)}, u32[]{:S(2)}, u32[]{:S(2)}) %collective-permute-start.22) | collective-permute-done | bytes 32800 | tf_op jit(solution)/shard_map/ppermute | solution.py:531
  74.0 2.5 %second.1 = (f32[16,16,128]{2,1,0:T(8,128)S(1)}, f32[128,16,128]{2,1,0:T(8,128)S(1)}, f32[16,128]{1,0:T(8,128)S(1)}, f32[2,4,16,128]{3,2,1,0:T(8,128)S(1)}, f32[...) custom-call(s32[288]{0:T(512)S(1)} %positions.1.pos.links, ...), custom_call_target="tpu_custom_call" | custom-call | tf_op jit(solution)/shard_map/second/pallas_call | solution.py:598
  76.5 1.4 %collective-permute-start.28 = (f32[16,16,128]{2,1,0:T(8,128)S(1)}, f32[16,16,128]{2,1,0:T(8,128)S(1)}, u32[]{:S(2)}, u32[]{:S(2)}) collective-permute-start(f32[16,16,128]{2,1,0:T(8,128)S(1)} %get-tuple-element.48.rest_8_), channel_id=1, source_target_pairs={{0,16},{8,24},{16,0},{24,8},{1,17},{9,25},{17,1},{25,9},{2,18},{10... | collective-permute-start | bytes 393224 | tf_op jit(solution)/shard_map/ppermute | solution.py:531
  77.9 1.8 %collective-permute-start.27 = (f32[16,16,128]{2,1,0:T(8,128)S(1)}, f32[16,16,128]{2,1,0:T(8,128)S(1)}, u32[]{:S(2)}, u32[]{:S(2)}) collective-permute-start(f32[16,16,128]{2,1,0:T(8,128)S(1)} %get-tuple-element.48.rest_8_), channel_id=1, source_target_pairs={{0,8},{8,0},{16,24},{24,16},{1,9},{9,1},{17,25},{25,17},{2,10},{10... | collective-permute-start | bytes 393224 | tf_op jit(solution)/shard_map/ppermute | solution.py:531
  79.7 6.2 %collective-permute-done.28.rest_10_ = f32[16,16,128]{2,1,0:T(8,128)S(1)} collective-permute-done((f32[16,16,128]{2,1,0:T(8,128)S(1)}, f32[16,16,128]{2,1,0:T(8,128)S(1)}, u32[]{:S(2)}, u32[]{:S(2)}) %collective-permute-start.28) | collective-permute-done | bytes 131104 | tf_op jit(solution)/shard_map/ppermute | solution.py:531
  87.0 1.6 %collective-permute-start.35 = (f32[2,4,16,128]{3,2,1,0:T(8,128)S(1)}, f32[2,4,16,128]{3,2,1,0:T(8,128)S(1)}, u32[]{:S(2)}, u32[]{:S(2)}) collective-permute-start(f32[2,4,16,128]{3,2,1,0:T(8,128)S(1)} %get-tuple-element.46), channel_id=1, source_target_pairs={{0,2},{1,3},{2,0},{3,1},{4,6},{5,7},{6,4},{7,5},{8,10},{9,11},{10,... | collective-permute-start | bytes 196616 | tf_op jit(solution)/shard_map/ppermute | solution.py:608
  88.6 1.6 %collective-permute-done.34.rest_1_ = f32[2,4,16,128]{3,2,1,0:T(8,128)S(1)} collective-permute-done((f32[2,4,16,128]{3,2,1,0:T(8,128)S(1)}, f32[2,4,16,128]{3,2,1,0:T(8,128)S(1)}, u32[]{:S(2)}, u32[]{:S(2)}) %collective-permute-start.34) | collective-permute-done | bytes 65568 | tf_op jit(solution)/shard_map/ppermute | solution.py:608
  91.3 2.1 %collective-permute-start.36 = (f32[2,4,16,128]{3,2,1,0:T(8,128)S(1)}, f32[2,4,16,128]{3,2,1,0:T(8,128)S(1)}, u32[]{:S(2)}, u32[]{:S(2)}) collective-permute-start(f32[2,4,16,128]{3,2,1,0:T(8,128)S(1)} %get-tuple-element.47), channel_id=1, source_target_pairs={{0,3},{1,2},{2,1},{3,0},{4,7},{5,6},{6,5},{7,4},{8,11},{9,10},{10,... | collective-permute-start | bytes 196616 | tf_op jit(solution)/shard_map/ppermute | solution.py:608
  93.4 3.3 %collective-permute-done.36.rest_3_ = f32[2,4,16,128]{3,2,1,0:T(8,128)S(1)} collective-permute-done((f32[2,4,16,128]{3,2,1,0:T(8,128)S(1)}, f32[2,4,16,128]{3,2,1,0:T(8,128)S(1)}, u32[]{:S(2)}, u32[]{:S(2)}) %collective-permute-start.36) | collective-permute-done | bytes 65568 | tf_op jit(solution)/shard_map/ppermute | solution.py:608
  96.7 2.5 %third.1 = f32[32,2,128]{2,1,0:T(2,128)S(1)} custom-call(s32[288]{0:T(512)S(1)} %positions.1.pos.links, f32[128,16,128]{2,1,0:T(8,128)S(1)} %get-tuple-element.41.basis, f32[16,128]{1,0:T(8,128)S(1)} %get-tuple-element.42.coeffs, f32[16,16,128]{2,1,0:T(8,128)S(1)} %bitcast.11, f32[16,16,128]{2,1,0:T(8,128)S(1)} %collective-permute-done.rest_1_, ...), custom_call_target="tpu_custom_call" | custom-call | tf_op jit(solution)/shard_map/third/pallas_call | solution.py:615
  99.2 11.3 %all_to_all.10.info = f32[32,2,128]{2,1,0:T(2,128)S(1)} all-to-all(f32[32,2,128]{2,1,0:T(2,128)S(1)} %third.1), channel_id=1, replica_groups=mesh['z'=4,'core'=2,'sub'=4] {'z','core','sub'}, dimensions={0} | all-to-all | bytes 65536 | tf_op jit(solution)/shard_map/all_to_all | solution.py:626
  (65 shorter events, 14.3 us)
Async XLA Ops:
  1.4 35.5 %collective-permute-start.9 = (f32[2,64,1152]{2,1,0:T(8,128)S(1)}, f32[2,64,1152]{2,1,0:T(8,128)S(1)}, u32[]{:S(2)}, u32[]{:S(2)}) collective-permute-start(f32[2,64,1152]{2,1,0:T(8,128)S(1)} %get-tuple-element.34.rest_8_), channel_id=1, source_target_pairs={{0,2},{1,3},{2,0},{3,1},{4,6},{5,7},{6,4},{7,5},{8,10},{9,11},{10,... | collective-permute-start | bytes 1769480 | tf_op jit(solution)/shard_map/ppermute | solution.py:501
  4.5 32.5 %collective-permute-start.8 = (f32[2,64,1152]{2,1,0:T(8,128)S(1)}, f32[2,64,1152]{2,1,0:T(8,128)S(1)}, u32[]{:S(2)}, u32[]{:S(2)}) collective-permute-start(f32[2,64,1152]{2,1,0:T(8,128)S(1)} %get-tuple-element.35.rest_9_), channel_id=1, source_target_pairs={{0,1},{1,0},{2,3},{3,2},{4,5},{5,4},{6,7},{7,6},{8,9},{9,8},{10,11... | collective-permute-start | bytes 1769480 | tf_op jit(solution)/shard_map/ppermute | solution.py:500
  7.7 13.0 %all-to-all-start = ((f32[4,4,16,128]{3,2,1,0:T(8,128)}), f32[4,4,16,128]{3,2,1,0:T(8,128)S(1)}, u32[]{:S(2)}, u32[]{:S(2)}) async-start(f32[4,4,16,128]{3,2,1,0:T(8,128)} %get-tuple-element.33), calls=%async_computation | async-start | bytes 262144 | tf_op jit(solution)/shard_map/all_to_all | solution.py:522
  21.3 8.0 %collective-permute-start.1 = (f32[16,16,128]{2,1,0:T(8,128)S(1)}, f32[16,16,128]{2,1,0:T(8,128)S(1)}, u32[]{:S(2)}, u32[]{:S(2)}) collective-permute-start(f32[16,16,128]{2,1,0:T(8,128)S(1)} %bitcast.6), channel_id=1, source_target_pairs={{0,16},{8,24},{16,0},{24,8},{1,17},{9,25},{17,1},{25,9},{2,18},{10... | collective-permute-start | bytes 393224 | tf_op jit(solution)/shard_map/ppermute | solution.py:531
  23.9 6.0 %collective-permute-start = (f32[16,16,128]{2,1,0:T(8,128)S(1)}, f32[16,16,128]{2,1,0:T(8,128)S(1)}, u32[]{:S(2)}, u32[]{:S(2)}) collective-permute-start(f32[16,16,128]{2,1,0:T(8,128)S(1)} %bitcast.7), channel_id=1, source_target_pairs={{0,8},{8,0},{16,24},{24,16},{1,9},{9,1},{17,25},{25,17},{2,10},{10... | collective-permute-start | bytes 393224 | tf_op jit(solution)/shard_map/ppermute | solution.py:531
  25.5 6.5 %collective-permute-start.3 = (f32[16,16,128]{2,1,0:T(8,128)S(1)}, f32[16,16,128]{2,1,0:T(8,128)S(1)}, u32[]{:S(2)}, u32[]{:S(2)}) collective-permute-start(f32[16,16,128]{2,1,0:T(8,128)S(1)} %bitcast.8), channel_id=1, source_target_pairs={{0,4},{4,0},{1,5},{5,1},{2,6},{6,2},{3,7},{7,3},{8,12},{12,8},{9,1... | collective-permute-start | bytes 393224 | tf_op jit(solution)/shard_map/ppermute | solution.py:541
  29.2 16.0 %collective-permute-start.10 = (f32[2,64,1152]{2,1,0:T(8,128)S(1)}, f32[2,64,1152]{2,1,0:T(8,128)}, u32[]{:S(2)}, u32[]{:S(2)}) collective-permute-start(f32[2,64,1152]{2,1,0:T(8,128)S(1)} %get-tuple-element.35.rest_9_), channel_id=1, source_target_pairs={{0,2},{1,3},{2,0},{3,1},{4,6},{5,7},{6,4},{7,5},{8,10},{9,11},{10,... | collective-permute-start | bytes 1769480 | tf_op jit(solution)/shard_map/ppermute | solution.py:503
  29.9 15.7 %collective-permute-start.7 = (f32[2,64,1152]{2,1,0:T(8,128)S(1)}, f32[2,64,1152]{2,1,0:T(8,128)}, u32[]{:S(2)}, u32[]{:S(2)}) collective-permute-start(f32[2,64,1152]{2,1,0:T(8,128)S(1)} %get-tuple-element.34.rest_8_), channel_id=1, source_target_pairs={{0,1},{1,0},{2,3},{3,2},{4,5},{5,4},{6,7},{7,6},{8,9},{9,8},{10,11... | collective-permute-start | bytes 1769480 | tf_op jit(solution)/shard_map/ppermute | solution.py:502
  31.9 5.0 %collective-permute-start.2 = (f32[16,16,128]{2,1,0:T(8,128)S(1)}, f32[16,16,128]{2,1,0:T(8,128)S(1)}, u32[]{:S(2)}, u32[]{:S(2)}) collective-permute-start(f32[16,16,128]{2,1,0:T(8,128)S(1)} %collective-permute-done.1.rest_2_), channel_id=1, source_target_pairs={{0,8},{8,0},{16,24},{24,16},{1,9},{9,1},{17,25},{25,17},{2,10},{10... | collective-permute-start | bytes 393224 | tf_op jit(solution)/shard_map/ppermute | solution.py:531
  36.9 24.0 %collective-permute-start.18 = (f32[2,64,1152]{2,1,0:T(8,128)S(1)}, f32[2,64,1152]{2,1,0:T(8,128)}, u32[]{:S(2)}, u32[]{:S(2)}) collective-permute-start(f32[2,64,1152]{2,1,0:T(8,128)S(1)} %collective-permute-done.9.rest_12_), channel_id=1, source_target_pairs={{0,1},{1,0},{2,3},{3,2},{4,5},{5,4},{6,7},{7,6},{8,9},{9,8},{10,11... | collective-permute-start | bytes 1769480 | tf_op jit(solution)/shard_map/ppermute | solution.py:545
  37.0 24.5 %collective-permute-start.19 = (f32[2,64,1152]{2,1,0:T(8,128)S(1)}, f32[2,64,1152]{2,1,0:T(8,128)}, u32[]{:S(2)}, u32[]{:S(2)}) collective-permute-start(f32[2,64,1152]{2,1,0:T(8,128)S(1)} %collective-permute-done.8.rest_11_), channel_id=1, source_target_pairs={{0,2},{1,3},{2,0},{3,1},{4,6},{5,7},{6,4},{7,5},{8,10},{9,11},{10,... | collective-permute-start | bytes 1769480 | tf_op jit(solution)/shard_map/ppermute | solution.py:546
  39.6 5.6 %collective-permute-start.6 = (f32[16,16,128]{2,1,0:T(8,128)S(1)}, f32[16,16,128]{2,1,0:T(8,128)S(1)}, u32[]{:S(2)}, u32[]{:S(2)}) collective-permute-start(f32[16,16,128]{2,1,0:T(8,128)S(1)} %collective-permute-done.2.rest_3_), channel_id=1, source_target_pairs={{0,4},{4,0},{1,5},{5,1},{2,6},{6,2},{3,7},{7,3},{8,12},{12,8},{9,1... | collective-permute-start | bytes 393224 | tf_op jit(solution)/shard_map/ppermute | solution.py:541
  48.6 7.7 %collective-permute-start.12 = (f32[12,16,128]{2,1,0:T(8,128)S(1)}, f32[12,16,128]{2,1,0:T(8,128)S(1)}, u32[]{:S(2)}, u32[]{:S(2)}) collective-permute-start(f32[12,16,128]{2,1,0:T(8,128)S(1)} %get-tuple-element.36.rest_8_), channel_id=1, source_target_pairs={{0,16},{8,24},{16,0},{24,8},{1,17},{9,25},{17,1},{25,9},{2,18},{10... | collective-permute-start | bytes 294920 | tf_op jit(solution)/shard_map/ppermute | solution.py:531
  50.2 6.4 %collective-permute-start.11 = (f32[12,16,128]{2,1,0:T(8,128)S(1)}, f32[12,16,128]{2,1,0:T(8,128)S(1)}, u32[]{:S(2)}, u32[]{:S(2)}) collective-permute-start(f32[12,16,128]{2,1,0:T(8,128)S(1)} %get-tuple-element.36.rest_8_), channel_id=1, source_target_pairs={{0,8},{8,0},{16,24},{24,16},{1,9},{9,1},{17,25},{25,17},{2,10},{10... | collective-permute-start | bytes 294920 | tf_op jit(solution)/shard_map/ppermute | solution.py:531
  56.3 4.6 %collective-permute-start.13 = (f32[12,16,128]{2,1,0:T(8,128)S(1)}, f32[12,16,128]{2,1,0:T(8,128)S(1)}, u32[]{:S(2)}, u32[]{:S(2)}) collective-permute-start(f32[12,16,128]{2,1,0:T(8,128)S(1)} %collective-permute-done.12.rest_10_), channel_id=1, source_target_pairs={{0,8},{8,0},{16,24},{24,16},{1,9},{9,1},{17,25},{25,17},{2,10},{10... | collective-permute-start | bytes 294920 | tf_op jit(solution)/shard_map/ppermute | solution.py:531
  56.6 8.8 %collective-permute-start.14 = (f32[12,16,128]{2,1,0:T(8,128)S(1)}, f32[12,16,128]{2,1,0:T(8,128)S(1)}, u32[]{:S(2)}, u32[]{:S(2)}) collective-permute-start(f32[12,16,128]{2,1,0:T(8,128)S(1)} %get-tuple-element.36.rest_8_), channel_id=1, source_target_pairs={{0,4},{4,0},{1,5},{5,1},{2,6},{6,2},{3,7},{7,3},{8,12},{12,8},{9,1... | collective-permute-start | bytes 294920 | tf_op jit(solution)/shard_map/ppermute | solution.py:541
  56.6 12.6 %collective-permute-start.15 = (f32[12,16,128]{2,1,0:T(8,128)S(1)}, f32[12,16,128]{2,1,0:T(8,128)S(1)}, u32[]{:S(2)}, u32[]{:S(2)}) collective-permute-start(f32[12,16,128]{2,1,0:T(8,128)S(1)} %collective-permute-done.11.rest_9_), channel_id=1, source_target_pairs={{0,4},{4,0},{1,5},{5,1},{2,6},{6,2},{3,7},{7,3},{8,12},{12,8},{9,1... | collective-permute-start | bytes 294920 | tf_op jit(solution)/shard_map/ppermute | solution.py:541
  60.9 8.3 %collective-permute-start.16 = (f32[12,16,128]{2,1,0:T(8,128)S(1)}, f32[12,16,128]{2,1,0:T(8,128)S(1)}, u32[]{:S(2)}, u32[]{:S(2)}) collective-permute-start(f32[12,16,128]{2,1,0:T(8,128)S(1)} %collective-permute-done.12.rest_10_), channel_id=1, source_target_pairs={{0,4},{4,0},{1,5},{5,1},{2,6},{6,2},{3,7},{7,3},{8,12},{12,8},{9,1... | collective-permute-start | bytes 294920 | tf_op jit(solution)/shard_map/ppermute | solution.py:541
  60.9 11.8 %collective-permute-start.17 = (f32[12,16,128]{2,1,0:T(8,128)S(1)}, f32[12,16,128]{2,1,0:T(8,128)S(1)}, u32[]{:S(2)}, u32[]{:S(2)}) collective-permute-start(f32[12,16,128]{2,1,0:T(8,128)S(1)} %collective-permute-done.13.rest_11_), channel_id=1, source_target_pairs={{0,4},{4,0},{1,5},{5,1},{2,6},{6,2},{3,7},{7,3},{8,12},{12,8},{9,1... | collective-permute-start | bytes 294920 | tf_op jit(solution)/shard_map/ppermute | solution.py:541
  63.6 5.2 %collective-permute-start.21 = (f32[4,16,128]{2,1,0:T(8,128)S(1)}, f32[4,16,128]{2,1,0:T(8,128)S(1)}, u32[]{:S(2)}, u32[]{:S(2)}) collective-permute-start(f32[4,16,128]{2,1,0:T(8,128)S(1)} %get-tuple-element.38.rest_16_), channel_id=1, source_target_pairs={{0,16},{8,24},{16,0},{24,8},{1,17},{9,25},{17,1},{25,9},{2,18},{10... | collective-permute-start | bytes 98312 | tf_op jit(solution)/shard_map/ppermute | solution.py:531
  65.4 4.3 %collective-permute-start.20 = (f32[4,16,128]{2,1,0:T(8,128)S(1)}, f32[4,16,128]{2,1,0:T(8,128)S(1)}, u32[]{:S(2)}, u32[]{:S(2)}) collective-permute-start(f32[4,16,128]{2,1,0:T(8,128)S(1)} %get-tuple-element.38.rest_16_), channel_id=1, source_target_pairs={{0,8},{8,0},{16,24},{24,16},{1,9},{9,1},{17,25},{25,17},{2,10},{10... | collective-permute-start | bytes 98312 | tf_op jit(solution)/shard_map/ppermute | solution.py:531
  68.8 3.9 %collective-permute-start.22 = (f32[4,16,128]{2,1,0:T(8,128)S(1)}, f32[4,16,128]{2,1,0:T(8,128)S(1)}, u32[]{:S(2)}, u32[]{:S(2)}) collective-permute-start(f32[4,16,128]{2,1,0:T(8,128)S(1)} %collective-permute-done.21.rest_18_), channel_id=1, source_target_pairs={{0,8},{8,0},{16,24},{24,16},{1,9},{9,1},{17,25},{25,17},{2,10},{10... | collective-permute-start | bytes 98312 | tf_op jit(solution)/shard_map/ppermute | solution.py:531
  76.5 9.4 %collective-permute-start.28 = (f32[16,16,128]{2,1,0:T(8,128)S(1)}, f32[16,16,128]{2,1,0:T(8,128)S(1)}, u32[]{:S(2)}, u32[]{:S(2)}) collective-permute-start(f32[16,16,128]{2,1,0:T(8,128)S(1)} %get-tuple-element.48.rest_8_), channel_id=1, source_target_pairs={{0,16},{8,24},{16,0},{24,8},{1,17},{9,25},{17,1},{25,9},{2,18},{10... | collective-permute-start | bytes 393224 | tf_op jit(solution)/shard_map/ppermute | solution.py:531
  77.9 12.3 %collective-permute-start.27 = (f32[16,16,128]{2,1,0:T(8,128)S(1)}, f32[16,16,128]{2,1,0:T(8,128)S(1)}, u32[]{:S(2)}, u32[]{:S(2)}) collective-permute-start(f32[16,16,128]{2,1,0:T(8,128)S(1)} %get-tuple-element.48.rest_8_), channel_id=1, source_target_pairs={{0,8},{8,0},{16,24},{24,16},{1,9},{9,1},{17,25},{25,17},{2,10},{10... | collective-permute-start | bytes 393224 | tf_op jit(solution)/shard_map/ppermute | solution.py:531
  85.9 5.4 %collective-permute-start.29 = (f32[16,16,128]{2,1,0:T(8,128)S(1)}, f32[16,16,128]{2,1,0:T(8,128)S(1)}, u32[]{:S(2)}, u32[]{:S(2)}) collective-permute-start(f32[16,16,128]{2,1,0:T(8,128)S(1)} %collective-permute-done.28.rest_10_), channel_id=1, source_target_pairs={{0,8},{8,0},{16,24},{24,16},{1,9},{9,1},{17,25},{25,17},{2,10},{10... | collective-permute-start | bytes 393224 | tf_op jit(solution)/shard_map/ppermute | solution.py:531
  85.9 4.3 %collective-permute-start.34 = (f32[2,4,16,128]{3,2,1,0:T(8,128)S(1)}, f32[2,4,16,128]{3,2,1,0:T(8,128)S(1)}, u32[]{:S(2)}, u32[]{:S(2)}) collective-permute-start(f32[2,4,16,128]{3,2,1,0:T(8,128)S(1)} %get-tuple-element.45), channel_id=1, source_target_pairs={{0,1},{1,0},{2,3},{3,2},{4,5},{5,4},{6,7},{7,6},{8,9},{9,8},{10,11... | collective-permute-start | bytes 196616 | tf_op jit(solution)/shard_map/ppermute | solution.py:608
  87.0 4.3 %collective-permute-start.35 = (f32[2,4,16,128]{3,2,1,0:T(8,128)S(1)}, f32[2,4,16,128]{3,2,1,0:T(8,128)S(1)}, u32[]{:S(2)}, u32[]{:S(2)}) collective-permute-start(f32[2,4,16,128]{3,2,1,0:T(8,128)S(1)} %get-tuple-element.46), channel_id=1, source_target_pairs={{0,2},{1,3},{2,0},{3,1},{4,6},{5,7},{6,4},{7,5},{8,10},{9,11},{10,... | collective-permute-start | bytes 196616 | tf_op jit(solution)/shard_map/ppermute | solution.py:608
  88.6 8.1 %collective-permute-start.30 = (f32[16,16,128]{2,1,0:T(8,128)S(1)}, f32[16,16,128]{2,1,0:T(8,128)S(1)}, u32[]{:S(2)}, u32[]{:S(2)}) collective-permute-start(f32[16,16,128]{2,1,0:T(8,128)S(1)} %get-tuple-element.48.rest_8_), channel_id=1, source_target_pairs={{0,4},{4,0},{1,5},{5,1},{2,6},{6,2},{3,7},{7,3},{8,12},{12,8},{9,1... | collective-permute-start | bytes 393224 | tf_op jit(solution)/shard_map/ppermute | solution.py:541
  90.1 6.5 %collective-permute-start.32 = (f32[16,16,128]{2,1,0:T(8,128)S(1)}, f32[16,16,128]{2,1,0:T(8,128)S(1)}, u32[]{:S(2)}, u32[]{:S(2)}) collective-permute-start(f32[16,16,128]{2,1,0:T(8,128)S(1)} %collective-permute-done.28.rest_10_), channel_id=1, source_target_pairs={{0,4},{4,0},{1,5},{5,1},{2,6},{6,2},{3,7},{7,3},{8,12},{12,8},{9,1... | collective-permute-start | bytes 393224 | tf_op jit(solution)/shard_map/ppermute | solution.py:541
  90.2 6.5 %collective-permute-start.31 = (f32[16,16,128]{2,1,0:T(8,128)S(1)}, f32[16,16,128]{2,1,0:T(8,128)S(1)}, u32[]{:S(2)}, u32[]{:S(2)}) collective-permute-start(f32[16,16,128]{2,1,0:T(8,128)S(1)} %collective-permute-done.27.rest_9_), channel_id=1, source_target_pairs={{0,4},{4,0},{1,5},{5,1},{2,6},{6,2},{3,7},{7,3},{8,12},{12,8},{9,1... | collective-permute-start | bytes 393224 | tf_op jit(solution)/shard_map/ppermute | solution.py:541
  91.3 5.4 %collective-permute-start.33 = (f32[16,16,128]{2,1,0:T(8,128)S(1)}, f32[16,16,128]{2,1,0:T(8,128)S(1)}, u32[]{:S(2)}, u32[]{:S(2)}) collective-permute-start(f32[16,16,128]{2,1,0:T(8,128)S(1)} %collective-permute-done.29.rest_11_), channel_id=1, source_target_pairs={{0,4},{4,0},{1,5},{5,1},{2,6},{6,2},{3,7},{7,3},{8,12},{12,8},{9,1... | collective-permute-start | bytes 393224 | tf_op jit(solution)/shard_map/ppermute | solution.py:541
  91.3 5.4 %collective-permute-start.36 = (f32[2,4,16,128]{3,2,1,0:T(8,128)S(1)}, f32[2,4,16,128]{3,2,1,0:T(8,128)S(1)}, u32[]{:S(2)}, u32[]{:S(2)}) collective-permute-start(f32[2,4,16,128]{3,2,1,0:T(8,128)S(1)} %get-tuple-element.47), channel_id=1, source_target_pairs={{0,3},{1,2},{2,1},{3,0},{4,7},{5,6},{6,5},{7,4},{8,11},{9,10},{10,... | collective-permute-start | bytes 196616 | tf_op jit(solution)/shard_map/ppermute | solution.py:608
  (9 other events, 96.4 us)
